TPU v7x, 32 devices: a whole 2x2x4 slice. The times are simulated.
32 devices in a mesh: dp: 8 (over y, x, core), mp: 4 (over z).
Axes of the slice: x: 2, y: 2, z: 4, core: 2. Of those that a mesh axis runs over, the one named last changes fastest.
Arguments:
- block_input: bfloat16 [16384, 768], P(('dp', 'mp')), may hold values from -6 to 6
- clusters: int32 [16384, 12], P(('dp', 'mp')), may hold values from 0 to 99
- ln1_gain: float32 [768], replicated, may hold values from 0.5 to 1.5
- ln1_bias: float32 [768], replicated, may hold values from -1.75 to 1.75
- w_query: bfloat16 [768, 768], replicated, may hold values from -0.875 to 0.875
- query_bias: float32 [768], replicated, may hold values from -8 to 8
- w_keyval: bfloat16 [768, 1536], replicated, may hold values from -0.21875 to 0.21875
- value_bias: float32 [768], replicated, may hold values from -0.625 to 0.625
- w_out: bfloat16 [768, 768], replicated, may hold values from -1.75 to 1.75
- out_bias: float32 [768], replicated, may hold values from -1.75 to 1.75
- ln2_gain: float32 [768], replicated, may hold values from 0.5 to 1.5
- ln2_bias: float32 [768], replicated, may hold values from -1.75 to 1.75
- w_up: bfloat16 [768, 3072], P(None, 'mp'), may hold values from -0.21875 to 0.21875
- up_bias: bfloat16 [3072], P('mp'), may hold values from -1.75 to 1.75
- w_down: bfloat16 [3072, 768], P('mp'), may hold values from -0.109375 to 0.109375
- down_bias: float32 [768], replicated, may hold values from -1.75 to 1.75
- cotangent: bfloat16 [16384, 768], P(('dp', 'mp')), may hold values from -6 to 6
Outputs:
- block_output: bfloat16 [16384, 768], P(('dp', 'mp'))
- input_grad: float32 [16384, 768], P(('dp', 'mp'))
- ln1_gain_grad: float32 [768], P(('dp', 'mp'))
- ln1_bias_grad: float32 [768], P(('dp', 'mp'))
- w_query_grad: float32 [768, 768], P(('dp', 'mp'))
- query_bias_grad: float32 [768], P(('dp', 'mp'))
- w_keyval_grad: float32 [768, 1536], P(('dp', 'mp'))
- value_bias_grad: float32 [768], P(('dp', 'mp'))
- w_out_grad: float32 [768, 768], P(('dp', 'mp'))
- out_bias_grad: float32 [768], P(('dp', 'mp'))
- ln2_gain_grad: float32 [768], P(('dp', 'mp'))
- ln2_bias_grad: float32 [768], P(('dp', 'mp'))
- w_up_grad: float32 [768, 3072], P('dp', 'mp')
- up_bias_grad: float32 [3072], P(('dp', 'mp'))
- w_down_grad: float32 [3072, 768], P('mp', 'dp')
- down_bias_grad: float32 [768], P(('dp', 'mp'))
All inputs are finite; a program needn't handle non-finite values.
Results may differ from a plain program's by a relative error of at most 0.03.
Values may be sent and summed in bfloat16 or wider, within the bound.
A program may use at most 128 MiB of HBM per device.

v0:
```python
import math

import jax
import jax.numpy as jnp
from jax import lax
from jax.sharding import PartitionSpec as P

FF = 3072
CLUSTERS = 100


epsilon = 1e-05


def norm_forward(inputs, gain_vec, offset):
    center = inputs - jnp.mean(inputs, axis=-1, keepdims=True)
    factor = lax.rsqrt(jnp.mean(center * center, axis=-1, keepdims=True) + epsilon)
    standard = center * factor
    return (standard * gain_vec + offset, standard, factor)


def norm_backward(upstream, standard, factor, gain_vec):
    scaled = upstream * gain_vec
    centred = scaled - jnp.mean(scaled, axis=-1, keepdims=True)
    centred = centred - standard * jnp.mean(scaled * standard, axis=-1, keepdims=True)
    return (factor * centred, jnp.sum(upstream * standard, axis=0), jnp.sum(upstream, axis=0))


def gelu_parts(before):
    cumulative = 0.5 * (1.0 + jax.scipy.special.erf(before / math.sqrt(2.0)))
    density = jnp.exp(-0.5 * before * before) / math.sqrt(2.0 * math.pi)
    return (before * cumulative, cumulative + before * density)


def on_device(
    block_input,
    clusters,
    ln1_gain,
    ln1_bias,
    w_query,
    query_bias,
    w_keyval,
    value_bias,
    w_out,
    out_bias,
    ln2_gain,
    ln2_bias,
    w_up,
    up_bias,
    w_down,
    down_bias,
    cotangent,
):
    group_size = lax.axis_size("mp")
    tok_rows = block_input.shape[0]
    model_width = block_input.shape[1]
    head_count = clusters.shape[1]
    head_dim = model_width // head_count
    local_heads = head_count // group_size
    score_scale = float(head_dim) ** (-0.5)
    inputs = block_input.astype(jnp.float32)
    normed_one, standard_one, factor_one = norm_forward(inputs, ln1_gain, ln1_bias)
    first = normed_one.astype(jnp.bfloat16)
    queries = (jnp.dot(first, w_query, preferred_element_type=jnp.float32) + query_bias).astype(
        jnp.bfloat16
    )
    keyval = jnp.dot(first, w_keyval, preferred_element_type=jnp.float32)
    keyval = (keyval + jnp.concatenate([jnp.zeros_like(value_bias), value_bias])).astype(
        jnp.bfloat16
    )
    member_float = (
        clusters.T[:, None, :] == jnp.arange(CLUSTERS, dtype=jnp.int32)[None, :, None]
    ).astype(jnp.float32)
    membership = member_float.astype(jnp.bfloat16)
    query_sums = jnp.einsum(
        "hct,thd->hcd",
        membership,
        queries.reshape(tok_rows, head_count, head_dim),
        preferred_element_type=jnp.float32,
    )
    cluster_sizes = jnp.sum(member_float, axis=2)
    query_sums, cluster_sizes = (
        lax.psum_scatter(
            query_sums.astype(jnp.bfloat16), "mp", scatter_dimension=0, tiled=True
        ).astype(jnp.float32),
        lax.psum_scatter(
            cluster_sizes.astype(jnp.bfloat16), "mp", scatter_dimension=0, tiled=True
        ).astype(jnp.float32),
    )
    divisor = jnp.maximum(cluster_sizes, 1.0)
    centroids = (query_sums / divisor[:, :, None]).astype(jnp.bfloat16)
    packed = keyval.reshape(tok_rows, 2, group_size, local_heads * head_dim)
    arrived = lax.all_to_all(packed, "mp", split_axis=2, concat_axis=0, tiled=True)
    length = arrived.shape[0]
    key_rows = arrived[:, 0, 0].reshape(length, local_heads, head_dim)
    value_rows = arrived[:, 1, 0].reshape(length, local_heads, head_dim)
    scores = score_scale * jnp.einsum(
        "hcd,jhd->hcj", centroids, key_rows, preferred_element_type=jnp.float32
    )
    score_peak = jnp.max(scores, axis=-1, keepdims=True)
    exponent = jnp.exp(scores - score_peak)
    denominator = jnp.sum(exponent, axis=-1, keepdims=True)
    probs = exponent / denominator
    logsum = score_peak + jnp.log(denominator)
    summary = jnp.einsum(
        "hcj,jhd->hcd", probs.astype(jnp.bfloat16), value_rows, preferred_element_type=jnp.float32
    ).astype(jnp.bfloat16)
    everyone = lax.all_gather(summary, "mp", axis=0, tiled=True)
    spread = (
        jnp.einsum("hct,hcd->thd", membership, everyone, preferred_element_type=jnp.float32)
        .astype(jnp.bfloat16)
        .reshape(tok_rows, model_width)
    )
    attended = jnp.dot(spread, w_out, preferred_element_type=jnp.float32) + out_bias
    middle = inputs + attended
    normed_two, standard_two, factor_two = norm_forward(middle, ln2_gain, ln2_bias)
    second = normed_two.astype(jnp.bfloat16)
    gathered = lax.all_gather(second, "mp", axis=0, tiled=True)
    before = jnp.dot(gathered, w_up, preferred_element_type=jnp.float32) + up_bias.astype(
        jnp.float32
    )
    activated, gelu_slope = gelu_parts(before)
    hidden = activated.astype(jnp.bfloat16)
    result = lax.psum_scatter(
        jnp.dot(hidden, w_down, preferred_element_type=jnp.float32).astype(jnp.bfloat16),
        "mp",
        scatter_dimension=0,
        tiled=True,
    ).astype(jnp.float32)
    block_output = (middle + result + down_bias).astype(jnp.bfloat16)
    upstream = cotangent.astype(jnp.float32)
    grad_down_bias = jnp.sum(upstream, axis=0)
    grad_rows = lax.all_gather(cotangent, "mp", axis=0, tiled=True)
    grad_down = jnp.einsum("tf,td->fd", hidden, grad_rows, preferred_element_type=jnp.float32)
    grad_hidden = jnp.einsum("td,fd->tf", grad_rows, w_down, preferred_element_type=jnp.float32)
    grad_before = (grad_hidden * gelu_slope).astype(jnp.bfloat16)
    bias_part = jnp.sum(grad_before.astype(jnp.float32), axis=0)
    grad_up = jnp.einsum("td,tf->df", gathered, grad_before, preferred_element_type=jnp.float32)
    grad_second = lax.psum_scatter(
        jnp.einsum("tf,df->td", grad_before, w_up, preferred_element_type=jnp.float32).astype(
            jnp.bfloat16
        ),
        "mp",
        scatter_dimension=0,
        tiled=True,
    ).astype(jnp.float32)
    grad_up_bias = lax.dynamic_update_slice(
        jnp.zeros((FF,), jnp.float32), bias_part, (lax.axis_index("mp") * bias_part.shape[0],)
    )
    middle_norm_grad, grad_gain_two, grad_shift_two = norm_backward(
        grad_second, standard_two, factor_two, ln2_gain
    )
    grad_middle = upstream + middle_norm_grad
    attn_grad = grad_middle.astype(jnp.bfloat16)
    grad_out_bias = jnp.sum(attn_grad.astype(jnp.float32), axis=0)
    grad_w_out = jnp.einsum("td,te->de", spread, attn_grad, preferred_element_type=jnp.float32)
    grad_spread = jnp.einsum(
        "te,de->td", attn_grad, w_out, preferred_element_type=jnp.float32
    ).astype(jnp.bfloat16)
    summary_grad = jnp.einsum(
        "hct,thd->hcd",
        membership,
        grad_spread.reshape(tok_rows, head_count, head_dim),
        preferred_element_type=jnp.float32,
    )
    summary_grad = lax.psum_scatter(
        summary_grad.astype(jnp.bfloat16), "mp", scatter_dimension=0, tiled=True
    )
    scores_again = score_scale * jnp.einsum(
        "hcd,jhd->hcj", centroids, key_rows, preferred_element_type=jnp.float32
    )
    probs_again = jnp.exp(scores_again - logsum)
    grad_values = jnp.einsum(
        "hcj,hcd->jhd",
        probs_again.astype(jnp.bfloat16),
        summary_grad,
        preferred_element_type=jnp.float32,
    )
    grad_probs = jnp.einsum(
        "hcd,jhd->hcj", summary_grad, value_rows, preferred_element_type=jnp.float32
    )
    grad_scores = probs_again * (
        grad_probs - jnp.sum(probs_again * grad_probs, axis=-1, keepdims=True)
    )
    grad_scores = grad_scores.astype(jnp.bfloat16)
    grad_centroids = (
        score_scale
        * jnp.einsum("hcj,jhd->hcd", grad_scores, key_rows, preferred_element_type=jnp.float32)
    ).astype(jnp.bfloat16)
    grad_keys = score_scale * jnp.einsum(
        "hcj,hcd->jhd", grad_scores, centroids, preferred_element_type=jnp.float32
    )
    grad_kv = jnp.stack(
        [
            grad_keys.reshape(length, local_heads * head_dim),
            grad_values.reshape(length, local_heads * head_dim),
        ],
        axis=1,
    )
    grad_kv = grad_kv.astype(jnp.bfloat16)[:, :, None, :]
    returned = lax.all_to_all(grad_kv, "mp", split_axis=0, concat_axis=2, tiled=True)
    grad_keyval = returned.reshape(tok_rows, 2 * model_width)
    per_member = grad_centroids.astype(jnp.float32) / divisor[:, :, None]
    all_member = lax.all_gather(per_member.astype(jnp.bfloat16), "mp", axis=0, tiled=True).astype(
        per_member.dtype
    )
    grad_queries = jnp.einsum(
        "hct,hcd->thd", member_float, all_member, precision=lax.Precision.HIGHEST
    )
    grad_queries = grad_queries.reshape(tok_rows, model_width).astype(jnp.bfloat16)
    grad_query_bias = jnp.sum(grad_queries.astype(jnp.float32), axis=0)
    grad_value_bias = jnp.sum(grad_keyval[:, model_width:].astype(jnp.float32), axis=0)
    grad_w_query = jnp.einsum("td,te->de", first, grad_queries, preferred_element_type=jnp.float32)
    grad_w_keyval = jnp.einsum("td,te->de", first, grad_keyval, preferred_element_type=jnp.float32)
    grad_first = jnp.einsum("te,de->td", grad_queries, w_query, preferred_element_type=jnp.float32)
    grad_first = grad_first + jnp.einsum(
        "te,de->td", grad_keyval, w_keyval, preferred_element_type=jnp.float32
    )
    input_norm_grad, grad_gain_one, grad_shift_one = norm_backward(
        grad_first, standard_one, factor_one, ln1_gain
    )
    input_grad = grad_middle + input_norm_grad
    shared = (
        lax.psum_scatter(grad_gain_one, ("dp", "mp"), scatter_dimension=0, tiled=True),
        lax.psum_scatter(grad_shift_one, ("dp", "mp"), scatter_dimension=0, tiled=True),
        lax.psum_scatter(grad_w_query, ("dp", "mp"), scatter_dimension=0, tiled=True),
        lax.psum_scatter(grad_query_bias, ("dp", "mp"), scatter_dimension=0, tiled=True),
        lax.psum_scatter(grad_w_keyval, ("dp", "mp"), scatter_dimension=0, tiled=True),
        lax.psum_scatter(grad_value_bias, ("dp", "mp"), scatter_dimension=0, tiled=True),
        lax.psum_scatter(grad_w_out, ("dp", "mp"), scatter_dimension=0, tiled=True),
        lax.psum_scatter(grad_out_bias, ("dp", "mp"), scatter_dimension=0, tiled=True),
        lax.psum_scatter(grad_gain_two, ("dp", "mp"), scatter_dimension=0, tiled=True),
        lax.psum_scatter(grad_shift_two, ("dp", "mp"), scatter_dimension=0, tiled=True),
        lax.psum_scatter(grad_up_bias, ("dp", "mp"), scatter_dimension=0, tiled=True),
        lax.psum_scatter(grad_down_bias, ("dp", "mp"), scatter_dimension=0, tiled=True),
    )
    up_share, down_share = (
        lax.psum_scatter(grad_up, "dp", scatter_dimension=0, tiled=True),
        lax.psum_scatter(grad_down, "dp", scatter_dimension=1, tiled=True),
    )
    return (
        block_output,
        input_grad,
        shared[0],
        shared[1],
        shared[2],
        shared[3],
        shared[4],
        shared[5],
        shared[6],
        shared[7],
        shared[8],
        shared[9],
        up_share,
        shared[10],
        down_share,
        shared[11],
    )


def solution(mesh):
    placed = (
        P(("dp", "mp"), None),
        P(("dp", "mp"), None),
        P(),
        P(),
        P(),
        P(),
        P(),
        P(),
        P(),
        P(),
        P(),
        P(),
        P(None, "mp"),
        P("mp"),
        P("mp", None),
        P(),
        P(("dp", "mp"), None),
    )
    return jax.shard_map(
        on_device,
        mesh=mesh,
        in_specs=placed,
        out_specs=(
            P(("dp", "mp"), None),
            P(("dp", "mp"), None),
            P(("dp", "mp")),
            P(("dp", "mp")),
            P(("dp", "mp"), None),
            P(("dp", "mp")),
            P(("dp", "mp"), None),
            P(("dp", "mp")),
            P(("dp", "mp"), None),
            P(("dp", "mp")),
            P(("dp", "mp")),
            P(("dp", "mp")),
            P("dp", "mp"),
            P(("dp", "mp")),
            P("mp", "dp"),
            P(("dp", "mp")),
        ),
        check_vma=False,
    )
```

profile of v0, /device:TPU:0, one launch (start us, length us, event | category | flops | bytes accessed | tf_op | source)
XLA Modules:
  0.0 804.2 jit_solution(6892211009984966623)
XLA Ops:
  18.2 6.5 all-to-all-start
  24.7 3.1 add_convert_fusion.2
  34.1 25.4 %all-reduce.1 = bf16[12,100]{1,0:T(8,128)(2,1)S(1)} all-reduce(bf16[12,100]{1,0:T(8,128)(2,1)S(1)} %convert_reduce_fusion.1), channel_id=3, replica_groups=mesh['dp'=8,'mp'=4] {'mp'}, use_global_device_ids=true, to_apply=%region_4.0.clone | all-reduce | flops 1200 | bytes 4800
  59.5 5.7 all-to-all-done
  72.3 15.2 %all_gather.12 = bf16[12,100,64]{1,2,0:T(8,128)(2,1)S(1)} all-gather(bf16[3,100,64]{1,2,0:T(8,128)(2,1)S(1)} %fusion.49), channel_id=1, replica_groups=mesh['dp'=8,'mp'=4] {'mp'}, dimensions={0}, use_global_device_ids=true | all-gather | bytes 192000 | tf_op jit(solution)/shard_map/all_gather | solution.py:108
  92.3 62.2 %all-gather.3.cloned.1.call-done = bf16[2048,768]{1,0:T(8,128)(2,1)} async-done(((bf16[512,768]{1,0:T(8,128)(2,1)}), bf16[2048,768]{1,0:T(8,128)(2,1)}) %all-gather.3.cloned.1.call-update) | async-done | bytes 3145744 | tf_op jit(solution)/shard_map/all_gather | solution.py:118
  154.5 6.9 multiply_convert_fusion
  161.4 56.8 %all-gather.5.cloned.1.call-done = bf16[2048,768]{1,0:T(8,128)(2,1)} async-done(((bf16[512,768]{1,0:T(8,128)(2,1)}), bf16[2048,768]{1,0:T(8,128)(2,1)}) %all-gather.5.cloned.1.call-update) | async-done | bytes 3145744 | tf_op jit(solution)/shard_map/all_gather | solution.py:133
  218.2 7.0 convert_reduce_fusion
  226.9 4.0 convolution_convert_fusion
  231.0 6.5 convolution_convert_fusion.1
  237.6 52.6 %reduce-scatter.14.cloned.1.call-done = bf16[512,768]{1,0:T(8,128)(2,1)} async-done(((bf16[2048,768]{1,0:T(8,128)(2,1)}), bf16[512,768]{1,0:T(8,128)(2,1)}) %reduce-scatter.14.cloned.1.call-update) | async-done | bytes 786448 | tf_op jit(solution)/shard_map/reduce_scatter | solution.py:139
  292.6 60.1 %reduce-scatter.12.cloned.1.call-done = bf16[512,768]{1,0:T(8,128)(2,1)} async-done(((bf16[2048,768]{1,0:T(8,128)(2,1)}), bf16[512,768]{1,0:T(8,128)(2,1)}) %reduce-scatter.12.cloned.1.call-update) | async-done | bytes 786448 | tf_op jit(solution)/shard_map/reduce_scatter | solution.py:124
  352.7 3.9 convert_reduce_fusion.5
  364.4 6.9 fusion.64
  371.4 6.9 fusion.65
  378.4 3.9 fusion.51
  383.8 2.9 multiply_reduce_fusion
  389.8 5.9 copy.51
  395.7 3.5 convolution_convert_fusion.2
  399.2 5.9 copy.52
  407.1 14.0 %all_gather.15 = bf16[12,100,64]{1,2,0:T(8,128)(2,1)S(1)} all-gather(bf16[3,100,64]{1,2,0:T(8,128)(2,1)S(1)} %fusion.50), channel_id=1, replica_groups=mesh['dp'=8,'mp'=4] {'mp'}, dimensions={0}, use_global_device_ids=true | all-gather | bytes 192000 | tf_op jit(solution)/shard_map/all_gather | solution.py:204
  425.5 6.3 pad_maximum_fusion
  431.7 48.1 %all_to_all.33 = bf16[2048,2,1,192]{3,1,2,0:T(2,128)(2,1)} all-to-all(bf16[2048,2,1,192]{3,1,2,0:T(2,128)(2,1)S(1)} %pad_maximum_fusion), channel_id=1, replica_groups=mesh['dp'=8,'mp'=4] {'mp'}, dimensions={0} | all-to-all | bytes 3145728 | tf_op jit(solution)/shard_map/all_to_all | solution.py:201
  479.8 6.5 copy.55
  489.2 3.8 fusion.54
  494.8 3.0 fusion.63
  500.3 39.8 %all-reduce.11 = (f32[768]{0:T(1024)S(1)}, f32[768]{0:T(1024)S(1)}, f32[768]{0:T(1024)S(1)}, f32[768]{0:T(1024)S(1)}, f32[768]{0:T(1024)S(1)}, /*index=5*/f32[76...) all-reduce(f32[768]{0:T(1024)S(1)} %get-tuple-element.18, ...), channel_id=7, replica_groups=mesh['dp'=8,'mp'=4] {'dp','mp'}, use_global_device_ids=true, to_apply=%region_18.0.clone | all-reduce | flops 9216 | bytes 73728
  545.3 3.6 fusion.28
  548.9 31.3 %reduce-scatter.22.cloned.1.call-done = f32[24,768]{1,0:T(8,128)} async-done(((f32[768,768]{1,0:T(8,128)}), f32[24,768]{1,0:T(8,128)}) %reduce-scatter.22.cloned.1.call-update) | async-done | bytes 73744 | tf_op jit(solution)/shard_map/reduce_scatter | solution.py:230
  580.2 104.4 %reduce-scatter.18.cloned.1.call-done = f32[24,768]{1,0:T(8,128)} async-done(((f32[768,768]{1,0:T(8,128)}), f32[24,768]{1,0:T(8,128)}) %reduce-scatter.18.cloned.1.call-update) | async-done | bytes 73744 | tf_op jit(solution)/shard_map/reduce_scatter | solution.py:226
  684.6 112.6 %reduce-scatter.20.cloned.1.call-done = f32[24,1536]{1,0:T(8,128)} async-done(((f32[768,1536]{1,0:T(8,128)}), f32[24,1536]{1,0:T(8,128)}) %reduce-scatter.20.cloned.1.call-update) | async-done | bytes 147472 | tf_op jit(solution)/shard_map/reduce_scatter | solution.py:228
  (139 shorter events, 63.8 us)
Async XLA Ops:
  7.2 3.1 copy-start
  7.2 3.1 copy-start.5
  7.2 3.0 copy-start.17
  7.2 3.0 copy-start.16
  7.2 3.0 copy-start.25
  18.2 6.5 copy-start.23
  18.2 47.0 %all-to-all-start = ((bf16[512,2,4,192]{0,3,1,2:T(8,128)(2,1)}), bf16[512,2,4,192]{0,3,1,2:T(8,128)(2,1)}, u32[]{:S(2)}, u32[]{:S(2)}) async-start(bf16[512,2,4,192]{0,3,1,2:T(8,128)(2,1)} %copy.48), calls=%async_computation.1 | async-start | bytes 3145728 | tf_op jit(solution)/shard_map/all_to_all | solution.py:93
  24.7 43.4 %reduce-scatter.10.cloned.1.call-start = ((), (), s32[]{:S(2)}) async-start(), calls=%async_computation.11 | async-start | bytes 245760 | tf_op jit(solution)/shard_map/reduce_scatter | solution.py:83
  27.7 2.3 copy-start.13
  27.7 4.8 copy-start.28
  32.5 122.0 %all-gather.3.cloned.1.call-start = ((), (), s32[]{:S(2)}) async-start(), calls=%async_computation.12 | async-start | bytes 3932160 | tf_op jit(solution)/shard_map/all_gather | solution.py:118
  69.9 2.4 copy-start.1
  71.5 16.4 %copy-start.20 = (bf16[768,768]{1,0:T(8,128)(2,1)S(1)}, bf16[768,768]{1,0:T(8,128)(2,1)}, u32[]{:S(2)}) copy-start(bf16[768,768]{1,0:T(8,128)(2,1)} %param.25) | copy-start | bytes 3538948
  71.5 16.4 %copy-start.24 = (f32[768]{0:T(1024)S(1)}, f32[768]{0:T(1024)}, u32[]{:S(2)}) copy-start(f32[768]{0:T(1024)} %param.26) | copy-start | bytes 9220
  90.1 2.2 copy-start.18
  91.3 126.9 %all-gather.5.cloned.1.call-start = ((), (), s32[]{:S(2)}) async-start(), calls=%async_computation.14 | async-start | bytes 3932160 | tf_op jit(solution)/shard_map/all_gather | solution.py:133
  92.0 198.1 %reduce-scatter.14.cloned.1.call-start = ((), (), s32[]{:S(2)}) async-start(), calls=%async_computation.15 | async-start | bytes 3932160 | tf_op jit(solution)/shard_map/reduce_scatter | solution.py:139
  218.2 8.7 %copy-start.19 = (bf16[768,768]{1,0:T(8,128)(2,1)S(1)}, bf16[768,768]{1,0:T(8,128)(2,1)}, u32[]{:S(2)}) copy-start(bf16[768,768]{1,0:T(8,128)(2,1)} %param.29) | copy-start | bytes 3538948
  230.9 121.7 %reduce-scatter.12.cloned.1.call-start = ((), (), s32[]{:S(2)}) async-start(), calls=%async_computation.13 | async-start | bytes 3932160 | tf_op jit(solution)/shard_map/reduce_scatter | solution.py:124
  237.5 115.1 %copy-start.15 = (f32[768]{0:T(1024)S(1)}, f32[768]{0:T(1024)}, u32[]{:S(2)}) copy-start(f32[768]{0:T(1024)} %param.32) | copy-start | bytes 9220
  237.5 146.3 %reduce-scatter.16.cloned.1.call-start = ((), (), s32[]{:S(2)}) async-start(), calls=%async_computation.16 | async-start | bytes 245760 | tf_op jit(solution)/shard_map/reduce_scatter | solution.py:166
  352.7 5.1 copy-start.21
  364.1 184.8 %reduce-scatter.24.cloned.1.call-start = ((), (), s32[]{:S(2)}) async-start(), calls=%async_computation.20 | async-start | bytes 2654208 | tf_op jit(solution)/shard_map/reduce_scatter | solution.py:238
  371.3 177.6 %reduce-scatter.26.cloned.1.call-start = ((), (), s32[]{:S(2)}) async-start(), calls=%async_computation.21 | async-start | bytes 2654208 | tf_op jit(solution)/shard_map/reduce_scatter | solution.py:239
  378.3 201.9 %reduce-scatter.22.cloned.1.call-start = ((), (), s32[]{:S(2)}) async-start(), calls=%async_computation.19 | async-start | bytes 2433024 | tf_op jit(solution)/shard_map/reduce_scatter | solution.py:230
  382.3 302.3 %reduce-scatter.18.cloned.1.call-start = ((), (), s32[]{:S(2)}) async-start(), calls=%async_computation.17 | async-start | bytes 2433024 | tf_op jit(solution)/shard_map/reduce_scatter | solution.py:226
  383.8 2.9 copy-start.2
  386.7 1.7 copy-start.11
  389.8 5.9 copy-start.10
  425.4 371.8 %reduce-scatter.20.cloned.1.call-start = ((), (), s32[]{:S(2)}) async-start(), calls=%async_computation.18 | async-start | bytes 4866048 | tf_op jit(solution)/shard_map/reduce_scatter | solution.py:228
  494.7 3.0 copy-start.22
  494.8 3.0 copy-start.27
  (10 other events, 12.0 us)
Sparse Core Ops, SparseCore 0:
  32.6 33.3 reduce-scatter.9
  91.4 62.9 all-gather.2
  156.0 62.0 all-gather.4
  231.1 59.0 reduce-scatter.13
  292.3 60.3 reduce-scatter.11
  364.3 19.5 reduce-scatter.15
  387.7 40.5 reduce-scatter.23
  432.2 42.3 reduce-scatter.25
  480.5 99.6 reduce-scatter.21
  585.9 98.6 reduce-scatter.17
  690.7 106.4 reduce-scatter.19
where the time goes:
time: 812 us; the launch traced here: 804 us
  waiting for transfers between devices  488 us (60%)
  blocking collectives  142 us (17%)
  matrix products  80.7 us (10%)
  local copies, waits for them, and re-layouts  46.9 us (6%)
  other arithmetic  23.5 us (3%)
  between operations  15.4 us (2%)
    reduce_scatter x1, waiting for transfers between devices, on_device(): lax.psum_scatter(grad_w_keyval, ('dp', 'mp'), scatter_dimension=0, tiled=...  113 us
    reduce_scatter x1, waiting for transfers between devices, on_device(): lax.psum_scatter(grad_w_query, ('dp', 'mp'), scatter_dimension=0, tiled=T...  104 us
    unnamed x2, blocking collectives  65.2 us
    all_gather x1, waiting for transfers between devices, on_device(): gathered = lax.all_gather(second, 'mp', axis=0, tiled=True)  62.2 us
    reduce_scatter x1, waiting for transfers between devices, on_device(): lax.psum_scatter(jnp.dot(hidden, w_down, preferred_element_type=jnp.float...  60.1 us
    all_gather x1, waiting for transfers between devices, on_device(): grad_rows = lax.all_gather(cotangent, 'mp', axis=0, tiled=True)  56.8 us
    reduce_scatter x1, waiting for transfers between devices, on_device(): lax.psum_scatter(jnp.einsum('tf,df->td', grad_before, w_up, preferred_ele...  52.6 us
    all_to_all x1, blocking collectives, on_device(): lax.all_to_all(grad_kv, 'mp', split_axis=0, concat_axis=2, tiled=True)  48.1 us
  transfers between devices with their start and end apart: 12, of which 9 were waited for; matrix products, arithmetic and copies ran while one was open for 13% of the time, Pallas kernels for 0%

commit v1 on v0

--- a/solution.py
+++ b/solution.py
@@ -5,7 +5,6 @@
 from jax import lax
 from jax.sharding import PartitionSpec as P
 
-FF = 3072
 CLUSTERS = 100
 
 
@@ -79,14 +78,14 @@
         preferred_element_type=jnp.float32,
     )
     cluster_sizes = jnp.sum(member_float, axis=2)
-    query_sums, cluster_sizes = (
-        lax.psum_scatter(
-            query_sums.astype(jnp.bfloat16), "mp", scatter_dimension=0, tiled=True
-        ).astype(jnp.float32),
-        lax.psum_scatter(
-            cluster_sizes.astype(jnp.bfloat16), "mp", scatter_dimension=0, tiled=True
-        ).astype(jnp.float32),
-    )
+    sums_and_sizes = lax.psum_scatter(
+        jnp.concatenate([query_sums, cluster_sizes[:, :, None]], axis=2),
+        "mp",
+        scatter_dimension=0,
+        tiled=True,
+    )
+    query_sums = sums_and_sizes[:, :, :head_dim]
+    cluster_sizes = sums_and_sizes[:, :, head_dim]
     divisor = jnp.maximum(cluster_sizes, 1.0)
     centroids = (query_sums / divisor[:, :, None]).astype(jnp.bfloat16)
     packed = keyval.reshape(tok_rows, 2, group_size, local_heads * head_dim)
@@ -131,7 +130,7 @@
     upstream = cotangent.astype(jnp.float32)
     grad_down_bias = jnp.sum(upstream, axis=0)
     grad_rows = lax.all_gather(cotangent, "mp", axis=0, tiled=True)
-    grad_down = jnp.einsum("tf,td->fd", hidden, grad_rows, preferred_element_type=jnp.float32)
+    grad_down_t = jnp.einsum("td,tf->df", grad_rows, hidden, preferred_element_type=jnp.float32)
     grad_hidden = jnp.einsum("td,fd->tf", grad_rows, w_down, preferred_element_type=jnp.float32)
     grad_before = (grad_hidden * gelu_slope).astype(jnp.bfloat16)
     bias_part = jnp.sum(grad_before.astype(jnp.float32), axis=0)
@@ -145,7 +144,9 @@
         tiled=True,
     ).astype(jnp.float32)
     grad_up_bias = lax.dynamic_update_slice(
-        jnp.zeros((FF,), jnp.float32), bias_part, (lax.axis_index("mp") * bias_part.shape[0],)
+        jnp.zeros((group_size * bias_part.shape[0],), jnp.float32),
+        bias_part,
+        (lax.axis_index("mp") * bias_part.shape[0],),
     )
     middle_norm_grad, grad_gain_two, grad_shift_two = norm_backward(
         grad_second, standard_two, factor_two, ln2_gain
@@ -190,19 +191,32 @@
     grad_keys = score_scale * jnp.einsum(
         "hcj,hcd->jhd", grad_scores, centroids, preferred_element_type=jnp.float32
     )
-    grad_kv = jnp.stack(
+    grad_kv = jnp.concatenate(
         [
             grad_keys.reshape(length, local_heads * head_dim),
             grad_values.reshape(length, local_heads * head_dim),
         ],
         axis=1,
-    )
-    grad_kv = grad_kv.astype(jnp.bfloat16)[:, :, None, :]
-    returned = lax.all_to_all(grad_kv, "mp", split_axis=0, concat_axis=2, tiled=True)
-    grad_keyval = returned.reshape(tok_rows, 2 * model_width)
-    per_member = grad_centroids.astype(jnp.float32) / divisor[:, :, None]
-    all_member = lax.all_gather(per_member.astype(jnp.bfloat16), "mp", axis=0, tiled=True).astype(
-        per_member.dtype
+    ).astype(jnp.bfloat16)
+    kv_width = 2 * local_heads * head_dim
+    per_member = (grad_centroids.astype(jnp.float32) / divisor[:, :, None]).astype(jnp.bfloat16)
+    member_rows = per_member.size // kv_width
+    outgoing = jnp.concatenate(
+        [
+            grad_kv.reshape(group_size, tok_rows, kv_width),
+            jnp.broadcast_to(
+                per_member.reshape(1, member_rows, kv_width), (group_size, member_rows, kv_width)
+            ),
+        ],
+        axis=1,
+    )
+    incoming = lax.all_to_all(outgoing, "mp", split_axis=0, concat_axis=0, tiled=True)
+    returned = incoming[:, :tok_rows].reshape(group_size, tok_rows, 2, local_heads * head_dim)
+    grad_keyval = returned.transpose(1, 2, 0, 3).reshape(tok_rows, 2 * model_width)
+    all_member = (
+        incoming[:, tok_rows:]
+        .reshape(head_count, CLUSTERS, head_dim)
+        .astype(jnp.float32)
     )
     grad_queries = jnp.einsum(
         "hct,hcd->thd", member_float, all_member, precision=lax.Precision.HIGHEST
@@ -220,41 +234,60 @@
         grad_first, standard_one, factor_one, ln1_gain
     )
     input_grad = grad_middle + input_norm_grad
-    shared = (
-        lax.psum_scatter(grad_gain_one, ("dp", "mp"), scatter_dimension=0, tiled=True),
-        lax.psum_scatter(grad_shift_one, ("dp", "mp"), scatter_dimension=0, tiled=True),
-        lax.psum_scatter(grad_w_query, ("dp", "mp"), scatter_dimension=0, tiled=True),
-        lax.psum_scatter(grad_query_bias, ("dp", "mp"), scatter_dimension=0, tiled=True),
-        lax.psum_scatter(grad_w_keyval, ("dp", "mp"), scatter_dimension=0, tiled=True),
-        lax.psum_scatter(grad_value_bias, ("dp", "mp"), scatter_dimension=0, tiled=True),
-        lax.psum_scatter(grad_w_out, ("dp", "mp"), scatter_dimension=0, tiled=True),
-        lax.psum_scatter(grad_out_bias, ("dp", "mp"), scatter_dimension=0, tiled=True),
-        lax.psum_scatter(grad_gain_two, ("dp", "mp"), scatter_dimension=0, tiled=True),
-        lax.psum_scatter(grad_shift_two, ("dp", "mp"), scatter_dimension=0, tiled=True),
-        lax.psum_scatter(grad_up_bias, ("dp", "mp"), scatter_dimension=0, tiled=True),
-        lax.psum_scatter(grad_down_bias, ("dp", "mp"), scatter_dimension=0, tiled=True),
-    )
-    up_share, down_share = (
-        lax.psum_scatter(grad_up, "dp", scatter_dimension=0, tiled=True),
-        lax.psum_scatter(grad_down, "dp", scatter_dimension=1, tiled=True),
-    )
+    vectors = jnp.stack(
+        [
+            grad_gain_one,
+            grad_shift_one,
+            grad_query_bias,
+            grad_value_bias,
+            grad_out_bias,
+            grad_gain_two,
+            grad_shift_two,
+            grad_down_bias,
+        ],
+        axis=1,
+    )
+    up_bias_cols = grad_up_bias.reshape(model_width, -1)
+    packed_grads = jnp.concatenate(
+        [grad_w_query, grad_w_keyval, grad_w_out, vectors, up_bias_cols], axis=1
+    )
+    reduced = lax.psum_scatter(
+        lax.psum_scatter(packed_grads, "dp", scatter_dimension=0, tiled=True),
+        "mp",
+        scatter_dimension=0,
+        tiled=True,
+    )
+    ff_grads = lax.psum_scatter(
+        jnp.concatenate([grad_up, grad_down_t], axis=1), "dp", scatter_dimension=0, tiled=True
+    )
+    ff_width = grad_up.shape[1]
+    up_share = ff_grads[:, :ff_width]
+    down_share = ff_grads[:, ff_width:].T
+    col = 0
+    pieces = []
+    for width in (model_width, 2 * model_width, model_width):
+        pieces.append(reduced[:, col : col + width])
+        col += width
+    vec = [reduced[:, col + i] for i in range(8)]
+    col += 8
+    up_bias_share = reduced[:, col:].reshape(-1)
     return (
         block_output,
         input_grad,
-        shared[0],
-        shared[1],
-        shared[2],
-        shared[3],
-        shared[4],
-        shared[5],
-        shared[6],
-        shared[7],
-        shared[8],
-        shared[9],
+        vec[0],
+        vec[1],
+        pieces[0],
+        vec[2],
+        pieces[1],
+        vec[3],
+        pieces[2],
+        vec[4],
+        vec[5],
+        vec[6],
         up_share,
-        shared[10],
+        up_bias_share,
         down_share,
-        shared[11],
+        vec[7],
     )
 
 

time: 812 us -> 727 us (0.90)
  blocking collectives: 142 us -> 13.8 us
  local copies, waits for them, and re-layouts: 46.9 us -> 76.7 us
  waiting for transfers between devices: 488 us -> 499 us
    reduce_scatter x6 -> x1, waiting for transfers between devices: 248 us -> 59.1 us  [on_device(): lax.psum_scatter(packed_grads, 'dp', scatter_dimension=0, tiled=True)]
    unnamed x11 -> x12, waiting for transfers between devices: 0.84 us -> 161 us
    unnamed x2 -> x0, blocking collectives: 65.2 us -> none
    all_to_all x1 -> x0, blocking collectives: 48.1 us -> none  [on_device(): lax.all_to_all(grad_kv, 'mp', split_axis=0, concat_axis=2, tiled=True)]
    all_to_all x0 -> x1, waiting for transfers between devices: none -> 27.7 us  [on_device(): lax.all_to_all(outgoing, 'mp', split_axis=0, concat_axis=0, tiled=True)]
    concatenate x0 -> x5, local copies, waits for them, and re-layouts: none -> 23 us  [the longest x1 12.4 us: on_device(): jnp.concatenate([grad_w_query, grad_w_keyval, grad_w_out, vectors, up_bia...]
    reduce_scatter x1, waiting for transfers between devices: 1.48 us -> 19.7 us  [on_device(): lax.psum_scatter(summary_grad.astype(jnp.bfloat16), 'mp', scatter_dimensi...]
    all_gather x1 -> x0, blocking collectives: 14 us -> none  [on_device(): lax.all_gather(per_member.astype(jnp.bfloat16), 'mp', axis=0, tiled=True)]
  transfers between devices with their start and end apart: 12 -> 11, of which waited for: 9 -> 10; matrix products, arithmetic and copies ran while one was open for 13% -> 8% of each run, Pallas kernels for 0% -> 0%
where the time goes in v1:
time: 727 us; the launch traced here: 720 us
  waiting for transfers between devices  499 us (69%)
  matrix products  76.8 us (11%)
  local copies, waits for them, and re-layouts  76.7 us (11%)
  other arithmetic  25.1 us (3%)
  between operations  16 us (2%)
  blocking collectives  13.8 us (2%)
  starting transfers between devices  12.4 us (2%)
    unnamed x12, waiting for transfers between devices  161 us
    all_gather x1, waiting for transfers between devices, on_device(): gathered = lax.all_gather(second, 'mp', axis=0, tiled=True)  62.5 us
    reduce_scatter x1, waiting for transfers between devices, on_device(): lax.psum_scatter(jnp.dot(hidden, w_down, preferred_element_type=jnp.float...  59.5 us
    reduce_scatter x1, waiting for transfers between devices, on_device(): lax.psum_scatter(packed_grads, 'dp', scatter_dimension=0, tiled=True)  59.1 us
    all_gather x1, waiting for transfers between devices, on_device(): grad_rows = lax.all_gather(cotangent, 'mp', axis=0, tiled=True)  56.6 us
    reduce_scatter x1, waiting for transfers between devices, on_device(): lax.psum_scatter(jnp.einsum('tf,df->td', grad_before, w_up, preferred_ele...  52.4 us
    all_to_all x1, waiting for transfers between devices, on_device(): lax.all_to_all(outgoing, 'mp', split_axis=0, concat_axis=0, tiled=True)  27.7 us
    reduce_scatter x1, waiting for transfers between devices, on_device(): lax.psum_scatter(summary_grad.astype(jnp.bfloat16), 'mp', scatter_dimensi...  19.7 us
  transfers between devices with their start and end apart: 11, of which 10 were waited for; matrix products, arithmetic and copies ran while one was open for 8% of the time, Pallas kernels for 0%

profile of v1, /device:TPU:0, one launch (start us, length us, event | category | flops | bytes accessed | tf_op | source)
XLA Modules:
  0.0 719.6 jit_solution(4960925814419219149)
XLA Ops:
  18.2 6.5 all-to-all-start
  25.1 3.1 add_convert_fusion.2
  34.3 49.1 %all-reduce.6.cloned.1.call-done = f32[12,100,65]{1,2,0:T(8,128)} async-done(((f32[12,100,65]{1,2,0:T(8,128)}), f32[12,100,65]{1,2,0:T(8,128)}) %all-reduce.6.cloned.1.call-update) | async-done | bytes 312016
  89.1 13.8 %all_gather.9 = bf16[12,100,64]{1,2,0:T(8,128)(2,1)S(1)} all-gather(bf16[3,100,64]{1,2,0:T(8,128)(2,1)S(1)} %fusion.50), channel_id=1, replica_groups=mesh['dp'=8,'mp'=4] {'mp'}, dimensions={0}, use_global_device_ids=true | all-gather | bytes 192000 | tf_op jit(solution)/shard_map/all_gather | solution.py:107
  108.1 62.5 %all-gather.3.cloned.1.call-done = bf16[2048,768]{1,0:T(8,128)(2,1)} async-done(((bf16[512,768]{1,0:T(8,128)(2,1)}), bf16[2048,768]{1,0:T(8,128)(2,1)}) %all-gather.3.cloned.1.call-update) | async-done | bytes 3145744 | tf_op jit(solution)/shard_map/all_gather | solution.py:117
  170.6 7.1 multiply_convert_fusion
  177.7 56.6 %all-gather.5.cloned.1.call-done = bf16[2048,768]{1,0:T(8,128)(2,1)} async-done(((bf16[512,768]{1,0:T(8,128)(2,1)}), bf16[2048,768]{1,0:T(8,128)(2,1)}) %all-gather.5.cloned.1.call-update) | async-done | bytes 3145744 | tf_op jit(solution)/shard_map/all_gather | solution.py:132
  234.3 7.1 convert_reduce_fusion
  243.1 4.0 convolution_convert_fusion
  247.2 6.5 convolution_convert_fusion.1
  254.0 52.4 %reduce-scatter.10.cloned.1.call-done = bf16[512,768]{1,0:T(8,128)(2,1)} async-done(((bf16[2048,768]{1,0:T(8,128)(2,1)}), bf16[512,768]{1,0:T(8,128)(2,1)}) %reduce-scatter.10.cloned.1.call-update) | async-done | bytes 786448 | tf_op jit(solution)/shard_map/reduce_scatter | solution.py:138
  306.3 3.0 fusion.36
  309.3 59.5 %reduce-scatter.8.cloned.1.call-done = bf16[512,768]{1,0:T(8,128)(2,1)} async-done(((bf16[2048,768]{1,0:T(8,128)(2,1)}), bf16[512,768]{1,0:T(8,128)(2,1)}) %reduce-scatter.8.cloned.1.call-update) | async-done | bytes 786448 | tf_op jit(solution)/shard_map/reduce_scatter | solution.py:123
  368.8 4.5 convert_reduce_fusion.5
  380.9 19.7 %reduce-scatter.12.cloned.1.call-done = bf16[3,100,64]{1,2,0:T(8,128)(2,1)} async-done(((bf16[12,100,64]{1,2,0:T(8,128)(2,1)}), bf16[3,100,64]{1,2,0:T(8,128)(2,1)}) %reduce-scatter.12.cloned.1.call-update) | async-done | bytes 38416 | tf_op jit(solution)/shard_map/reduce_scatter | solution.py:167
  400.5 3.3 fusion.9
  403.9 3.0 concatenate.27
  421.6 3.3 pad_maximum_fusion.1
  424.9 4.4 all-to-all-start.1
  436.8 3.3 fusion.53
  440.2 27.7 %all-to-all-done.1 = bf16[4,562,384]{2,1,0:T(8,128)(2,1)} async-done(((bf16[4,562,384]{2,1,0:T(8,128)(2,1)}), bf16[4,562,384]{2,1,0:T(8,128)(2,1)}, u32[]{:S(2)}, u32[]{:S(2)}) %all-to-all-start.1) | async-done | bytes 1726496 | tf_op jit(solution)/shard_map/all_to_all | solution.py:213
  477.6 3.9 fusion.58
  489.6 3.8 fusion.60
  493.5 3.0 fusion.31
  498.3 12.4 %concatenate.30 = f32[768,3084]{1,0:T(8,128)} concatenate(f32[768,768]{1,0:T(8,128)} %fusion.60, f32[768,1536]{1,0:T(8,128)} %fusion.58, f32[768,768]{1,0:T(8,128)} %fusion.53, f32[768,1]{1,0:T(8,128)} %stack.32, f32[768,1]{1,0:T(8,128)} %stack.33, f32[768,1]{1,0:T(8,128)} %stack.34, f32[768,1]{1,0:T(8,128)} %stack.35, f32[768,1]{1,0:T(8,128)} %stack.36, f32[768,1]{1,0:T(8,128)} %stack.37, ...), dimensions={1} | concatenate | bytes 18948096 | tf_op jit(solution)/shard_map/concatenate | solution.py:251
  511.0 5.7 convolution_bitcast_fusion
  519.6 3.1 pad_maximum_fusion
  522.7 6.6 copy.108
  529.4 59.1 %reduce-scatter.14.cloned.1.call-done = f32[96,3084]{1,0:T(8,128)} async-done(((f32[768,3084]{1,0:T(8,128)}), f32[96,3084]{1,0:T(8,128)}) %reduce-scatter.14.cloned.1.call-update) | async-done | bytes 1184272 | tf_op jit(solution)/shard_map/reduce_scatter | solution.py:255
  589.3 56.6 %reduce-scatter.16.cloned.1.call-done = f32[96,1536]{1,0:T(8,128)} async-done(((f32[768,1536]{1,0:T(8,128)}), f32[96,1536]{1,0:T(8,128)}) %reduce-scatter.16.cloned.1.call-update) | async-done | bytes 589840
  647.8 3.6 fusion.30
  651.3 54.8 %all-reduce.8.cloned.1.call-done = f32[96,3084]{1,0:T(8,128)} async-done(((f32[96,3084]{1,0:T(8,128)}), f32[96,3084]{1,0:T(8,128)}) %all-reduce.8.cloned.1.call-update) | async-done | bytes 1184272
  (168 shorter events, 90.6 us)
Async XLA Ops:
  7.2 3.1 copy-start
  7.2 3.1 copy-start.6
  7.2 3.1 copy-start.19
  10.2 14.8 %copy-start.15 = (f32[512]{0:T(512)}, f32[512]{0:T(512)S(1)}, u32[]{:S(2)}) copy-start(f32[512]{0:T(512)S(1)} %add_rsqrt_fusion.1) | copy-start | bytes 6148
  18.2 6.5 copy-start.13
  18.2 6.9 copy-start.31
  18.2 65.9 %all-to-all-start = ((bf16[512,2,4,192]{0,3,1,2:T(8,128)(2,1)}), bf16[512,2,4,192]{0,3,1,2:T(8,128)(2,1)}, u32[]{:S(2)}, u32[]{:S(2)}) async-start(bf16[512,2,4,192]{0,3,1,2:T(8,128)(2,1)} %copy.84), calls=%async_computation | async-start | bytes 3145728 | tf_op jit(solution)/shard_map/all_to_all | solution.py:92
  24.7 58.7 %all-reduce.6.cloned.1.call-start = ((), (), s32[]{:S(2)}) async-start(), calls=%async_computation.14 | async-start | bytes 884736
  33.0 137.6 %all-gather.3.cloned.1.call-start = ((), (), s32[]{:S(2)}) async-start(), calls=%async_computation.7 | async-start | bytes 3932160 | tf_op jit(solution)/shard_map/all_gather | solution.py:117
  88.0 15.4 %copy-start.28 = (bf16[768,768]{1,0:T(8,128)(2,1)S(1)}, bf16[768,768]{1,0:T(8,128)(2,1)}, u32[]{:S(2)}) copy-start(bf16[768,768]{1,0:T(8,128)(2,1)} %param.25) | copy-start | bytes 3538948
  88.1 15.4 %copy-start.32 = (f32[768]{0:T(1024)S(1)}, f32[768]{0:T(1024)}, u32[]{:S(2)}) copy-start(f32[768]{0:T(1024)} %param.26) | copy-start | bytes 9220
  106.8 127.5 %all-gather.5.cloned.1.call-start = ((), (), s32[]{:S(2)}) async-start(), calls=%async_computation.9 | async-start | bytes 3932160 | tf_op jit(solution)/shard_map/all_gather | solution.py:132
  107.5 198.8 %reduce-scatter.10.cloned.1.call-start = ((), (), s32[]{:S(2)}) async-start(), calls=%async_computation.10 | async-start | bytes 3932160 | tf_op jit(solution)/shard_map/reduce_scatter | solution.py:138
  234.3 8.8 %copy-start.27 = (bf16[768,768]{1,0:T(8,128)(2,1)S(1)}, bf16[768,768]{1,0:T(8,128)(2,1)}, u32[]{:S(2)}) copy-start(bf16[768,768]{1,0:T(8,128)(2,1)} %param.29) | copy-start | bytes 3538948
  247.1 121.7 %reduce-scatter.8.cloned.1.call-start = ((), (), s32[]{:S(2)}) async-start(), calls=%async_computation.8 | async-start | bytes 3932160 | tf_op jit(solution)/shard_map/reduce_scatter | solution.py:123
  253.7 115.1 %copy-start.18 = (f32[768]{0:T(1024)S(1)}, f32[768]{0:T(1024)}, u32[]{:S(2)}) copy-start(f32[768]{0:T(1024)} %param.32) | copy-start | bytes 9220
  253.7 146.8 %reduce-scatter.12.cloned.1.call-start = ((), (), s32[]{:S(2)}) async-start(), calls=%async_computation.11 | async-start | bytes 245760 | tf_op jit(solution)/shard_map/reduce_scatter | solution.py:167
  368.8 5.7 copy-start.29
  403.9 5.3 copy-start.12
  424.9 43.0 %all-to-all-start.1 = ((bf16[4,562,384]{2,1,0:T(8,128)(2,1)}), bf16[4,562,384]{2,1,0:T(8,128)(2,1)}, u32[]{:S(2)}, u32[]{:S(2)}) async-start(bf16[4,562,384]{2,1,0:T(8,128)(2,1)} %pad_maximum_fusion.1), calls=%async_computation.4 | async-start | bytes 3489792 | tf_op jit(solution)/shard_map/all_to_all | solution.py:213
  429.3 159.3 %reduce-scatter.14.cloned.1.call-start = ((), (), s32[]{:S(2)}) async-start(), calls=%async_computation.12 | async-start | bytes 11059200 | tf_op jit(solution)/shard_map/reduce_scatter | solution.py:255
  430.3 6.6 copy-start.5
  489.6 3.8 copy-start.11
  489.6 3.8 copy-start.21
  489.6 3.8 copy-start.30
  489.6 3.8 copy-start.36
  510.7 135.1 %reduce-scatter.16.cloned.1.call-start = ((), (), s32[]{:S(2)}) async-start(), calls=%async_computation.13 | async-start | bytes 5308416
  511.0 5.7 copy-start.26
  511.0 5.7 copy-start.38
  529.4 118.4 %copy-start.25 = (f32[512]{0:T(512)S(1)}, f32[512]{0:T(512)}, u32[]{:S(2)}) copy-start(f32[512]{0:T(512)} %get-tuple-element.83) | copy-start | bytes 6148
  529.4 118.4 %copy-start.24 = (f32[512]{0:T(512)S(1)}, f32[512]{0:T(512)}, u32[]{:S(2)}) copy-start(f32[512]{0:T(512)} %get-tuple-element.84) | copy-start | bytes 6148
  529.4 176.7 %all-reduce.8.cloned.1.call-start = ((), (), s32[]{:S(2)}) async-start(), calls=%async_computation.15 | async-start | bytes 2457600
  (18 other events, 35.7 us)
Sparse Core Ops, SparseCore 0:
  33.1 50.2 all-reduce.5
  106.9 63.6 all-gather.2
  172.2 62.0 all-gather.4
  247.2 59.0 reduce-scatter.9
  308.5 60.2 reduce-scatter.7
  381.0 19.5 reduce-scatter.11
  510.8 77.6 reduce-scatter.13
  592.0 53.7 reduce-scatter.15
  648.2 57.8 all-reduce.7

commit v2 on v1

--- a/solution.py
+++ b/solution.py
@@ -4,6 +4,7 @@
 import jax.numpy as jnp
 from jax import lax
 from jax.sharding import PartitionSpec as P
+
 
 CLUSTERS = 100
 
@@ -31,7 +32,53 @@
     return (before * cumulative, cumulative + before * density)
 
 
-def on_device(
+def ring_shift(x, group_size):
+    return lax.ppermute(x, "mp", [(i, (i + 1) % group_size) for i in range(group_size)])
+
+
+def ring_gather(x, group_size):
+    me = lax.axis_index("mp")
+    out = jnp.zeros((group_size,) + x.shape, x.dtype)
+    out = lax.dynamic_update_index_in_dim(out, x, me, 0)
+    cur = x
+    for step in range(1, group_size):
+        cur = ring_shift(cur, group_size)
+        out = lax.dynamic_update_index_in_dim(
+            out, cur, jnp.remainder(me + group_size - step, group_size), 0
+        )
+    return out.reshape((group_size * x.shape[0],) + x.shape[1:])
+
+
+def ring_reduce(partial, group_size, wire_dtype):
+    me = lax.axis_index("mp")
+    blocks = partial.reshape((group_size, -1) + partial.shape[1:])
+
+    def block(owner):
+        return lax.dynamic_index_in_dim(
+            blocks, jnp.remainder(owner + 2 * group_size, group_size), 0, keepdims=False
+        )
+
+    acc = block(me - 1).astype(wire_dtype)
+    for step in range(1, group_size - 1):
+        arrived = ring_shift(acc, group_size)
+        acc = (arrived.astype(jnp.float32) + block(me - 1 - step)).astype(wire_dtype)
+    arrived = ring_shift(acc, group_size)
+    return arrived.astype(jnp.float32) + block(me)
+
+
+def scatter_sum(partial, group_size):
+    pieces = partial.reshape((group_size, -1) + partial.shape[1:])
+    arrived = lax.all_to_all(pieces, "mp", split_axis=0, concat_axis=0, tiled=True)
+    return jnp.sum(arrived, axis=0)
+
+
+def broadcast_gather(local, group_size):
+    sent = jnp.broadcast_to(local[None], (group_size,) + local.shape)
+    arrived = lax.all_to_all(sent, "mp", split_axis=0, concat_axis=0, tiled=True)
+    return arrived.reshape((group_size * local.shape[0],) + local.shape[1:])
+
+
+def block_body(
     block_input,
     clusters,
     ln1_gain,
@@ -57,12 +104,15 @@
     head_dim = model_width // head_count
     local_heads = head_count // group_size
     score_scale = float(head_dim) ** (-0.5)
+
+    grad_rows = ring_gather(cotangent, group_size)
+
     inputs = block_input.astype(jnp.float32)
     normed_one, standard_one, factor_one = norm_forward(inputs, ln1_gain, ln1_bias)
     first = normed_one.astype(jnp.bfloat16)
-    queries = (jnp.dot(first, w_query, preferred_element_type=jnp.float32) + query_bias).astype(
-        jnp.bfloat16
-    )
+    queries = (
+        jnp.dot(first, w_query, preferred_element_type=jnp.float32) + query_bias
+    ).astype(jnp.bfloat16)
     keyval = jnp.dot(first, w_keyval, preferred_element_type=jnp.float32)
     keyval = (keyval + jnp.concatenate([jnp.zeros_like(value_bias), value_bias])).astype(
         jnp.bfloat16
@@ -78,18 +128,17 @@
         preferred_element_type=jnp.float32,
     )
     cluster_sizes = jnp.sum(member_float, axis=2)
-    sums_and_sizes = lax.psum_scatter(
-        jnp.concatenate([query_sums, cluster_sizes[:, :, None]], axis=2),
-        "mp",
-        scatter_dimension=0,
-        tiled=True,
-    )
+    packed = keyval.reshape(tok_rows, 2, group_size, local_heads * head_dim)
+
+    sums_and_sizes = scatter_sum(
+        jnp.concatenate([query_sums, cluster_sizes[:, :, None]], axis=2), group_size
+    )
+    arrived = lax.all_to_all(packed, "mp", split_axis=2, concat_axis=0, tiled=True)
+
     query_sums = sums_and_sizes[:, :, :head_dim]
     cluster_sizes = sums_and_sizes[:, :, head_dim]
     divisor = jnp.maximum(cluster_sizes, 1.0)
     centroids = (query_sums / divisor[:, :, None]).astype(jnp.bfloat16)
-    packed = keyval.reshape(tok_rows, 2, group_size, local_heads * head_dim)
-    arrived = lax.all_to_all(packed, "mp", split_axis=2, concat_axis=0, tiled=True)
     length = arrived.shape[0]
     key_rows = arrived[:, 0, 0].reshape(length, local_heads, head_dim)
     value_rows = arrived[:, 1, 0].reshape(length, local_heads, head_dim)
@@ -102,9 +151,14 @@
     probs = exponent / denominator
     logsum = score_peak + jnp.log(denominator)
     summary = jnp.einsum(
-        "hcj,jhd->hcd", probs.astype(jnp.bfloat16), value_rows, preferred_element_type=jnp.float32
-    ).astype(jnp.bfloat16)
-    everyone = lax.all_gather(summary, "mp", axis=0, tiled=True)
+        "hcj,jhd->hcd",
+        probs.astype(jnp.bfloat16),
+        value_rows,
+        preferred_element_type=jnp.float32,
+    ).astype(jnp.bfloat16)
+
+    everyone = broadcast_gather(summary, group_size)
+
     spread = (
         jnp.einsum("hct,hcd->thd", membership, everyone, preferred_element_type=jnp.float32)
         .astype(jnp.bfloat16)
@@ -114,27 +168,17 @@
     middle = inputs + attended
     normed_two, standard_two, factor_two = norm_forward(middle, ln2_gain, ln2_bias)
     second = normed_two.astype(jnp.bfloat16)
+    residual = lax.optimization_barrier(middle + down_bias)
+
     gathered = lax.all_gather(second, "mp", axis=0, tiled=True)
+
     before = jnp.dot(gathered, w_up, preferred_element_type=jnp.float32) + up_bias.astype(
         jnp.float32
     )
     activated, gelu_slope = gelu_parts(before)
     hidden = activated.astype(jnp.bfloat16)
-    result = lax.psum_scatter(
-        jnp.dot(hidden, w_down, preferred_element_type=jnp.float32).astype(jnp.bfloat16),
-        "mp",
-        scatter_dimension=0,
-        tiled=True,
-    ).astype(jnp.float32)
-    block_output = (middle + result + down_bias).astype(jnp.bfloat16)
-    upstream = cotangent.astype(jnp.float32)
-    grad_down_bias = jnp.sum(upstream, axis=0)
-    grad_rows = lax.all_gather(cotangent, "mp", axis=0, tiled=True)
-    grad_down_t = jnp.einsum("td,tf->df", grad_rows, hidden, preferred_element_type=jnp.float32)
     grad_hidden = jnp.einsum("td,fd->tf", grad_rows, w_down, preferred_element_type=jnp.float32)
     grad_before = (grad_hidden * gelu_slope).astype(jnp.bfloat16)
-    bias_part = jnp.sum(grad_before.astype(jnp.float32), axis=0)
-    grad_up = jnp.einsum("td,tf->df", gathered, grad_before, preferred_element_type=jnp.float32)
     grad_second = lax.psum_scatter(
         jnp.einsum("tf,df->td", grad_before, w_up, preferred_element_type=jnp.float32).astype(
             jnp.bfloat16
@@ -143,11 +187,25 @@
         scatter_dimension=0,
         tiled=True,
     ).astype(jnp.float32)
+
+    out_partial = jnp.dot(hidden, w_down, preferred_element_type=jnp.float32)
+    result = ring_reduce(out_partial, group_size, jnp.bfloat16)
+    block_output = (residual + result).astype(jnp.bfloat16)
+
+    upstream = cotangent.astype(jnp.float32)
+    grad_down_bias = jnp.sum(upstream, axis=0)
+    grad_down_t = jnp.einsum("td,tf->df", grad_rows, hidden, preferred_element_type=jnp.float32)
+    bias_part = jnp.sum(grad_before.astype(jnp.float32), axis=0)
+    grad_up = jnp.einsum("td,tf->df", gathered, grad_before, preferred_element_type=jnp.float32)
     grad_up_bias = lax.dynamic_update_slice(
         jnp.zeros((group_size * bias_part.shape[0],), jnp.float32),
         bias_part,
         (lax.axis_index("mp") * bias_part.shape[0],),
     )
+    ff_grads = lax.psum_scatter(
+        jnp.concatenate([grad_up, grad_down_t], axis=1), "dp", scatter_dimension=0, tiled=True
+    )
+
     middle_norm_grad, grad_gain_two, grad_shift_two = norm_backward(
         grad_second, standard_two, factor_two, ln2_gain
     )
@@ -164,9 +222,9 @@
         grad_spread.reshape(tok_rows, head_count, head_dim),
         preferred_element_type=jnp.float32,
     )
-    summary_grad = lax.psum_scatter(
-        summary_grad.astype(jnp.bfloat16), "mp", scatter_dimension=0, tiled=True
-    )
+
+    summary_grad = scatter_sum(summary_grad, group_size).astype(jnp.bfloat16)
+
     scores_again = score_scale * jnp.einsum(
         "hcd,jhd->hcj", centroids, key_rows, preferred_element_type=jnp.float32
     )
@@ -199,24 +257,27 @@
         axis=1,
     ).astype(jnp.bfloat16)
     kv_width = 2 * local_heads * head_dim
-    per_member = (grad_centroids.astype(jnp.float32) / divisor[:, :, None]).astype(jnp.bfloat16)
+    per_member = (grad_centroids.astype(jnp.float32) / divisor[:, :, None]).astype(
+        jnp.bfloat16
+    )
     member_rows = per_member.size // kv_width
     outgoing = jnp.concatenate(
         [
             grad_kv.reshape(group_size, tok_rows, kv_width),
             jnp.broadcast_to(
-                per_member.reshape(1, member_rows, kv_width), (group_size, member_rows, kv_width)
+                per_member.reshape(1, member_rows, kv_width),
+                (group_size, member_rows, kv_width),
             ),
         ],
         axis=1,
     )
+
     incoming = lax.all_to_all(outgoing, "mp", split_axis=0, concat_axis=0, tiled=True)
+
     returned = incoming[:, :tok_rows].reshape(group_size, tok_rows, 2, local_heads * head_dim)
     grad_keyval = returned.transpose(1, 2, 0, 3).reshape(tok_rows, 2 * model_width)
     all_member = (
-        incoming[:, tok_rows:]
-        .reshape(head_count, CLUSTERS, head_dim)
-        .astype(jnp.float32)
+        incoming[:, tok_rows:].reshape(head_count, CLUSTERS, head_dim).astype(jnp.float32)
     )
     grad_queries = jnp.einsum(
         "hct,hcd->thd", member_float, all_member, precision=lax.Precision.HIGHEST
@@ -251,14 +312,9 @@
     packed_grads = jnp.concatenate(
         [grad_w_query, grad_w_keyval, grad_w_out, vectors, up_bias_cols], axis=1
     )
-    reduced = lax.psum_scatter(
-        lax.psum_scatter(packed_grads, "dp", scatter_dimension=0, tiled=True),
-        "mp",
-        scatter_dimension=0,
-        tiled=True,
-    )
-    ff_grads = lax.psum_scatter(
-        jnp.concatenate([grad_up, grad_down_t], axis=1), "dp", scatter_dimension=0, tiled=True
+
+    reduced = scatter_sum(
+        lax.psum_scatter(packed_grads, "dp", scatter_dimension=0, tiled=True), group_size
     )
     ff_width = grad_up.shape[1]
     up_share = ff_grads[:, :ff_width]
@@ -312,7 +368,7 @@
         P(("dp", "mp"), None),
     )
     return jax.shard_map(
-        on_device,
+        block_body,
         mesh=mesh,
         in_specs=placed,
         out_specs=(

time: 727 us -> 574 us (0.79)
  waiting for transfers between devices: 499 us -> 315 us
  starting transfers between devices: 12.4 us -> 41.7 us
  other arithmetic: 25.1 us -> 34.4 us
  matrix products: 76.8 us -> 67.7 us
    ppermute x0 -> x6, waiting for transfers between devices: none -> 131 us  [ring_shift(): lax.ppermute(x, 'mp', [(i, (i + 1) % group_size) for i in range(group_siz...]
    reduce_scatter x4 -> x2, waiting for transfers between devices: 191 us -> 65 us  [the longest x1 58.8 us: block_body(): lax.psum_scatter(jnp.einsum('tf,df->td', grad_before, w_up, preferred_ele...]
    unnamed x12 -> x5, waiting for transfers between devices: 161 us -> 38.3 us
    all_gather x2 -> x1, waiting for transfers between devices: 119 us -> 0.01 us  [block_body(): gathered = lax.all_gather(second, 'mp', axis=0, tiled=True)]
    all_to_all x2 -> x5, waiting for transfers between devices: 27.7 us -> 80.7 us  [the longest x1 35.4 us: block_body(): lax.all_to_all(packed, 'mp', split_axis=2, concat_axis=0, tiled=True)]
    ppermute x0 -> x6, starting transfers between devices: none -> 17.3 us  [ring_shift(): lax.ppermute(x, 'mp', [(i, (i + 1) % group_size) for i in range(group_siz...]
    all_gather x1 -> x0, blocking collectives: 13.8 us -> none  [on_device(): everyone = lax.all_gather(summary, 'mp', axis=0, tiled=True)]
    all_to_all x2 -> x5, starting transfers between devices: 10.9 us -> 23.9 us  [the longest x3 15 us: scatter_sum(): lax.all_to_all(pieces, 'mp', split_axis=0, concat_axis=0, tiled=True)]
  transfers between devices with their start and end apart: 11 -> 15, of which waited for: 10 -> 13; matrix products, arithmetic and copies ran while one was open for 8% -> 11% of each run, Pallas kernels for 0% -> 0%
where the time goes in v2:
time: 574 us; the launch traced here: 565 us
  waiting for transfers between devices  315 us (55%)
  local copies, waits for them, and re-layouts  82.1 us (14%)
  matrix products  67.7 us (12%)
  starting transfers between devices  41.7 us (7%)
  other arithmetic  34.4 us (6%)
  between operations  14.7 us (3%)
  blocking collectives  9.55 us (2%)
    ppermute x6, waiting for transfers between devices, ring_shift(): lax.ppermute(x, 'mp', [(i, (i + 1) % group_size) for i in range(group_siz...  131 us
    reduce_scatter x1, waiting for transfers between devices, block_body(): lax.psum_scatter(jnp.einsum('tf,df->td', grad_before, w_up, preferred_ele...  58.8 us
    unnamed x5, waiting for transfers between devices  38.3 us
    all_to_all x1, waiting for transfers between devices, block_body(): lax.all_to_all(packed, 'mp', split_axis=2, concat_axis=0, tiled=True)  35.4 us
    all_to_all x1, waiting for transfers between devices, block_body(): lax.all_to_all(outgoing, 'mp', split_axis=0, concat_axis=0, tiled=True)  29.5 us
    unnamed x111, local copies, waits for them, and re-layouts  18.5 us
    ppermute x6, starting transfers between devices, ring_shift(): lax.ppermute(x, 'mp', [(i, (i + 1) % group_size) for i in range(group_siz...  17.3 us
    all_to_all x3, waiting for transfers between devices, scatter_sum(): lax.all_to_all(pieces, 'mp', split_axis=0, concat_axis=0, tiled=True)  15.8 us
  transfers between devices with their start and end apart: 15, of which 13 were waited for; matrix products, arithmetic and copies ran while one was open for 11% of the time, Pallas kernels for 0%

profile of v2, /device:TPU:0, one launch (start us, length us, event | category | flops | bytes accessed | tf_op | source)
XLA Modules:
  0.0 565.4 jit_solution(9097362014446873879)
XLA Ops:
  18.5 6.3 %all-to-all-start = ((f32[4,3,100,65]{2,3,1,0:T(8,128)}), f32[4,3,100,65]{2,3,1,0:T(8,128)}, u32[]{:S(2)}, u32[]{:S(2)}) async-start(f32[4,3,100,65]{2,3,1,0:T(8,128)} %pad_maximum_fusion.2), calls=%async_computation | async-start | bytes 884736 | tf_op jit(solution)/shard_map/all_to_all | solution.py:71
  32.8 4.9 all-to-all-done
  37.7 4.3 all-to-all-start.1
  43.2 35.4 %all-to-all-done.1 = bf16[512,2,4,192]{0,3,1,2:T(8,128)(2,1)} async-done(((bf16[512,2,4,192]{0,3,1,2:T(8,128)(2,1)}), bf16[512,2,4,192]{0,3,1,2:T(8,128)(2,1)}, u32[]{:S(2)}, u32[]{:S(2)}) %all-to-all-start.1) | async-done | bytes 1572896 | tf_op jit(solution)/shard_map/all_to_all | solution.py:136
  82.9 9.5 %all_to_all.43 = bf16[4,3,100,64]{2,3,1,0:T(8,128)(2,1)S(1)} all-to-all(bf16[4,3,100,64]{2,3,1,0:T(8,128)(2,1)S(1)} %broadcast_in_dim.23), channel_id=1, replica_groups=mesh['dp'=8,'mp'=4] {'mp'}, dimensions={0} | all-to-all | bytes 307200 | tf_op jit(solution)/shard_map/all_to_all | solution.py:77
  97.2 29.3 %collective-permute-done.3 = bf16[512,768]{1,0:T(8,128)(2,1)} collective-permute-done((bf16[512,768]{1,0:T(8,128)(2,1)}, bf16[512,768]{1,0:T(8,128)(2,1)}, u32[]{:S(2)}, u32[]{:S(2)}) %collective-permute-start.3) | collective-permute-done | bytes 786464 | tf_op jit(solution)/shard_map/ppermute | solution.py:36
  126.5 6.6 %collective-permute-start.4 = (bf16[512,768]{1,0:T(8,128)(2,1)}, bf16[512,768]{1,0:T(8,128)(2,1)}, u32[]{:S(2)}, u32[]{:S(2)}) collective-permute-start(bf16[512,768]{1,0:T(8,128)(2,1)} %collective-permute-done.3), channel_id=1, source_target_pairs={{0,1},{1,2},{2,3},{3,0},{4,5},{5,6},{6,7},{7,4},{8,9},{9,10},{10,1... | collective-permute-start | bytes 2359304 | tf_op jit(solution)/shard_map/ppermute | solution.py:36
  133.1 37.2 %collective-permute-done.4 = bf16[512,768]{1,0:T(8,128)(2,1)} collective-permute-done((bf16[512,768]{1,0:T(8,128)(2,1)}, bf16[512,768]{1,0:T(8,128)(2,1)}, u32[]{:S(2)}, u32[]{:S(2)}) %collective-permute-start.4) | collective-permute-done | bytes 786464 | tf_op jit(solution)/shard_map/ppermute | solution.py:36
  170.4 9.7 %collective-permute-start.5 = (bf16[512,768]{1,0:T(8,128)(2,1)}, bf16[512,768]{1,0:T(8,128)(2,1)S(1)}, u32[]{:S(2)}, u32[]{:S(2)}) collective-permute-start(bf16[512,768]{1,0:T(8,128)(2,1)} %collective-permute-done.4), channel_id=1, source_target_pairs={{0,1},{1,2},{2,3},{3,0},{4,5},{5,6},{6,7},{7,4},{8,9},{9,10},{10,1... | collective-permute-start | bytes 2359304 | tf_op jit(solution)/shard_map/ppermute | solution.py:36
  187.1 12.9 %collective-permute-done.5 = bf16[512,768]{1,0:T(8,128)(2,1)S(1)} collective-permute-done((bf16[512,768]{1,0:T(8,128)(2,1)}, bf16[512,768]{1,0:T(8,128)(2,1)S(1)}, u32[]{:S(2)}, u32[]{:S(2)}) %collective-permute-start.5) | collective-permute-done | bytes 786464 | tf_op jit(solution)/shard_map/ppermute | solution.py:36
  201.0 6.2 %multiply_convert_fusion = (bf16[2048,768]{1,0:T(8,128)(2,1)}, f32[2048,768]{1,0:T(8,128)S(1)}) fusion(f32[768]{0:T(1024)S(1)} %convert_element_type.142, bf16[2048,768]{1,0:T(8,128)(2,1)} %all-gather.2.cloned.1.call-done, bf16[768,768]{1,0:T(8,128)(2,1)} %param.29), kind=kOutput, calls=%fused_computation.8 | convolution fusion | flops 2425356288 | bytes 13765632 | tf_op jit(solution)/shard_map/dot_general | solution.py:175
  207.2 6.4 %convert_reduce_fusion = (f32[768]{0:T(1024)}, bf16[2048,768]{1,0:T(8,128)(2,1)S(1)}) fusion(f32[2048,768]{1,0:T(8,128)S(1)} %get-tuple-element.111, f32[768]{0:T(1024)S(1)} %convert_element_type.142, bf16[2048,768]{1,0:T(8,128)(2,1)} %bitcast.20, bf16[768,768]{1,0:T(8,128)(2,1)S(1)} %copy-done.44), kind=kOutput, calls=%fused_computation.7 | convolution fusion | flops 2436365568 | bytes 13768704 | tf_op jit(solution)/shard_map/td,fd->tf/dot_general | solution.py:180
  215.3 4.0 convolution_convert_fusion
  219.3 58.8 %reduce-scatter.6.cloned.1.call-done = bf16[512,768]{1,0:T(8,128)(2,1)} async-done(((bf16[2048,768]{1,0:T(8,128)(2,1)}), bf16[512,768]{1,0:T(8,128)(2,1)}) %reduce-scatter.6.cloned.1.call-update) | async-done | bytes 786448 | tf_op jit(solution)/shard_map/reduce_scatter | solution.py:182
  281.3 3.8 convert_reduce_fusion.5
  292.7 4.1 all-to-all-start.3
  297.5 10.9 %all-to-all-done.3 = f32[4,3,100,64]{2,3,1,0:T(8,128)S(1)} async-done(((f32[4,3,100,64]{2,3,1,0:T(8,128)}), f32[4,3,100,64]{2,3,1,0:T(8,128)S(1)}, u32[]{:S(2)}, u32[]{:S(2)}) %all-to-all-start.3) | async-done | bytes 307232 | tf_op jit(solution)/shard_map/all_to_all | solution.py:71
  330.9 4.5 all-to-all-start.4
  346.2 29.5 %all-to-all-done.4 = bf16[4,562,384]{2,1,0:T(8,128)(2,1)} async-done(((bf16[4,562,384]{2,1,0:T(8,128)(2,1)}), bf16[4,562,384]{2,1,0:T(8,128)(2,1)}, u32[]{:S(2)}, u32[]{:S(2)}) %all-to-all-start.4) | async-done | bytes 1726496 | tf_op jit(solution)/shard_map/all_to_all | solution.py:275
  385.4 3.9 fusion.65
  396.0 4.3 fusion.31
  402.1 11.7 %concatenate.37 = f32[768,3084]{1,0:T(8,128)} concatenate(f32[768,768]{1,0:T(8,128)} %fusion.67, f32[768,1536]{1,0:T(8,128)} %fusion.65, f32[768,768]{1,0:T(8,128)S(1)} %copy-done.8, f32[768,1]{1,0:T(8,128)} %stack.32, f32[768,1]{1,0:T(8,128)} %stack.33, f32[768,1]{1,0:T(8,128)} %stack.34, f32[768,1]{1,0:T(8,128)} %stack.35, f32[768,1]{1,0:T(8,128)} %stack.36, f32[768,1]{1,0:T(8,128)} %stack.37, ...), dimensions={1} | concatenate | bytes 18948096 | tf_op jit(solution)/shard_map/concatenate | solution.py:312
  414.1 5.6 fusion.78
  425.7 6.6 %copy.108 = f32[768,1536]{1,0:T(8,128)} copy(f32[768,1536]{0,1:T(8,128)} %pad_maximum_fusion) | data formatting | bytes 9437184
  433.6 4.6 fusion.75
  441.3 20.5 %collective-permute-done = bf16[512,768]{1,0:T(8,128)(2,1)S(1)} collective-permute-done((bf16[512,768]{1,0:T(8,128)(2,1)S(1)}, bf16[512,768]{1,0:T(8,128)(2,1)S(1)}, u32[]{:S(2)}, u32[]{:S(2)}) %collective-permute-start) | collective-permute-done | bytes 786464 | tf_op jit(solution)/shard_map/ppermute | solution.py:36
  463.4 19.6 %collective-permute-done.1 = bf16[512,768]{1,0:T(8,128)(2,1)S(1)} collective-permute-done((bf16[512,768]{1,0:T(8,128)(2,1)S(1)}, bf16[512,768]{1,0:T(8,128)(2,1)S(1)}, u32[]{:S(2)}, u32[]{:S(2)}) %collective-permute-start.1) | collective-permute-done | bytes 786464 | tf_op jit(solution)/shard_map/ppermute | solution.py:36
  485.5 6.2 %reduce-scatter.8.cloned.1.call-done = f32[96,3084]{1,0:T(8,128)} async-done(((f32[768,3084]{1,0:T(8,128)}), f32[96,3084]{1,0:T(8,128)}) %reduce-scatter.8.cloned.1.call-update) | async-done | bytes 1184272 | tf_op jit(solution)/shard_map/reduce_scatter | solution.py:317
  491.7 4.6 all-to-all-start.5
  496.2 11.7 %collective-permute-done.2 = bf16[512,768]{1,0:T(8,128)(2,1)S(1)} collective-permute-done((bf16[512,768]{1,0:T(8,128)(2,1)}, bf16[512,768]{1,0:T(8,128)(2,1)S(1)}, u32[]{:S(2)}, u32[]{:S(2)}) %collective-permute-start.2) | collective-permute-done | bytes 786464 | tf_op jit(solution)/shard_map/ppermute | solution.py:36
  510.5 38.2 %reduce-scatter.10.cloned.1.call-done = f32[96,1536]{1,0:T(8,128)} async-done(((f32[768,1536]{1,0:T(8,128)}), f32[96,1536]{1,0:T(8,128)}) %reduce-scatter.10.cloned.1.call-update) | async-done | bytes 589840
  550.7 3.7 fusion.30
  (213 shorter events, 124.9 us)
Async XLA Ops:
  7.2 17.7 %copy-start = (bf16[768,1536]{1,0:T(8,128)(2,1)S(1)}, bf16[768,1536]{1,0:T(8,128)(2,1)}, u32[]{:S(2)}) copy-start(bf16[768,1536]{1,0:T(8,128)(2,1)} %param.23) | copy-start | bytes 7077892
  10.2 14.7 %copy-start.27 = (f32[512]{0:T(512)}, f32[512]{0:T(512)S(1)}, u32[]{:S(2)}) copy-start(f32[512]{0:T(512)S(1)} %add_rsqrt_fusion.1) | copy-start | bytes 6148
  16.0 8.9 %copy-start.34 = (f32[768]{0:T(1024)S(1)}, f32[768]{0:T(1024)}, u32[]{:S(2)}) copy-start(f32[768]{0:T(1024)} %param.24) | copy-start | bytes 9220
  18.5 19.2 %all-to-all-start = ((f32[4,3,100,65]{2,3,1,0:T(8,128)}), f32[4,3,100,65]{2,3,1,0:T(8,128)}, u32[]{:S(2)}, u32[]{:S(2)}) async-start(f32[4,3,100,65]{2,3,1,0:T(8,128)} %pad_maximum_fusion.2), calls=%async_computation | async-start | bytes 884736 | tf_op jit(solution)/shard_map/all_to_all | solution.py:71
  37.7 40.9 %all-to-all-start.1 = ((bf16[512,2,4,192]{0,3,1,2:T(8,128)(2,1)}), bf16[512,2,4,192]{0,3,1,2:T(8,128)(2,1)}, u32[]{:S(2)}, u32[]{:S(2)}) async-start(bf16[512,2,4,192]{0,3,1,2:T(8,128)(2,1)} %copy.84), calls=%async_computation.1 | async-start | bytes 3145728 | tf_op jit(solution)/shard_map/all_to_all | solution.py:136
  42.1 159.0 %all-gather.2.cloned.1.call-start = ((), (), s32[]{:S(2)}) async-start(), calls=%async_computation.9 | async-start | bytes 3932160 | tf_op jit(solution)/shard_map/all_gather | solution.py:173
  43.2 37.2 %copy-start.18 = (f32[3,100,65]{1,2,0:T(8,128)}, f32[3,100,65]{1,2,0:T(8,128)S(1)}, u32[]{:S(2)}) copy-start(f32[3,100,65]{1,2,0:T(8,128)S(1)} %reduce_sum.210) | copy-start | bytes 234004
  82.8 10.1 %copy-start.41 = (bf16[768,768]{1,0:T(8,128)(2,1)S(1)}, bf16[768,768]{1,0:T(8,128)(2,1)}, u32[]{:S(2)}) copy-start(bf16[768,768]{1,0:T(8,128)(2,1)} %param.25) | copy-start | bytes 3538948
  82.8 10.1 %copy-start.47 = (f32[768]{0:T(1024)S(1)}, f32[768]{0:T(1024)}, u32[]{:S(2)}) copy-start(f32[768]{0:T(1024)} %param.26) | copy-start | bytes 9220
  95.1 38.1 %copy-start.36 = (bf16[768]{0:T(1024)(128)(2,1)S(1)}, bf16[768]{0:T(1024)(128)(2,1)}, u32[]{:S(2)}) copy-start(bf16[768]{0:T(1024)(128)(2,1)} %param.30) | copy-start | bytes 4612
  96.3 181.8 %reduce-scatter.6.cloned.1.call-start = ((), (), s32[]{:S(2)}) async-start(), calls=%async_computation.10 | async-start | bytes 3932160 | tf_op jit(solution)/shard_map/reduce_scatter | solution.py:182
  96.3 30.1 %collective-permute-start.3 = (bf16[512,768]{1,0:T(8,128)(2,1)}, bf16[512,768]{1,0:T(8,128)(2,1)}, u32[]{:S(2)}, u32[]{:S(2)}) collective-permute-start(bf16[512,768]{1,0:T(8,128)(2,1)} %param.33), channel_id=1, source_target_pairs={{0,1},{1,2},{2,3},{3,0},{4,5},{5,6},{6,7},{7,4},{8,9},{9,10},{10,1... | collective-permute-start | bytes 2359304 | tf_op jit(solution)/shard_map/ppermute | solution.py:36
  126.5 43.9 %collective-permute-start.4 = (bf16[512,768]{1,0:T(8,128)(2,1)}, bf16[512,768]{1,0:T(8,128)(2,1)}, u32[]{:S(2)}, u32[]{:S(2)}) collective-permute-start(bf16[512,768]{1,0:T(8,128)(2,1)} %collective-permute-done.3), channel_id=1, source_target_pairs={{0,1},{1,2},{2,3},{3,0},{4,5},{5,6},{6,7},{7,4},{8,9},{9,10},{10,1... | collective-permute-start | bytes 2359304 | tf_op jit(solution)/shard_map/ppermute | solution.py:36
  133.1 48.8 %copy-start.12 = (bf16[512,768]{1,0:T(8,128)(2,1)S(1)}, bf16[512,768]{1,0:T(8,128)(2,1)}, u32[]{:S(2)}) copy-start(bf16[512,768]{1,0:T(8,128)(2,1)} %param.33) | copy-start | bytes 2359300
  170.4 29.6 %collective-permute-start.5 = (bf16[512,768]{1,0:T(8,128)(2,1)}, bf16[512,768]{1,0:T(8,128)(2,1)S(1)}, u32[]{:S(2)}, u32[]{:S(2)}) collective-permute-start(bf16[512,768]{1,0:T(8,128)(2,1)} %collective-permute-done.4), channel_id=1, source_target_pairs={{0,1},{1,2},{2,3},{3,0},{4,5},{5,6},{6,7},{7,4},{8,9},{9,10},{10,1... | collective-permute-start | bytes 2359304 | tf_op jit(solution)/shard_map/ppermute | solution.py:36
  201.0 6.2 %copy-start.44 = (bf16[768,768]{1,0:T(8,128)(2,1)S(1)}, bf16[768,768]{1,0:T(8,128)(2,1)}, u32[]{:S(2)}) copy-start(bf16[768,768]{1,0:T(8,128)(2,1)} %param.31) | copy-start | bytes 3538948
  207.2 8.0 %copy-start.40 = (bf16[768,768]{1,0:T(8,128)(2,1)S(1)}, bf16[768,768]{1,0:T(8,128)(2,1)}, u32[]{:S(2)}) copy-start(bf16[768,768]{1,0:T(8,128)(2,1)} %param.29) | copy-start | bytes 3538948
  219.3 62.0 %copy-start.30 = (f32[768]{0:T(1024)S(1)}, f32[768]{0:T(1024)}, u32[]{:S(2)}) copy-start(f32[768]{0:T(1024)} %param.32) | copy-start | bytes 9220
  292.7 15.7 %all-to-all-start.3 = ((f32[4,3,100,64]{2,3,1,0:T(8,128)}), f32[4,3,100,64]{2,3,1,0:T(8,128)S(1)}, u32[]{:S(2)}, u32[]{:S(2)}) async-start(f32[4,3,100,64]{2,3,1,0:T(8,128)} %bitcast.123), calls=%async_computation.4 | async-start | bytes 786432 | tf_op jit(solution)/shard_map/all_to_all | solution.py:71
  330.9 44.8 %all-to-all-start.4 = ((bf16[4,562,384]{2,1,0:T(8,128)(2,1)}), bf16[4,562,384]{2,1,0:T(8,128)(2,1)}, u32[]{:S(2)}, u32[]{:S(2)}) async-start(bf16[4,562,384]{2,1,0:T(8,128)(2,1)} %pad_maximum_fusion.1), calls=%async_computation.5 | async-start | bytes 3489792 | tf_op jit(solution)/shard_map/all_to_all | solution.py:275
  335.4 156.2 %reduce-scatter.8.cloned.1.call-start = ((), (), s32[]{:S(2)}) async-start(), calls=%async_computation.11 | async-start | bytes 11059200 | tf_op jit(solution)/shard_map/reduce_scatter | solution.py:317
  336.4 6.5 %copy-start.7 = (f32[512,768]{1,0:T(8,128)S(1)}, f32[512,768]{1,0:T(8,128)}, u32[]{:S(2)}) copy-start(f32[512,768]{1,0:T(8,128)} %copy-done.6) | copy-start | bytes 4718596
  413.8 135.0 %reduce-scatter.10.cloned.1.call-start = ((), (), s32[]{:S(2)}) async-start(), calls=%async_computation.12 | async-start | bytes 5308416
  441.2 20.5 %collective-permute-start = (bf16[512,768]{1,0:T(8,128)(2,1)S(1)}, bf16[512,768]{1,0:T(8,128)(2,1)S(1)}, u32[]{:S(2)}, u32[]{:S(2)}) collective-permute-start(bf16[512,768]{1,0:T(8,128)(2,1)S(1)} %fusion.55), channel_id=1, source_target_pairs={{0,1},{1,2},{2,3},{3,0},{4,5},{5,6},{6,7},{7,4},{8,9},{9,10},{10,1... | collective-permute-start | bytes 2359304 | tf_op jit(solution)/shard_map/ppermute | solution.py:36
  463.3 19.7 %collective-permute-start.1 = (bf16[512,768]{1,0:T(8,128)(2,1)S(1)}, bf16[512,768]{1,0:T(8,128)(2,1)S(1)}, u32[]{:S(2)}, u32[]{:S(2)}) collective-permute-start(bf16[512,768]{1,0:T(8,128)(2,1)S(1)} %fusion.40), channel_id=1, source_target_pairs={{0,1},{1,2},{2,3},{3,0},{4,5},{5,6},{6,7},{7,4},{8,9},{9,10},{10,1... | collective-permute-start | bytes 2359304 | tf_op jit(solution)/shard_map/ppermute | solution.py:36
  485.4 22.5 %copy-start.10 = (f32[512,768]{1,0:T(8,128)S(1)}, f32[512,768]{1,0:T(8,128)}, u32[]{:S(2)}) copy-start(f32[512,768]{1,0:T(8,128)} %get-tuple-element.98) | copy-start | bytes 4718596
  485.5 22.5 %collective-permute-start.2 = (bf16[512,768]{1,0:T(8,128)(2,1)}, bf16[512,768]{1,0:T(8,128)(2,1)S(1)}, u32[]{:S(2)}, u32[]{:S(2)}) collective-permute-start(bf16[512,768]{1,0:T(8,128)(2,1)} %fusion.39), channel_id=1, source_target_pairs={{0,1},{1,2},{2,3},{3,0},{4,5},{5,6},{6,7},{7,4},{8,9},{9,10},{10,1... | collective-permute-start | bytes 2359304 | tf_op jit(solution)/shard_map/ppermute | solution.py:36
  491.7 62.8 %all-to-all-start.5 = ((f32[4,24,3084]{2,1,0:T(8,128)}), f32[4,24,3084]{2,1,0:T(8,128)}, u32[]{:S(2)}, u32[]{:S(2)}) async-start(f32[4,24,3084]{2,1,0:T(8,128)} %bitcast.116), calls=%async_computation.7 | async-start | bytes 2457600 | tf_op jit(solution)/shard_map/all_to_all | solution.py:71
  496.2 54.4 %copy-start.38 = (f32[512]{0:T(512)S(1)}, f32[512]{0:T(512)}, u32[]{:S(2)}) copy-start(f32[512]{0:T(512)} %get-tuple-element.83) | copy-start | bytes 6148
  496.2 54.4 %copy-start.37 = (f32[512]{0:T(512)S(1)}, f32[512]{0:T(512)}, u32[]{:S(2)}) copy-start(f32[512]{0:T(512)} %get-tuple-element.84) | copy-start | bytes 6148
  496.2 54.5 %copy-start.33 = (f32[768]{0:T(1024)S(1)}, f32[768]{0:T(1024)}, u32[]{:S(2)}) copy-start(f32[768]{0:T(1024)} %param.19) | copy-start | bytes 9220
  550.7 8.0 %copy-start.1 = (bf16[768,1536]{1,0:T(8,128)(2,1)S(1)}, bf16[768,1536]{1,0:T(8,128)(2,1)}, u32[]{:S(2)}) copy-start(bf16[768,1536]{1,0:T(8,128)(2,1)} %param.23) | copy-start | bytes 7077892
  (37 other events, 103.1 us)
Sparse Core Ops, SparseCore 0:
  96.4 87.6 all-gather.1
  219.4 58.6 reduce-scatter.5
  413.9 77.6 reduce-scatter.7
  495.0 53.7 reduce-scatter.9

commit v3 on v2

--- a/solution.py
+++ b/solution.py
@@ -49,9 +49,11 @@
     return out.reshape((group_size * x.shape[0],) + x.shape[1:])
 
 
-def ring_reduce(partial, group_size, wire_dtype):
+def ring_reduce(partial, group_size, wire_dtype, after):
     me = lax.axis_index("mp")
-    blocks = partial.reshape((group_size, -1) + partial.shape[1:])
+    blocks, _ = lax.optimization_barrier(
+        (partial.reshape((group_size, -1) + partial.shape[1:]), after)
+    )
 
     def block(owner):
         return lax.dynamic_index_in_dim(
@@ -189,8 +191,6 @@
     ).astype(jnp.float32)
 
     out_partial = jnp.dot(hidden, w_down, preferred_element_type=jnp.float32)
-    result = ring_reduce(out_partial, group_size, jnp.bfloat16)
-    block_output = (residual + result).astype(jnp.bfloat16)
 
     upstream = cotangent.astype(jnp.float32)
     grad_down_bias = jnp.sum(upstream, axis=0)
@@ -203,7 +203,7 @@
         (lax.axis_index("mp") * bias_part.shape[0],),
     )
     ff_grads = lax.psum_scatter(
-        jnp.concatenate([grad_up, grad_down_t], axis=1), "dp", scatter_dimension=0, tiled=True
+        jnp.stack([grad_up, grad_down_t]), "dp", scatter_dimension=1, tiled=True
     )
 
     middle_norm_grad, grad_gain_two, grad_shift_two = norm_backward(
@@ -273,6 +273,9 @@
     )
 
     incoming = lax.all_to_all(outgoing, "mp", split_axis=0, concat_axis=0, tiled=True)
+
+    result = ring_reduce(out_partial, group_size, jnp.bfloat16, incoming)
+    block_output = (residual + result).astype(jnp.bfloat16)
 
     returned = incoming[:, :tok_rows].reshape(group_size, tok_rows, 2, local_heads * head_dim)
     grad_keyval = returned.transpose(1, 2, 0, 3).reshape(tok_rows, 2 * model_width)
@@ -316,9 +319,8 @@
     reduced = scatter_sum(
         lax.psum_scatter(packed_grads, "dp", scatter_dimension=0, tiled=True), group_size
     )
-    ff_width = grad_up.shape[1]
-    up_share = ff_grads[:, :ff_width]
-    down_share = ff_grads[:, ff_width:].T
+    up_share = ff_grads[0]
+    down_share = ff_grads[1].T
     col = 0
     pieces = []
     for width in (model_width, 2 * model_width, model_width):

time: 574 us -> 600 us (1.045)
  waiting for transfers between devices: 315 us -> 343 us
    reduce_scatter x0 -> x1, waiting for transfers between devices: none -> 52.4 us  [block_body(): lax.psum_scatter(jnp.stack([grad_up, grad_down_t]), 'dp', scatter_dimensi...]
    unnamed x5 -> x4, waiting for transfers between devices: 38.3 us -> 0.07 us
    reduce_scatter x1, waiting for transfers between devices: 6.19 us -> 32.9 us  [block_body(): lax.psum_scatter(packed_grads, 'dp', scatter_dimension=0, tiled=True)]
    ppermute x6, waiting for transfers between devices: 131 us -> 118 us  [ring_shift(): lax.ppermute(x, 'mp', [(i, (i + 1) % group_size) for i in range(group_siz...]
    unnamed x111 -> x108, local copies, waits for them, and re-layouts: 18.5 us -> 10.3 us
  transfers between devices with their start and end apart: 15 -> 15, of which waited for: 13 -> 12; matrix products, arithmetic and copies ran while one was open for 11% -> 10% of each run, Pallas kernels for 0% -> 0%
where the time goes in v3:
time: 600 us; the launch traced here: 592 us
  waiting for transfers between devices  343 us (57%)
  local copies, waits for them, and re-layouts  77.9 us (13%)
  matrix products  70.7 us (12%)
  starting transfers between devices  42.9 us (7%)
  other arithmetic  33.2 us (6%)
  between operations  14.7 us (2%)
  blocking collectives  9.55 us (2%)
    ppermute x6, waiting for transfers between devices, ring_shift(): lax.ppermute(x, 'mp', [(i, (i + 1) % group_size) for i in range(group_siz...  118 us
    reduce_scatter x1, waiting for transfers between devices, block_body(): lax.psum_scatter(jnp.einsum('tf,df->td', grad_before, w_up, preferred_ele...  58.8 us
    reduce_scatter x1, waiting for transfers between devices, block_body(): lax.psum_scatter(jnp.stack([grad_up, grad_down_t]), 'dp', scatter_dimensi...  52.4 us
    all_to_all x1, waiting for transfers between devices, block_body(): lax.all_to_all(packed, 'mp', split_axis=2, concat_axis=0, tiled=True)  35.4 us
    reduce_scatter x1, waiting for transfers between devices, block_body(): lax.psum_scatter(packed_grads, 'dp', scatter_dimension=0, tiled=True)  32.9 us
    all_to_all x1, waiting for transfers between devices, block_body(): lax.all_to_all(outgoing, 'mp', split_axis=0, concat_axis=0, tiled=True)  29.5 us
    ppermute x6, starting transfers between devices, ring_shift(): lax.ppermute(x, 'mp', [(i, (i + 1) % group_size) for i in range(group_siz...  18.4 us
    all_to_all x3, waiting for transfers between devices, scatter_sum(): lax.all_to_all(pieces, 'mp', split_axis=0, concat_axis=0, tiled=True)  15.8 us
  transfers between devices with their start and end apart: 15, of which 12 were waited for; matrix products, arithmetic and copies ran while one was open for 10% of the time, Pallas kernels for 0%

profile of v3, /device:TPU:0, one launch (start us, length us, event | category | flops | bytes accessed | tf_op | source)
XLA Modules:
  0.0 592.0 jit_solution(1005368471742867411)
XLA Ops:
  18.5 6.3 %all-to-all-start = ((f32[4,3,100,65]{2,3,1,0:T(8,128)}), f32[4,3,100,65]{2,3,1,0:T(8,128)}, u32[]{:S(2)}, u32[]{:S(2)}) async-start(f32[4,3,100,65]{2,3,1,0:T(8,128)} %pad_maximum_fusion.2), calls=%async_computation | async-start | bytes 884736 | tf_op jit(solution)/shard_map/all_to_all | solution.py:73
  32.8 4.9 all-to-all-done
  37.7 4.3 all-to-all-start.1
  43.2 35.4 %all-to-all-done.1 = bf16[512,2,4,192]{0,3,1,2:T(8,128)(2,1)} async-done(((bf16[512,2,4,192]{0,3,1,2:T(8,128)(2,1)}), bf16[512,2,4,192]{0,3,1,2:T(8,128)(2,1)}, u32[]{:S(2)}, u32[]{:S(2)}) %all-to-all-start.1) | async-done | bytes 1572896 | tf_op jit(solution)/shard_map/all_to_all | solution.py:138
  82.8 9.5 %all_to_all.43 = bf16[4,3,100,64]{2,3,1,0:T(8,128)(2,1)S(1)} all-to-all(bf16[4,3,100,64]{2,3,1,0:T(8,128)(2,1)S(1)} %broadcast_in_dim.23), channel_id=1, replica_groups=mesh['dp'=8,'mp'=4] {'mp'}, dimensions={0} | all-to-all | bytes 307200 | tf_op jit(solution)/shard_map/all_to_all | solution.py:79
  97.2 29.3 %collective-permute-done = bf16[512,768]{1,0:T(8,128)(2,1)} collective-permute-done((bf16[512,768]{1,0:T(8,128)(2,1)}, bf16[512,768]{1,0:T(8,128)(2,1)}, u32[]{:S(2)}, u32[]{:S(2)}) %collective-permute-start) | collective-permute-done | bytes 786464 | tf_op jit(solution)/shard_map/ppermute | solution.py:36
  126.4 6.6 %collective-permute-start.1 = (bf16[512,768]{1,0:T(8,128)(2,1)}, bf16[512,768]{1,0:T(8,128)(2,1)}, u32[]{:S(2)}, u32[]{:S(2)}) collective-permute-start(bf16[512,768]{1,0:T(8,128)(2,1)} %collective-permute-done), channel_id=1, source_target_pairs={{0,1},{1,2},{2,3},{3,0},{4,5},{5,6},{6,7},{7,4},{8,9},{9,10},{10,1... | collective-permute-start | bytes 2359304 | tf_op jit(solution)/shard_map/ppermute | solution.py:36
  133.1 37.3 %collective-permute-done.1 = bf16[512,768]{1,0:T(8,128)(2,1)} collective-permute-done((bf16[512,768]{1,0:T(8,128)(2,1)}, bf16[512,768]{1,0:T(8,128)(2,1)}, u32[]{:S(2)}, u32[]{:S(2)}) %collective-permute-start.1) | collective-permute-done | bytes 786464 | tf_op jit(solution)/shard_map/ppermute | solution.py:36
  170.4 9.4 %collective-permute-start.2 = (bf16[512,768]{1,0:T(8,128)(2,1)}, bf16[512,768]{1,0:T(8,128)(2,1)S(1)}, u32[]{:S(2)}, u32[]{:S(2)}) collective-permute-start(bf16[512,768]{1,0:T(8,128)(2,1)} %collective-permute-done.1), channel_id=1, source_target_pairs={{0,1},{1,2},{2,3},{3,0},{4,5},{5,6},{6,7},{7,4},{8,9},{9,10},{10,1... | collective-permute-start | bytes 2359304 | tf_op jit(solution)/shard_map/ppermute | solution.py:36
  186.8 13.2 %collective-permute-done.2 = bf16[512,768]{1,0:T(8,128)(2,1)S(1)} collective-permute-done((bf16[512,768]{1,0:T(8,128)(2,1)}, bf16[512,768]{1,0:T(8,128)(2,1)S(1)}, u32[]{:S(2)}, u32[]{:S(2)}) %collective-permute-start.2) | collective-permute-done | bytes 786464 | tf_op jit(solution)/shard_map/ppermute | solution.py:36
  201.0 6.2 %multiply_convert_fusion = (bf16[2048,768]{1,0:T(8,128)(2,1)}, f32[2048,768]{1,0:T(8,128)S(1)}) fusion(f32[768]{0:T(1024)S(1)} %convert_element_type.142, bf16[2048,768]{1,0:T(8,128)(2,1)} %all-gather.2.cloned.1.call-done, bf16[768,768]{1,0:T(8,128)(2,1)} %param.29), kind=kOutput, calls=%fused_computation.8 | convolution fusion | flops 2425356288 | bytes 13765632 | tf_op jit(solution)/shard_map/dot_general | solution.py:177
  207.2 6.4 %convert_reduce_fusion = (f32[768]{0:T(1024)}, bf16[2048,768]{1,0:T(8,128)(2,1)S(1)}) fusion(f32[2048,768]{1,0:T(8,128)S(1)} %get-tuple-element.49, f32[768]{0:T(1024)S(1)} %convert_element_type.142, bf16[2048,768]{1,0:T(8,128)(2,1)} %bitcast.16, bf16[768,768]{1,0:T(8,128)(2,1)S(1)} %copy-done.45), kind=kOutput, calls=%fused_computation.7 | convolution fusion | flops 2436365568 | bytes 13768704 | tf_op jit(solution)/shard_map/td,fd->tf/dot_general | solution.py:182
  215.2 4.0 convolution_convert_fusion
  219.3 58.8 %reduce-scatter.4.cloned.1.call-done = bf16[512,768]{1,0:T(8,128)(2,1)} async-done(((bf16[2048,768]{1,0:T(8,128)(2,1)}), bf16[512,768]{1,0:T(8,128)(2,1)}) %reduce-scatter.4.cloned.1.call-update) | async-done | bytes 786448 | tf_op jit(solution)/shard_map/reduce_scatter | solution.py:184
  281.2 3.8 convert_reduce_fusion.5
  292.6 4.1 all-to-all-start.3
  297.5 10.9 %all-to-all-done.3 = f32[4,3,100,64]{2,3,1,0:T(8,128)S(1)} async-done(((f32[4,3,100,64]{2,3,1,0:T(8,128)}), f32[4,3,100,64]{2,3,1,0:T(8,128)S(1)}, u32[]{:S(2)}, u32[]{:S(2)}) %all-to-all-start.3) | async-done | bytes 307232 | tf_op jit(solution)/shard_map/all_to_all | solution.py:73
  309.0 3.5 fusion.9
  327.6 3.3 pad_maximum_fusion.1
  330.9 4.5 all-to-all-start.4
  342.9 3.3 fusion.60
  346.2 29.5 %all-to-all-done.4 = bf16[4,562,384]{2,1,0:T(8,128)(2,1)} async-done(((bf16[4,562,384]{2,1,0:T(8,128)(2,1)}), bf16[4,562,384]{2,1,0:T(8,128)(2,1)}, u32[]{:S(2)}, u32[]{:S(2)}) %all-to-all-start.4) | async-done | bytes 1726496 | tf_op jit(solution)/shard_map/all_to_all | solution.py:275
  385.4 3.9 fusion.65
  397.5 3.8 fusion.67
  406.2 12.4 %concatenate.34 = f32[768,3084]{1,0:T(8,128)} concatenate(f32[768,768]{1,0:T(8,128)} %fusion.67, f32[768,1536]{1,0:T(8,128)} %fusion.65, f32[768,768]{1,0:T(8,128)} %fusion.60, f32[768,1]{1,0:T(8,128)} %stack.44, f32[768,1]{1,0:T(8,128)} %stack.45, f32[768,1]{1,0:T(8,128)} %stack.46, f32[768,1]{1,0:T(8,128)} %stack.47, f32[768,1]{1,0:T(8,128)} %stack.48, f32[768,1]{1,0:T(8,128)} %stack.49, ...), dimensions={1} | concatenate | bytes 18948096 | tf_op jit(solution)/shard_map/concatenate | solution.py:315
  418.9 5.7 convolution_bitcast_fusion
  430.4 5.9 fusion.75
  439.9 20.8 %collective-permute-done.3 = bf16[512,768]{1,0:T(8,128)(2,1)} collective-permute-done((bf16[512,768]{1,0:T(8,128)(2,1)}, bf16[512,768]{1,0:T(8,128)(2,1)}, u32[]{:S(2)}, u32[]{:S(2)}) %collective-permute-start.3) | collective-permute-done | bytes 786464 | tf_op jit(solution)/shard_map/ppermute | solution.py:36
  463.6 32.9 %reduce-scatter.6.cloned.1.call-done = f32[96,3084]{1,0:T(8,128)} async-done(((f32[768,3084]{1,0:T(8,128)}), f32[96,3084]{1,0:T(8,128)}) %reduce-scatter.6.cloned.1.call-update) | async-done | bytes 1184272 | tf_op jit(solution)/shard_map/reduce_scatter | solution.py:320
  496.5 4.6 all-to-all-start.5
  501.1 52.4 %reduce-scatter.8.cloned.1.call-done = f32[2,96,768]{2,1,0:T(8,128)} async-done(((f32[2,768,768]{2,1,0:T(8,128)}), f32[2,96,768]{2,1,0:T(8,128)}) %reduce-scatter.8.cloned.1.call-update) | async-done | bytes 589840 | tf_op jit(solution)/shard_map/reduce_scatter | solution.py:205
  560.7 17.7 %collective-permute-done.5 = bf16[512,768]{1,0:T(8,128)(2,1)S(1)} collective-permute-done((bf16[512,768]{1,0:T(8,128)(2,1)S(1)}, bf16[512,768]{1,0:T(8,128)(2,1)S(1)}, u32[]{:S(2)}, u32[]{:S(2)}) %collective-permute-start.5) | collective-permute-done | bytes 786464 | tf_op jit(solution)/shard_map/ppermute | solution.py:36
  (210 shorter events, 122.7 us)
Async XLA Ops:
  7.2 17.7 %copy-start = (bf16[768,1536]{1,0:T(8,128)(2,1)S(1)}, bf16[768,1536]{1,0:T(8,128)(2,1)}, u32[]{:S(2)}) copy-start(bf16[768,1536]{1,0:T(8,128)(2,1)} %param.23) | copy-start | bytes 7077892
  10.2 14.7 %copy-start.26 = (f32[512]{0:T(512)}, f32[512]{0:T(512)S(1)}, u32[]{:S(2)}) copy-start(f32[512]{0:T(512)S(1)} %add_rsqrt_fusion.1) | copy-start | bytes 6148
  16.0 8.9 %copy-start.35 = (f32[768]{0:T(1024)S(1)}, f32[768]{0:T(1024)}, u32[]{:S(2)}) copy-start(f32[768]{0:T(1024)} %param.24) | copy-start | bytes 9220
  18.5 19.2 %all-to-all-start = ((f32[4,3,100,65]{2,3,1,0:T(8,128)}), f32[4,3,100,65]{2,3,1,0:T(8,128)}, u32[]{:S(2)}, u32[]{:S(2)}) async-start(f32[4,3,100,65]{2,3,1,0:T(8,128)} %pad_maximum_fusion.2), calls=%async_computation | async-start | bytes 884736 | tf_op jit(solution)/shard_map/all_to_all | solution.py:73
  37.7 40.9 %all-to-all-start.1 = ((bf16[512,2,4,192]{0,3,1,2:T(8,128)(2,1)}), bf16[512,2,4,192]{0,3,1,2:T(8,128)(2,1)}, u32[]{:S(2)}, u32[]{:S(2)}) async-start(bf16[512,2,4,192]{0,3,1,2:T(8,128)(2,1)} %copy.78), calls=%async_computation.1 | async-start | bytes 3145728 | tf_op jit(solution)/shard_map/all_to_all | solution.py:138
  42.1 158.9 %all-gather.2.cloned.1.call-start = ((), (), s32[]{:S(2)}) async-start(), calls=%async_computation.9 | async-start | bytes 3932160 | tf_op jit(solution)/shard_map/all_gather | solution.py:175
  43.2 37.2 %copy-start.18 = (f32[3,100,65]{1,2,0:T(8,128)}, f32[3,100,65]{1,2,0:T(8,128)S(1)}, u32[]{:S(2)}) copy-start(f32[3,100,65]{1,2,0:T(8,128)S(1)} %reduce_sum.210) | copy-start | bytes 234004
  82.8 10.1 %copy-start.42 = (bf16[768,768]{1,0:T(8,128)(2,1)S(1)}, bf16[768,768]{1,0:T(8,128)(2,1)}, u32[]{:S(2)}) copy-start(bf16[768,768]{1,0:T(8,128)(2,1)} %param.25) | copy-start | bytes 3538948
  82.8 10.1 %copy-start.47 = (f32[768]{0:T(1024)S(1)}, f32[768]{0:T(1024)}, u32[]{:S(2)}) copy-start(f32[768]{0:T(1024)} %param.26) | copy-start | bytes 9220
  95.0 38.0 %copy-start.37 = (bf16[768]{0:T(1024)(128)(2,1)S(1)}, bf16[768]{0:T(1024)(128)(2,1)}, u32[]{:S(2)}) copy-start(bf16[768]{0:T(1024)(128)(2,1)} %param.30) | copy-start | bytes 4612
  96.2 181.8 %reduce-scatter.4.cloned.1.call-start = ((), (), s32[]{:S(2)}) async-start(), calls=%async_computation.10 | async-start | bytes 3932160 | tf_op jit(solution)/shard_map/reduce_scatter | solution.py:184
  96.3 30.1 %collective-permute-start = (bf16[512,768]{1,0:T(8,128)(2,1)}, bf16[512,768]{1,0:T(8,128)(2,1)}, u32[]{:S(2)}, u32[]{:S(2)}) collective-permute-start(bf16[512,768]{1,0:T(8,128)(2,1)} %param.33), channel_id=1, source_target_pairs={{0,1},{1,2},{2,3},{3,0},{4,5},{5,6},{6,7},{7,4},{8,9},{9,10},{10,1... | collective-permute-start | bytes 2359304 | tf_op jit(solution)/shard_map/ppermute | solution.py:36
  126.4 43.9 %collective-permute-start.1 = (bf16[512,768]{1,0:T(8,128)(2,1)}, bf16[512,768]{1,0:T(8,128)(2,1)}, u32[]{:S(2)}, u32[]{:S(2)}) collective-permute-start(bf16[512,768]{1,0:T(8,128)(2,1)} %collective-permute-done), channel_id=1, source_target_pairs={{0,1},{1,2},{2,3},{3,0},{4,5},{5,6},{6,7},{7,4},{8,9},{9,10},{10,1... | collective-permute-start | bytes 2359304 | tf_op jit(solution)/shard_map/ppermute | solution.py:36
  133.1 48.6 %copy-start.11 = (bf16[512,768]{1,0:T(8,128)(2,1)S(1)}, bf16[512,768]{1,0:T(8,128)(2,1)}, u32[]{:S(2)}) copy-start(bf16[512,768]{1,0:T(8,128)(2,1)} %param.33) | copy-start | bytes 2359300
  170.4 29.6 %collective-permute-start.2 = (bf16[512,768]{1,0:T(8,128)(2,1)}, bf16[512,768]{1,0:T(8,128)(2,1)S(1)}, u32[]{:S(2)}, u32[]{:S(2)}) collective-permute-start(bf16[512,768]{1,0:T(8,128)(2,1)} %collective-permute-done.1), channel_id=1, source_target_pairs={{0,1},{1,2},{2,3},{3,0},{4,5},{5,6},{6,7},{7,4},{8,9},{9,10},{10,1... | collective-permute-start | bytes 2359304 | tf_op jit(solution)/shard_map/ppermute | solution.py:36
  201.0 6.2 %copy-start.45 = (bf16[768,768]{1,0:T(8,128)(2,1)S(1)}, bf16[768,768]{1,0:T(8,128)(2,1)}, u32[]{:S(2)}) copy-start(bf16[768,768]{1,0:T(8,128)(2,1)} %param.31) | copy-start | bytes 3538948
  207.2 8.0 %copy-start.41 = (bf16[768,768]{1,0:T(8,128)(2,1)S(1)}, bf16[768,768]{1,0:T(8,128)(2,1)}, u32[]{:S(2)}) copy-start(bf16[768,768]{1,0:T(8,128)(2,1)} %param.29) | copy-start | bytes 3538948
  219.2 62.0 %copy-start.30 = (f32[768]{0:T(1024)S(1)}, f32[768]{0:T(1024)}, u32[]{:S(2)}) copy-start(f32[768]{0:T(1024)} %param.32) | copy-start | bytes 9220
  281.2 4.9 copy-start.43
  292.6 15.7 %all-to-all-start.3 = ((f32[4,3,100,64]{2,3,1,0:T(8,128)}), f32[4,3,100,64]{2,3,1,0:T(8,128)S(1)}, u32[]{:S(2)}, u32[]{:S(2)}) async-start(f32[4,3,100,64]{2,3,1,0:T(8,128)} %bitcast.129), calls=%async_computation.4 | async-start | bytes 786432 | tf_op jit(solution)/shard_map/all_to_all | solution.py:73
  330.9 44.8 %all-to-all-start.4 = ((bf16[4,562,384]{2,1,0:T(8,128)(2,1)}), bf16[4,562,384]{2,1,0:T(8,128)(2,1)}, u32[]{:S(2)}, u32[]{:S(2)}) async-start(bf16[4,562,384]{2,1,0:T(8,128)(2,1)} %pad_maximum_fusion.1), calls=%async_computation.5 | async-start | bytes 3489792 | tf_op jit(solution)/shard_map/all_to_all | solution.py:275
  335.4 161.1 %reduce-scatter.6.cloned.1.call-start = ((), (), s32[]{:S(2)}) async-start(), calls=%async_computation.11 | async-start | bytes 11059200 | tf_op jit(solution)/shard_map/reduce_scatter | solution.py:320
  336.4 6.5 %copy-start.6 = (f32[512,768]{1,0:T(8,128)S(1)}, f32[512,768]{1,0:T(8,128)}, u32[]{:S(2)}) copy-start(f32[512,768]{1,0:T(8,128)} %copy-done.5) | copy-start | bytes 4718596
  418.6 134.9 %reduce-scatter.8.cloned.1.call-start = ((), (), s32[]{:S(2)}) async-start(), calls=%async_computation.12 | async-start | bytes 5308416 | tf_op jit(solution)/shard_map/reduce_scatter | solution.py:205
  418.9 5.7 copy-start.40
  418.9 5.7 copy-start.52
  439.9 20.8 %collective-permute-start.3 = (bf16[512,768]{1,0:T(8,128)(2,1)}, bf16[512,768]{1,0:T(8,128)(2,1)}, u32[]{:S(2)}, u32[]{:S(2)}) collective-permute-start(bf16[512,768]{1,0:T(8,128)(2,1)} %fusion.55), channel_id=1, source_target_pairs={{0,1},{1,2},{2,3},{3,0},{4,5},{5,6},{6,7},{7,4},{8,9},{9,10},{10,1... | collective-permute-start | bytes 2359304 | tf_op jit(solution)/shard_map/ppermute | solution.py:36
  463.6 91.8 %collective-permute-start.4 = (bf16[512,768]{1,0:T(8,128)(2,1)}, bf16[512,768]{1,0:T(8,128)(2,1)}, u32[]{:S(2)}, u32[]{:S(2)}) collective-permute-start(bf16[512,768]{1,0:T(8,128)(2,1)} %fusion.40), channel_id=1, source_target_pairs={{0,1},{1,2},{2,3},{3,0},{4,5},{5,6},{6,7},{7,4},{8,9},{9,10},{10,1... | collective-permute-start | bytes 2359304 | tf_op jit(solution)/shard_map/ppermute | solution.py:36
  496.5 84.6 %all-to-all-start.5 = ((f32[4,24,3084]{2,1,0:T(8,128)}), f32[4,24,3084]{2,1,0:T(8,128)}, u32[]{:S(2)}, u32[]{:S(2)}) async-start(f32[4,24,3084]{2,1,0:T(8,128)} %bitcast.122), calls=%async_computation.7 | async-start | bytes 2457600 | tf_op jit(solution)/shard_map/all_to_all | solution.py:73
  553.5 5.4 copy-start.39
  557.4 21.0 %collective-permute-start.5 = (bf16[512,768]{1,0:T(8,128)(2,1)S(1)}, bf16[512,768]{1,0:T(8,128)(2,1)S(1)}, u32[]{:S(2)}, u32[]{:S(2)}) collective-permute-start(bf16[512,768]{1,0:T(8,128)(2,1)S(1)} %fusion.39), channel_id=1, source_target_pairs={{0,1},{1,2},{2,3},{3,0},{4,5},{5,6},{6,7},{7,4},{8,9},{9,10},{10,1... | collective-permute-start | bytes 2359304 | tf_op jit(solution)/shard_map/ppermute | solution.py:36
  558.9 19.4 %copy-start.9 = (f32[512,768]{1,0:T(8,128)S(1)}, f32[512,768]{1,0:T(8,128)}, u32[]{:S(2)}) copy-start(f32[512,768]{1,0:T(8,128)} %get-tuple-element.36) | copy-start | bytes 4718596
  (36 other events, 95.9 us)
Sparse Core Ops, SparseCore 0:
  96.4 87.6 all-gather.1
  219.4 58.6 reduce-scatter.3
  418.7 77.6 reduce-scatter.5
  499.8 53.7 reduce-scatter.7

commit v4 on v3

--- a/solution.py
+++ b/solution.py
@@ -47,25 +47,6 @@
             out, cur, jnp.remainder(me + group_size - step, group_size), 0
         )
     return out.reshape((group_size * x.shape[0],) + x.shape[1:])
-
-
-def ring_reduce(partial, group_size, wire_dtype, after):
-    me = lax.axis_index("mp")
-    blocks, _ = lax.optimization_barrier(
-        (partial.reshape((group_size, -1) + partial.shape[1:]), after)
-    )
-
-    def block(owner):
-        return lax.dynamic_index_in_dim(
-            blocks, jnp.remainder(owner + 2 * group_size, group_size), 0, keepdims=False
-        )
-
-    acc = block(me - 1).astype(wire_dtype)
-    for step in range(1, group_size - 1):
-        arrived = ring_shift(acc, group_size)
-        acc = (arrived.astype(jnp.float32) + block(me - 1 - step)).astype(wire_dtype)
-    arrived = ring_shift(acc, group_size)
-    return arrived.astype(jnp.float32) + block(me)
 
 
 def scatter_sum(partial, group_size):
@@ -206,6 +187,16 @@
         jnp.stack([grad_up, grad_down_t]), "dp", scatter_dimension=1, tiled=True
     )
 
+    result = lax.psum_scatter(
+        out_partial.astype(jnp.bfloat16), "mp", scatter_dimension=0, tiled=True
+    ).astype(jnp.float32)
+    block_output = (residual + result).astype(jnp.bfloat16)
+
+    scores_again = score_scale * jnp.einsum(
+        "hcd,jhd->hcj", centroids, key_rows, preferred_element_type=jnp.float32
+    )
+    probs_again = jnp.exp(scores_again - logsum)
+
     middle_norm_grad, grad_gain_two, grad_shift_two = norm_backward(
         grad_second, standard_two, factor_two, ln2_gain
     )
@@ -225,10 +216,6 @@
 
     summary_grad = scatter_sum(summary_grad, group_size).astype(jnp.bfloat16)
 
-    scores_again = score_scale * jnp.einsum(
-        "hcd,jhd->hcj", centroids, key_rows, preferred_element_type=jnp.float32
-    )
-    probs_again = jnp.exp(scores_again - logsum)
     grad_values = jnp.einsum(
         "hcj,hcd->jhd",
         probs_again.astype(jnp.bfloat16),
@@ -273,9 +260,6 @@
     )
 
     incoming = lax.all_to_all(outgoing, "mp", split_axis=0, concat_axis=0, tiled=True)
-
-    result = ring_reduce(out_partial, group_size, jnp.bfloat16, incoming)
-    block_output = (residual + result).astype(jnp.bfloat16)
 
     returned = incoming[:, :tok_rows].reshape(group_size, tok_rows, 2, local_heads * head_dim)
     grad_keyval = returned.transpose(1, 2, 0, 3).reshape(tok_rows, 2 * model_width)

time: 600 us -> 661 us (1.10)
  waiting for transfers between devices: 343 us -> 410 us
    reduce_scatter x0 -> x1, waiting for transfers between devices: none -> 76 us  [block_body(): lax.psum_scatter(out_partial.astype(jnp.bfloat16), 'mp', scatter_dimensio...]
    ppermute x6 -> x3, waiting for transfers between devices: 118 us -> 79.6 us  [ring_shift(): lax.ppermute(x, 'mp', [(i, (i + 1) % group_size) for i in range(group_siz...]
    reduce_scatter x1, waiting for transfers between devices: 32.9 us -> 58.1 us  [block_body(): lax.psum_scatter(packed_grads, 'dp', scatter_dimension=0, tiled=True)]
    ppermute x6 -> x3, starting transfers between devices: 18.4 us -> 16.9 us  [ring_shift(): lax.ppermute(x, 'mp', [(i, (i + 1) % group_size) for i in range(group_siz...]
  transfers between devices with their start and end apart: 15 -> 13, of which waited for: 12 -> 11; matrix products, arithmetic and copies ran while one was open for 10% -> 8% of each run, Pallas kernels for 0% -> 0%
where the time goes in v4:
time: 661 us; the launch traced here: 653 us
  waiting for transfers between devices  410 us (62%)
  local copies, waits for them, and re-layouts  74.4 us (11%)
  matrix products  73 us (11%)
  starting transfers between devices  41.4 us (6%)
  other arithmetic  29.7 us (4%)
  between operations  14.6 us (2%)
  blocking collectives  9.55 us (1%)
    ppermute x3, waiting for transfers between devices, ring_shift(): lax.ppermute(x, 'mp', [(i, (i + 1) % group_size) for i in range(group_siz...  79.6 us
    reduce_scatter x1, waiting for transfers between devices, block_body(): lax.psum_scatter(out_partial.astype(jnp.bfloat16), 'mp', scatter_dimensio...  76 us
    reduce_scatter x1, waiting for transfers between devices, block_body(): lax.psum_scatter(jnp.einsum('tf,df->td', grad_before, w_up, preferred_ele...  58.9 us
    reduce_scatter x1, waiting for transfers between devices, block_body(): lax.psum_scatter(packed_grads, 'dp', scatter_dimension=0, tiled=True)  58.1 us
    reduce_scatter x1, waiting for transfers between devices, block_body(): lax.psum_scatter(jnp.stack([grad_up, grad_down_t]), 'dp', scatter_dimensi...  56.9 us
    all_to_all x1, waiting for transfers between devices, block_body(): lax.all_to_all(packed, 'mp', split_axis=2, concat_axis=0, tiled=True)  35.4 us
    all_to_all x1, waiting for transfers between devices, block_body(): lax.all_to_all(outgoing, 'mp', split_axis=0, concat_axis=0, tiled=True)  29.4 us
    ppermute x3, starting transfers between devices, ring_shift(): lax.ppermute(x, 'mp', [(i, (i + 1) % group_size) for i in range(group_siz...  16.9 us
  transfers between devices with their start and end apart: 13, of which 11 were waited for; matrix products, arithmetic and copies ran while one was open for 8% of the time, Pallas kernels for 0%

profile of v4, /device:TPU:0, one launch (start us, length us, event | category | flops | bytes accessed | tf_op | source)
XLA Modules:
  0.0 652.9 jit_solution(8904600303848215366)
XLA Ops:
  18.5 6.3 all-to-all-start
  32.8 4.9 all-to-all-done
  37.7 4.3 all-to-all-start.1
  43.2 35.4 %all-to-all-done.1 = bf16[512,2,4,192]{0,3,1,2:T(8,128)(2,1)} async-done(((bf16[512,2,4,192]{0,3,1,2:T(8,128)(2,1)}), bf16[512,2,4,192]{0,3,1,2:T(8,128)(2,1)}, u32[]{:S(2)}, u32[]{:S(2)}) %all-to-all-start.1) | async-done | bytes 1572896 | tf_op jit(solution)/shard_map/all_to_all | solution.py:119
  82.8 9.5 %all_to_all.43 = bf16[4,3,100,64]{2,3,1,0:T(8,128)(2,1)S(1)} all-to-all(bf16[4,3,100,64]{2,3,1,0:T(8,128)(2,1)S(1)} %broadcast_in_dim.23), channel_id=1, replica_groups=mesh['dp'=8,'mp'=4] {'mp'}, dimensions={0} | all-to-all | bytes 307200 | tf_op jit(solution)/shard_map/all_to_all | solution.py:60
  97.1 29.3 %collective-permute-done = bf16[512,768]{1,0:T(8,128)(2,1)} collective-permute-done((bf16[512,768]{1,0:T(8,128)(2,1)}, bf16[512,768]{1,0:T(8,128)(2,1)}, u32[]{:S(2)}, u32[]{:S(2)}) %collective-permute-start) | collective-permute-done | bytes 786464 | tf_op jit(solution)/shard_map/ppermute | solution.py:36
  126.4 6.6 %collective-permute-start.1 = (bf16[512,768]{1,0:T(8,128)(2,1)}, bf16[512,768]{1,0:T(8,128)(2,1)}, u32[]{:S(2)}, u32[]{:S(2)}) collective-permute-start(bf16[512,768]{1,0:T(8,128)(2,1)} %collective-permute-done), channel_id=1, source_target_pairs={{0,1},{1,2},{2,3},{3,0},{4,5},{5,6},{6,7},{7,4},{8,9},{9,10},{10,1... | collective-permute-start | bytes 2359304 | tf_op jit(solution)/shard_map/ppermute | solution.py:36
  133.0 37.3 %collective-permute-done.1 = bf16[512,768]{1,0:T(8,128)(2,1)} collective-permute-done((bf16[512,768]{1,0:T(8,128)(2,1)}, bf16[512,768]{1,0:T(8,128)(2,1)}, u32[]{:S(2)}, u32[]{:S(2)}) %collective-permute-start.1) | collective-permute-done | bytes 786464 | tf_op jit(solution)/shard_map/ppermute | solution.py:36
  170.3 9.4 %collective-permute-start.2 = (bf16[512,768]{1,0:T(8,128)(2,1)}, bf16[512,768]{1,0:T(8,128)(2,1)S(1)}, u32[]{:S(2)}, u32[]{:S(2)}) collective-permute-start(bf16[512,768]{1,0:T(8,128)(2,1)} %collective-permute-done.1), channel_id=1, source_target_pairs={{0,1},{1,2},{2,3},{3,0},{4,5},{5,6},{6,7},{7,4},{8,9},{9,10},{10,1... | collective-permute-start | bytes 2359304 | tf_op jit(solution)/shard_map/ppermute | solution.py:36
  186.8 13.1 %collective-permute-done.2 = bf16[512,768]{1,0:T(8,128)(2,1)S(1)} collective-permute-done((bf16[512,768]{1,0:T(8,128)(2,1)}, bf16[512,768]{1,0:T(8,128)(2,1)S(1)}, u32[]{:S(2)}, u32[]{:S(2)}) %collective-permute-start.2) | collective-permute-done | bytes 786464 | tf_op jit(solution)/shard_map/ppermute | solution.py:36
  200.8 6.2 multiply_convert_fusion
  207.0 6.4 convert_reduce_fusion
  215.1 4.1 convolution_convert_fusion
  219.1 58.9 %reduce-scatter.7.cloned.1.call-done = bf16[512,768]{1,0:T(8,128)(2,1)} async-done(((bf16[2048,768]{1,0:T(8,128)(2,1)}), bf16[512,768]{1,0:T(8,128)(2,1)}) %reduce-scatter.7.cloned.1.call-update) | async-done | bytes 786448 | tf_op jit(solution)/shard_map/reduce_scatter | solution.py:165
  281.2 3.8 convert_reduce_fusion.5
  292.6 4.1 all-to-all-start.3
  297.4 10.9 %all-to-all-done.3 = f32[4,3,100,64]{2,3,1,0:T(8,128)S(1)} async-done(((f32[4,3,100,64]{2,3,1,0:T(8,128)}), f32[4,3,100,64]{2,3,1,0:T(8,128)S(1)}, u32[]{:S(2)}, u32[]{:S(2)}) %all-to-all-start.3) | async-done | bytes 307232 | tf_op jit(solution)/shard_map/all_to_all | solution.py:54
  309.0 3.5 fusion.9
  327.5 3.3 pad_maximum_fusion.1
  330.9 4.5 all-to-all-start.4
  342.9 3.4 fusion.55
  346.3 29.4 %all-to-all-done.4 = bf16[4,562,384]{2,1,0:T(8,128)(2,1)} async-done(((bf16[4,562,384]{2,1,0:T(8,128)(2,1)}), bf16[4,562,384]{2,1,0:T(8,128)(2,1)}, u32[]{:S(2)}, u32[]{:S(2)}) %all-to-all-start.4) | async-done | bytes 1726496 | tf_op jit(solution)/shard_map/all_to_all | solution.py:262
  385.4 3.9 fusion.60
  397.4 3.8 fusion.62
  406.1 12.4 %concatenate.34 = f32[768,3084]{1,0:T(8,128)} concatenate(f32[768,768]{1,0:T(8,128)} %fusion.62, f32[768,1536]{1,0:T(8,128)} %fusion.60, f32[768,768]{1,0:T(8,128)} %fusion.55, f32[768,1]{1,0:T(8,128)} %stack.44, f32[768,1]{1,0:T(8,128)} %stack.45, f32[768,1]{1,0:T(8,128)} %stack.46, f32[768,1]{1,0:T(8,128)} %stack.47, f32[768,1]{1,0:T(8,128)} %stack.48, f32[768,1]{1,0:T(8,128)} %stack.49, ...), dimensions={1} | concatenate | bytes 18948096 | tf_op jit(solution)/shard_map/concatenate | solution.py:299
  418.5 6.5 %convolution_convert_fusion.1 = bf16[2048,768]{1,0:T(8,128)(2,1)} fusion(bf16[2048,768]{1,0:T(8,128)(2,1)} %get-tuple-element.46, bf16[768,768]{1,0:T(8,128)(2,1)} %param.31), kind=kOutput, calls=%fused_computation.14 | convolution fusion | flops 2417491968 | bytes 7471104 | tf_op jit(solution)/shard_map/dot_general | solution.py:174
  425.4 7.2 %convolution_bitcast_fusion = f32[1,768,768]{2,1,0:T(8,128)S(1)} fusion(bf16[2048,768]{1,0:T(8,128)(2,1)} %bitcast.15, bf16[2048,768]{1,0:T(8,128)(2,1)} %get-tuple-element.46), kind=kOutput, calls=%fused_computation.53 | convolution fusion | flops 2415919104 | bytes 8650752 | tf_op jit(solution)/shard_map/td,tf->df/dot_general | solution.py:178
  438.2 58.1 %reduce-scatter.9.cloned.1.call-done = f32[96,3084]{1,0:T(8,128)} async-done(((f32[768,3084]{1,0:T(8,128)}), f32[96,3084]{1,0:T(8,128)}) %reduce-scatter.9.cloned.1.call-update) | async-done | bytes 1184272 | tf_op jit(solution)/shard_map/reduce_scatter | solution.py:304
  496.4 4.6 all-to-all-start.5
  501.0 76.0 %reduce-scatter.5.cloned.1.call-done = bf16[512,768]{1,0:T(8,128)(2,1)} async-done(((bf16[2048,768]{1,0:T(8,128)(2,1)}), bf16[512,768]{1,0:T(8,128)(2,1)}) %reduce-scatter.5.cloned.1.call-update) | async-done | bytes 786448 | tf_op jit(solution)/shard_map/reduce_scatter | solution.py:190
  579.6 56.9 %reduce-scatter.11.cloned.1.call-done = f32[2,96,768]{2,1,0:T(8,128)} async-done(((f32[2,768,768]{2,1,0:T(8,128)}), f32[2,96,768]{2,1,0:T(8,128)}) %reduce-scatter.11.cloned.1.call-update) | async-done | bytes 589840 | tf_op jit(solution)/shard_map/reduce_scatter | solution.py:186
  638.4 3.6 fusion.30
  (192 shorter events, 110.7 us)
Async XLA Ops:
  7.2 17.7 %copy-start = (bf16[768,1536]{1,0:T(8,128)(2,1)S(1)}, bf16[768,1536]{1,0:T(8,128)(2,1)}, u32[]{:S(2)}) copy-start(bf16[768,1536]{1,0:T(8,128)(2,1)} %param.23) | copy-start | bytes 7077892
  10.2 14.7 %copy-start.22 = (f32[512]{0:T(512)}, f32[512]{0:T(512)S(1)}, u32[]{:S(2)}) copy-start(f32[512]{0:T(512)S(1)} %add_rsqrt_fusion.1) | copy-start | bytes 6148
  16.0 8.9 %copy-start.29 = (f32[768]{0:T(1024)S(1)}, f32[768]{0:T(1024)}, u32[]{:S(2)}) copy-start(f32[768]{0:T(1024)} %param.24) | copy-start | bytes 9220
  18.5 19.2 %all-to-all-start = ((f32[4,3,100,65]{2,3,1,0:T(8,128)}), f32[4,3,100,65]{2,3,1,0:T(8,128)}, u32[]{:S(2)}, u32[]{:S(2)}) async-start(f32[4,3,100,65]{2,3,1,0:T(8,128)} %pad_maximum_fusion.2), calls=%async_computation | async-start | bytes 884736 | tf_op jit(solution)/shard_map/all_to_all | solution.py:54
  37.7 40.9 %all-to-all-start.1 = ((bf16[512,2,4,192]{0,3,1,2:T(8,128)(2,1)}), bf16[512,2,4,192]{0,3,1,2:T(8,128)(2,1)}, u32[]{:S(2)}, u32[]{:S(2)}) async-start(bf16[512,2,4,192]{0,3,1,2:T(8,128)(2,1)} %copy.78), calls=%async_computation.1 | async-start | bytes 3145728 | tf_op jit(solution)/shard_map/all_to_all | solution.py:119
  42.1 158.8 %all-gather.2.cloned.1.call-start = ((), (), s32[]{:S(2)}) async-start(), calls=%async_computation.10 | async-start | bytes 3932160 | tf_op jit(solution)/shard_map/all_gather | solution.py:156
  43.2 37.2 %copy-start.14 = (f32[3,100,65]{1,2,0:T(8,128)}, f32[3,100,65]{1,2,0:T(8,128)S(1)}, u32[]{:S(2)}) copy-start(f32[3,100,65]{1,2,0:T(8,128)S(1)} %reduce_sum.210) | copy-start | bytes 234004
  82.7 10.1 %copy-start.36 = (bf16[768,768]{1,0:T(8,128)(2,1)S(1)}, bf16[768,768]{1,0:T(8,128)(2,1)}, u32[]{:S(2)}) copy-start(bf16[768,768]{1,0:T(8,128)(2,1)} %param.25) | copy-start | bytes 3538948
  82.7 10.1 %copy-start.41 = (f32[768]{0:T(1024)S(1)}, f32[768]{0:T(1024)}, u32[]{:S(2)}) copy-start(f32[768]{0:T(1024)} %param.26) | copy-start | bytes 9220
  95.0 38.0 %copy-start.31 = (bf16[768]{0:T(1024)(128)(2,1)S(1)}, bf16[768]{0:T(1024)(128)(2,1)}, u32[]{:S(2)}) copy-start(bf16[768]{0:T(1024)(128)(2,1)} %param.30) | copy-start | bytes 4612
  96.2 181.9 %reduce-scatter.7.cloned.1.call-start = ((), (), s32[]{:S(2)}) async-start(), calls=%async_computation.12 | async-start | bytes 3932160 | tf_op jit(solution)/shard_map/reduce_scatter | solution.py:165
  96.2 30.1 %collective-permute-start = (bf16[512,768]{1,0:T(8,128)(2,1)}, bf16[512,768]{1,0:T(8,128)(2,1)}, u32[]{:S(2)}, u32[]{:S(2)}) collective-permute-start(bf16[512,768]{1,0:T(8,128)(2,1)} %param.33), channel_id=1, source_target_pairs={{0,1},{1,2},{2,3},{3,0},{4,5},{5,6},{6,7},{7,4},{8,9},{9,10},{10,1... | collective-permute-start | bytes 2359304 | tf_op jit(solution)/shard_map/ppermute | solution.py:36
  126.4 43.9 %collective-permute-start.1 = (bf16[512,768]{1,0:T(8,128)(2,1)}, bf16[512,768]{1,0:T(8,128)(2,1)}, u32[]{:S(2)}, u32[]{:S(2)}) collective-permute-start(bf16[512,768]{1,0:T(8,128)(2,1)} %collective-permute-done), channel_id=1, source_target_pairs={{0,1},{1,2},{2,3},{3,0},{4,5},{5,6},{6,7},{7,4},{8,9},{9,10},{10,1... | collective-permute-start | bytes 2359304 | tf_op jit(solution)/shard_map/ppermute | solution.py:36
  133.0 48.6 %copy-start.8 = (bf16[512,768]{1,0:T(8,128)(2,1)S(1)}, bf16[512,768]{1,0:T(8,128)(2,1)}, u32[]{:S(2)}) copy-start(bf16[512,768]{1,0:T(8,128)(2,1)} %param.33) | copy-start | bytes 2359300
  170.3 29.6 %collective-permute-start.2 = (bf16[512,768]{1,0:T(8,128)(2,1)}, bf16[512,768]{1,0:T(8,128)(2,1)S(1)}, u32[]{:S(2)}, u32[]{:S(2)}) collective-permute-start(bf16[512,768]{1,0:T(8,128)(2,1)} %collective-permute-done.1), channel_id=1, source_target_pairs={{0,1},{1,2},{2,3},{3,0},{4,5},{5,6},{6,7},{7,4},{8,9},{9,10},{10,1... | collective-permute-start | bytes 2359304 | tf_op jit(solution)/shard_map/ppermute | solution.py:36
  200.8 6.2 copy-start.39
  207.0 8.0 %copy-start.35 = (bf16[768,768]{1,0:T(8,128)(2,1)S(1)}, bf16[768,768]{1,0:T(8,128)(2,1)}, u32[]{:S(2)}) copy-start(bf16[768,768]{1,0:T(8,128)(2,1)} %param.29) | copy-start | bytes 3538948
  219.1 62.1 %copy-start.25 = (f32[768]{0:T(1024)S(1)}, f32[768]{0:T(1024)}, u32[]{:S(2)}) copy-start(f32[768]{0:T(1024)} %param.32) | copy-start | bytes 9220
  281.2 5.0 copy-start.37
  292.6 15.7 %all-to-all-start.3 = ((f32[4,3,100,64]{2,3,1,0:T(8,128)}), f32[4,3,100,64]{2,3,1,0:T(8,128)S(1)}, u32[]{:S(2)}, u32[]{:S(2)}) async-start(f32[4,3,100,64]{2,3,1,0:T(8,128)} %bitcast.108), calls=%async_computation.5 | async-start | bytes 786432 | tf_op jit(solution)/shard_map/all_to_all | solution.py:54
  330.8 4.8 copy-start.30
  330.9 44.8 %all-to-all-start.4 = ((bf16[4,562,384]{2,1,0:T(8,128)(2,1)}), bf16[4,562,384]{2,1,0:T(8,128)(2,1)}, u32[]{:S(2)}, u32[]{:S(2)}) async-start(bf16[4,562,384]{2,1,0:T(8,128)(2,1)} %pad_maximum_fusion.1), calls=%async_computation.6 | async-start | bytes 3489792 | tf_op jit(solution)/shard_map/all_to_all | solution.py:262
  335.4 161.0 %reduce-scatter.9.cloned.1.call-start = ((), (), s32[]{:S(2)}) async-start(), calls=%async_computation.13 | async-start | bytes 11059200 | tf_op jit(solution)/shard_map/reduce_scatter | solution.py:304
  336.3 6.6 %copy-start.6 = (f32[512,768]{1,0:T(8,128)S(1)}, f32[512,768]{1,0:T(8,128)}, u32[]{:S(2)}) copy-start(f32[512,768]{1,0:T(8,128)} %copy-done.5) | copy-start | bytes 4718596
  397.4 3.8 copy-start.44
  418.5 158.4 %reduce-scatter.5.cloned.1.call-start = ((), (), s32[]{:S(2)}) async-start(), calls=%async_computation.11 | async-start | bytes 3932160 | tf_op jit(solution)/shard_map/reduce_scatter | solution.py:190
  425.1 211.4 %reduce-scatter.11.cloned.1.call-start = ((), (), s32[]{:S(2)}) async-start(), calls=%async_computation.14 | async-start | bytes 5308416 | tf_op jit(solution)/shard_map/reduce_scatter | solution.py:186
  425.4 7.2 %copy-start.34 = (bf16[2048,768]{1,0:T(8,128)(2,1)S(1)}, bf16[2048,768]{1,0:T(8,128)(2,1)}, u32[]{:S(2)}) copy-start(bf16[2048,768]{1,0:T(8,128)(2,1)} %all-gather.2.cloned.1.call-done) | copy-start | bytes 9437188
  425.4 7.5 %copy-start.46 = (bf16[2048,768]{1,0:T(8,128)(2,1)S(1)}, bf16[2048,768]{1,0:T(8,128)(2,1)}, u32[]{:S(2)}) copy-start(bf16[2048,768]{1,0:T(8,128)(2,1)} %copy-done.45) | copy-start | bytes 9437188
  496.4 145.6 %all-to-all-start.5 = ((f32[4,24,3084]{2,1,0:T(8,128)}), f32[4,24,3084]{2,1,0:T(8,128)}, u32[]{:S(2)}, u32[]{:S(2)}) async-start(f32[4,24,3084]{2,1,0:T(8,128)} %bitcast.101), calls=%async_computation.8 | async-start | bytes 2457600 | tf_op jit(solution)/shard_map/all_to_all | solution.py:54
  500.9 137.4 %copy-start.33 = (f32[512]{0:T(512)S(1)}, f32[512]{0:T(512)}, u32[]{:S(2)}) copy-start(f32[512]{0:T(512)} %get-tuple-element.19) | copy-start | bytes 6148
  501.0 137.4 %copy-start.32 = (f32[512]{0:T(512)S(1)}, f32[512]{0:T(512)}, u32[]{:S(2)}) copy-start(f32[512]{0:T(512)} %get-tuple-element.20) | copy-start | bytes 6148
  (28 other events, 66.6 us)
Sparse Core Ops, SparseCore 0:
  96.3 87.6 all-gather.1
  219.3 58.7 reduce-scatter.6
  418.6 77.6 reduce-scatter.8
  498.5 78.3 reduce-scatter.4
  580.2 56.1 reduce-scatter.10

commit v5 on v4

--- a/solution.py
+++ b/solution.py
@@ -52,7 +52,7 @@
 def scatter_sum(partial, group_size):
     pieces = partial.reshape((group_size, -1) + partial.shape[1:])
     arrived = lax.all_to_all(pieces, "mp", split_axis=0, concat_axis=0, tiled=True)
-    return jnp.sum(arrived, axis=0)
+    return jnp.sum(arrived.astype(jnp.float32), axis=0)
 
 
 def broadcast_gather(local, group_size):
@@ -183,14 +183,6 @@
         bias_part,
         (lax.axis_index("mp") * bias_part.shape[0],),
     )
-    ff_grads = lax.psum_scatter(
-        jnp.stack([grad_up, grad_down_t]), "dp", scatter_dimension=1, tiled=True
-    )
-
-    result = lax.psum_scatter(
-        out_partial.astype(jnp.bfloat16), "mp", scatter_dimension=0, tiled=True
-    ).astype(jnp.float32)
-    block_output = (residual + result).astype(jnp.bfloat16)
 
     scores_again = score_scale * jnp.einsum(
         "hcd,jhd->hcj", centroids, key_rows, preferred_element_type=jnp.float32
@@ -212,6 +204,10 @@
         membership,
         grad_spread.reshape(tok_rows, head_count, head_dim),
         preferred_element_type=jnp.float32,
+    )
+
+    ff_grads = lax.psum_scatter(
+        jnp.stack([grad_up, grad_down_t, grad_w_out]), "dp", scatter_dimension=1, tiled=True
     )
 
     summary_grad = scatter_sum(summary_grad, group_size).astype(jnp.bfloat16)
@@ -260,6 +256,10 @@
     )
 
     incoming = lax.all_to_all(outgoing, "mp", split_axis=0, concat_axis=0, tiled=True)
+
+    out_pieces, _ = lax.optimization_barrier((out_partial.astype(jnp.bfloat16), incoming))
+    result = scatter_sum(out_pieces, group_size)
+    block_output = (residual + result).astype(jnp.bfloat16)
 
     returned = incoming[:, :tok_rows].reshape(group_size, tok_rows, 2, local_heads * head_dim)
     grad_keyval = returned.transpose(1, 2, 0, 3).reshape(tok_rows, 2 * model_width)
@@ -296,12 +296,15 @@
         axis=1,
     )
     up_bias_cols = grad_up_bias.reshape(model_width, -1)
-    packed_grads = jnp.concatenate(
-        [grad_w_query, grad_w_keyval, grad_w_out, vectors, up_bias_cols], axis=1
-    )
-
+    packed_grads = jnp.concatenate([grad_w_query, grad_w_keyval, vectors, up_bias_cols], axis=1)
+
+    dp_reduced = lax.psum_scatter(packed_grads, "dp", scatter_dimension=0, tiled=True)
+    attn_width = grad_w_query.shape[1] + grad_w_keyval.shape[1]
     reduced = scatter_sum(
-        lax.psum_scatter(packed_grads, "dp", scatter_dimension=0, tiled=True), group_size
+        jnp.concatenate(
+            [dp_reduced[:, :attn_width], ff_grads[2], dp_reduced[:, attn_width:]], axis=1
+        ),
+        group_size,
     )
     up_share = ff_grads[0]
     down_share = ff_grads[1].T

time: 661 us -> 573 us (0.87)
  waiting for transfers between devices: 410 us -> 298 us
  starting transfers between devices: 41.4 us -> 56.2 us
    reduce_scatter x2 -> x1, waiting for transfers between devices: 133 us -> 0.02 us  [block_body(): lax.psum_scatter(jnp.stack([grad_up, grad_down_t, grad_w_out]), 'dp', sca...]
    all_to_all x3 -> x4, waiting for transfers between devices: 15.8 us -> 50.6 us  [scatter_sum(): lax.all_to_all(pieces, 'mp', split_axis=0, concat_axis=0, tiled=True)]
    ppermute x3, starting transfers between devices: 16.9 us -> 27.7 us  [ring_shift(): lax.ppermute(x, 'mp', [(i, (i + 1) % group_size) for i in range(group_siz...]
    reduce_scatter x1, waiting for transfers between devices: 58.9 us -> 48.7 us  [block_body(): lax.psum_scatter(jnp.einsum('tf,df->td', grad_before, w_up, preferred_ele...]
    all_to_all x3 -> x4, starting transfers between devices: 15.1 us -> 19.2 us  [scatter_sum(): lax.all_to_all(pieces, 'mp', split_axis=0, concat_axis=0, tiled=True)]
  transfers between devices with their start and end apart: 13 -> 13, of which waited for: 11 -> 11; matrix products, arithmetic and copies ran while one was open for 8% -> 23% of each run, Pallas kernels for 0% -> 0%
where the time goes in v5:
time: 573 us; the launch traced here: 565 us
  waiting for transfers between devices  298 us (52%)
  local copies, waits for them, and re-layouts  76.3 us (13%)
  matrix products  76.1 us (13%)
  starting transfers between devices  56.2 us (10%)
  other arithmetic  33.9 us (6%)
  between operations  14.8 us (3%)
  blocking collectives  9.55 us (2%)
    ppermute x3, waiting for transfers between devices, ring_shift(): lax.ppermute(x, 'mp', [(i, (i + 1) % group_size) for i in range(group_siz...  76.9 us
    reduce_scatter x1, waiting for transfers between devices, block_body(): lax.psum_scatter(packed_grads, 'dp', scatter_dimension=0, tiled=True)  53 us
    all_to_all x4, waiting for transfers between devices, scatter_sum(): lax.all_to_all(pieces, 'mp', split_axis=0, concat_axis=0, tiled=True)  50.6 us
    reduce_scatter x1, waiting for transfers between devices, block_body(): lax.psum_scatter(jnp.einsum('tf,df->td', grad_before, w_up, preferred_ele...  48.7 us
    all_to_all x1, waiting for transfers between devices, block_body(): lax.all_to_all(packed, 'mp', split_axis=2, concat_axis=0, tiled=True)  35.4 us
    all_to_all x1, waiting for transfers between devices, block_body(): lax.all_to_all(outgoing, 'mp', split_axis=0, concat_axis=0, tiled=True)  33.1 us
    ppermute x3, starting transfers between devices, ring_shift(): lax.ppermute(x, 'mp', [(i, (i + 1) % group_size) for i in range(group_siz...  27.7 us
    all_to_all x4, starting transfers between devices, scatter_sum(): lax.all_to_all(pieces, 'mp', split_axis=0, concat_axis=0, tiled=True)  19.2 us
  transfers between devices with their start and end apart: 13, of which 11 were waited for; matrix products, arithmetic and copies ran while one was open for 23% of the time, Pallas kernels for 0%

profile of v5, /device:TPU:0, one launch (start us, length us, event | category | flops | bytes accessed | tf_op | source)
XLA Modules:
  0.0 564.8 jit_solution(12807224478875882254)
XLA Ops:
  18.5 6.3 %all-to-all-start = ((f32[4,3,100,65]{2,3,1,0:T(8,128)}), f32[4,3,100,65]{2,3,1,0:T(8,128)}, u32[]{:S(2)}, u32[]{:S(2)}) async-start(f32[4,3,100,65]{2,3,1,0:T(8,128)} %pad_maximum_fusion.3), calls=%async_computation | async-start | bytes 884736 | tf_op jit(solution)/shard_map/all_to_all | solution.py:54
  32.8 4.9 all-to-all-done
  37.7 4.3 all-to-all-start.1
  43.2 35.4 %all-to-all-done.1 = bf16[512,2,4,192]{0,3,1,2:T(8,128)(2,1)} async-done(((bf16[512,2,4,192]{0,3,1,2:T(8,128)(2,1)}), bf16[512,2,4,192]{0,3,1,2:T(8,128)(2,1)}, u32[]{:S(2)}, u32[]{:S(2)}) %all-to-all-start.1) | async-done | bytes 1572896 | tf_op jit(solution)/shard_map/all_to_all | solution.py:119
  82.8 9.5 %all_to_all.48 = bf16[4,3,100,64]{2,3,1,0:T(8,128)(2,1)S(1)} all-to-all(bf16[4,3,100,64]{2,3,1,0:T(8,128)(2,1)S(1)} %broadcast_in_dim.23), channel_id=1, replica_groups=mesh['dp'=8,'mp'=4] {'mp'}, dimensions={0} | all-to-all | bytes 307200 | tf_op jit(solution)/shard_map/all_to_all | solution.py:60
  97.2 29.2 %collective-permute-done = bf16[512,768]{1,0:T(8,128)(2,1)} collective-permute-done((bf16[512,768]{1,0:T(8,128)(2,1)}, bf16[512,768]{1,0:T(8,128)(2,1)}, u32[]{:S(2)}, u32[]{:S(2)}) %collective-permute-start) | collective-permute-done | bytes 786464 | tf_op jit(solution)/shard_map/ppermute | solution.py:36
  126.4 6.7 %collective-permute-start.1 = (bf16[512,768]{1,0:T(8,128)(2,1)}, bf16[512,768]{1,0:T(8,128)(2,1)}, u32[]{:S(2)}, u32[]{:S(2)}) collective-permute-start(bf16[512,768]{1,0:T(8,128)(2,1)} %collective-permute-done), channel_id=1, source_target_pairs={{0,1},{1,2},{2,3},{3,0},{4,5},{5,6},{6,7},{7,4},{8,9},{9,10},{10,1... | collective-permute-start | bytes 2359304 | tf_op jit(solution)/shard_map/ppermute | solution.py:36
  133.1 37.2 %collective-permute-done.1 = bf16[512,768]{1,0:T(8,128)(2,1)} collective-permute-done((bf16[512,768]{1,0:T(8,128)(2,1)}, bf16[512,768]{1,0:T(8,128)(2,1)}, u32[]{:S(2)}, u32[]{:S(2)}) %collective-permute-start.1) | collective-permute-done | bytes 786464 | tf_op jit(solution)/shard_map/ppermute | solution.py:36
  170.3 20.2 %collective-permute-start.2 = (bf16[512,768]{1,0:T(8,128)(2,1)}, bf16[512,768]{1,0:T(8,128)(2,1)S(1)}, u32[]{:S(2)}, u32[]{:S(2)}) collective-permute-start(bf16[512,768]{1,0:T(8,128)(2,1)} %collective-permute-done.1), channel_id=1, source_target_pairs={{0,1},{1,2},{2,3},{3,0},{4,5},{5,6},{6,7},{7,4},{8,9},{9,10},{10,1... | collective-permute-start | bytes 2359304 | tf_op jit(solution)/shard_map/ppermute | solution.py:36
  197.4 10.5 %collective-permute-done.2 = bf16[512,768]{1,0:T(8,128)(2,1)S(1)} collective-permute-done((bf16[512,768]{1,0:T(8,128)(2,1)}, bf16[512,768]{1,0:T(8,128)(2,1)S(1)}, u32[]{:S(2)}, u32[]{:S(2)}) %collective-permute-start.2) | collective-permute-done | bytes 786464 | tf_op jit(solution)/shard_map/ppermute | solution.py:36
  208.9 6.2 %multiply_convert_fusion = (bf16[2048,768]{1,0:T(8,128)(2,1)}, f32[2048,768]{1,0:T(8,128)S(1)}) fusion(f32[768]{0:T(1024)S(1)} %convert_element_type.127, bf16[2048,768]{1,0:T(8,128)(2,1)} %all-gather.2.cloned.1.call-done, bf16[768,768]{1,0:T(8,128)(2,1)} %param.29), kind=kOutput, calls=%fused_computation.10 | convolution fusion | flops 2425356288 | bytes 13765632 | tf_op jit(solution)/shard_map/dot_general | solution.py:158
  215.1 6.4 %convert_reduce_fusion = (f32[768]{0:T(1024)}, bf16[2048,768]{1,0:T(8,128)(2,1)S(1)}) fusion(f32[2048,768]{1,0:T(8,128)S(1)} %get-tuple-element.50, f32[768]{0:T(1024)S(1)} %convert_element_type.127, bf16[2048,768]{1,0:T(8,128)(2,1)} %bitcast.15, bf16[768,768]{1,0:T(8,128)(2,1)S(1)} %copy-done.41), kind=kOutput, calls=%fused_computation.8 | convolution fusion | flops 2436365568 | bytes 13768704 | tf_op jit(solution)/shard_map/td,fd->tf/dot_general | solution.py:163
  223.2 4.0 convolution_convert_fusion
  227.3 7.0 %convolution_bitcast_fusion = f32[1,768,768]{2,1,0:T(8,128)} fusion(bf16[2048,768]{1,0:T(8,128)(2,1)} %bitcast.15, bf16[2048,768]{1,0:T(8,128)(2,1)} %get-tuple-element.49), kind=kOutput, calls=%fused_computation.54 | convolution fusion | flops 2415919104 | bytes 8650752 | tf_op jit(solution)/shard_map/td,tf->df/dot_general | solution.py:178
  234.3 4.2 convolution_bitcast_fusion.1
  238.5 48.7 %reduce-scatter.4.cloned.1.call-done = bf16[512,768]{1,0:T(8,128)(2,1)} async-done(((bf16[2048,768]{1,0:T(8,128)(2,1)}), bf16[512,768]{1,0:T(8,128)(2,1)}) %reduce-scatter.4.cloned.1.call-update) | async-done | bytes 786448 | tf_op jit(solution)/shard_map/reduce_scatter | solution.py:165
  290.4 3.8 convert_reduce_fusion.6
  301.1 3.4 convolution_convert_fusion.3
  309.4 3.8 all-to-all-start.3
  313.9 11.0 %all-to-all-done.3 = f32[4,3,100,64]{2,3,1,0:T(8,128)S(1)} async-done(((f32[4,3,100,64]{2,3,1,0:T(8,128)}), f32[4,3,100,64]{2,3,1,0:T(8,128)S(1)}, u32[]{:S(2)}, u32[]{:S(2)}) %all-to-all-start.3) | async-done | bytes 307232 | tf_op jit(solution)/shard_map/all_to_all | solution.py:54
  325.6 3.7 fusion.9
  351.5 4.6 all-to-all-start.4
  363.5 33.1 %all-to-all-done.4 = bf16[4,562,384]{2,1,0:T(8,128)(2,1)} async-done(((bf16[4,562,384]{2,1,0:T(8,128)(2,1)}), bf16[4,562,384]{2,1,0:T(8,128)(2,1)}, u32[]{:S(2)}, u32[]{:S(2)}) %all-to-all-start.4) | async-done | bytes 1726496 | tf_op jit(solution)/shard_map/all_to_all | solution.py:258
  424.6 3.8 fusion.59
  428.4 10.0 %concatenate.44 = f32[768,2316]{1,0:T(8,128)} concatenate(f32[768,768]{1,0:T(8,128)} %fusion.61, f32[768,1536]{1,0:T(8,128)} %fusion.59, f32[768,1]{1,0:T(8,128)} %stack.48, f32[768,1]{1,0:T(8,128)} %stack.49, f32[768,1]{1,0:T(8,128)} %stack.50, f32[768,1]{1,0:T(8,128)} %stack.51, f32[768,1]{1,0:T(8,128)} %stack.52, f32[768,1]{1,0:T(8,128)} %stack.53, f32[768,1]{1,0:T(8,128)} %stack.54, ...), dimensions={1} | concatenate | bytes 14229504 | tf_op jit(solution)/shard_map/concatenate | solution.py:299
  438.5 6.5 %convolution_convert_fusion.1 = bf16[2048,768]{1,0:T(8,128)(2,1)} fusion(bf16[2048,768]{1,0:T(8,128)(2,1)} %get-tuple-element.49, bf16[768,768]{1,0:T(8,128)(2,1)} %param.31), kind=kOutput, calls=%fused_computation.15 | convolution fusion | flops 2417491968 | bytes 7471104 | tf_op jit(solution)/shard_map/dot_general | solution.py:174
  445.0 4.7 all-to-all-start.5
  452.0 53.0 %reduce-scatter.6.cloned.1.call-done = f32[96,2316]{1,0:T(8,128)} async-done(((f32[768,2316]{1,0:T(8,128)}), f32[96,2316]{1,0:T(8,128)}) %reduce-scatter.6.cloned.1.call-update) | async-done | bytes 889360 | tf_op jit(solution)/shard_map/reduce_scatter | solution.py:301
  507.3 12.7 %all-to-all-done.5 = bf16[4,512,768]{2,1,0:T(8,128)(2,1)} async-done(((bf16[4,512,768]{2,1,0:T(8,128)(2,1)}), bf16[4,512,768]{2,1,0:T(8,128)(2,1)}, u32[]{:S(2)}, u32[]{:S(2)}) %all-to-all-start.5) | async-done | bytes 3145760 | tf_op jit(solution)/shard_map/all_to_all | solution.py:54
  520.0 4.3 all-to-all-start.6
  524.4 3.6 fusion.30
  531.6 21.9 %all-to-all-done.6 = f32[4,24,3084]{2,1,0:T(8,128)} async-done(((f32[4,24,3084]{2,1,0:T(8,128)}), f32[4,24,3084]{2,1,0:T(8,128)}, u32[]{:S(2)}, u32[]{:S(2)}) %all-to-all-start.6) | async-done | bytes 1184288 | tf_op jit(solution)/shard_map/all_to_all | solution.py:54
  (199 shorter events, 124.9 us)
Async XLA Ops:
  7.2 17.7 %copy-start = (bf16[768,1536]{1,0:T(8,128)(2,1)S(1)}, bf16[768,1536]{1,0:T(8,128)(2,1)}, u32[]{:S(2)}) copy-start(bf16[768,1536]{1,0:T(8,128)(2,1)} %param.23) | copy-start | bytes 7077892
  10.2 14.7 %copy-start.25 = (f32[512]{0:T(512)}, f32[512]{0:T(512)S(1)}, u32[]{:S(2)}) copy-start(f32[512]{0:T(512)S(1)} %add_rsqrt_fusion.1) | copy-start | bytes 6148
  16.0 8.9 %copy-start.32 = (f32[768]{0:T(1024)S(1)}, f32[768]{0:T(1024)}, u32[]{:S(2)}) copy-start(f32[768]{0:T(1024)} %param.24) | copy-start | bytes 9220
  18.5 19.2 %all-to-all-start = ((f32[4,3,100,65]{2,3,1,0:T(8,128)}), f32[4,3,100,65]{2,3,1,0:T(8,128)}, u32[]{:S(2)}, u32[]{:S(2)}) async-start(f32[4,3,100,65]{2,3,1,0:T(8,128)} %pad_maximum_fusion.3), calls=%async_computation | async-start | bytes 884736 | tf_op jit(solution)/shard_map/all_to_all | solution.py:54
  37.7 40.9 %all-to-all-start.1 = ((bf16[512,2,4,192]{0,3,1,2:T(8,128)(2,1)}), bf16[512,2,4,192]{0,3,1,2:T(8,128)(2,1)}, u32[]{:S(2)}, u32[]{:S(2)}) async-start(bf16[512,2,4,192]{0,3,1,2:T(8,128)(2,1)} %copy.75), calls=%async_computation.1 | async-start | bytes 3145728 | tf_op jit(solution)/shard_map/all_to_all | solution.py:119
  42.1 166.8 %all-gather.2.cloned.1.call-start = ((), (), s32[]{:S(2)}) async-start(), calls=%async_computation.10 | async-start | bytes 3932160 | tf_op jit(solution)/shard_map/all_gather | solution.py:156
  43.2 37.2 %copy-start.16 = (f32[3,100,65]{1,2,0:T(8,128)}, f32[3,100,65]{1,2,0:T(8,128)S(1)}, u32[]{:S(2)}) copy-start(f32[3,100,65]{1,2,0:T(8,128)S(1)} %reduce_sum.219) | copy-start | bytes 234004
  82.8 10.1 %copy-start.39 = (bf16[768,768]{1,0:T(8,128)(2,1)S(1)}, bf16[768,768]{1,0:T(8,128)(2,1)}, u32[]{:S(2)}) copy-start(bf16[768,768]{1,0:T(8,128)(2,1)} %param.25) | copy-start | bytes 3538948
  82.8 10.1 %copy-start.43 = (f32[768]{0:T(1024)S(1)}, f32[768]{0:T(1024)}, u32[]{:S(2)}) copy-start(f32[768]{0:T(1024)} %param.26) | copy-start | bytes 9220
  95.0 38.1 %copy-start.34 = (bf16[768]{0:T(1024)(128)(2,1)S(1)}, bf16[768]{0:T(1024)(128)(2,1)}, u32[]{:S(2)}) copy-start(bf16[768]{0:T(1024)(128)(2,1)} %param.30) | copy-start | bytes 4612
  96.2 191.0 %reduce-scatter.4.cloned.1.call-start = ((), (), s32[]{:S(2)}) async-start(), calls=%async_computation.11 | async-start | bytes 3932160 | tf_op jit(solution)/shard_map/reduce_scatter | solution.py:165
  96.3 30.1 %collective-permute-start = (bf16[512,768]{1,0:T(8,128)(2,1)}, bf16[512,768]{1,0:T(8,128)(2,1)}, u32[]{:S(2)}, u32[]{:S(2)}) collective-permute-start(bf16[512,768]{1,0:T(8,128)(2,1)} %param.33), channel_id=1, source_target_pairs={{0,1},{1,2},{2,3},{3,0},{4,5},{5,6},{6,7},{7,4},{8,9},{9,10},{10,1... | collective-permute-start | bytes 2359304 | tf_op jit(solution)/shard_map/ppermute | solution.py:36
  126.4 43.9 %collective-permute-start.1 = (bf16[512,768]{1,0:T(8,128)(2,1)}, bf16[512,768]{1,0:T(8,128)(2,1)}, u32[]{:S(2)}, u32[]{:S(2)}) collective-permute-start(bf16[512,768]{1,0:T(8,128)(2,1)} %collective-permute-done), channel_id=1, source_target_pairs={{0,1},{1,2},{2,3},{3,0},{4,5},{5,6},{6,7},{7,4},{8,9},{9,10},{10,1... | collective-permute-start | bytes 2359304 | tf_op jit(solution)/shard_map/ppermute | solution.py:36
  133.1 59.2 %copy-start.10 = (bf16[512,768]{1,0:T(8,128)(2,1)S(1)}, bf16[512,768]{1,0:T(8,128)(2,1)}, u32[]{:S(2)}) copy-start(bf16[512,768]{1,0:T(8,128)(2,1)} %param.33) | copy-start | bytes 2359300
  170.3 37.6 %collective-permute-start.2 = (bf16[512,768]{1,0:T(8,128)(2,1)}, bf16[512,768]{1,0:T(8,128)(2,1)S(1)}, u32[]{:S(2)}, u32[]{:S(2)}) collective-permute-start(bf16[512,768]{1,0:T(8,128)(2,1)} %collective-permute-done.1), channel_id=1, source_target_pairs={{0,1},{1,2},{2,3},{3,0},{4,5},{5,6},{6,7},{7,4},{8,9},{9,10},{10,1... | collective-permute-start | bytes 2359304 | tf_op jit(solution)/shard_map/ppermute | solution.py:36
  208.9 6.2 %copy-start.41 = (bf16[768,768]{1,0:T(8,128)(2,1)S(1)}, bf16[768,768]{1,0:T(8,128)(2,1)}, u32[]{:S(2)}) copy-start(bf16[768,768]{1,0:T(8,128)(2,1)} %param.31) | copy-start | bytes 3538948
  215.1 8.1 %copy-start.38 = (bf16[768,768]{1,0:T(8,128)(2,1)S(1)}, bf16[768,768]{1,0:T(8,128)(2,1)}, u32[]{:S(2)}) copy-start(bf16[768,768]{1,0:T(8,128)(2,1)} %param.29) | copy-start | bytes 3538948
  227.2 222.5 %reduce-scatter.8.cloned.1.call-start = ((), (), s32[]{:S(2)}) async-start(), calls=%async_computation.13 | async-start | bytes 7962624 | tf_op jit(solution)/shard_map/reduce_scatter | solution.py:209
  227.3 7.1 %copy-start.37 = (bf16[2048,768]{1,0:T(8,128)(2,1)S(1)}, bf16[2048,768]{1,0:T(8,128)(2,1)}, u32[]{:S(2)}) copy-start(bf16[2048,768]{1,0:T(8,128)(2,1)} %all-gather.2.cloned.1.call-done) | copy-start | bytes 9437188
  227.3 7.0 %copy-start.47 = (bf16[2048,768]{1,0:T(8,128)(2,1)S(1)}, bf16[2048,768]{1,0:T(8,128)(2,1)}, u32[]{:S(2)}) copy-start(bf16[2048,768]{1,0:T(8,128)(2,1)} %copy-done.46) | copy-start | bytes 9437188
  238.5 51.9 %copy-start.28 = (f32[768]{0:T(1024)S(1)}, f32[768]{0:T(1024)}, u32[]{:S(2)}) copy-start(f32[768]{0:T(1024)} %param.32) | copy-start | bytes 9220
  290.4 5.0 copy-start.19
  309.4 15.5 %all-to-all-start.3 = ((f32[4,3,100,64]{2,3,1,0:T(8,128)}), f32[4,3,100,64]{2,3,1,0:T(8,128)S(1)}, u32[]{:S(2)}, u32[]{:S(2)}) async-start(f32[4,3,100,64]{2,3,1,0:T(8,128)} %bitcast.116), calls=%async_computation.4 | async-start | bytes 786432 | tf_op jit(solution)/shard_map/all_to_all | solution.py:54
  329.2 5.3 copy-start.21
  351.5 4.9 copy-start.33
  351.5 45.2 %all-to-all-start.4 = ((bf16[4,562,384]{2,1,0:T(8,128)(2,1)}), bf16[4,562,384]{2,1,0:T(8,128)(2,1)}, u32[]{:S(2)}, u32[]{:S(2)}) async-start(bf16[4,562,384]{2,1,0:T(8,128)(2,1)} %pad_maximum_fusion.1), calls=%async_computation.5 | async-start | bytes 3489792 | tf_op jit(solution)/shard_map/all_to_all | solution.py:258
  356.0 148.9 %reduce-scatter.6.cloned.1.call-start = ((), (), s32[]{:S(2)}) async-start(), calls=%async_computation.12 | async-start | bytes 8404992 | tf_op jit(solution)/shard_map/reduce_scatter | solution.py:301
  445.0 75.0 %all-to-all-start.5 = ((bf16[4,512,768]{2,1,0:T(8,128)(2,1)}), bf16[4,512,768]{2,1,0:T(8,128)(2,1)}, u32[]{:S(2)}, u32[]{:S(2)}) async-start(bf16[4,512,768]{2,1,0:T(8,128)(2,1)} %bitcast.104), calls=%async_computation.6 | async-start | bytes 6291456 | tf_op jit(solution)/shard_map/all_to_all | solution.py:54
  507.3 17.0 %copy-start.36 = (f32[512]{0:T(512)S(1)}, f32[512]{0:T(512)}, u32[]{:S(2)}) copy-start(f32[512]{0:T(512)} %get-tuple-element.21) | copy-start | bytes 6148
  507.3 17.0 %copy-start.35 = (f32[512]{0:T(512)S(1)}, f32[512]{0:T(512)}, u32[]{:S(2)}) copy-start(f32[512]{0:T(512)} %get-tuple-element.22) | copy-start | bytes 6148
  507.3 17.1 %copy-start.31 = (f32[768]{0:T(1024)S(1)}, f32[768]{0:T(1024)}, u32[]{:S(2)}) copy-start(f32[768]{0:T(1024)} %param.19) | copy-start | bytes 9220
  520.0 33.5 %all-to-all-start.6 = ((f32[4,24,3084]{2,1,0:T(8,128)}), f32[4,24,3084]{2,1,0:T(8,128)}, u32[]{:S(2)}, u32[]{:S(2)}) async-start(f32[4,24,3084]{2,1,0:T(8,128)} %pad_maximum_fusion.2), calls=%async_computation.9 | async-start | bytes 2457600 | tf_op jit(solution)/shard_map/all_to_all | solution.py:54
  (31 other events, 68.7 us)
Sparse Core Ops, SparseCore 0:
  96.4 86.9 all-gather.1
  227.4 59.8 reduce-scatter.3
  301.3 65.2 reduce-scatter.7
  438.6 66.3 reduce-scatter.5

commit v6 on v5

--- a/solution.py
+++ b/solution.py
@@ -113,10 +113,10 @@
     cluster_sizes = jnp.sum(member_float, axis=2)
     packed = keyval.reshape(tok_rows, 2, group_size, local_heads * head_dim)
 
+    arrived = lax.all_to_all(packed, "mp", split_axis=2, concat_axis=0, tiled=True)
     sums_and_sizes = scatter_sum(
         jnp.concatenate([query_sums, cluster_sizes[:, :, None]], axis=2), group_size
     )
-    arrived = lax.all_to_all(packed, "mp", split_axis=2, concat_axis=0, tiled=True)
 
     query_sums = sums_and_sizes[:, :, :head_dim]
     cluster_sizes = sums_and_sizes[:, :, head_dim]
@@ -272,8 +272,12 @@
     grad_queries = grad_queries.reshape(tok_rows, model_width).astype(jnp.bfloat16)
     grad_query_bias = jnp.sum(grad_queries.astype(jnp.float32), axis=0)
     grad_value_bias = jnp.sum(grad_keyval[:, model_width:].astype(jnp.float32), axis=0)
-    grad_w_query = jnp.einsum("td,te->de", first, grad_queries, preferred_element_type=jnp.float32)
-    grad_w_keyval = jnp.einsum("td,te->de", first, grad_keyval, preferred_element_type=jnp.float32)
+    grad_w_attn = jnp.einsum(
+        "td,te->de",
+        first,
+        jnp.concatenate([grad_queries, grad_keyval], axis=1),
+        preferred_element_type=jnp.float32,
+    )
     grad_first = jnp.einsum("te,de->td", grad_queries, w_query, preferred_element_type=jnp.float32)
     grad_first = grad_first + jnp.einsum(
         "te,de->td", grad_keyval, w_keyval, preferred_element_type=jnp.float32
@@ -296,10 +300,10 @@
         axis=1,
     )
     up_bias_cols = grad_up_bias.reshape(model_width, -1)
-    packed_grads = jnp.concatenate([grad_w_query, grad_w_keyval, vectors, up_bias_cols], axis=1)
+    packed_grads = jnp.concatenate([grad_w_attn, vectors, up_bias_cols], axis=1)
 
     dp_reduced = lax.psum_scatter(packed_grads, "dp", scatter_dimension=0, tiled=True)
-    attn_width = grad_w_query.shape[1] + grad_w_keyval.shape[1]
+    attn_width = grad_w_attn.shape[1]
     reduced = scatter_sum(
         jnp.concatenate(
             [dp_reduced[:, :attn_width], ff_grads[2], dp_reduced[:, attn_width:]], axis=1

time: 573 us -> 563 us (0.983)
  starting transfers between devices: 56.2 us -> 46 us
    ppermute x3, starting transfers between devices: 27.7 us -> 17.6 us  [ring_shift(): lax.ppermute(x, 'mp', [(i, (i + 1) % group_size) for i in range(group_siz...]
where the time goes in v6:
time: 563 us; the launch traced here: 554 us
  waiting for transfers between devices  299 us (53%)
  local copies, waits for them, and re-layouts  76.3 us (14%)
  matrix products  75.2 us (13%)
  starting transfers between devices  46 us (8%)
  other arithmetic  33.8 us (6%)
  between operations  14.6 us (3%)
  blocking collectives  9.55 us (2%)
    ppermute x3, waiting for transfers between devices, ring_shift(): lax.ppermute(x, 'mp', [(i, (i + 1) % group_size) for i in range(group_siz...  78.9 us
    reduce_scatter x1, waiting for transfers between devices, block_body(): lax.psum_scatter(packed_grads, 'dp', scatter_dimension=0, tiled=True)  53 us
    all_to_all x4, waiting for transfers between devices, scatter_sum(): lax.all_to_all(pieces, 'mp', split_axis=0, concat_axis=0, tiled=True)  50.6 us
    reduce_scatter x1, waiting for transfers between devices, block_body(): lax.psum_scatter(jnp.einsum('tf,df->td', grad_before, w_up, preferred_ele...  47.7 us
    all_to_all x1, waiting for transfers between devices, block_body(): lax.all_to_all(packed, 'mp', split_axis=2, concat_axis=0, tiled=True)  35.4 us
    all_to_all x1, waiting for transfers between devices, block_body(): lax.all_to_all(outgoing, 'mp', split_axis=0, concat_axis=0, tiled=True)  33.2 us
    all_to_all x4, starting transfers between devices, scatter_sum(): lax.all_to_all(pieces, 'mp', split_axis=0, concat_axis=0, tiled=True)  19.1 us
    ppermute x3, starting transfers between devices, ring_shift(): lax.ppermute(x, 'mp', [(i, (i + 1) % group_size) for i in range(group_siz...  17.6 us
  transfers between devices with their start and end apart: 13, of which 11 were waited for; matrix products, arithmetic and copies ran while one was open for 23% of the time, Pallas kernels for 0%

profile of v6, /device:TPU:0, one launch (start us, length us, event | category | flops | bytes accessed | tf_op | source)
XLA Modules:
  0.0 554.4 jit_solution(17168007241399821700)
XLA Ops:
  18.5 6.3 %all-to-all-start = ((f32[4,3,100,65]{2,3,1,0:T(8,128)}), f32[4,3,100,65]{2,3,1,0:T(8,128)}, u32[]{:S(2)}, u32[]{:S(2)}) async-start(f32[4,3,100,65]{2,3,1,0:T(8,128)} %pad_maximum_fusion.3), calls=%async_computation | async-start | bytes 884736 | tf_op jit(solution)/shard_map/all_to_all | solution.py:54
  32.8 4.9 all-to-all-done
  37.7 4.3 all-to-all-start.1
  43.2 35.4 %all-to-all-done.1 = bf16[512,2,4,192]{0,3,1,2:T(8,128)(2,1)} async-done(((bf16[512,2,4,192]{0,3,1,2:T(8,128)(2,1)}), bf16[512,2,4,192]{0,3,1,2:T(8,128)(2,1)}, u32[]{:S(2)}, u32[]{:S(2)}) %all-to-all-start.1) | async-done | bytes 1572896 | tf_op jit(solution)/shard_map/all_to_all | solution.py:116
  82.8 9.5 %all_to_all.48 = bf16[4,3,100,64]{2,3,1,0:T(8,128)(2,1)S(1)} all-to-all(bf16[4,3,100,64]{2,3,1,0:T(8,128)(2,1)S(1)} %broadcast_in_dim.23), channel_id=1, replica_groups=mesh['dp'=8,'mp'=4] {'mp'}, dimensions={0} | all-to-all | bytes 307200 | tf_op jit(solution)/shard_map/all_to_all | solution.py:60
  97.2 29.3 %collective-permute-done = bf16[512,768]{1,0:T(8,128)(2,1)} collective-permute-done((bf16[512,768]{1,0:T(8,128)(2,1)}, bf16[512,768]{1,0:T(8,128)(2,1)}, u32[]{:S(2)}, u32[]{:S(2)}) %collective-permute-start) | collective-permute-done | bytes 786464 | tf_op jit(solution)/shard_map/ppermute | solution.py:36
  126.4 6.7 %collective-permute-start.1 = (bf16[512,768]{1,0:T(8,128)(2,1)}, bf16[512,768]{1,0:T(8,128)(2,1)}, u32[]{:S(2)}, u32[]{:S(2)}) collective-permute-start(bf16[512,768]{1,0:T(8,128)(2,1)} %collective-permute-done), channel_id=1, source_target_pairs={{0,1},{1,2},{2,3},{3,0},{4,5},{5,6},{6,7},{7,4},{8,9},{9,10},{10,1... | collective-permute-start | bytes 2359304 | tf_op jit(solution)/shard_map/ppermute | solution.py:36
  133.1 37.2 %collective-permute-done.1 = bf16[512,768]{1,0:T(8,128)(2,1)} collective-permute-done((bf16[512,768]{1,0:T(8,128)(2,1)}, bf16[512,768]{1,0:T(8,128)(2,1)}, u32[]{:S(2)}, u32[]{:S(2)}) %collective-permute-start.1) | collective-permute-done | bytes 786464 | tf_op jit(solution)/shard_map/ppermute | solution.py:36
  170.3 10.0 %collective-permute-start.2 = (bf16[512,768]{1,0:T(8,128)(2,1)}, bf16[512,768]{1,0:T(8,128)(2,1)S(1)}, u32[]{:S(2)}, u32[]{:S(2)}) collective-permute-start(bf16[512,768]{1,0:T(8,128)(2,1)} %collective-permute-done.1), channel_id=1, source_target_pairs={{0,1},{1,2},{2,3},{3,0},{4,5},{5,6},{6,7},{7,4},{8,9},{9,10},{10,1... | collective-permute-start | bytes 2359304 | tf_op jit(solution)/shard_map/ppermute | solution.py:36
  187.5 12.5 %collective-permute-done.2 = bf16[512,768]{1,0:T(8,128)(2,1)S(1)} collective-permute-done((bf16[512,768]{1,0:T(8,128)(2,1)}, bf16[512,768]{1,0:T(8,128)(2,1)S(1)}, u32[]{:S(2)}, u32[]{:S(2)}) %collective-permute-start.2) | collective-permute-done | bytes 786464 | tf_op jit(solution)/shard_map/ppermute | solution.py:36
  200.9 6.2 %multiply_convert_fusion = (bf16[2048,768]{1,0:T(8,128)(2,1)}, f32[2048,768]{1,0:T(8,128)S(1)}) fusion(f32[768]{0:T(1024)S(1)} %convert_element_type.127, bf16[2048,768]{1,0:T(8,128)(2,1)} %all-gather.2.cloned.1.call-done, bf16[768,768]{1,0:T(8,128)(2,1)} %param.29), kind=kOutput, calls=%fused_computation.10 | convolution fusion | flops 2425356288 | bytes 13765632 | tf_op jit(solution)/shard_map/dot_general | solution.py:158
  207.1 6.4 %convert_reduce_fusion = (f32[768]{0:T(1024)}, bf16[2048,768]{1,0:T(8,128)(2,1)S(1)}) fusion(f32[2048,768]{1,0:T(8,128)S(1)} %get-tuple-element.50, f32[768]{0:T(1024)S(1)} %convert_element_type.127, bf16[2048,768]{1,0:T(8,128)(2,1)} %bitcast.15, bf16[768,768]{1,0:T(8,128)(2,1)S(1)} %copy-done.41), kind=kOutput, calls=%fused_computation.8 | convolution fusion | flops 2436365568 | bytes 13768704 | tf_op jit(solution)/shard_map/td,fd->tf/dot_general | solution.py:163
  215.2 4.0 convolution_convert_fusion
  219.3 7.1 %convolution_bitcast_fusion = f32[1,768,768]{2,1,0:T(8,128)} fusion(bf16[2048,768]{1,0:T(8,128)(2,1)} %bitcast.15, bf16[2048,768]{1,0:T(8,128)(2,1)} %get-tuple-element.49), kind=kOutput, calls=%fused_computation.58 | convolution fusion | flops 2415919104 | bytes 8650752 | tf_op jit(solution)/shard_map/td,tf->df/dot_general | solution.py:178
  226.3 4.2 convolution_bitcast_fusion.1
  230.5 47.7 %reduce-scatter.4.cloned.1.call-done = bf16[512,768]{1,0:T(8,128)(2,1)} async-done(((bf16[2048,768]{1,0:T(8,128)(2,1)}), bf16[512,768]{1,0:T(8,128)(2,1)}) %reduce-scatter.4.cloned.1.call-update) | async-done | bytes 786448 | tf_op jit(solution)/shard_map/reduce_scatter | solution.py:165
  281.4 3.8 convert_reduce_fusion.6
  292.1 3.4 convolution_convert_fusion.3
  300.3 3.8 all-to-all-start.3
  304.8 11.0 %all-to-all-done.3 = f32[4,3,100,64]{2,3,1,0:T(8,128)S(1)} async-done(((f32[4,3,100,64]{2,3,1,0:T(8,128)}), f32[4,3,100,64]{2,3,1,0:T(8,128)S(1)}, u32[]{:S(2)}, u32[]{:S(2)}) %all-to-all-start.3) | async-done | bytes 307232 | tf_op jit(solution)/shard_map/all_to_all | solution.py:54
  316.4 3.7 fusion.9
  342.4 4.5 all-to-all-start.4
  354.4 33.2 %all-to-all-done.4 = bf16[4,562,384]{2,1,0:T(8,128)(2,1)} async-done(((bf16[4,562,384]{2,1,0:T(8,128)(2,1)}), bf16[4,562,384]{2,1,0:T(8,128)(2,1)}, u32[]{:S(2)}, u32[]{:S(2)}) %all-to-all-start.4) | async-done | bytes 1726496 | tf_op jit(solution)/shard_map/all_to_all | solution.py:258
  412.9 5.3 fusion.11
  418.2 10.1 %concatenate.48 = f32[768,2316]{1,0:T(8,128)} concatenate(f32[768,2304]{1,0:T(8,128)} %fusion.11, f32[768,1]{1,0:T(8,128)} %stack.48, f32[768,1]{1,0:T(8,128)} %stack.49, f32[768,1]{1,0:T(8,128)} %stack.50, f32[768,1]{1,0:T(8,128)} %stack.51, f32[768,1]{1,0:T(8,128)} %stack.52, f32[768,1]{1,0:T(8,128)} %stack.53, f32[768,1]{1,0:T(8,128)} %stack.54, f32[768,1]{1,0:T(8,128)} %stack.55, ...), dimensions={1} | concatenate | bytes 14229504 | tf_op jit(solution)/shard_map/concatenate | solution.py:303
  428.3 6.6 %convolution_convert_fusion.1 = bf16[2048,768]{1,0:T(8,128)(2,1)} fusion(bf16[2048,768]{1,0:T(8,128)(2,1)} %get-tuple-element.49, bf16[768,768]{1,0:T(8,128)(2,1)} %param.31), kind=kOutput, calls=%fused_computation.15 | convolution fusion | flops 2417491968 | bytes 7471104 | tf_op jit(solution)/shard_map/dot_general | solution.py:174
  434.8 4.7 all-to-all-start.5
  441.8 53.0 %reduce-scatter.6.cloned.1.call-done = f32[96,2316]{1,0:T(8,128)} async-done(((f32[768,2316]{1,0:T(8,128)}), f32[96,2316]{1,0:T(8,128)}) %reduce-scatter.6.cloned.1.call-update) | async-done | bytes 889360 | tf_op jit(solution)/shard_map/reduce_scatter | solution.py:305
  497.1 12.8 %all-to-all-done.5 = bf16[4,512,768]{2,1,0:T(8,128)(2,1)} async-done(((bf16[4,512,768]{2,1,0:T(8,128)(2,1)}), bf16[4,512,768]{2,1,0:T(8,128)(2,1)}, u32[]{:S(2)}, u32[]{:S(2)}) %all-to-all-start.5) | async-done | bytes 3145760 | tf_op jit(solution)/shard_map/all_to_all | solution.py:54
  509.9 4.3 all-to-all-start.6
  514.2 3.6 fusion.34
  521.5 21.9 %all-to-all-done.6 = f32[4,24,3084]{2,1,0:T(8,128)} async-done(((f32[4,24,3084]{2,1,0:T(8,128)}), f32[4,24,3084]{2,1,0:T(8,128)}, u32[]{:S(2)}, u32[]{:S(2)}) %all-to-all-start.6) | async-done | bytes 1184288 | tf_op jit(solution)/shard_map/all_to_all | solution.py:54
  (198 shorter events, 122.5 us)
Async XLA Ops:
  7.2 17.7 %copy-start = (bf16[768,1536]{1,0:T(8,128)(2,1)S(1)}, bf16[768,1536]{1,0:T(8,128)(2,1)}, u32[]{:S(2)}) copy-start(bf16[768,1536]{1,0:T(8,128)(2,1)} %param.23) | copy-start | bytes 7077892
  10.2 14.7 %copy-start.25 = (f32[512]{0:T(512)}, f32[512]{0:T(512)S(1)}, u32[]{:S(2)}) copy-start(f32[512]{0:T(512)S(1)} %add_rsqrt_fusion.1) | copy-start | bytes 6148
  16.0 8.9 %copy-start.32 = (f32[768]{0:T(1024)S(1)}, f32[768]{0:T(1024)}, u32[]{:S(2)}) copy-start(f32[768]{0:T(1024)} %param.24) | copy-start | bytes 9220
  18.5 19.2 %all-to-all-start = ((f32[4,3,100,65]{2,3,1,0:T(8,128)}), f32[4,3,100,65]{2,3,1,0:T(8,128)}, u32[]{:S(2)}, u32[]{:S(2)}) async-start(f32[4,3,100,65]{2,3,1,0:T(8,128)} %pad_maximum_fusion.3), calls=%async_computation | async-start | bytes 884736 | tf_op jit(solution)/shard_map/all_to_all | solution.py:54
  37.7 40.9 %all-to-all-start.1 = ((bf16[512,2,4,192]{0,3,1,2:T(8,128)(2,1)}), bf16[512,2,4,192]{0,3,1,2:T(8,128)(2,1)}, u32[]{:S(2)}, u32[]{:S(2)}) async-start(bf16[512,2,4,192]{0,3,1,2:T(8,128)(2,1)} %copy.73), calls=%async_computation.1 | async-start | bytes 3145728 | tf_op jit(solution)/shard_map/all_to_all | solution.py:116
  42.1 158.8 %all-gather.2.cloned.1.call-start = ((), (), s32[]{:S(2)}) async-start(), calls=%async_computation.10 | async-start | bytes 3932160 | tf_op jit(solution)/shard_map/all_gather | solution.py:156
  43.2 37.2 %copy-start.16 = (f32[3,100,65]{1,2,0:T(8,128)}, f32[3,100,65]{1,2,0:T(8,128)S(1)}, u32[]{:S(2)}) copy-start(f32[3,100,65]{1,2,0:T(8,128)S(1)} %reduce_sum.219) | copy-start | bytes 234004
  82.8 10.1 %copy-start.39 = (bf16[768,768]{1,0:T(8,128)(2,1)S(1)}, bf16[768,768]{1,0:T(8,128)(2,1)}, u32[]{:S(2)}) copy-start(bf16[768,768]{1,0:T(8,128)(2,1)} %param.25) | copy-start | bytes 3538948
  82.8 10.1 %copy-start.43 = (f32[768]{0:T(1024)S(1)}, f32[768]{0:T(1024)}, u32[]{:S(2)}) copy-start(f32[768]{0:T(1024)} %param.26) | copy-start | bytes 9220
  95.0 38.1 %copy-start.34 = (bf16[768]{0:T(1024)(128)(2,1)S(1)}, bf16[768]{0:T(1024)(128)(2,1)}, u32[]{:S(2)}) copy-start(bf16[768]{0:T(1024)(128)(2,1)} %param.30) | copy-start | bytes 4612
  96.2 181.9 %reduce-scatter.4.cloned.1.call-start = ((), (), s32[]{:S(2)}) async-start(), calls=%async_computation.11 | async-start | bytes 3932160 | tf_op jit(solution)/shard_map/reduce_scatter | solution.py:165
  96.3 30.1 %collective-permute-start = (bf16[512,768]{1,0:T(8,128)(2,1)}, bf16[512,768]{1,0:T(8,128)(2,1)}, u32[]{:S(2)}, u32[]{:S(2)}) collective-permute-start(bf16[512,768]{1,0:T(8,128)(2,1)} %param.33), channel_id=1, source_target_pairs={{0,1},{1,2},{2,3},{3,0},{4,5},{5,6},{6,7},{7,4},{8,9},{9,10},{10,1... | collective-permute-start | bytes 2359304 | tf_op jit(solution)/shard_map/ppermute | solution.py:36
  126.4 43.9 %collective-permute-start.1 = (bf16[512,768]{1,0:T(8,128)(2,1)}, bf16[512,768]{1,0:T(8,128)(2,1)}, u32[]{:S(2)}, u32[]{:S(2)}) collective-permute-start(bf16[512,768]{1,0:T(8,128)(2,1)} %collective-permute-done), channel_id=1, source_target_pairs={{0,1},{1,2},{2,3},{3,0},{4,5},{5,6},{6,7},{7,4},{8,9},{9,10},{10,1... | collective-permute-start | bytes 2359304 | tf_op jit(solution)/shard_map/ppermute | solution.py:36
  133.1 49.1 %copy-start.10 = (bf16[512,768]{1,0:T(8,128)(2,1)S(1)}, bf16[512,768]{1,0:T(8,128)(2,1)}, u32[]{:S(2)}) copy-start(bf16[512,768]{1,0:T(8,128)(2,1)} %param.33) | copy-start | bytes 2359300
  170.3 29.7 %collective-permute-start.2 = (bf16[512,768]{1,0:T(8,128)(2,1)}, bf16[512,768]{1,0:T(8,128)(2,1)S(1)}, u32[]{:S(2)}, u32[]{:S(2)}) collective-permute-start(bf16[512,768]{1,0:T(8,128)(2,1)} %collective-permute-done.1), channel_id=1, source_target_pairs={{0,1},{1,2},{2,3},{3,0},{4,5},{5,6},{6,7},{7,4},{8,9},{9,10},{10,1... | collective-permute-start | bytes 2359304 | tf_op jit(solution)/shard_map/ppermute | solution.py:36
  200.9 6.2 %copy-start.41 = (bf16[768,768]{1,0:T(8,128)(2,1)S(1)}, bf16[768,768]{1,0:T(8,128)(2,1)}, u32[]{:S(2)}) copy-start(bf16[768,768]{1,0:T(8,128)(2,1)} %param.31) | copy-start | bytes 3538948
  207.1 8.1 %copy-start.38 = (bf16[768,768]{1,0:T(8,128)(2,1)S(1)}, bf16[768,768]{1,0:T(8,128)(2,1)}, u32[]{:S(2)}) copy-start(bf16[768,768]{1,0:T(8,128)(2,1)} %param.29) | copy-start | bytes 3538948
  219.2 220.4 %reduce-scatter.8.cloned.1.call-start = ((), (), s32[]{:S(2)}) async-start(), calls=%async_computation.13 | async-start | bytes 7962624 | tf_op jit(solution)/shard_map/reduce_scatter | solution.py:209
  219.3 7.1 %copy-start.37 = (bf16[2048,768]{1,0:T(8,128)(2,1)S(1)}, bf16[2048,768]{1,0:T(8,128)(2,1)}, u32[]{:S(2)}) copy-start(bf16[2048,768]{1,0:T(8,128)(2,1)} %all-gather.2.cloned.1.call-done) | copy-start | bytes 9437188
  219.3 7.1 %copy-start.47 = (bf16[2048,768]{1,0:T(8,128)(2,1)S(1)}, bf16[2048,768]{1,0:T(8,128)(2,1)}, u32[]{:S(2)}) copy-start(bf16[2048,768]{1,0:T(8,128)(2,1)} %copy-done.46) | copy-start | bytes 9437188
  230.5 50.8 %copy-start.28 = (f32[768]{0:T(1024)S(1)}, f32[768]{0:T(1024)}, u32[]{:S(2)}) copy-start(f32[768]{0:T(1024)} %param.32) | copy-start | bytes 9220
  300.3 15.5 %all-to-all-start.3 = ((f32[4,3,100,64]{2,3,1,0:T(8,128)}), f32[4,3,100,64]{2,3,1,0:T(8,128)S(1)}, u32[]{:S(2)}, u32[]{:S(2)}) async-start(f32[4,3,100,64]{2,3,1,0:T(8,128)} %bitcast.114), calls=%async_computation.4 | async-start | bytes 786432 | tf_op jit(solution)/shard_map/all_to_all | solution.py:54
  320.1 5.3 copy-start.21
  342.4 45.1 %all-to-all-start.4 = ((bf16[4,562,384]{2,1,0:T(8,128)(2,1)}), bf16[4,562,384]{2,1,0:T(8,128)(2,1)}, u32[]{:S(2)}, u32[]{:S(2)}) async-start(bf16[4,562,384]{2,1,0:T(8,128)(2,1)} %pad_maximum_fusion.1), calls=%async_computation.5 | async-start | bytes 3489792 | tf_op jit(solution)/shard_map/all_to_all | solution.py:258
  347.0 147.8 %reduce-scatter.6.cloned.1.call-start = ((), (), s32[]{:S(2)}) async-start(), calls=%async_computation.12 | async-start | bytes 8404992 | tf_op jit(solution)/shard_map/reduce_scatter | solution.py:305
  408.0 4.9 copy-start.9
  408.0 4.9 copy-start.45
  434.8 75.1 %all-to-all-start.5 = ((bf16[4,512,768]{2,1,0:T(8,128)(2,1)}), bf16[4,512,768]{2,1,0:T(8,128)(2,1)}, u32[]{:S(2)}, u32[]{:S(2)}) async-start(bf16[4,512,768]{2,1,0:T(8,128)(2,1)} %bitcast.102), calls=%async_computation.6 | async-start | bytes 6291456 | tf_op jit(solution)/shard_map/all_to_all | solution.py:54
  497.1 17.1 %copy-start.36 = (f32[512]{0:T(512)S(1)}, f32[512]{0:T(512)}, u32[]{:S(2)}) copy-start(f32[512]{0:T(512)} %get-tuple-element.21) | copy-start | bytes 6148
  497.1 17.1 %copy-start.35 = (f32[512]{0:T(512)S(1)}, f32[512]{0:T(512)}, u32[]{:S(2)}) copy-start(f32[512]{0:T(512)} %get-tuple-element.22) | copy-start | bytes 6148
  497.1 17.1 %copy-start.31 = (f32[768]{0:T(1024)S(1)}, f32[768]{0:T(1024)}, u32[]{:S(2)}) copy-start(f32[768]{0:T(1024)} %param.19) | copy-start | bytes 9220
  509.9 33.5 %all-to-all-start.6 = ((f32[4,24,3084]{2,1,0:T(8,128)}), f32[4,24,3084]{2,1,0:T(8,128)}, u32[]{:S(2)}, u32[]{:S(2)}) async-start(f32[4,24,3084]{2,1,0:T(8,128)} %pad_maximum_fusion.2), calls=%async_computation.9 | async-start | bytes 2457600 | tf_op jit(solution)/shard_map/all_to_all | solution.py:54
  (31 other events, 71.0 us)
Sparse Core Ops, SparseCore 0:
  96.4 87.6 all-gather.1
  219.3 58.8 reduce-scatter.3
  292.2 65.2 reduce-scatter.7
  428.4 66.3 reduce-scatter.5

commit v7 on v6

--- a/solution.py
+++ b/solution.py
@@ -218,6 +218,11 @@
         summary_grad,
         preferred_element_type=jnp.float32,
     )
+    half_width = local_heads * head_dim
+    values_out = grad_values.astype(jnp.bfloat16).reshape(group_size, tok_rows, half_width)
+
+    values_in = lax.all_to_all(values_out, "mp", split_axis=0, concat_axis=0, tiled=True)
+
     grad_probs = jnp.einsum(
         "hcd,jhd->hcj", summary_grad, value_rows, preferred_element_type=jnp.float32
     )
@@ -232,24 +237,16 @@
     grad_keys = score_scale * jnp.einsum(
         "hcj,hcd->jhd", grad_scores, centroids, preferred_element_type=jnp.float32
     )
-    grad_kv = jnp.concatenate(
-        [
-            grad_keys.reshape(length, local_heads * head_dim),
-            grad_values.reshape(length, local_heads * head_dim),
-        ],
-        axis=1,
-    ).astype(jnp.bfloat16)
-    kv_width = 2 * local_heads * head_dim
     per_member = (grad_centroids.astype(jnp.float32) / divisor[:, :, None]).astype(
         jnp.bfloat16
     )
-    member_rows = per_member.size // kv_width
+    member_rows = per_member.size // half_width
     outgoing = jnp.concatenate(
         [
-            grad_kv.reshape(group_size, tok_rows, kv_width),
+            grad_keys.astype(jnp.bfloat16).reshape(group_size, tok_rows, half_width),
             jnp.broadcast_to(
-                per_member.reshape(1, member_rows, kv_width),
-                (group_size, member_rows, kv_width),
+                per_member.reshape(1, member_rows, half_width),
+                (group_size, member_rows, half_width),
             ),
         ],
         axis=1,
@@ -261,8 +258,9 @@
     result = scatter_sum(out_pieces, group_size)
     block_output = (residual + result).astype(jnp.bfloat16)
 
-    returned = incoming[:, :tok_rows].reshape(group_size, tok_rows, 2, local_heads * head_dim)
-    grad_keyval = returned.transpose(1, 2, 0, 3).reshape(tok_rows, 2 * model_width)
+    keys_back = incoming[:, :tok_rows].transpose(1, 0, 2).reshape(tok_rows, model_width)
+    values_back = values_in.transpose(1, 0, 2).reshape(tok_rows, model_width)
+    grad_keyval = jnp.concatenate([keys_back, values_back], axis=1)
     all_member = (
         incoming[:, tok_rows:].reshape(head_count, CLUSTERS, head_dim).astype(jnp.float32)
     )

time: 563 us -> 546 us (0.970)
  waiting for transfers between devices: 299 us -> 285 us
    all_to_all x1, waiting for transfers between devices: 33.2 us -> 15 us  [block_body(): lax.all_to_all(outgoing, 'mp', split_axis=0, concat_axis=0, tiled=True)]
    concatenate x4 -> x0, local copies, waits for them, and re-layouts: 10.6 us -> none  [block_body(): jnp.concatenate([grad_keys.reshape(length, local_heads * head_dim), grad_...]
    reshape x0 -> x4, local copies, waits for them, and re-layouts: none -> 10.4 us  [the longest x2 5.27 us: block_body(): grad_keys.astype(jnp.bfloat16).reshape(group_size, tok_rows, half_width)]
  transfers between devices with their start and end apart: 13 -> 14, of which waited for: 11 -> 12; matrix products, arithmetic and copies ran while one was open for 23% -> 22% of each run, Pallas kernels for 0% -> 0%
where the time goes in v7:
time: 546 us; the launch traced here: 538 us
  waiting for transfers between devices  285 us (52%)
  matrix products  75.4 us (14%)
  local copies, waits for them, and re-layouts  71.1 us (13%)
  starting transfers between devices  49 us (9%)
  other arithmetic  32.8 us (6%)
  between operations  14.9 us (3%)
  blocking collectives  9.55 us (2%)
    ppermute x3, waiting for transfers between devices, ring_shift(): lax.ppermute(x, 'mp', [(i, (i + 1) % group_size) for i in range(group_siz...  79.7 us
    reduce_scatter x1, waiting for transfers between devices, block_body(): lax.psum_scatter(packed_grads, 'dp', scatter_dimension=0, tiled=True)  53.2 us
    all_to_all x4, waiting for transfers between devices, scatter_sum(): lax.all_to_all(pieces, 'mp', split_axis=0, concat_axis=0, tiled=True)  49.8 us
    reduce_scatter x1, waiting for transfers between devices, block_body(): lax.psum_scatter(jnp.einsum('tf,df->td', grad_before, w_up, preferred_ele...  47.7 us
    all_to_all x1, waiting for transfers between devices, block_body(): lax.all_to_all(packed, 'mp', split_axis=2, concat_axis=0, tiled=True)  35.4 us
    all_to_all x4, starting transfers between devices, scatter_sum(): lax.all_to_all(pieces, 'mp', split_axis=0, concat_axis=0, tiled=True)  19 us
    ppermute x3, starting transfers between devices, ring_shift(): lax.ppermute(x, 'mp', [(i, (i + 1) % group_size) for i in range(group_siz...  16.9 us
    all_to_all x1, waiting for transfers between devices, block_body(): lax.all_to_all(outgoing, 'mp', split_axis=0, concat_axis=0, tiled=True)  15 us
  transfers between devices with their start and end apart: 14, of which 12 were waited for; matrix products, arithmetic and copies ran while one was open for 22% of the time, Pallas kernels for 0%

profile of v7, /device:TPU:0, one launch (start us, length us, event | category | flops | bytes accessed | tf_op | source)
XLA Modules:
  0.0 537.6 jit_solution(7702280956940320897)
XLA Ops:
  19.1 6.3 %all-to-all-start = ((f32[4,3,100,65]{2,3,1,0:T(8,128)}), f32[4,3,100,65]{2,3,1,0:T(8,128)}, u32[]{:S(2)}, u32[]{:S(2)}) async-start(f32[4,3,100,65]{2,3,1,0:T(8,128)} %pad_maximum_fusion.3), calls=%async_computation | async-start | bytes 884736 | tf_op jit(solution)/shard_map/all_to_all | solution.py:54
  34.1 4.2 all-to-all-done
  38.3 4.4 all-to-all-start.1
  43.8 35.4 %all-to-all-done.1 = bf16[512,2,4,192]{0,3,1,2:T(8,128)(2,1)} async-done(((bf16[512,2,4,192]{0,3,1,2:T(8,128)(2,1)}), bf16[512,2,4,192]{0,3,1,2:T(8,128)(2,1)}, u32[]{:S(2)}, u32[]{:S(2)}) %all-to-all-start.1) | async-done | bytes 1572896 | tf_op jit(solution)/shard_map/all_to_all | solution.py:116
  83.4 9.5 %all_to_all.53 = bf16[4,3,100,64]{2,3,1,0:T(8,128)(2,1)S(1)} all-to-all(bf16[4,3,100,64]{2,3,1,0:T(8,128)(2,1)S(1)} %broadcast_in_dim.23), channel_id=1, replica_groups=mesh['dp'=8,'mp'=4] {'mp'}, dimensions={0} | all-to-all | bytes 307200 | tf_op jit(solution)/shard_map/all_to_all | solution.py:60
  97.8 29.3 %collective-permute-done = bf16[512,768]{1,0:T(8,128)(2,1)} collective-permute-done((bf16[512,768]{1,0:T(8,128)(2,1)}, bf16[512,768]{1,0:T(8,128)(2,1)}, u32[]{:S(2)}, u32[]{:S(2)}) %collective-permute-start) | collective-permute-done | bytes 786464 | tf_op jit(solution)/shard_map/ppermute | solution.py:36
  127.0 6.7 %collective-permute-start.1 = (bf16[512,768]{1,0:T(8,128)(2,1)}, bf16[512,768]{1,0:T(8,128)(2,1)}, u32[]{:S(2)}, u32[]{:S(2)}) collective-permute-start(bf16[512,768]{1,0:T(8,128)(2,1)} %collective-permute-done), channel_id=1, source_target_pairs={{0,1},{1,2},{2,3},{3,0},{4,5},{5,6},{6,7},{7,4},{8,9},{9,10},{10,1... | collective-permute-start | bytes 2359304 | tf_op jit(solution)/shard_map/ppermute | solution.py:36
  133.7 37.2 %collective-permute-done.1 = bf16[512,768]{1,0:T(8,128)(2,1)} collective-permute-done((bf16[512,768]{1,0:T(8,128)(2,1)}, bf16[512,768]{1,0:T(8,128)(2,1)}, u32[]{:S(2)}, u32[]{:S(2)}) %collective-permute-start.1) | collective-permute-done | bytes 786464 | tf_op jit(solution)/shard_map/ppermute | solution.py:36
  170.9 9.3 %collective-permute-start.2 = (bf16[512,768]{1,0:T(8,128)(2,1)}, bf16[512,768]{1,0:T(8,128)(2,1)S(1)}, u32[]{:S(2)}, u32[]{:S(2)}) collective-permute-start(bf16[512,768]{1,0:T(8,128)(2,1)} %collective-permute-done.1), channel_id=1, source_target_pairs={{0,1},{1,2},{2,3},{3,0},{4,5},{5,6},{6,7},{7,4},{8,9},{9,10},{10,1... | collective-permute-start | bytes 2359304 | tf_op jit(solution)/shard_map/ppermute | solution.py:36
  187.3 13.2 %collective-permute-done.2 = bf16[512,768]{1,0:T(8,128)(2,1)S(1)} collective-permute-done((bf16[512,768]{1,0:T(8,128)(2,1)}, bf16[512,768]{1,0:T(8,128)(2,1)S(1)}, u32[]{:S(2)}, u32[]{:S(2)}) %collective-permute-start.2) | collective-permute-done | bytes 786464 | tf_op jit(solution)/shard_map/ppermute | solution.py:36
  201.5 6.2 %multiply_convert_fusion = (bf16[2048,768]{1,0:T(8,128)(2,1)}, f32[2048,768]{1,0:T(8,128)S(1)}) fusion(f32[768]{0:T(1024)S(1)} %convert_element_type.138, bf16[2048,768]{1,0:T(8,128)(2,1)} %all-gather.2.cloned.1.call-done, bf16[768,768]{1,0:T(8,128)(2,1)} %param.29), kind=kOutput, calls=%fused_computation.10 | convolution fusion | flops 2425356288 | bytes 13765632 | tf_op jit(solution)/shard_map/dot_general | solution.py:158
  207.7 6.4 %convert_reduce_fusion = (f32[768]{0:T(1024)}, bf16[2048,768]{1,0:T(8,128)(2,1)S(1)}) fusion(f32[2048,768]{1,0:T(8,128)S(1)} %get-tuple-element.50, f32[768]{0:T(1024)S(1)} %convert_element_type.138, bf16[2048,768]{1,0:T(8,128)(2,1)} %bitcast.15, bf16[768,768]{1,0:T(8,128)(2,1)S(1)} %copy-done.48), kind=kOutput, calls=%fused_computation.8 | convolution fusion | flops 2436365568 | bytes 13768704 | tf_op jit(solution)/shard_map/td,fd->tf/dot_general | solution.py:163
  215.8 4.0 convolution_convert_fusion
  219.9 7.1 %convolution_bitcast_fusion = f32[1,768,768]{2,1,0:T(8,128)} fusion(bf16[2048,768]{1,0:T(8,128)(2,1)} %bitcast.15, bf16[2048,768]{1,0:T(8,128)(2,1)} %get-tuple-element.49), kind=kOutput, calls=%fused_computation.59 | convolution fusion | flops 2415919104 | bytes 8650752 | tf_op jit(solution)/shard_map/td,tf->df/dot_general | solution.py:178
  227.0 4.2 convolution_bitcast_fusion.1
  231.1 47.7 %reduce-scatter.4.cloned.1.call-done = bf16[512,768]{1,0:T(8,128)(2,1)} async-done(((bf16[2048,768]{1,0:T(8,128)(2,1)}), bf16[512,768]{1,0:T(8,128)(2,1)}) %reduce-scatter.4.cloned.1.call-update) | async-done | bytes 786448 | tf_op jit(solution)/shard_map/reduce_scatter | solution.py:165
  282.0 3.8 convert_reduce_fusion.6
  300.9 3.6 all-to-all-start.3
  305.2 11.0 %all-to-all-done.3 = f32[4,3,100,64]{2,3,1,0:T(8,128)S(1)} async-done(((f32[4,3,100,64]{2,3,1,0:T(8,128)}), f32[4,3,100,64]{2,3,1,0:T(8,128)S(1)}, u32[]{:S(2)}, u32[]{:S(2)}) %all-to-all-start.3) | async-done | bytes 307232 | tf_op jit(solution)/shard_map/all_to_all | solution.py:54
  316.9 3.8 fusion.9
  325.8 4.4 all-to-all-start.6
  345.9 4.1 all-to-all-done.6
  350.0 4.2 all-to-all-start.4
  363.1 15.0 %all-to-all-done.4 = bf16[4,612,192]{1,2,0:T(8,128)(2,1)} async-done(((bf16[4,612,192]{1,2,0:T(8,128)(2,1)}), bf16[4,612,192]{1,2,0:T(8,128)(2,1)}, u32[]{:S(2)}, u32[]{:S(2)}) %all-to-all-start.4) | async-done | bytes 940064 | tf_op jit(solution)/shard_map/all_to_all | solution.py:255
  394.4 6.9 %fusion.11 = f32[768,2304]{1,0:T(8,128)} fusion(bf16[512,768]{0,1:T(8,128)(2,1)} %bitcast.26, bf16[512,768]{0,1:T(8,128)(2,1)} %bitcast.109, bf16[512,768]{0,1:T(8,128)(2,1)} %bitcast.111, bf16[512,768]{1,0:T(8,128)(2,1)S(1)} %copy-done.6, f32[768]{0:T(1024)} %param.20, f32[768]{0:T(1024)} %param.19, f32[512]{0:T(512)S(1)} %copy-done.32, f32[512]{0:T(512)S(1)} %copy-done.29), kind=kOutput, calls=%fused_computation.37 | convolution fusion | flops 1821376512 | bytes 10233856 | tf_op jit(solution)/shard_map/td,te->de/dot_general | solution.py:273
  401.4 10.1 %concatenate.41 = f32[768,2316]{1,0:T(8,128)} concatenate(f32[768,2304]{1,0:T(8,128)} %fusion.11, f32[768,1]{1,0:T(8,128)} %stack.48, f32[768,1]{1,0:T(8,128)} %stack.49, f32[768,1]{1,0:T(8,128)} %stack.50, f32[768,1]{1,0:T(8,128)} %stack.51, f32[768,1]{1,0:T(8,128)} %stack.52, f32[768,1]{1,0:T(8,128)} %stack.53, f32[768,1]{1,0:T(8,128)} %stack.54, f32[768,1]{1,0:T(8,128)} %stack.55, ...), dimensions={1} | concatenate | bytes 14229504 | tf_op jit(solution)/shard_map/concatenate | solution.py:301
  411.5 6.5 %convolution_convert_fusion.1 = bf16[2048,768]{1,0:T(8,128)(2,1)} fusion(bf16[2048,768]{1,0:T(8,128)(2,1)} %get-tuple-element.49, bf16[768,768]{1,0:T(8,128)(2,1)} %param.31), kind=kOutput, calls=%fused_computation.15 | convolution fusion | flops 2417491968 | bytes 7471104 | tf_op jit(solution)/shard_map/dot_general | solution.py:174
  418.0 4.7 all-to-all-start.5
  424.9 53.2 %reduce-scatter.6.cloned.1.call-done = f32[96,2316]{1,0:T(8,128)} async-done(((f32[768,2316]{1,0:T(8,128)}), f32[96,2316]{1,0:T(8,128)}) %reduce-scatter.6.cloned.1.call-update) | async-done | bytes 889360 | tf_op jit(solution)/shard_map/reduce_scatter | solution.py:303
  480.4 12.6 %all-to-all-done.5 = bf16[4,512,768]{2,1,0:T(8,128)(2,1)} async-done(((bf16[4,512,768]{2,1,0:T(8,128)(2,1)}), bf16[4,512,768]{2,1,0:T(8,128)(2,1)}, u32[]{:S(2)}, u32[]{:S(2)}) %all-to-all-start.5) | async-done | bytes 3145760 | tf_op jit(solution)/shard_map/all_to_all | solution.py:54
  493.0 4.3 all-to-all-start.7
  504.6 21.9 %all-to-all-done.7 = f32[4,24,3084]{2,1,0:T(8,128)} async-done(((f32[4,24,3084]{2,1,0:T(8,128)}), f32[4,24,3084]{2,1,0:T(8,128)}, u32[]{:S(2)}, u32[]{:S(2)}) %all-to-all-start.7) | async-done | bytes 1184288 | tf_op jit(solution)/shard_map/all_to_all | solution.py:54
  (212 shorter events, 121.4 us)
Async XLA Ops:
  7.2 18.3 %copy-start = (bf16[768,1536]{1,0:T(8,128)(2,1)S(1)}, bf16[768,1536]{1,0:T(8,128)(2,1)}, u32[]{:S(2)}) copy-start(bf16[768,1536]{1,0:T(8,128)(2,1)} %param.23) | copy-start | bytes 7077892
  18.3 7.2 %copy-start.39 = (f32[768]{0:T(1024)S(1)}, f32[768]{0:T(1024)}, u32[]{:S(2)}) copy-start(f32[768]{0:T(1024)} %param.24) | copy-start | bytes 9220
  18.3 7.2 %copy-start.36 = (f32[768]{0:T(1024)S(1)}, f32[768]{0:T(1024)}, u32[]{:S(2)}) copy-start(f32[768]{0:T(1024)} %param.19) | copy-start | bytes 9220
  19.1 19.2 %all-to-all-start = ((f32[4,3,100,65]{2,3,1,0:T(8,128)}), f32[4,3,100,65]{2,3,1,0:T(8,128)}, u32[]{:S(2)}, u32[]{:S(2)}) async-start(f32[4,3,100,65]{2,3,1,0:T(8,128)} %pad_maximum_fusion.3), calls=%async_computation | async-start | bytes 884736 | tf_op jit(solution)/shard_map/all_to_all | solution.py:54
  38.3 40.9 %all-to-all-start.1 = ((bf16[512,2,4,192]{0,3,1,2:T(8,128)(2,1)}), bf16[512,2,4,192]{0,3,1,2:T(8,128)(2,1)}, u32[]{:S(2)}, u32[]{:S(2)}) async-start(bf16[512,2,4,192]{0,3,1,2:T(8,128)(2,1)} %copy.56), calls=%async_computation.1 | async-start | bytes 3145728 | tf_op jit(solution)/shard_map/all_to_all | solution.py:116
  42.7 158.8 %all-gather.2.cloned.1.call-start = ((), (), s32[]{:S(2)}) async-start(), calls=%async_computation.11 | async-start | bytes 3932160 | tf_op jit(solution)/shard_map/all_gather | solution.py:156
  43.8 37.2 %copy-start.17 = (f32[3,100,65]{1,2,0:T(8,128)}, f32[3,100,65]{1,2,0:T(8,128)S(1)}, u32[]{:S(2)}) copy-start(f32[3,100,65]{1,2,0:T(8,128)S(1)} %reduce_sum.219) | copy-start | bytes 234004
  82.5 10.5 %copy-start.25 = (s32[512,12]{0,1:T(8,128)S(1)}, s32[512,12]{0,1:T(8,128)}, u32[]{:S(2)}) copy-start(s32[512,12]{0,1:T(8,128)} %param.18) | copy-start | bytes 73732
  83.4 10.1 %copy-start.46 = (bf16[768,768]{1,0:T(8,128)(2,1)S(1)}, bf16[768,768]{1,0:T(8,128)(2,1)}, u32[]{:S(2)}) copy-start(bf16[768,768]{1,0:T(8,128)(2,1)} %param.25) | copy-start | bytes 3538948
  83.4 10.1 %copy-start.50 = (f32[768]{0:T(1024)S(1)}, f32[768]{0:T(1024)}, u32[]{:S(2)}) copy-start(f32[768]{0:T(1024)} %param.26) | copy-start | bytes 9220
  95.6 38.1 %copy-start.41 = (bf16[768]{0:T(1024)(128)(2,1)S(1)}, bf16[768]{0:T(1024)(128)(2,1)}, u32[]{:S(2)}) copy-start(bf16[768]{0:T(1024)(128)(2,1)} %param.30) | copy-start | bytes 4612
  96.8 182.0 %reduce-scatter.4.cloned.1.call-start = ((), (), s32[]{:S(2)}) async-start(), calls=%async_computation.12 | async-start | bytes 3932160 | tf_op jit(solution)/shard_map/reduce_scatter | solution.py:165
  96.9 30.1 %collective-permute-start = (bf16[512,768]{1,0:T(8,128)(2,1)}, bf16[512,768]{1,0:T(8,128)(2,1)}, u32[]{:S(2)}, u32[]{:S(2)}) collective-permute-start(bf16[512,768]{1,0:T(8,128)(2,1)} %param.33), channel_id=1, source_target_pairs={{0,1},{1,2},{2,3},{3,0},{4,5},{5,6},{6,7},{7,4},{8,9},{9,10},{10,1... | collective-permute-start | bytes 2359304 | tf_op jit(solution)/shard_map/ppermute | solution.py:36
  127.0 43.8 %collective-permute-start.1 = (bf16[512,768]{1,0:T(8,128)(2,1)}, bf16[512,768]{1,0:T(8,128)(2,1)}, u32[]{:S(2)}, u32[]{:S(2)}) collective-permute-start(bf16[512,768]{1,0:T(8,128)(2,1)} %collective-permute-done), channel_id=1, source_target_pairs={{0,1},{1,2},{2,3},{3,0},{4,5},{5,6},{6,7},{7,4},{8,9},{9,10},{10,1... | collective-permute-start | bytes 2359304 | tf_op jit(solution)/shard_map/ppermute | solution.py:36
  133.7 48.4 %copy-start.10 = (bf16[512,768]{1,0:T(8,128)(2,1)S(1)}, bf16[512,768]{1,0:T(8,128)(2,1)}, u32[]{:S(2)}) copy-start(bf16[512,768]{1,0:T(8,128)(2,1)} %param.33) | copy-start | bytes 2359300
  170.9 29.7 %collective-permute-start.2 = (bf16[512,768]{1,0:T(8,128)(2,1)}, bf16[512,768]{1,0:T(8,128)(2,1)S(1)}, u32[]{:S(2)}, u32[]{:S(2)}) collective-permute-start(bf16[512,768]{1,0:T(8,128)(2,1)} %collective-permute-done.1), channel_id=1, source_target_pairs={{0,1},{1,2},{2,3},{3,0},{4,5},{5,6},{6,7},{7,4},{8,9},{9,10},{10,1... | collective-permute-start | bytes 2359304 | tf_op jit(solution)/shard_map/ppermute | solution.py:36
  207.7 8.1 %copy-start.45 = (bf16[768,768]{1,0:T(8,128)(2,1)S(1)}, bf16[768,768]{1,0:T(8,128)(2,1)}, u32[]{:S(2)}) copy-start(bf16[768,768]{1,0:T(8,128)(2,1)} %param.29) | copy-start | bytes 3538948
  219.8 202.9 %reduce-scatter.8.cloned.1.call-start = ((), (), s32[]{:S(2)}) async-start(), calls=%async_computation.14 | async-start | bytes 7962624 | tf_op jit(solution)/shard_map/reduce_scatter | solution.py:209
  219.9 7.1 %copy-start.44 = (bf16[2048,768]{1,0:T(8,128)(2,1)S(1)}, bf16[2048,768]{1,0:T(8,128)(2,1)}, u32[]{:S(2)}) copy-start(bf16[2048,768]{1,0:T(8,128)(2,1)} %all-gather.2.cloned.1.call-done) | copy-start | bytes 9437188
  219.9 7.1 %copy-start.53 = (bf16[2048,768]{1,0:T(8,128)(2,1)S(1)}, bf16[2048,768]{1,0:T(8,128)(2,1)}, u32[]{:S(2)}) copy-start(bf16[2048,768]{1,0:T(8,128)(2,1)} %copy-done.52) | copy-start | bytes 9437188
  231.1 50.8 %copy-start.34 = (f32[768]{0:T(1024)S(1)}, f32[768]{0:T(1024)}, u32[]{:S(2)}) copy-start(f32[768]{0:T(1024)} %param.32) | copy-start | bytes 9220
  300.9 15.3 %all-to-all-start.3 = ((f32[4,3,100,64]{2,3,1,0:T(8,128)}), f32[4,3,100,64]{2,3,1,0:T(8,128)S(1)}, u32[]{:S(2)}, u32[]{:S(2)}) async-start(f32[4,3,100,64]{2,3,1,0:T(8,128)} %bitcast.114), calls=%async_computation.4 | async-start | bytes 786432 | tf_op jit(solution)/shard_map/all_to_all | solution.py:54
  323.7 6.6 %copy-start.23 = (bf16[3,100,64]{1,2,0:T(8,128)(2,1)S(1)}, bf16[3,100,64]{1,2,0:T(8,128)(2,1)}, u32[]{:S(2)}) copy-start(bf16[3,100,64]{1,2,0:T(8,128)(2,1)} %reduce_sum.225) | copy-start | bytes 115204
  325.8 24.1 %all-to-all-start.6 = ((bf16[4,512,192]{1,2,0:T(8,128)(2,1)}), bf16[4,512,192]{1,2,0:T(8,128)(2,1)}, u32[]{:S(2)}, u32[]{:S(2)}) async-start(bf16[4,512,192]{1,2,0:T(8,128)(2,1)} %copy.64), calls=%async_computation.7 | async-start | bytes 1572864 | tf_op jit(solution)/shard_map/all_to_all | solution.py:224
  343.6 10.6 %copy-start.40 = (f32[768]{0:T(1024)S(1)}, f32[768]{0:T(1024)}, u32[]{:S(2)}) copy-start(f32[768]{0:T(1024)} %get-tuple-element.56) | copy-start | bytes 9220
  350.0 28.2 %all-to-all-start.4 = ((bf16[4,612,192]{1,2,0:T(8,128)(2,1)}), bf16[4,612,192]{1,2,0:T(8,128)(2,1)}, u32[]{:S(2)}, u32[]{:S(2)}) async-start(bf16[4,612,192]{1,2,0:T(8,128)(2,1)} %pad_maximum_fusion.2), calls=%async_computation.5 | async-start | bytes 1966080 | tf_op jit(solution)/shard_map/all_to_all | solution.py:255
  354.2 123.9 %reduce-scatter.6.cloned.1.call-start = ((), (), s32[]{:S(2)}) async-start(), calls=%async_computation.13 | async-start | bytes 8404992 | tf_op jit(solution)/shard_map/reduce_scatter | solution.py:303
  418.0 75.0 %all-to-all-start.5 = ((bf16[4,512,768]{2,1,0:T(8,128)(2,1)}), bf16[4,512,768]{2,1,0:T(8,128)(2,1)}, u32[]{:S(2)}, u32[]{:S(2)}) async-start(bf16[4,512,768]{2,1,0:T(8,128)(2,1)} %bitcast.100), calls=%async_computation.6 | async-start | bytes 6291456 | tf_op jit(solution)/shard_map/all_to_all | solution.py:54
  480.4 16.9 %copy-start.43 = (f32[512]{0:T(512)S(1)}, f32[512]{0:T(512)}, u32[]{:S(2)}) copy-start(f32[512]{0:T(512)} %get-tuple-element.21) | copy-start | bytes 6148
  480.4 16.9 %copy-start.42 = (f32[512]{0:T(512)S(1)}, f32[512]{0:T(512)}, u32[]{:S(2)}) copy-start(f32[512]{0:T(512)} %get-tuple-element.22) | copy-start | bytes 6148
  480.4 16.9 %copy-start.38 = (f32[768]{0:T(1024)S(1)}, f32[768]{0:T(1024)}, u32[]{:S(2)}) copy-start(f32[768]{0:T(1024)} %param.19) | copy-start | bytes 9220
  493.0 33.5 %all-to-all-start.7 = ((f32[4,24,3084]{2,1,0:T(8,128)}), f32[4,24,3084]{2,1,0:T(8,128)}, u32[]{:S(2)}, u32[]{:S(2)}) async-start(f32[4,24,3084]{2,1,0:T(8,128)} %pad_maximum_fusion.1), calls=%async_computation.10 | async-start | bytes 2457600 | tf_op jit(solution)/shard_map/all_to_all | solution.py:54
  (38 other events, 86.1 us)
Sparse Core Ops, SparseCore 0:
  97.0 87.7 all-gather.1
  219.9 58.8 reduce-scatter.3
  292.8 65.2 reduce-scatter.7
  411.6 66.4 reduce-scatter.5

commit v8 on v7

--- a/solution.py
+++ b/solution.py
@@ -30,23 +30,6 @@
     cumulative = 0.5 * (1.0 + jax.scipy.special.erf(before / math.sqrt(2.0)))
     density = jnp.exp(-0.5 * before * before) / math.sqrt(2.0 * math.pi)
     return (before * cumulative, cumulative + before * density)
-
-
-def ring_shift(x, group_size):
-    return lax.ppermute(x, "mp", [(i, (i + 1) % group_size) for i in range(group_size)])
-
-
-def ring_gather(x, group_size):
-    me = lax.axis_index("mp")
-    out = jnp.zeros((group_size,) + x.shape, x.dtype)
-    out = lax.dynamic_update_index_in_dim(out, x, me, 0)
-    cur = x
-    for step in range(1, group_size):
-        cur = ring_shift(cur, group_size)
-        out = lax.dynamic_update_index_in_dim(
-            out, cur, jnp.remainder(me + group_size - step, group_size), 0
-        )
-    return out.reshape((group_size * x.shape[0],) + x.shape[1:])
 
 
 def scatter_sum(partial, group_size):
@@ -88,7 +71,7 @@
     local_heads = head_count // group_size
     score_scale = float(head_dim) ** (-0.5)
 
-    grad_rows = ring_gather(cotangent, group_size)
+    grad_rows = lax.all_gather(cotangent, "mp", axis=0, tiled=True)
 
     inputs = block_input.astype(jnp.float32)
     normed_one, standard_one, factor_one = norm_forward(inputs, ln1_gain, ln1_bias)
@@ -111,20 +94,40 @@
         preferred_element_type=jnp.float32,
     )
     cluster_sizes = jnp.sum(member_float, axis=2)
-    packed = keyval.reshape(tok_rows, 2, group_size, local_heads * head_dim)
+    size_high = jnp.floor(cluster_sizes / 256.0)
+    size_low = cluster_sizes - 256.0 * size_high
+    partial = jnp.concatenate(
+        [query_sums, size_high[:, :, None], size_low[:, :, None]], axis=2
+    ).reshape(group_size, -1)
+    partial_size = partial.shape[1]
+    half_width = local_heads * head_dim
+    extra_rows = -(-partial_size // (2 * half_width))
+    partial = jnp.pad(partial, ((0, 0), (0, extra_rows * 2 * half_width - partial_size)))
+    extra = (
+        partial.reshape(group_size, extra_rows, 2, half_width)
+        .transpose(1, 2, 0, 3)
+        .astype(jnp.bfloat16)
+    )
+    packed = jnp.concatenate([keyval.reshape(tok_rows, 2, group_size, half_width), extra], axis=0)
 
     arrived = lax.all_to_all(packed, "mp", split_axis=2, concat_axis=0, tiled=True)
-    sums_and_sizes = scatter_sum(
-        jnp.concatenate([query_sums, cluster_sizes[:, :, None]], axis=2), group_size
-    )
-
+
+    blocks = arrived.reshape(group_size, tok_rows + extra_rows, 2, half_width)
+    sums_and_sizes = jnp.sum(
+        blocks[:, tok_rows:]
+        .reshape(group_size, -1)[:, :partial_size]
+        .reshape(group_size, local_heads, CLUSTERS, head_dim + 2)
+        .astype(jnp.float32),
+        axis=0,
+    )
     query_sums = sums_and_sizes[:, :, :head_dim]
-    cluster_sizes = sums_and_sizes[:, :, head_dim]
+    cluster_sizes = 256.0 * sums_and_sizes[:, :, head_dim] + sums_and_sizes[:, :, head_dim + 1]
     divisor = jnp.maximum(cluster_sizes, 1.0)
     centroids = (query_sums / divisor[:, :, None]).astype(jnp.bfloat16)
-    length = arrived.shape[0]
-    key_rows = arrived[:, 0, 0].reshape(length, local_heads, head_dim)
-    value_rows = arrived[:, 1, 0].reshape(length, local_heads, head_dim)
+    kv_rows = blocks[:, :tok_rows].reshape(group_size * tok_rows, 2, half_width)
+    length = kv_rows.shape[0]
+    key_rows = kv_rows[:, 0].reshape(length, local_heads, head_dim)
+    value_rows = kv_rows[:, 1].reshape(length, local_heads, head_dim)
     scores = score_scale * jnp.einsum(
         "hcd,jhd->hcj", centroids, key_rows, preferred_element_type=jnp.float32
     )

time: 546 us -> 577 us (1.057)
  blocking collectives: 9.55 us -> 61.5 us
  starting transfers between devices: 49 us -> 21.7 us
    ppermute x3 -> x0, waiting for transfers between devices: 79.7 us -> none  [ring_shift(): lax.ppermute(x, 'mp', [(i, (i + 1) % group_size) for i in range(group_siz...]
    all_gather x1, waiting for transfers between devices: 0.01 us -> 61.5 us  [block_body(): gathered = lax.all_gather(second, 'mp', axis=0, tiled=True)]
    all_gather x0 -> x1, waiting for transfers between devices: none -> 56.7 us  [block_body(): grad_rows = lax.all_gather(cotangent, 'mp', axis=0, tiled=True)]
    all_to_all x0 -> x1, blocking collectives: none -> 51.5 us  [block_body(): lax.all_to_all(packed, 'mp', split_axis=2, concat_axis=0, tiled=True)]
    all_to_all x1 -> x0, waiting for transfers between devices: 35.4 us -> none  [block_body(): lax.all_to_all(packed, 'mp', split_axis=2, concat_axis=0, tiled=True)]
    ppermute x3 -> x0, starting transfers between devices: 16.9 us -> none  [ring_shift(): lax.ppermute(x, 'mp', [(i, (i + 1) % group_size) for i in range(group_siz...]
    all_to_all x4 -> x3, starting transfers between devices: 19 us -> 12.7 us  [scatter_sum(): lax.all_to_all(pieces, 'mp', split_axis=0, concat_axis=0, tiled=True)]
    dynamic_update_slice x4 -> x0, local copies, waits for them, and re-layouts: 6.12 us -> none  [the longest x3 5.11 us: ring_gather(): lax.dynamic_update_index_in_dim(out, cur, jnp.remainder(me + group_size -...]
  transfers between devices with their start and end apart: 14 -> 10, of which waited for: 12 -> 9; matrix products, arithmetic and copies ran while one was open for 22% -> 20% of each run, Pallas kernels for 0% -> 0%
where the time goes in v8:
time: 577 us; the launch traced here: 567 us
  waiting for transfers between devices  284 us (49%)
  matrix products  78.9 us (14%)
  local copies, waits for them, and re-layouts  72.2 us (13%)
  blocking collectives  61.5 us (11%)
  other arithmetic  33.8 us (6%)
  starting transfers between devices  21.7 us (4%)
  between operations  14.9 us (3%)
    all_gather x1, waiting for transfers between devices, block_body(): gathered = lax.all_gather(second, 'mp', axis=0, tiled=True)  61.5 us
    all_gather x1, waiting for transfers between devices, block_body(): grad_rows = lax.all_gather(cotangent, 'mp', axis=0, tiled=True)  56.7 us
    reduce_scatter x1, waiting for transfers between devices, block_body(): lax.psum_scatter(packed_grads, 'dp', scatter_dimension=0, tiled=True)  53.2 us
    all_to_all x1, blocking collectives, block_body(): lax.all_to_all(packed, 'mp', split_axis=2, concat_axis=0, tiled=True)  51.5 us
    reduce_scatter x1, waiting for transfers between devices, block_body(): lax.psum_scatter(jnp.einsum('tf,df->td', grad_before, w_up, preferred_ele...  47.8 us
    all_to_all x3, waiting for transfers between devices, scatter_sum(): lax.all_to_all(pieces, 'mp', split_axis=0, concat_axis=0, tiled=True)  45.6 us
    all_to_all x1, waiting for transfers between devices, block_body(): lax.all_to_all(outgoing, 'mp', split_axis=0, concat_axis=0, tiled=True)  14.4 us
    all_to_all x3, starting transfers between devices, scatter_sum(): lax.all_to_all(pieces, 'mp', split_axis=0, concat_axis=0, tiled=True)  12.7 us
  transfers between devices with their start and end apart: 10, of which 9 were waited for; matrix products, arithmetic and copies ran while one was open for 20% of the time, Pallas kernels for 0%

profile of v8, /device:TPU:0, one launch (start us, length us, event | category | flops | bytes accessed | tf_op | source)
XLA Modules:
  0.0 567.1 jit_solution(12615391880565470032)
XLA Ops:
  10.3 3.1 add_convert_fusion.2
  24.5 3.3 fusion.6
  32.3 51.5 %all_to_all.45 = bf16[564,2,4,192]{0,3,1,2:T(8,128)(2,1)S(1)} all-to-all(bf16[564,2,4,192]{0,3,1,2:T(8,128)(2,1)S(1)} %copy.87), channel_id=1, replica_groups=mesh['dp'=8,'mp'=4] {'mp'}, dimensions={2} | all-to-all | bytes 3465216 | tf_op jit(solution)/shard_map/all_to_all | solution.py:113
  95.2 10.0 %all_to_all.46 = bf16[4,3,100,64]{2,3,1,0:T(8,128)(2,1)S(1)} all-to-all(bf16[4,3,100,64]{2,3,1,0:T(8,128)(2,1)S(1)} %broadcast_in_dim.8), channel_id=1, replica_groups=mesh['dp'=8,'mp'=4] {'mp'}, dimensions={0} | all-to-all | bytes 307200 | tf_op jit(solution)/shard_map/all_to_all | solution.py:43
  110.1 61.5 %all-gather.3.cloned.1.call-done = bf16[2048,768]{1,0:T(8,128)(2,1)} async-done(((bf16[512,768]{1,0:T(8,128)(2,1)}), bf16[2048,768]{1,0:T(8,128)(2,1)}) %all-gather.3.cloned.1.call-update) | async-done | bytes 3145744 | tf_op jit(solution)/shard_map/all_gather | solution.py:159
  171.6 6.9 %multiply_convert_fusion = (bf16[2048,768]{1,0:T(8,128)(2,1)}, f32[2048,768]{1,0:T(8,128)}) fusion(f32[768]{0:T(1024)S(1)} %convert_element_type.154, bf16[2048,768]{1,0:T(8,128)(2,1)} %all-gather.3.cloned.1.call-done, bf16[768,768]{1,0:T(8,128)(2,1)} %param.29), kind=kOutput, calls=%fused_computation.10 | convolution fusion | flops 2425356288 | bytes 13765632 | tf_op jit(solution)/shard_map/dot_general | solution.py:161
  178.5 56.7 %all-gather.5.cloned.1.call-done = bf16[2048,768]{1,0:T(8,128)(2,1)} async-done(((bf16[512,768]{1,0:T(8,128)(2,1)}), bf16[2048,768]{1,0:T(8,128)(2,1)}) %all-gather.5.cloned.1.call-update) | async-done | bytes 3145744 | tf_op jit(solution)/shard_map/all_gather | solution.py:74
  235.3 8.1 %convert_reduce_fusion = (f32[768]{0:T(1024)}, bf16[2048,768]{1,0:T(8,128)(2,1)S(1)}) fusion(f32[2048,768]{1,0:T(8,128)} %get-tuple-element.52, f32[768]{0:T(1024)S(1)} %convert_element_type.154, bf16[2048,768]{1,0:T(8,128)(2,1)} %all-gather.5.cloned.1.call-done, bf16[768,768]{1,0:T(8,128)(2,1)} %param.31), kind=kOutput, calls=%fused_computation.8 | convolution fusion | flops 2436365568 | bytes 13768704 | tf_op jit(solution)/shard_map/td,fd->tf/dot_general | solution.py:166
  245.1 4.0 convolution_convert_fusion
  249.2 7.1 %convolution_bitcast_fusion.1 = f32[1,768,768]{2,1,0:T(8,128)} fusion(bf16[2048,768]{1,0:T(8,128)(2,1)} %all-gather.3.cloned.1.call-done, bf16[2048,768]{1,0:T(8,128)(2,1)} %copy-done.45), kind=kOutput, calls=%fused_computation.61 | convolution fusion | flops 2415919104 | bytes 8650752 | tf_op jit(solution)/shard_map/td,tf->df/dot_general | solution.py:183
  256.3 4.2 convolution_bitcast_fusion
  260.5 47.8 %reduce-scatter.4.cloned.1.call-done = bf16[512,768]{1,0:T(8,128)(2,1)} async-done(((bf16[2048,768]{1,0:T(8,128)(2,1)}), bf16[512,768]{1,0:T(8,128)(2,1)}) %reduce-scatter.4.cloned.1.call-update) | async-done | bytes 786448 | tf_op jit(solution)/shard_map/reduce_scatter | solution.py:168
  308.3 3.1 fusion.42
  311.5 3.8 convert_reduce_fusion.6
  318.8 3.4 pad_maximum_fusion
  322.2 3.5 convolution_convert_fusion.3
  330.5 3.6 all-to-all-start.2
  334.8 11.0 %all-to-all-done.2 = f32[4,3,100,64]{2,3,1,0:T(8,128)S(1)} async-done(((f32[4,3,100,64]{2,3,1,0:T(8,128)}), f32[4,3,100,64]{2,3,1,0:T(8,128)S(1)}, u32[]{:S(2)}, u32[]{:S(2)}) %all-to-all-start.2) | async-done | bytes 307232 | tf_op jit(solution)/shard_map/all_to_all | solution.py:37
  346.5 3.8 fusion.9
  355.5 4.4 all-to-all-start.5
  375.4 4.2 all-to-all-done.5
  379.6 4.2 all-to-all-start.3
  393.4 14.4 %all-to-all-done.3 = bf16[4,612,192]{1,2,0:T(8,128)(2,1)} async-done(((bf16[4,612,192]{1,2,0:T(8,128)(2,1)}), bf16[4,612,192]{1,2,0:T(8,128)(2,1)}, u32[]{:S(2)}, u32[]{:S(2)}) %all-to-all-start.3) | async-done | bytes 940064 | tf_op jit(solution)/shard_map/all_to_all | solution.py:258
  424.1 6.8 %fusion.11 = f32[768,2304]{1,0:T(8,128)} fusion(bf16[512,768]{0,1:T(8,128)(2,1)} %bitcast.24, bf16[512,768]{0,1:T(8,128)(2,1)} %bitcast.107, bf16[512,768]{0,1:T(8,128)(2,1)} %bitcast.109, bf16[512,768]{1,0:T(8,128)(2,1)S(1)} %copy-done.6, f32[768]{0:T(1024)} %param.20, f32[768]{0:T(1024)} %param.19, f32[512]{0:T(512)S(1)} %copy-done.28, ...), kind=kOutput, calls=%fused_computation.37 | convolution fusion | flops 1821376512 | bytes 10233856 | tf_op jit(solution)/shard_map/td,te->de/dot_general | solution.py:276
  430.9 10.1 %concatenate.39 = f32[768,2316]{1,0:T(8,128)} concatenate(f32[768,2304]{1,0:T(8,128)} %fusion.11, f32[768,1]{1,0:T(8,128)} %stack.48, f32[768,1]{1,0:T(8,128)} %stack.49, f32[768,1]{1,0:T(8,128)} %stack.50, f32[768,1]{1,0:T(8,128)} %stack.51, f32[768,1]{1,0:T(8,128)} %stack.52, f32[768,1]{1,0:T(8,128)} %stack.53, f32[768,1]{1,0:T(8,128)} %stack.54, f32[768,1]{1,0:T(8,128)} %stack.55, ...), dimensions={1} | concatenate | bytes 14229504 | tf_op jit(solution)/shard_map/concatenate | solution.py:304
  441.0 6.5 %convolution_convert_fusion.1 = bf16[2048,768]{1,0:T(8,128)(2,1)} fusion(bf16[2048,768]{1,0:T(8,128)(2,1)} %get-tuple-element.51, bf16[768,768]{1,0:T(8,128)(2,1)} %param.31), kind=kOutput, calls=%fused_computation.15 | convolution fusion | flops 2417491968 | bytes 7471104 | tf_op jit(solution)/shard_map/dot_general | solution.py:177
  447.5 4.8 all-to-all-start.4
  454.4 53.2 %reduce-scatter.6.cloned.1.call-done = f32[96,2316]{1,0:T(8,128)} async-done(((f32[768,2316]{1,0:T(8,128)}), f32[96,2316]{1,0:T(8,128)}) %reduce-scatter.6.cloned.1.call-update) | async-done | bytes 889360 | tf_op jit(solution)/shard_map/reduce_scatter | solution.py:306
  509.9 12.7 %all-to-all-done.4 = bf16[4,512,768]{2,1,0:T(8,128)(2,1)} async-done(((bf16[4,512,768]{2,1,0:T(8,128)(2,1)}), bf16[4,512,768]{2,1,0:T(8,128)(2,1)}, u32[]{:S(2)}, u32[]{:S(2)}) %all-to-all-start.4) | async-done | bytes 3145760 | tf_op jit(solution)/shard_map/all_to_all | solution.py:37
  522.5 4.3 all-to-all-start.6
  526.9 3.6 fusion.36
  534.1 21.9 %all-to-all-done.6 = f32[4,24,3084]{2,1,0:T(8,128)} async-done(((f32[4,24,3084]{2,1,0:T(8,128)}), f32[4,24,3084]{2,1,0:T(8,128)}, u32[]{:S(2)}, u32[]{:S(2)}) %all-to-all-start.6) | async-done | bytes 1184288 | tf_op jit(solution)/shard_map/all_to_all | solution.py:37
  (198 shorter events, 104.6 us)
Async XLA Ops:
  7.2 17.3 %copy-start = (bf16[768,1536]{1,0:T(8,128)(2,1)S(1)}, bf16[768,1536]{1,0:T(8,128)(2,1)}, u32[]{:S(2)}) copy-start(bf16[768,1536]{1,0:T(8,128)(2,1)} %param.23) | copy-start | bytes 7077892
  7.2 3.1 copy-start.6
  7.2 3.1 copy-start.31
  7.2 3.1 copy-start.44
  7.2 3.1 copy-start.42
  7.2 164.4 %all-gather.3.cloned.1.call-start = ((), (), s32[]{:S(2)}) async-start(), calls=%async_computation.10 | async-start | bytes 3932160 | tf_op jit(solution)/shard_map/all_gather | solution.py:159
  10.3 14.2 %copy-start.27 = (f32[512]{0:T(512)}, f32[512]{0:T(512)S(1)}, u32[]{:S(2)}) copy-start(f32[512]{0:T(512)S(1)} %add_rsqrt_fusion.1) | copy-start | bytes 6148
  94.4 10.8 %copy-start.23 = (s32[512,12]{0,1:T(8,128)S(1)}, s32[512,12]{0,1:T(8,128)}, u32[]{:S(2)}) copy-start(s32[512,12]{0,1:T(8,128)} %param.18) | copy-start | bytes 73732
  95.1 10.6 %copy-start.40 = (bf16[768,768]{1,0:T(8,128)(2,1)S(1)}, bf16[768,768]{1,0:T(8,128)(2,1)}, u32[]{:S(2)}) copy-start(bf16[768,768]{1,0:T(8,128)(2,1)} %param.25) | copy-start | bytes 3538948
  95.1 10.6 %copy-start.43 = (f32[768]{0:T(1024)S(1)}, f32[768]{0:T(1024)}, u32[]{:S(2)}) copy-start(f32[768]{0:T(1024)} %param.26) | copy-start | bytes 9220
  109.1 126.2 %all-gather.5.cloned.1.call-start = ((), (), s32[]{:S(2)}) async-start(), calls=%async_computation.11 | async-start | bytes 3932160 | tf_op jit(solution)/shard_map/all_gather | solution.py:74
  109.8 198.5 %reduce-scatter.4.cloned.1.call-start = ((), (), s32[]{:S(2)}) async-start(), calls=%async_computation.12 | async-start | bytes 3932160 | tf_op jit(solution)/shard_map/reduce_scatter | solution.py:168
  235.3 9.8 %copy-start.39 = (bf16[768,768]{1,0:T(8,128)(2,1)S(1)}, bf16[768,768]{1,0:T(8,128)(2,1)}, u32[]{:S(2)}) copy-start(bf16[768,768]{1,0:T(8,128)(2,1)} %param.29) | copy-start | bytes 3538948
  249.1 203.1 %reduce-scatter.8.cloned.1.call-start = ((), (), s32[]{:S(2)}) async-start(), calls=%async_computation.14 | async-start | bytes 7962624 | tf_op jit(solution)/shard_map/reduce_scatter | solution.py:212
  249.2 7.1 %copy-start.38 = (bf16[2048,768]{1,0:T(8,128)(2,1)S(1)}, bf16[2048,768]{1,0:T(8,128)(2,1)}, u32[]{:S(2)}) copy-start(bf16[2048,768]{1,0:T(8,128)(2,1)} %all-gather.5.cloned.1.call-done) | copy-start | bytes 9437188
  249.2 7.1 %copy-start.46 = (bf16[2048,768]{1,0:T(8,128)(2,1)S(1)}, bf16[2048,768]{1,0:T(8,128)(2,1)}, u32[]{:S(2)}) copy-start(bf16[2048,768]{1,0:T(8,128)(2,1)} %get-tuple-element.51) | copy-start | bytes 9437188
  260.5 51.0 %copy-start.30 = (f32[768]{0:T(1024)S(1)}, f32[768]{0:T(1024)}, u32[]{:S(2)}) copy-start(f32[768]{0:T(1024)} %param.32) | copy-start | bytes 9220
  308.3 3.2 copy-start.4
  308.3 3.2 copy-start.10
  311.5 5.0 copy-start.18
  330.5 15.4 %all-to-all-start.2 = ((f32[4,3,100,64]{2,3,1,0:T(8,128)}), f32[4,3,100,64]{2,3,1,0:T(8,128)S(1)}, u32[]{:S(2)}, u32[]{:S(2)}) async-start(f32[4,3,100,64]{2,3,1,0:T(8,128)} %bitcast.112), calls=%async_computation.3 | async-start | bytes 786432 | tf_op jit(solution)/shard_map/all_to_all | solution.py:37
  353.3 6.6 %copy-start.21 = (bf16[3,100,64]{1,2,0:T(8,128)(2,1)S(1)}, bf16[3,100,64]{1,2,0:T(8,128)(2,1)}, u32[]{:S(2)}) copy-start(bf16[3,100,64]{1,2,0:T(8,128)(2,1)} %reduce_sum.231) | copy-start | bytes 115204
  355.5 24.1 %all-to-all-start.5 = ((bf16[4,512,192]{1,2,0:T(8,128)(2,1)}), bf16[4,512,192]{1,2,0:T(8,128)(2,1)}, u32[]{:S(2)}, u32[]{:S(2)}) async-start(bf16[4,512,192]{1,2,0:T(8,128)(2,1)} %copy.97), calls=%async_computation.6 | async-start | bytes 1572864 | tf_op jit(solution)/shard_map/all_to_all | solution.py:227
  373.2 10.7 %copy-start.34 = (f32[768]{0:T(1024)S(1)}, f32[768]{0:T(1024)}, u32[]{:S(2)}) copy-start(f32[768]{0:T(1024)} %get-tuple-element.58) | copy-start | bytes 9220
  379.6 28.2 %all-to-all-start.3 = ((bf16[4,612,192]{1,2,0:T(8,128)(2,1)}), bf16[4,612,192]{1,2,0:T(8,128)(2,1)}, u32[]{:S(2)}, u32[]{:S(2)}) async-start(bf16[4,612,192]{1,2,0:T(8,128)(2,1)} %pad_maximum_fusion.3), calls=%async_computation.4 | async-start | bytes 1966080 | tf_op jit(solution)/shard_map/all_to_all | solution.py:258
  383.8 123.7 %reduce-scatter.6.cloned.1.call-start = ((), (), s32[]{:S(2)}) async-start(), calls=%async_computation.13 | async-start | bytes 8404992 | tf_op jit(solution)/shard_map/reduce_scatter | solution.py:306
  414.3 3.8 copy-start.19
  447.5 75.1 %all-to-all-start.4 = ((bf16[4,512,768]{2,1,0:T(8,128)(2,1)}), bf16[4,512,768]{2,1,0:T(8,128)(2,1)}, u32[]{:S(2)}, u32[]{:S(2)}) async-start(bf16[4,512,768]{2,1,0:T(8,128)(2,1)} %bitcast.96), calls=%async_computation.5 | async-start | bytes 6291456 | tf_op jit(solution)/shard_map/all_to_all | solution.py:37
  509.9 17.0 %copy-start.37 = (f32[512]{0:T(512)S(1)}, f32[512]{0:T(512)}, u32[]{:S(2)}) copy-start(f32[512]{0:T(512)} %get-tuple-element.21) | copy-start | bytes 6148
  509.9 17.0 %copy-start.36 = (f32[512]{0:T(512)S(1)}, f32[512]{0:T(512)}, u32[]{:S(2)}) copy-start(f32[512]{0:T(512)} %get-tuple-element.22) | copy-start | bytes 6148
  509.9 17.0 %copy-start.33 = (f32[768]{0:T(1024)S(1)}, f32[768]{0:T(1024)}, u32[]{:S(2)}) copy-start(f32[768]{0:T(1024)} %param.19) | copy-start | bytes 9220
  522.5 33.5 %all-to-all-start.6 = ((f32[4,24,3084]{2,1,0:T(8,128)}), f32[4,24,3084]{2,1,0:T(8,128)}, u32[]{:S(2)}, u32[]{:S(2)}) async-start(f32[4,24,3084]{2,1,0:T(8,128)} %pad_maximum_fusion.2), calls=%async_computation.9 | async-start | bytes 2457600 | tf_op jit(solution)/shard_map/all_to_all | solution.py:37
  (27 other events, 50.8 us)
Sparse Core Ops, SparseCore 0:
  109.2 62.3 all-gather.2
  173.2 62.0 all-gather.4
  249.2 59.0 reduce-scatter.3
  322.4 65.2 reduce-scatter.7
  441.1 66.4 reduce-scatter.5

commit v9 on v7

--- a/solution.py
+++ b/solution.py
@@ -30,23 +30,6 @@
     cumulative = 0.5 * (1.0 + jax.scipy.special.erf(before / math.sqrt(2.0)))
     density = jnp.exp(-0.5 * before * before) / math.sqrt(2.0 * math.pi)
     return (before * cumulative, cumulative + before * density)
-
-
-def ring_shift(x, group_size):
-    return lax.ppermute(x, "mp", [(i, (i + 1) % group_size) for i in range(group_size)])
-
-
-def ring_gather(x, group_size):
-    me = lax.axis_index("mp")
-    out = jnp.zeros((group_size,) + x.shape, x.dtype)
-    out = lax.dynamic_update_index_in_dim(out, x, me, 0)
-    cur = x
-    for step in range(1, group_size):
-        cur = ring_shift(cur, group_size)
-        out = lax.dynamic_update_index_in_dim(
-            out, cur, jnp.remainder(me + group_size - step, group_size), 0
-        )
-    return out.reshape((group_size * x.shape[0],) + x.shape[1:])
 
 
 def scatter_sum(partial, group_size):
@@ -88,7 +71,7 @@
     local_heads = head_count // group_size
     score_scale = float(head_dim) ** (-0.5)
 
-    grad_rows = ring_gather(cotangent, group_size)
+    grad_rows = lax.all_gather(cotangent, "mp", axis=0, tiled=True)
 
     inputs = block_input.astype(jnp.float32)
     normed_one, standard_one, factor_one = norm_forward(inputs, ln1_gain, ln1_bias)
@@ -155,12 +138,15 @@
 
     gathered = lax.all_gather(second, "mp", axis=0, tiled=True)
 
+    grad_hidden = lax.optimization_barrier(
+        jnp.einsum("td,fd->tf", grad_rows, w_down, preferred_element_type=jnp.float32)
+    )
+
     before = jnp.dot(gathered, w_up, preferred_element_type=jnp.float32) + up_bias.astype(
         jnp.float32
     )
     activated, gelu_slope = gelu_parts(before)
     hidden = activated.astype(jnp.bfloat16)
-    grad_hidden = jnp.einsum("td,fd->tf", grad_rows, w_down, preferred_element_type=jnp.float32)
     grad_before = (grad_hidden * gelu_slope).astype(jnp.bfloat16)
     grad_second = lax.psum_scatter(
         jnp.einsum("tf,df->td", grad_before, w_up, preferred_element_type=jnp.float32).astype(

time: 546 us -> 541 us (level)
  starting transfers between devices: 49 us -> 32.8 us
  waiting for transfers between devices: 285 us -> 295 us
  local copies, waits for them, and re-layouts: 71.1 us -> 63.2 us
    ppermute x3 -> x0, waiting for transfers between devices: 79.7 us -> none  [ring_shift(): lax.ppermute(x, 'mp', [(i, (i + 1) % group_size) for i in range(group_siz...]
    all_gather x1, waiting for transfers between devices: 0.01 us -> 57.1 us  [block_body(): gathered = lax.all_gather(second, 'mp', axis=0, tiled=True)]
    all_to_all x1, waiting for transfers between devices: 35.4 us -> 66.8 us  [block_body(): lax.all_to_all(packed, 'mp', split_axis=2, concat_axis=0, tiled=True)]
    ppermute x3 -> x0, starting transfers between devices: 16.9 us -> none  [ring_shift(): lax.ppermute(x, 'mp', [(i, (i + 1) % group_size) for i in range(group_siz...]
    dynamic_update_slice x4 -> x0, local copies, waits for them, and re-layouts: 6.12 us -> none  [the longest x3 5.11 us: ring_gather(): lax.dynamic_update_index_in_dim(out, cur, jnp.remainder(me + group_size -...]
  transfers between devices with their start and end apart: 14 -> 12, of which waited for: 12 -> 11; matrix products, arithmetic and copies ran while one was open for 22% -> 24% of each run, Pallas kernels for 0% -> 0%
where the time goes in v9:
time: 541 us; the launch traced here: 533 us
  waiting for transfers between devices  295 us (55%)
  matrix products  80.6 us (15%)
  local copies, waits for them, and re-layouts  63.2 us (12%)
  starting transfers between devices  32.8 us (6%)
  other arithmetic  32.7 us (6%)
  between operations  14.9 us (3%)
  blocking collectives  13.6 us (3%)
    all_to_all x1, waiting for transfers between devices, block_body(): lax.all_to_all(packed, 'mp', split_axis=2, concat_axis=0, tiled=True)  66.8 us
    all_gather x1, waiting for transfers between devices, block_body(): gathered = lax.all_gather(second, 'mp', axis=0, tiled=True)  57.1 us
    reduce_scatter x1, waiting for transfers between devices, block_body(): lax.psum_scatter(packed_grads, 'dp', scatter_dimension=0, tiled=True)  53.1 us
    all_to_all x4, waiting for transfers between devices, scatter_sum(): lax.all_to_all(pieces, 'mp', split_axis=0, concat_axis=0, tiled=True)  49.9 us
    reduce_scatter x1, waiting for transfers between devices, block_body(): lax.psum_scatter(jnp.einsum('tf,df->td', grad_before, w_up, preferred_ele...  47.6 us
    all_to_all x4, starting transfers between devices, scatter_sum(): lax.all_to_all(pieces, 'mp', split_axis=0, concat_axis=0, tiled=True)  19 us
    all_to_all x1, waiting for transfers between devices, block_body(): lax.all_to_all(outgoing, 'mp', split_axis=0, concat_axis=0, tiled=True)  15 us
    all_to_all x1, blocking collectives, broadcast_gather(): lax.all_to_all(sent, 'mp', split_axis=0, concat_axis=0, tiled=True)  13.6 us
  transfers between devices with their start and end apart: 12, of which 11 were waited for; matrix products, arithmetic and copies ran while one was open for 24% of the time, Pallas kernels for 0%

profile of v9, /device:TPU:0, one launch (start us, length us, event | category | flops | bytes accessed | tf_op | source)
XLA Modules:
  0.0 533.0 jit_solution(3776588233498210275)
XLA Ops:
  19.1 6.3 %all-to-all-start = ((f32[4,3,100,65]{2,3,1,0:T(8,128)}), f32[4,3,100,65]{2,3,1,0:T(8,128)}, u32[]{:S(2)}, u32[]{:S(2)}) async-start(f32[4,3,100,65]{2,3,1,0:T(8,128)} %pad_maximum_fusion.3), calls=%async_computation | async-start | bytes 884736 | tf_op jit(solution)/shard_map/all_to_all | solution.py:37
  25.5 3.3 fusion.6
  34.1 4.2 all-to-all-done
  38.3 4.3 all-to-all-start.1
  44.5 66.8 %all-to-all-done.1 = bf16[512,2,4,192]{0,3,1,2:T(8,128)(2,1)} async-done(((bf16[512,2,4,192]{0,3,1,2:T(8,128)(2,1)}), bf16[512,2,4,192]{0,3,1,2:T(8,128)(2,1)}, u32[]{:S(2)}, u32[]{:S(2)}) %all-to-all-start.1) | async-done | bytes 1572896 | tf_op jit(solution)/shard_map/all_to_all | solution.py:99
  115.6 13.6 %all_to_all.53 = bf16[4,3,100,64]{2,3,1,0:T(8,128)(2,1)S(1)} all-to-all(bf16[4,3,100,64]{2,3,1,0:T(8,128)(2,1)S(1)} %broadcast_in_dim.8), channel_id=1, replica_groups=mesh['dp'=8,'mp'=4] {'mp'}, dimensions={0} | all-to-all | bytes 307200 | tf_op jit(solution)/shard_map/all_to_all | solution.py:43
  134.3 7.5 %fusion.79 = f32[2048,768]{1,0:T(8,128)} fusion(bf16[2048,768]{1,0:T(8,128)(2,1)} %all-gather.5.cloned.1.call-done, bf16[768,768]{1,0:T(8,128)(2,1)} %param.31), kind=kOutput, calls=%fused_computation.141 | convolution fusion | flops 2415919104 | bytes 10616832 | tf_op jit(solution)/shard_map/td,fd->tf/dot_general | solution.py:142
  141.8 57.1 %all-gather.3.cloned.1.call-done = bf16[2048,768]{1,0:T(8,128)(2,1)} async-done(((bf16[512,768]{1,0:T(8,128)(2,1)}), bf16[2048,768]{1,0:T(8,128)(2,1)}) %all-gather.3.cloned.1.call-update) | async-done | bytes 3145744 | tf_op jit(solution)/shard_map/all_gather | solution.py:139
  199.0 10.2 %convert_reduce_fusion = (f32[768]{0:T(1024)}, bf16[2048,768]{1,0:T(8,128)(2,1)S(1)}, bf16[2048,768]{1,0:T(8,128)(2,1)}) fusion(f32[2048,768]{1,0:T(8,128)} %fusion.79, f32[768]{0:T(1024)S(1)} %convert_element_type.138, bf16[2048,768]{1,0:T(8,128)(2,1)} %all-gather.3.cloned.1.call-done, bf16[768,768]{1,0:T(8,128)(2,1)} %param.29), kind=kOutput, calls=%fused_computation.8 | convolution fusion | flops 2439511296 | bytes 16914432 | tf_op jit(solution)/shard_map/dot_general | solution.py:145
  210.9 4.0 convolution_convert_fusion
  215.2 7.1 %convolution_bitcast_fusion.1 = f32[1,768,768]{2,1,0:T(8,128)} fusion(bf16[2048,768]{1,0:T(8,128)(2,1)} %all-gather.3.cloned.1.call-done, bf16[2048,768]{1,0:T(8,128)(2,1)} %copy-done.50), kind=kOutput, calls=%fused_computation.60 | convolution fusion | flops 2415919104 | bytes 8650752 | tf_op jit(solution)/shard_map/td,tf->df/dot_general | solution.py:166
  222.3 4.2 convolution_bitcast_fusion
  226.5 47.6 %reduce-scatter.4.cloned.1.call-done = bf16[512,768]{1,0:T(8,128)(2,1)} async-done(((bf16[2048,768]{1,0:T(8,128)(2,1)}), bf16[512,768]{1,0:T(8,128)(2,1)}) %reduce-scatter.4.cloned.1.call-update) | async-done | bytes 786448 | tf_op jit(solution)/shard_map/reduce_scatter | solution.py:151
  277.3 3.7 convert_reduce_fusion.6
  284.6 3.4 pad_maximum_fusion
  288.0 3.4 convolution_convert_fusion.3
  296.2 3.6 all-to-all-start.3
  300.5 11.0 %all-to-all-done.3 = f32[4,3,100,64]{2,3,1,0:T(8,128)S(1)} async-done(((f32[4,3,100,64]{2,3,1,0:T(8,128)}), f32[4,3,100,64]{2,3,1,0:T(8,128)S(1)}, u32[]{:S(2)}, u32[]{:S(2)}) %all-to-all-start.3) | async-done | bytes 307232 | tf_op jit(solution)/shard_map/all_to_all | solution.py:37
  312.2 3.8 fusion.9
  321.2 4.4 all-to-all-start.6
  341.2 4.1 all-to-all-done.6
  345.3 4.2 all-to-all-start.4
  358.5 15.0 %all-to-all-done.4 = bf16[4,612,192]{1,2,0:T(8,128)(2,1)} async-done(((bf16[4,612,192]{1,2,0:T(8,128)(2,1)}), bf16[4,612,192]{1,2,0:T(8,128)(2,1)}, u32[]{:S(2)}, u32[]{:S(2)}) %all-to-all-start.4) | async-done | bytes 940064 | tf_op jit(solution)/shard_map/all_to_all | solution.py:241
  389.8 6.9 %fusion.11 = f32[768,2304]{1,0:T(8,128)} fusion(bf16[512,768]{0,1:T(8,128)(2,1)} %bitcast.21, bf16[512,768]{0,1:T(8,128)(2,1)} %bitcast.102, bf16[512,768]{0,1:T(8,128)(2,1)} %bitcast.104, bf16[512,768]{1,0:T(8,128)(2,1)S(1)} %copy-done.6, f32[768]{0:T(1024)} %param.20, f32[768]{0:T(1024)} %param.19, f32[512]{0:T(512)S(1)} %copy-done.31, f32[512]{0:T(512)S(1)} %copy-done.28), kind=kOutput, calls=%fused_computation.37 | convolution fusion | flops 1821376512 | bytes 10233856 | tf_op jit(solution)/shard_map/td,te->de/dot_general | solution.py:259
  396.7 10.1 %concatenate.41 = f32[768,2316]{1,0:T(8,128)} concatenate(f32[768,2304]{1,0:T(8,128)} %fusion.11, f32[768,1]{1,0:T(8,128)} %stack.48, f32[768,1]{1,0:T(8,128)} %stack.49, f32[768,1]{1,0:T(8,128)} %stack.50, f32[768,1]{1,0:T(8,128)} %stack.51, f32[768,1]{1,0:T(8,128)} %stack.52, f32[768,1]{1,0:T(8,128)} %stack.53, f32[768,1]{1,0:T(8,128)} %stack.54, f32[768,1]{1,0:T(8,128)} %stack.55, ...), dimensions={1} | concatenate | bytes 14229504 | tf_op jit(solution)/shard_map/concatenate | solution.py:287
  406.7 6.6 %convolution_convert_fusion.1 = bf16[2048,768]{1,0:T(8,128)(2,1)} fusion(bf16[2048,768]{1,0:T(8,128)(2,1)} %get-tuple-element.38, bf16[768,768]{1,0:T(8,128)(2,1)} %param.31), kind=kOutput, calls=%fused_computation.15 | convolution fusion | flops 2417491968 | bytes 7471104 | tf_op jit(solution)/shard_map/dot_general | solution.py:160
  413.3 4.7 all-to-all-start.5
  420.2 53.1 %reduce-scatter.6.cloned.1.call-done = f32[96,2316]{1,0:T(8,128)} async-done(((f32[768,2316]{1,0:T(8,128)}), f32[96,2316]{1,0:T(8,128)}) %reduce-scatter.6.cloned.1.call-update) | async-done | bytes 889360 | tf_op jit(solution)/shard_map/reduce_scatter | solution.py:289
  475.6 12.7 %all-to-all-done.5 = bf16[4,512,768]{2,1,0:T(8,128)(2,1)} async-done(((bf16[4,512,768]{2,1,0:T(8,128)(2,1)}), bf16[4,512,768]{2,1,0:T(8,128)(2,1)}, u32[]{:S(2)}, u32[]{:S(2)}) %all-to-all-start.5) | async-done | bytes 3145760 | tf_op jit(solution)/shard_map/all_to_all | solution.py:37
  488.4 4.3 all-to-all-start.7
  492.7 3.6 fusion.36
  499.9 21.9 %all-to-all-done.7 = f32[4,24,3084]{2,1,0:T(8,128)} async-done(((f32[4,24,3084]{2,1,0:T(8,128)}), f32[4,24,3084]{2,1,0:T(8,128)}, u32[]{:S(2)}, u32[]{:S(2)}) %all-to-all-start.7) | async-done | bytes 1184288 | tf_op jit(solution)/shard_map/all_to_all | solution.py:37
  (200 shorter events, 100.9 us)
Async XLA Ops:
  7.2 18.3 %copy-start = (bf16[768,1536]{1,0:T(8,128)(2,1)S(1)}, bf16[768,1536]{1,0:T(8,128)(2,1)}, u32[]{:S(2)}) copy-start(bf16[768,1536]{1,0:T(8,128)(2,1)} %param.23) | copy-start | bytes 7077892
  7.2 3.6 copy-start.6
  7.2 3.6 copy-start.34
  18.3 7.2 %copy-start.38 = (f32[768]{0:T(1024)S(1)}, f32[768]{0:T(1024)}, u32[]{:S(2)}) copy-start(f32[768]{0:T(1024)} %param.24) | copy-start | bytes 9220
  18.3 7.2 %copy-start.35 = (f32[768]{0:T(1024)S(1)}, f32[768]{0:T(1024)}, u32[]{:S(2)}) copy-start(f32[768]{0:T(1024)} %param.19) | copy-start | bytes 9220
  19.1 19.2 %all-to-all-start = ((f32[4,3,100,65]{2,3,1,0:T(8,128)}), f32[4,3,100,65]{2,3,1,0:T(8,128)}, u32[]{:S(2)}, u32[]{:S(2)}) async-start(f32[4,3,100,65]{2,3,1,0:T(8,128)} %pad_maximum_fusion.3), calls=%async_computation | async-start | bytes 884736 | tf_op jit(solution)/shard_map/all_to_all | solution.py:37
  38.3 73.1 %all-to-all-start.1 = ((bf16[512,2,4,192]{0,3,1,2:T(8,128)(2,1)}), bf16[512,2,4,192]{0,3,1,2:T(8,128)(2,1)}, u32[]{:S(2)}, u32[]{:S(2)}) async-start(bf16[512,2,4,192]{0,3,1,2:T(8,128)(2,1)} %copy.58), calls=%async_computation.1 | async-start | bytes 3145728 | tf_op jit(solution)/shard_map/all_to_all | solution.py:99
  42.6 91.6 %all-gather.5.cloned.1.call-start = ((), (), s32[]{:S(2)}) async-start(), calls=%async_computation.12 | async-start | bytes 3932160 | tf_op jit(solution)/shard_map/all_gather | solution.py:74
  43.4 155.6 %all-gather.3.cloned.1.call-start = ((), (), s32[]{:S(2)}) async-start(), calls=%async_computation.11 | async-start | bytes 3932160 | tf_op jit(solution)/shard_map/all_gather | solution.py:139
  44.5 68.7 %copy-start.16 = (f32[3,100,65]{1,2,0:T(8,128)}, f32[3,100,65]{1,2,0:T(8,128)S(1)}, u32[]{:S(2)}) copy-start(f32[3,100,65]{1,2,0:T(8,128)S(1)} %reduce_sum.219) | copy-start | bytes 234004
  114.6 14.6 %copy-start.24 = (s32[512,12]{0,1:T(8,128)S(1)}, s32[512,12]{0,1:T(8,128)}, u32[]{:S(2)}) copy-start(s32[512,12]{0,1:T(8,128)} %param.18) | copy-start | bytes 73732
  115.5 14.2 %copy-start.45 = (bf16[768,768]{1,0:T(8,128)(2,1)S(1)}, bf16[768,768]{1,0:T(8,128)(2,1)}, u32[]{:S(2)}) copy-start(bf16[768,768]{1,0:T(8,128)(2,1)} %param.25) | copy-start | bytes 3538948
  115.5 14.2 %copy-start.48 = (f32[768]{0:T(1024)S(1)}, f32[768]{0:T(1024)}, u32[]{:S(2)}) copy-start(f32[768]{0:T(1024)} %param.26) | copy-start | bytes 9220
  133.1 141.1 %reduce-scatter.4.cloned.1.call-start = ((), (), s32[]{:S(2)}) async-start(), calls=%async_computation.13 | async-start | bytes 3932160 | tf_op jit(solution)/shard_map/reduce_scatter | solution.py:151
  199.0 12.0 %copy-start.44 = (bf16[768,768]{1,0:T(8,128)(2,1)S(1)}, bf16[768,768]{1,0:T(8,128)(2,1)}, u32[]{:S(2)}) copy-start(bf16[768,768]{1,0:T(8,128)(2,1)} %param.29) | copy-start | bytes 3538948
  215.0 203.1 %reduce-scatter.8.cloned.1.call-start = ((), (), s32[]{:S(2)}) async-start(), calls=%async_computation.15 | async-start | bytes 7962624 | tf_op jit(solution)/shard_map/reduce_scatter | solution.py:195
  215.2 7.2 %copy-start.43 = (bf16[2048,768]{1,0:T(8,128)(2,1)S(1)}, bf16[2048,768]{1,0:T(8,128)(2,1)}, u32[]{:S(2)}) copy-start(bf16[2048,768]{1,0:T(8,128)(2,1)} %all-gather.5.cloned.1.call-done) | copy-start | bytes 9437188
  215.2 7.1 %copy-start.51 = (bf16[2048,768]{1,0:T(8,128)(2,1)S(1)}, bf16[2048,768]{1,0:T(8,128)(2,1)}, u32[]{:S(2)}) copy-start(bf16[2048,768]{1,0:T(8,128)(2,1)} %get-tuple-element.38) | copy-start | bytes 9437188
  226.5 50.8 %copy-start.33 = (f32[768]{0:T(1024)S(1)}, f32[768]{0:T(1024)}, u32[]{:S(2)}) copy-start(f32[768]{0:T(1024)} %param.32) | copy-start | bytes 9220
  277.3 4.9 copy-start.19
  296.2 15.4 %all-to-all-start.3 = ((f32[4,3,100,64]{2,3,1,0:T(8,128)}), f32[4,3,100,64]{2,3,1,0:T(8,128)S(1)}, u32[]{:S(2)}, u32[]{:S(2)}) async-start(f32[4,3,100,64]{2,3,1,0:T(8,128)} %bitcast.107), calls=%async_computation.4 | async-start | bytes 786432 | tf_op jit(solution)/shard_map/all_to_all | solution.py:37
  319.0 6.6 %copy-start.22 = (bf16[3,100,64]{1,2,0:T(8,128)(2,1)S(1)}, bf16[3,100,64]{1,2,0:T(8,128)(2,1)}, u32[]{:S(2)}) copy-start(bf16[3,100,64]{1,2,0:T(8,128)(2,1)} %reduce_sum.225) | copy-start | bytes 115204
  321.2 24.1 %all-to-all-start.6 = ((bf16[4,512,192]{1,2,0:T(8,128)(2,1)}), bf16[4,512,192]{1,2,0:T(8,128)(2,1)}, u32[]{:S(2)}, u32[]{:S(2)}) async-start(bf16[4,512,192]{1,2,0:T(8,128)(2,1)} %copy.66), calls=%async_computation.7 | async-start | bytes 1572864 | tf_op jit(solution)/shard_map/all_to_all | solution.py:210
  339.0 10.6 %copy-start.39 = (f32[768]{0:T(1024)S(1)}, f32[768]{0:T(1024)}, u32[]{:S(2)}) copy-start(f32[768]{0:T(1024)} %get-tuple-element.34) | copy-start | bytes 9220
  345.3 28.2 %all-to-all-start.4 = ((bf16[4,612,192]{1,2,0:T(8,128)(2,1)}), bf16[4,612,192]{1,2,0:T(8,128)(2,1)}, u32[]{:S(2)}, u32[]{:S(2)}) async-start(bf16[4,612,192]{1,2,0:T(8,128)(2,1)} %pad_maximum_fusion.2), calls=%async_computation.5 | async-start | bytes 1966080 | tf_op jit(solution)/shard_map/all_to_all | solution.py:241
  349.5 123.8 %reduce-scatter.6.cloned.1.call-start = ((), (), s32[]{:S(2)}) async-start(), calls=%async_computation.14 | async-start | bytes 8404992 | tf_op jit(solution)/shard_map/reduce_scatter | solution.py:289
  380.0 3.8 copy-start.20
  413.3 75.0 %all-to-all-start.5 = ((bf16[4,512,768]{2,1,0:T(8,128)(2,1)}), bf16[4,512,768]{2,1,0:T(8,128)(2,1)}, u32[]{:S(2)}, u32[]{:S(2)}) async-start(bf16[4,512,768]{2,1,0:T(8,128)(2,1)} %bitcast.93), calls=%async_computation.6 | async-start | bytes 6291456 | tf_op jit(solution)/shard_map/all_to_all | solution.py:37
  475.6 17.0 %copy-start.42 = (f32[512]{0:T(512)S(1)}, f32[512]{0:T(512)}, u32[]{:S(2)}) copy-start(f32[512]{0:T(512)} %get-tuple-element.21) | copy-start | bytes 6148
  475.6 17.0 %copy-start.41 = (f32[512]{0:T(512)S(1)}, f32[512]{0:T(512)}, u32[]{:S(2)}) copy-start(f32[512]{0:T(512)} %get-tuple-element.22) | copy-start | bytes 6148
  475.6 17.1 %copy-start.37 = (f32[768]{0:T(1024)S(1)}, f32[768]{0:T(1024)}, u32[]{:S(2)}) copy-start(f32[768]{0:T(1024)} %param.19) | copy-start | bytes 9220
  488.4 33.5 %all-to-all-start.7 = ((f32[4,24,3084]{2,1,0:T(8,128)}), f32[4,24,3084]{2,1,0:T(8,128)}, u32[]{:S(2)}, u32[]{:S(2)}) async-start(f32[4,24,3084]{2,1,0:T(8,128)} %pad_maximum_fusion.1), calls=%async_computation.10 | async-start | bytes 2457600 | tf_op jit(solution)/shard_map/all_to_all | solution.py:37
  (34 other events, 65.7 us)
Sparse Core Ops, SparseCore 0:
  45.0 89.2 all-gather.4
  136.4 62.4 all-gather.2
  215.1 59.0 reduce-scatter.3
  288.1 65.2 reduce-scatter.7
  406.9 66.4 reduce-scatter.5

commit v10 on v9

--- a/solution.py
+++ b/solution.py
@@ -138,15 +138,12 @@
 
     gathered = lax.all_gather(second, "mp", axis=0, tiled=True)
 
-    grad_hidden = lax.optimization_barrier(
-        jnp.einsum("td,fd->tf", grad_rows, w_down, preferred_element_type=jnp.float32)
-    )
-
     before = jnp.dot(gathered, w_up, preferred_element_type=jnp.float32) + up_bias.astype(
         jnp.float32
     )
     activated, gelu_slope = gelu_parts(before)
     hidden = activated.astype(jnp.bfloat16)
+    grad_hidden = jnp.einsum("td,fd->tf", grad_rows, w_down, preferred_element_type=jnp.float32)
     grad_before = (grad_hidden * gelu_slope).astype(jnp.bfloat16)
     grad_second = lax.psum_scatter(
         jnp.einsum("tf,df->td", grad_before, w_up, preferred_element_type=jnp.float32).astype(
@@ -284,16 +281,14 @@
         axis=1,
     )
     up_bias_cols = grad_up_bias.reshape(model_width, -1)
-    packed_grads = jnp.concatenate([grad_w_attn, vectors, up_bias_cols], axis=1)
-
-    dp_reduced = lax.psum_scatter(packed_grads, "dp", scatter_dimension=0, tiled=True)
-    attn_width = grad_w_attn.shape[1]
-    reduced = scatter_sum(
-        jnp.concatenate(
-            [dp_reduced[:, :attn_width], ff_grads[2], dp_reduced[:, attn_width:]], axis=1
-        ),
-        group_size,
-    )
+    small_grads = jnp.concatenate([vectors, up_bias_cols], axis=1)
+
+    dp_reduced = lax.psum_scatter(grad_w_attn, "dp", scatter_dimension=0, tiled=True)
+    dp_rows = dp_reduced.shape[0]
+    small_sum = lax.dynamic_slice_in_dim(
+        lax.psum(small_grads, "dp"), lax.axis_index("dp") * dp_rows, dp_rows, 0
+    )
+    reduced = scatter_sum(jnp.concatenate([dp_reduced, ff_grads[2], small_sum], axis=1), group_size)
     up_share = ff_grads[0]
     down_share = ff_grads[1].T
     col = 0

time: 541 us -> 544 us (level)
  blocking collectives: 13.6 us -> 35.6 us
  local copies, waits for them, and re-layouts: 63.2 us -> 44.1 us
    all_gather x1, waiting for transfers between devices: 0.69 us -> 56.6 us  [block_body(): grad_rows = lax.all_gather(cotangent, 'mp', axis=0, tiled=True)]
    reduce_scatter x1, waiting for transfers between devices: 53.1 us -> 14.5 us  [block_body(): lax.psum_scatter(grad_w_attn, 'dp', scatter_dimension=0, tiled=True)]
    all_to_all x1, waiting for transfers between devices: 66.8 us -> 35.4 us  [block_body(): lax.all_to_all(packed, 'mp', split_axis=2, concat_axis=0, tiled=True)]
    psum x0 -> x1, blocking collectives: none -> 26.1 us  [block_body(): lax.psum(small_grads, 'dp')]
    concatenate x1 -> x2, local copies, waits for them, and re-layouts: 10.1 us -> 0.17 us  [the longest x1 0.11 us: block_body(): jnp.concatenate([dp_reduced, ff_grads[2], small_sum], axis=1)]
    all_to_all x1, waiting for transfers between devices: 4.14 us -> 12.2 us  [block_body(): lax.all_to_all(values_out, 'mp', split_axis=0, concat_axis=0, tiled=True)]
    another operation x8, local copies, waits for them, and re-layouts: 9.77 us -> 3.63 us  [block_body(): jnp.stack([grad_gain_one, grad_shift_one, grad_query_bias, grad_value_bia...]
  transfers between devices with their start and end apart: 12 -> 12, of which waited for: 11 -> 11; matrix products, arithmetic and copies ran while one was open for 24% -> 19% of each run, Pallas kernels for 0% -> 0%
where the time goes in v10:
time: 544 us; the launch traced here: 536 us
  waiting for transfers between devices  296 us (54%)
  matrix products  78.1 us (14%)
  local copies, waits for them, and re-layouts  44.1 us (8%)
  blocking collectives  35.6 us (7%)
  other arithmetic  33.9 us (6%)
  starting transfers between devices  33 us (6%)
  between operations  14.7 us (3%)
    all_gather x1, waiting for transfers between devices, block_body(): gathered = lax.all_gather(second, 'mp', axis=0, tiled=True)  61.4 us
    all_gather x1, waiting for transfers between devices, block_body(): grad_rows = lax.all_gather(cotangent, 'mp', axis=0, tiled=True)  56.6 us
    all_to_all x4, waiting for transfers between devices, scatter_sum(): lax.all_to_all(pieces, 'mp', split_axis=0, concat_axis=0, tiled=True)  51.5 us
    reduce_scatter x1, waiting for transfers between devices, block_body(): lax.psum_scatter(jnp.einsum('tf,df->td', grad_before, w_up, preferred_ele...  47.7 us
    all_to_all x1, waiting for transfers between devices, block_body(): lax.all_to_all(packed, 'mp', split_axis=2, concat_axis=0, tiled=True)  35.4 us
    psum x1, blocking collectives, block_body(): lax.psum(small_grads, 'dp')  26.1 us
    all_to_all x4, starting transfers between devices, scatter_sum(): lax.all_to_all(pieces, 'mp', split_axis=0, concat_axis=0, tiled=True)  19.5 us
    all_to_all x1, waiting for transfers between devices, block_body(): lax.all_to_all(outgoing, 'mp', split_axis=0, concat_axis=0, tiled=True)  16.2 us
  transfers between devices with their start and end apart: 12, of which 11 were waited for; matrix products, arithmetic and copies ran while one was open for 19% of the time, Pallas kernels for 0%

profile of v10, /device:TPU:0, one launch (start us, length us, event | category | flops | bytes accessed | tf_op | source)
XLA Modules:
  0.0 535.8 jit_solution(8544626904184541451)
XLA Ops:
  18.5 6.3 %all-to-all-start = ((f32[4,3,100,65]{2,3,1,0:T(8,128)}), f32[4,3,100,65]{2,3,1,0:T(8,128)}, u32[]{:S(2)}, u32[]{:S(2)}) async-start(f32[4,3,100,65]{2,3,1,0:T(8,128)} %pad_maximum_fusion.3), calls=%async_computation | async-start | bytes 884736 | tf_op jit(solution)/shard_map/all_to_all | solution.py:37
  32.8 4.9 all-to-all-done
  37.7 4.3 all-to-all-start.1
  43.2 35.4 %all-to-all-done.1 = bf16[512,2,4,192]{0,3,1,2:T(8,128)(2,1)} async-done(((bf16[512,2,4,192]{0,3,1,2:T(8,128)(2,1)}), bf16[512,2,4,192]{0,3,1,2:T(8,128)(2,1)}, u32[]{:S(2)}, u32[]{:S(2)}) %all-to-all-start.1) | async-done | bytes 1572896 | tf_op jit(solution)/shard_map/all_to_all | solution.py:99
  82.8 9.5 %all_to_all.53 = bf16[4,3,100,64]{2,3,1,0:T(8,128)(2,1)S(1)} all-to-all(bf16[4,3,100,64]{2,3,1,0:T(8,128)(2,1)S(1)} %broadcast_in_dim.8), channel_id=1, replica_groups=mesh['dp'=8,'mp'=4] {'mp'}, dimensions={0} | all-to-all | bytes 307200 | tf_op jit(solution)/shard_map/all_to_all | solution.py:43
  97.5 61.4 %all-gather.3.cloned.1.call-done = bf16[2048,768]{1,0:T(8,128)(2,1)} async-done(((bf16[512,768]{1,0:T(8,128)(2,1)}), bf16[2048,768]{1,0:T(8,128)(2,1)}) %all-gather.3.cloned.1.call-update) | async-done | bytes 3145744 | tf_op jit(solution)/shard_map/all_gather | solution.py:139
  158.9 7.1 %multiply_convert_fusion = (bf16[2048,768]{1,0:T(8,128)(2,1)}, f32[2048,768]{1,0:T(8,128)}) fusion(f32[768]{0:T(1024)S(1)} %convert_element_type.138, bf16[2048,768]{1,0:T(8,128)(2,1)} %all-gather.3.cloned.1.call-done, bf16[768,768]{1,0:T(8,128)(2,1)} %param.29), kind=kOutput, calls=%fused_computation.10 | convolution fusion | flops 2425356288 | bytes 13765632 | tf_op jit(solution)/shard_map/dot_general | solution.py:141
  166.0 56.6 %all-gather.5.cloned.1.call-done = bf16[2048,768]{1,0:T(8,128)(2,1)} async-done(((bf16[512,768]{1,0:T(8,128)(2,1)}), bf16[2048,768]{1,0:T(8,128)(2,1)}) %all-gather.5.cloned.1.call-update) | async-done | bytes 3145744 | tf_op jit(solution)/shard_map/all_gather | solution.py:74
  222.6 8.1 %convert_reduce_fusion = (f32[768]{0:T(1024)}, bf16[2048,768]{1,0:T(8,128)(2,1)S(1)}) fusion(f32[2048,768]{1,0:T(8,128)} %get-tuple-element.50, f32[768]{0:T(1024)S(1)} %convert_element_type.138, bf16[2048,768]{1,0:T(8,128)(2,1)} %all-gather.5.cloned.1.call-done, bf16[768,768]{1,0:T(8,128)(2,1)} %param.31), kind=kOutput, calls=%fused_computation.8 | convolution fusion | flops 2436365568 | bytes 13768704 | tf_op jit(solution)/shard_map/td,fd->tf/dot_general | solution.py:146
  232.4 4.0 convolution_convert_fusion
  236.5 7.1 %convolution_bitcast_fusion.1 = f32[1,768,768]{2,1,0:T(8,128)} fusion(bf16[2048,768]{1,0:T(8,128)(2,1)} %all-gather.3.cloned.1.call-done, bf16[2048,768]{1,0:T(8,128)(2,1)} %copy-done.44), kind=kOutput, calls=%fused_computation.60 | convolution fusion | flops 2415919104 | bytes 8650752 | tf_op jit(solution)/shard_map/td,tf->df/dot_general | solution.py:163
  243.6 4.3 convolution_bitcast_fusion
  247.9 47.7 %reduce-scatter.4.cloned.1.call-done = bf16[512,768]{1,0:T(8,128)(2,1)} async-done(((bf16[2048,768]{1,0:T(8,128)(2,1)}), bf16[512,768]{1,0:T(8,128)(2,1)}) %reduce-scatter.4.cloned.1.call-update) | async-done | bytes 786448 | tf_op jit(solution)/shard_map/reduce_scatter | solution.py:148
  298.8 3.8 convert_reduce_fusion.6
  306.1 3.4 pad_maximum_fusion
  309.5 3.4 convolution_convert_fusion.3
  317.7 3.8 all-to-all-start.3
  322.2 11.0 %all-to-all-done.3 = f32[4,3,100,64]{2,3,1,0:T(8,128)S(1)} async-done(((f32[4,3,100,64]{2,3,1,0:T(8,128)}), f32[4,3,100,64]{2,3,1,0:T(8,128)S(1)}, u32[]{:S(2)}, u32[]{:S(2)}) %all-to-all-start.3) | async-done | bytes 307232 | tf_op jit(solution)/shard_map/all_to_all | solution.py:37
  349.7 4.2 all-to-all-start.4
  353.9 3.3 fusion.9
  362.4 16.2 %all-to-all-done.4 = bf16[4,612,192]{1,2,0:T(8,128)(2,1)} async-done(((bf16[4,612,192]{1,2,0:T(8,128)(2,1)}), bf16[4,612,192]{1,2,0:T(8,128)(2,1)}, u32[]{:S(2)}, u32[]{:S(2)}) %all-to-all-start.4) | async-done | bytes 940064 | tf_op jit(solution)/shard_map/all_to_all | solution.py:238
  378.6 4.2 all-to-all-start.6
  390.3 12.2 %all-to-all-done.6 = bf16[4,512,192]{1,2,0:T(8,128)(2,1)} async-done(((bf16[4,512,192]{1,2,0:T(8,128)(2,1)}), bf16[4,512,192]{1,2,0:T(8,128)(2,1)}, u32[]{:S(2)}, u32[]{:S(2)}) %all-to-all-start.6) | async-done | bytes 786464 | tf_op jit(solution)/shard_map/all_to_all | solution.py:207
  402.5 6.9 %fusion.11 = f32[768,2304]{1,0:T(8,128)} fusion(bf16[512,768]{0,1:T(8,128)(2,1)} %bitcast.21, bf16[512,768]{0,1:T(8,128)(2,1)} %bitcast.102, bf16[512,768]{0,1:T(8,128)(2,1)} %bitcast.100, bf16[512,768]{1,0:T(8,128)(2,1)S(1)} %copy-done.6, f32[768]{0:T(1024)S(1)} %copy-done.43, f32[768]{0:T(1024)S(1)} %copy-done.31, f32[512]{0:T(512)S(1)} %copy-done.26, ...), kind=kOutput, calls=%fused_computation.37 | convolution fusion | flops 1821376512 | bytes 10233856 | tf_op jit(solution)/shard_map/td,te->de/dot_general | solution.py:256
  409.4 6.5 %convolution_convert_fusion.1 = bf16[2048,768]{1,0:T(8,128)(2,1)} fusion(bf16[2048,768]{1,0:T(8,128)(2,1)} %get-tuple-element.49, bf16[768,768]{1,0:T(8,128)(2,1)} %param.31), kind=kOutput, calls=%fused_computation.15 | convolution fusion | flops 2417491968 | bytes 7471104 | tf_op jit(solution)/shard_map/dot_general | solution.py:157
  415.9 5.1 all-to-all-start.5
  432.5 26.1 %psum.7 = f32[768,12]{0,1:T(8,128)S(1)} all-reduce(f32[768,12]{0,1:T(8,128)S(1)} %concatenate.43), channel_id=1, replica_groups=mesh['dp'=8,'mp'=4] {'dp'}, use_global_device_ids=true, to_apply=%region_27.0 | all-reduce | flops 9216 | bytes 73728 | tf_op jit(solution)/shard_map/psum | solution.py:289
  460.8 14.5 %reduce-scatter.6.cloned.1.call-done = f32[96,2304]{1,0:T(8,128)} async-done(((f32[768,2304]{1,0:T(8,128)}), f32[96,2304]{1,0:T(8,128)}) %reduce-scatter.6.cloned.1.call-update) | async-done | bytes 884752 | tf_op jit(solution)/shard_map/reduce_scatter | solution.py:286
  477.6 13.7 %all-to-all-done.5 = bf16[4,512,768]{2,1,0:T(8,128)(2,1)} async-done(((bf16[4,512,768]{2,1,0:T(8,128)(2,1)}), bf16[4,512,768]{2,1,0:T(8,128)(2,1)}, u32[]{:S(2)}, u32[]{:S(2)}) %all-to-all-start.5) | async-done | bytes 3145760 | tf_op jit(solution)/shard_map/all_to_all | solution.py:37
  491.3 4.3 all-to-all-start.7
  495.6 3.6 fusion.36
  502.8 22.0 %all-to-all-done.7 = f32[4,24,3084]{2,1,0:T(8,128)} async-done(((f32[4,24,3084]{2,1,0:T(8,128)}), f32[4,24,3084]{2,1,0:T(8,128)}, u32[]{:S(2)}, u32[]{:S(2)}) %all-to-all-start.7) | async-done | bytes 1184288 | tf_op jit(solution)/shard_map/all_to_all | solution.py:37
  (188 shorter events, 96.2 us)
Async XLA Ops:
  7.2 17.7 %copy-start = (bf16[768,1536]{1,0:T(8,128)(2,1)S(1)}, bf16[768,1536]{1,0:T(8,128)(2,1)}, u32[]{:S(2)}) copy-start(bf16[768,1536]{1,0:T(8,128)(2,1)} %param.23) | copy-start | bytes 7077892
  7.2 3.4 copy-start.6
  7.2 3.4 copy-start.30
  7.2 3.4 copy-start.42
  10.2 14.7 %copy-start.25 = (f32[512]{0:T(512)}, f32[512]{0:T(512)S(1)}, u32[]{:S(2)}) copy-start(f32[512]{0:T(512)S(1)} %add_rsqrt_fusion.1) | copy-start | bytes 6148
  16.0 8.9 %copy-start.33 = (f32[768]{0:T(1024)S(1)}, f32[768]{0:T(1024)}, u32[]{:S(2)}) copy-start(f32[768]{0:T(1024)} %param.24) | copy-start | bytes 9220
  18.5 19.2 %all-to-all-start = ((f32[4,3,100,65]{2,3,1,0:T(8,128)}), f32[4,3,100,65]{2,3,1,0:T(8,128)}, u32[]{:S(2)}, u32[]{:S(2)}) async-start(f32[4,3,100,65]{2,3,1,0:T(8,128)} %pad_maximum_fusion.3), calls=%async_computation | async-start | bytes 884736 | tf_op jit(solution)/shard_map/all_to_all | solution.py:37
  37.7 40.9 %all-to-all-start.1 = ((bf16[512,2,4,192]{0,3,1,2:T(8,128)(2,1)}), bf16[512,2,4,192]{0,3,1,2:T(8,128)(2,1)}, u32[]{:S(2)}, u32[]{:S(2)}) async-start(bf16[512,2,4,192]{0,3,1,2:T(8,128)(2,1)} %copy.73), calls=%async_computation.1 | async-start | bytes 3145728 | tf_op jit(solution)/shard_map/all_to_all | solution.py:99
  42.1 116.8 %all-gather.3.cloned.1.call-start = ((), (), s32[]{:S(2)}) async-start(), calls=%async_computation.11 | async-start | bytes 3932160 | tf_op jit(solution)/shard_map/all_gather | solution.py:139
  43.2 37.2 %copy-start.15 = (f32[3,100,65]{1,2,0:T(8,128)}, f32[3,100,65]{1,2,0:T(8,128)S(1)}, u32[]{:S(2)}) copy-start(f32[3,100,65]{1,2,0:T(8,128)S(1)} %reduce_sum.219) | copy-start | bytes 234004
  82.8 10.1 %copy-start.38 = (bf16[768,768]{1,0:T(8,128)(2,1)S(1)}, bf16[768,768]{1,0:T(8,128)(2,1)}, u32[]{:S(2)}) copy-start(bf16[768,768]{1,0:T(8,128)(2,1)} %param.25) | copy-start | bytes 3538948
  82.8 10.1 %copy-start.41 = (f32[768]{0:T(1024)S(1)}, f32[768]{0:T(1024)}, u32[]{:S(2)}) copy-start(f32[768]{0:T(1024)} %param.26) | copy-start | bytes 9220
  96.2 126.4 %all-gather.5.cloned.1.call-start = ((), (), s32[]{:S(2)}) async-start(), calls=%async_computation.12 | async-start | bytes 3932160 | tf_op jit(solution)/shard_map/all_gather | solution.py:74
  97.0 198.6 %reduce-scatter.4.cloned.1.call-start = ((), (), s32[]{:S(2)}) async-start(), calls=%async_computation.13 | async-start | bytes 3932160 | tf_op jit(solution)/shard_map/reduce_scatter | solution.py:148
  222.6 9.8 %copy-start.37 = (bf16[768,768]{1,0:T(8,128)(2,1)S(1)}, bf16[768,768]{1,0:T(8,128)(2,1)}, u32[]{:S(2)}) copy-start(bf16[768,768]{1,0:T(8,128)(2,1)} %param.29) | copy-start | bytes 3538948
  236.4 222.3 %reduce-scatter.8.cloned.1.call-start = ((), (), s32[]{:S(2)}) async-start(), calls=%async_computation.15 | async-start | bytes 7962624 | tf_op jit(solution)/shard_map/reduce_scatter | solution.py:192
  236.5 7.2 %copy-start.36 = (bf16[2048,768]{1,0:T(8,128)(2,1)S(1)}, bf16[2048,768]{1,0:T(8,128)(2,1)}, u32[]{:S(2)}) copy-start(bf16[2048,768]{1,0:T(8,128)(2,1)} %all-gather.5.cloned.1.call-done) | copy-start | bytes 9437188
  236.5 7.2 %copy-start.45 = (bf16[2048,768]{1,0:T(8,128)(2,1)S(1)}, bf16[2048,768]{1,0:T(8,128)(2,1)}, u32[]{:S(2)}) copy-start(bf16[2048,768]{1,0:T(8,128)(2,1)} %get-tuple-element.49) | copy-start | bytes 9437188
  247.9 50.9 %copy-start.29 = (f32[768]{0:T(1024)S(1)}, f32[768]{0:T(1024)}, u32[]{:S(2)}) copy-start(f32[768]{0:T(1024)} %param.32) | copy-start | bytes 9220
  298.8 4.9 copy-start.18
  317.7 15.5 %all-to-all-start.3 = ((f32[4,3,100,64]{2,3,1,0:T(8,128)}), f32[4,3,100,64]{2,3,1,0:T(8,128)S(1)}, u32[]{:S(2)}, u32[]{:S(2)}) async-start(f32[4,3,100,64]{2,3,1,0:T(8,128)} %bitcast.106), calls=%async_computation.4 | async-start | bytes 786432 | tf_op jit(solution)/shard_map/all_to_all | solution.py:37
  347.5 6.4 %copy-start.20 = (bf16[3,100,64]{1,2,0:T(8,128)(2,1)S(1)}, bf16[3,100,64]{1,2,0:T(8,128)(2,1)}, u32[]{:S(2)}) copy-start(bf16[3,100,64]{1,2,0:T(8,128)(2,1)} %reduce_sum.225) | copy-start | bytes 115204
  349.7 28.9 %all-to-all-start.4 = ((bf16[4,612,192]{1,2,0:T(8,128)(2,1)}), bf16[4,612,192]{1,2,0:T(8,128)(2,1)}, u32[]{:S(2)}, u32[]{:S(2)}) async-start(bf16[4,612,192]{1,2,0:T(8,128)(2,1)} %pad_maximum_fusion.2), calls=%async_computation.5 | async-start | bytes 1966080 | tf_op jit(solution)/shard_map/all_to_all | solution.py:238
  378.6 23.9 %all-to-all-start.6 = ((bf16[4,512,192]{1,2,0:T(8,128)(2,1)}), bf16[4,512,192]{1,2,0:T(8,128)(2,1)}, u32[]{:S(2)}, u32[]{:S(2)}) async-start(bf16[4,512,192]{1,2,0:T(8,128)(2,1)} %copy.81), calls=%async_computation.7 | async-start | bytes 1572864 | tf_op jit(solution)/shard_map/all_to_all | solution.py:207
  382.8 5.2 copy-start.22
  382.8 92.5 %reduce-scatter.6.cloned.1.call-start = ((), (), s32[]{:S(2)}) async-start(), calls=%async_computation.14 | async-start | bytes 7962624 | tf_op jit(solution)/shard_map/reduce_scatter | solution.py:286
  384.6 17.9 %copy-start.26 = (f32[512]{0:T(512)S(1)}, f32[512]{0:T(512)}, u32[]{:S(2)}) copy-start(f32[512]{0:T(512)} %copy-done.25) | copy-start | bytes 6148
  384.6 17.9 %copy-start.31 = (f32[768]{0:T(1024)S(1)}, f32[768]{0:T(1024)}, u32[]{:S(2)}) copy-start(f32[768]{0:T(1024)} %param.19) | copy-start | bytes 9220
  384.6 17.9 %copy-start.43 = (f32[768]{0:T(1024)S(1)}, f32[768]{0:T(1024)}, u32[]{:S(2)}) copy-start(f32[768]{0:T(1024)} %param.20) | copy-start | bytes 9220
  415.9 5.1 copy-start.34
  415.9 75.4 %all-to-all-start.5 = ((bf16[4,512,768]{2,1,0:T(8,128)(2,1)}), bf16[4,512,768]{2,1,0:T(8,128)(2,1)}, u32[]{:S(2)}, u32[]{:S(2)}) async-start(bf16[4,512,768]{2,1,0:T(8,128)(2,1)} %bitcast.91), calls=%async_computation.6 | async-start | bytes 6291456 | tf_op jit(solution)/shard_map/all_to_all | solution.py:37
  491.3 33.5 %all-to-all-start.7 = ((f32[4,24,3084]{2,1,0:T(8,128)}), f32[4,24,3084]{2,1,0:T(8,128)}, u32[]{:S(2)}, u32[]{:S(2)}) async-start(f32[4,24,3084]{2,1,0:T(8,128)} %pad_maximum_fusion.1), calls=%async_computation.10 | async-start | bytes 2457600 | tf_op jit(solution)/shard_map/all_to_all | solution.py:37
  (26 other events, 54.0 us)
Sparse Core Ops, SparseCore 0:
  96.4 62.5 all-gather.2
  160.5 62.0 all-gather.4
  236.6 59.0 reduce-scatter.3
  309.6 65.2 reduce-scatter.7
  409.5 65.7 reduce-scatter.5

commit v11 on v10

--- a/solution.py
+++ b/solution.py
@@ -71,7 +71,14 @@
     local_heads = head_count // group_size
     score_scale = float(head_dim) ** (-0.5)
 
-    grad_rows = lax.all_gather(cotangent, "mp", axis=0, tiled=True)
+    split = model_width // 2
+    grad_rows = jnp.concatenate(
+        [
+            lax.all_gather(cotangent[:, :split], "mp", axis=0, tiled=True),
+            lax.all_gather(cotangent[:, split:], "mp", axis=0, tiled=True),
+        ],
+        axis=1,
+    )
 
     inputs = block_input.astype(jnp.float32)
     normed_one, standard_one, factor_one = norm_forward(inputs, ln1_gain, ln1_bias)

time: 544 us -> 525 us (0.965)
  waiting for transfers between devices: 296 us -> 265 us
  local copies, waits for them, and re-layouts: 44.1 us -> 51.8 us
  blocking collectives: 35.6 us -> 42.6 us
    all_gather x1 -> x2, waiting for transfers between devices: 56.6 us -> 6.97 us  [the longest x1 6.95 us: block_body(): lax.all_gather(cotangent[:, split:], 'mp', axis=0, tiled=True)]
    all_to_all x1, waiting for transfers between devices: 35.4 us -> 55.3 us  [block_body(): lax.all_to_all(packed, 'mp', split_axis=2, concat_axis=0, tiled=True)]
    all_to_all x1, blocking collectives: 9.55 us -> 16.5 us  [broadcast_gather(): lax.all_to_all(sent, 'mp', split_axis=0, concat_axis=0, tiled=True)]
  transfers between devices with their start and end apart: 12 -> 13, of which waited for: 11 -> 11; matrix products, arithmetic and copies ran while one was open for 19% -> 22% of each run, Pallas kernels for 0% -> 0%
where the time goes in v11:
time: 525 us; the launch traced here: 517 us
  waiting for transfers between devices  265 us (50%)
  matrix products  75.3 us (14%)
  local copies, waits for them, and re-layouts  51.8 us (10%)
  blocking collectives  42.6 us (8%)
  other arithmetic  34 us (6%)
  starting transfers between devices  33.1 us (6%)
  between operations  15 us (3%)
    all_gather x1, waiting for transfers between devices, block_body(): gathered = lax.all_gather(second, 'mp', axis=0, tiled=True)  61.7 us
    all_to_all x1, waiting for transfers between devices, block_body(): lax.all_to_all(packed, 'mp', split_axis=2, concat_axis=0, tiled=True)  55.3 us
    all_to_all x4, waiting for transfers between devices, scatter_sum(): lax.all_to_all(pieces, 'mp', split_axis=0, concat_axis=0, tiled=True)  49.4 us
    reduce_scatter x1, waiting for transfers between devices, block_body(): lax.psum_scatter(jnp.einsum('tf,df->td', grad_before, w_up, preferred_ele...  47.8 us
    psum x1, blocking collectives, block_body(): lax.psum(small_grads, 'dp')  26.1 us
    all_to_all x4, starting transfers between devices, scatter_sum(): lax.all_to_all(pieces, 'mp', split_axis=0, concat_axis=0, tiled=True)  19.6 us
    all_to_all x1, blocking collectives, broadcast_gather(): lax.all_to_all(sent, 'mp', split_axis=0, concat_axis=0, tiled=True)  16.5 us
    all_to_all x1, waiting for transfers between devices, block_body(): lax.all_to_all(outgoing, 'mp', split_axis=0, concat_axis=0, tiled=True)  16.2 us
  transfers between devices with their start and end apart: 13, of which 11 were waited for; matrix products, arithmetic and copies ran while one was open for 22% of the time, Pallas kernels for 0%

profile of v11, /device:TPU:0, one launch (start us, length us, event | category | flops | bytes accessed | tf_op | source)
XLA Modules:
  0.0 516.6 jit_solution(8299102507063551991)
XLA Ops:
  18.5 6.5 %all-to-all-start = ((f32[4,3,100,65]{2,3,1,0:T(8,128)}), f32[4,3,100,65]{2,3,1,0:T(8,128)}, u32[]{:S(2)}, u32[]{:S(2)}) async-start(f32[4,3,100,65]{2,3,1,0:T(8,128)} %pad_maximum_fusion.3), calls=%async_computation | async-start | bytes 884736 | tf_op jit(solution)/shard_map/all_to_all | solution.py:37
  37.8 4.3 all-to-all-start.1
  44.1 55.3 %all-to-all-done.1 = bf16[512,2,4,192]{0,3,1,2:T(8,128)(2,1)} async-done(((bf16[512,2,4,192]{0,3,1,2:T(8,128)(2,1)}), bf16[512,2,4,192]{0,3,1,2:T(8,128)(2,1)}, u32[]{:S(2)}, u32[]{:S(2)}) %all-to-all-start.1) | async-done | bytes 1572896 | tf_op jit(solution)/shard_map/all_to_all | solution.py:106
  103.6 16.5 %all_to_all.53 = bf16[4,3,100,64]{2,3,1,0:T(8,128)(2,1)S(1)} all-to-all(bf16[4,3,100,64]{2,3,1,0:T(8,128)(2,1)S(1)} %broadcast_in_dim.8), channel_id=1, replica_groups=mesh['dp'=8,'mp'=4] {'mp'}, dimensions={0} | all-to-all | bytes 307200 | tf_op jit(solution)/shard_map/all_to_all | solution.py:43
  127.3 6.9 %all-gather.8.cloned.1.call-done = bf16[2048,384]{1,0:T(8,128)(2,1)} async-done(((bf16[512,384]{1,0:T(8,128)(2,1)}), bf16[2048,384]{1,0:T(8,128)(2,1)}) %all-gather.8.cloned.1.call-update) | async-done | bytes 1572880 | tf_op jit(solution)/shard_map/all_gather | solution.py:78
  137.0 61.7 %all-gather.4.cloned.1.call-done = bf16[2048,768]{1,0:T(8,128)(2,1)} async-done(((bf16[512,768]{1,0:T(8,128)(2,1)}), bf16[2048,768]{1,0:T(8,128)(2,1)}) %all-gather.4.cloned.1.call-update) | async-done | bytes 3145744 | tf_op jit(solution)/shard_map/all_gather | solution.py:146
  198.7 6.2 %multiply_convert_fusion = (bf16[2048,768]{1,0:T(8,128)(2,1)}, f32[2048,768]{1,0:T(8,128)S(1)}) fusion(f32[768]{0:T(1024)S(1)} %convert_element_type.138, bf16[2048,768]{1,0:T(8,128)(2,1)} %all-gather.4.cloned.1.call-done, bf16[768,768]{1,0:T(8,128)(2,1)} %param.29), kind=kOutput, calls=%fused_computation.10 | convolution fusion | flops 2425356288 | bytes 13765632 | tf_op jit(solution)/shard_map/dot_general | solution.py:148
  204.9 6.2 %convert_reduce_fusion = (f32[768]{0:T(1024)}, bf16[2048,768]{1,0:T(8,128)(2,1)S(1)}) fusion(f32[2048,768]{1,0:T(8,128)S(1)} %get-tuple-element.52, f32[768]{0:T(1024)S(1)} %convert_element_type.138, bf16[2048,768]{1,0:T(8,128)(2,1)S(1)} %copy-done.19, bf16[768,768]{1,0:T(8,128)(2,1)S(1)} %copy-done.40), kind=kOutput, calls=%fused_computation.8 | convolution fusion | flops 2436365568 | bytes 13768704 | tf_op jit(solution)/shard_map/td,fd->tf/dot_general | solution.py:153
  212.8 4.0 convolution_convert_fusion
  217.0 7.1 %convolution_bitcast_fusion = f32[1,768,768]{2,1,0:T(8,128)} fusion(bf16[2048,768]{1,0:T(8,128)(2,1)} %constant_dynamic-update-slice_fusion, bf16[2048,768]{1,0:T(8,128)(2,1)} %get-tuple-element.51), kind=kOutput, calls=%fused_computation.59 | convolution fusion | flops 2415919104 | bytes 8650752 | tf_op jit(solution)/shard_map/td,tf->df/dot_general | solution.py:168
  224.1 4.2 convolution_bitcast_fusion.1
  228.3 47.8 %reduce-scatter.4.cloned.1.call-done = bf16[512,768]{1,0:T(8,128)(2,1)} async-done(((bf16[2048,768]{1,0:T(8,128)(2,1)}), bf16[512,768]{1,0:T(8,128)(2,1)}) %reduce-scatter.4.cloned.1.call-update) | async-done | bytes 786448 | tf_op jit(solution)/shard_map/reduce_scatter | solution.py:155
  279.3 3.8 convert_reduce_fusion.6
  286.6 3.4 pad_maximum_fusion
  290.0 3.4 convolution_convert_fusion.3
  298.2 3.8 all-to-all-start.3
  302.7 11.0 %all-to-all-done.3 = f32[4,3,100,64]{2,3,1,0:T(8,128)S(1)} async-done(((f32[4,3,100,64]{2,3,1,0:T(8,128)}), f32[4,3,100,64]{2,3,1,0:T(8,128)S(1)}, u32[]{:S(2)}, u32[]{:S(2)}) %all-to-all-start.3) | async-done | bytes 307232 | tf_op jit(solution)/shard_map/all_to_all | solution.py:37
  314.3 3.2 multiply_reduce_fusion
  330.2 4.2 all-to-all-start.4
  334.5 3.3 fusion.9
  342.9 16.2 %all-to-all-done.4 = bf16[4,612,192]{1,2,0:T(8,128)(2,1)} async-done(((bf16[4,612,192]{1,2,0:T(8,128)(2,1)}), bf16[4,612,192]{1,2,0:T(8,128)(2,1)}, u32[]{:S(2)}, u32[]{:S(2)}) %all-to-all-start.4) | async-done | bytes 940064 | tf_op jit(solution)/shard_map/all_to_all | solution.py:245
  359.1 4.2 all-to-all-start.6
  370.9 12.2 %all-to-all-done.6 = bf16[4,512,192]{1,2,0:T(8,128)(2,1)} async-done(((bf16[4,512,192]{1,2,0:T(8,128)(2,1)}), bf16[4,512,192]{1,2,0:T(8,128)(2,1)}, u32[]{:S(2)}, u32[]{:S(2)}) %all-to-all-start.6) | async-done | bytes 786464 | tf_op jit(solution)/shard_map/all_to_all | solution.py:214
  383.1 6.8 %fusion.11 = f32[768,2304]{1,0:T(8,128)} fusion(bf16[512,768]{0,1:T(8,128)(2,1)} %bitcast.21, bf16[512,768]{0,1:T(8,128)(2,1)} %bitcast.100, bf16[512,768]{0,1:T(8,128)(2,1)} %bitcast.98, bf16[512,768]{1,0:T(8,128)(2,1)S(1)} %copy-done.6, f32[768]{0:T(1024)S(1)} %copy-done.45, f32[768]{0:T(1024)S(1)} %copy-done.32, f32[512]{0:T(512)S(1)} %copy-done.27, ...), kind=kOutput, calls=%fused_computation.37 | convolution fusion | flops 1821376512 | bytes 10233856 | tf_op jit(solution)/shard_map/td,te->de/dot_general | solution.py:263
  389.9 6.5 %convolution_convert_fusion.1 = bf16[2048,768]{1,0:T(8,128)(2,1)} fusion(bf16[2048,768]{1,0:T(8,128)(2,1)} %get-tuple-element.51, bf16[768,768]{1,0:T(8,128)(2,1)} %param.31), kind=kOutput, calls=%fused_computation.15 | convolution fusion | flops 2417491968 | bytes 7471104 | tf_op jit(solution)/shard_map/dot_general | solution.py:164
  396.4 5.1 all-to-all-start.5
  413.0 26.1 %psum.7 = f32[768,12]{0,1:T(8,128)S(1)} all-reduce(f32[768,12]{0,1:T(8,128)S(1)} %concatenate.47), channel_id=1, replica_groups=mesh['dp'=8,'mp'=4] {'dp'}, use_global_device_ids=true, to_apply=%region_27.0 | all-reduce | flops 9216 | bytes 73728 | tf_op jit(solution)/shard_map/psum | solution.py:296
  441.3 14.5 %reduce-scatter.6.cloned.1.call-done = f32[96,2304]{1,0:T(8,128)} async-done(((f32[768,2304]{1,0:T(8,128)}), f32[96,2304]{1,0:T(8,128)}) %reduce-scatter.6.cloned.1.call-update) | async-done | bytes 884752 | tf_op jit(solution)/shard_map/reduce_scatter | solution.py:293
  458.1 13.7 %all-to-all-done.5 = bf16[4,512,768]{2,1,0:T(8,128)(2,1)} async-done(((bf16[4,512,768]{2,1,0:T(8,128)(2,1)}), bf16[4,512,768]{2,1,0:T(8,128)(2,1)}, u32[]{:S(2)}, u32[]{:S(2)}) %all-to-all-start.5) | async-done | bytes 3145760 | tf_op jit(solution)/shard_map/all_to_all | solution.py:37
  471.8 4.3 all-to-all-start.7
  476.1 3.6 fusion.36
  483.3 22.0 %all-to-all-done.7 = f32[4,24,3084]{2,1,0:T(8,128)} async-done(((f32[4,24,3084]{2,1,0:T(8,128)}), f32[4,24,3084]{2,1,0:T(8,128)}, u32[]{:S(2)}, u32[]{:S(2)}) %all-to-all-start.7) | async-done | bytes 1184288 | tf_op jit(solution)/shard_map/all_to_all | solution.py:37
  (198 shorter events, 103.7 us)
Async XLA Ops:
  7.2 20.0 %copy-start = (bf16[768,1536]{1,0:T(8,128)(2,1)S(1)}, bf16[768,1536]{1,0:T(8,128)(2,1)}, u32[]{:S(2)}) copy-start(bf16[768,1536]{1,0:T(8,128)(2,1)} %param.23) | copy-start | bytes 7077892
  10.2 16.9 %copy-start.26 = (f32[512]{0:T(512)}, f32[512]{0:T(512)S(1)}, u32[]{:S(2)}) copy-start(f32[512]{0:T(512)S(1)} %add_rsqrt_fusion.1) | copy-start | bytes 6148
  18.5 8.6 %copy-start.34 = (f32[768]{0:T(1024)S(1)}, f32[768]{0:T(1024)}, u32[]{:S(2)}) copy-start(f32[768]{0:T(1024)} %param.24) | copy-start | bytes 9220
  18.5 19.3 %all-to-all-start = ((f32[4,3,100,65]{2,3,1,0:T(8,128)}), f32[4,3,100,65]{2,3,1,0:T(8,128)}, u32[]{:S(2)}, u32[]{:S(2)}) async-start(f32[4,3,100,65]{2,3,1,0:T(8,128)} %pad_maximum_fusion.3), calls=%async_computation | async-start | bytes 884736 | tf_op jit(solution)/shard_map/all_to_all | solution.py:37
  25.0 99.5 %all-gather.6.cloned.1.call-start = ((), (), s32[]{:S(2)}) async-start(), calls=%async_computation.12 | async-start | bytes 1966080 | tf_op jit(solution)/shard_map/all_gather | solution.py:77
  37.8 61.5 %all-to-all-start.1 = ((bf16[512,2,4,192]{0,3,1,2:T(8,128)(2,1)}), bf16[512,2,4,192]{0,3,1,2:T(8,128)(2,1)}, u32[]{:S(2)}, u32[]{:S(2)}) async-start(bf16[512,2,4,192]{0,3,1,2:T(8,128)(2,1)} %copy.70), calls=%async_computation.1 | async-start | bytes 3145728 | tf_op jit(solution)/shard_map/all_to_all | solution.py:106
  42.2 92.1 %all-gather.8.cloned.1.call-start = ((), (), s32[]{:S(2)}) async-start(), calls=%async_computation.13 | async-start | bytes 1966080 | tf_op jit(solution)/shard_map/all_gather | solution.py:78
  42.9 155.8 %all-gather.4.cloned.1.call-start = ((), (), s32[]{:S(2)}) async-start(), calls=%async_computation.11 | async-start | bytes 3932160 | tf_op jit(solution)/shard_map/all_gather | solution.py:146
  44.0 57.2 %copy-start.15 = (f32[3,100,65]{1,2,0:T(8,128)}, f32[3,100,65]{1,2,0:T(8,128)S(1)}, u32[]{:S(2)}) copy-start(f32[3,100,65]{1,2,0:T(8,128)S(1)} %reduce_sum.219) | copy-start | bytes 234004
  103.6 17.0 %copy-start.39 = (bf16[768,768]{1,0:T(8,128)(2,1)S(1)}, bf16[768,768]{1,0:T(8,128)(2,1)}, u32[]{:S(2)}) copy-start(bf16[768,768]{1,0:T(8,128)(2,1)} %param.25) | copy-start | bytes 3538948
  103.6 17.0 %copy-start.43 = (f32[768]{0:T(1024)S(1)}, f32[768]{0:T(1024)}, u32[]{:S(2)}) copy-start(f32[768]{0:T(1024)} %param.26) | copy-start | bytes 9220
  124.0 152.1 %reduce-scatter.4.cloned.1.call-start = ((), (), s32[]{:S(2)}) async-start(), calls=%async_computation.14 | async-start | bytes 3932160 | tf_op jit(solution)/shard_map/reduce_scatter | solution.py:155
  198.7 6.2 %copy-start.19 = (bf16[2048,768]{1,0:T(8,128)(2,1)S(1)}, bf16[2048,768]{1,0:T(8,128)(2,1)}, u32[]{:S(2)}) copy-start(bf16[2048,768]{1,0:T(8,128)(2,1)} %constant_dynamic-update-slice_fusion) | copy-start | bytes 9437188
  198.7 6.2 %copy-start.40 = (bf16[768,768]{1,0:T(8,128)(2,1)S(1)}, bf16[768,768]{1,0:T(8,128)(2,1)}, u32[]{:S(2)}) copy-start(bf16[768,768]{1,0:T(8,128)(2,1)} %param.31) | copy-start | bytes 3538948
  204.9 7.9 %copy-start.38 = (bf16[768,768]{1,0:T(8,128)(2,1)S(1)}, bf16[768,768]{1,0:T(8,128)(2,1)}, u32[]{:S(2)}) copy-start(bf16[768,768]{1,0:T(8,128)(2,1)} %param.29) | copy-start | bytes 3538948
  216.9 222.4 %reduce-scatter.8.cloned.1.call-start = ((), (), s32[]{:S(2)}) async-start(), calls=%async_computation.16 | async-start | bytes 7962624 | tf_op jit(solution)/shard_map/reduce_scatter | solution.py:199
  216.9 7.2 %copy-start.37 = (bf16[2048,768]{1,0:T(8,128)(2,1)S(1)}, bf16[2048,768]{1,0:T(8,128)(2,1)}, u32[]{:S(2)}) copy-start(bf16[2048,768]{1,0:T(8,128)(2,1)} %all-gather.4.cloned.1.call-done) | copy-start | bytes 9437188
  216.9 7.1 %copy-start.47 = (bf16[2048,768]{1,0:T(8,128)(2,1)S(1)}, bf16[2048,768]{1,0:T(8,128)(2,1)}, u32[]{:S(2)}) copy-start(bf16[2048,768]{1,0:T(8,128)(2,1)} %copy-done.46) | copy-start | bytes 9437188
  228.3 50.9 %copy-start.30 = (f32[768]{0:T(1024)S(1)}, f32[768]{0:T(1024)}, u32[]{:S(2)}) copy-start(f32[768]{0:T(1024)} %param.32) | copy-start | bytes 9220
  279.3 4.9 copy-start.18
  298.2 15.5 %all-to-all-start.3 = ((f32[4,3,100,64]{2,3,1,0:T(8,128)}), f32[4,3,100,64]{2,3,1,0:T(8,128)S(1)}, u32[]{:S(2)}, u32[]{:S(2)}) async-start(f32[4,3,100,64]{2,3,1,0:T(8,128)} %bitcast.104), calls=%async_computation.4 | async-start | bytes 786432 | tf_op jit(solution)/shard_map/all_to_all | solution.py:37
  328.0 6.5 %copy-start.21 = (bf16[3,100,64]{1,2,0:T(8,128)(2,1)S(1)}, bf16[3,100,64]{1,2,0:T(8,128)(2,1)}, u32[]{:S(2)}) copy-start(bf16[3,100,64]{1,2,0:T(8,128)(2,1)} %reduce_sum.225) | copy-start | bytes 115204
  330.2 28.9 %all-to-all-start.4 = ((bf16[4,612,192]{1,2,0:T(8,128)(2,1)}), bf16[4,612,192]{1,2,0:T(8,128)(2,1)}, u32[]{:S(2)}, u32[]{:S(2)}) async-start(bf16[4,612,192]{1,2,0:T(8,128)(2,1)} %pad_maximum_fusion.2), calls=%async_computation.5 | async-start | bytes 1966080 | tf_op jit(solution)/shard_map/all_to_all | solution.py:245
  359.1 23.9 %all-to-all-start.6 = ((bf16[4,512,192]{1,2,0:T(8,128)(2,1)}), bf16[4,512,192]{1,2,0:T(8,128)(2,1)}, u32[]{:S(2)}, u32[]{:S(2)}) async-start(bf16[4,512,192]{1,2,0:T(8,128)(2,1)} %copy.78), calls=%async_computation.7 | async-start | bytes 1572864 | tf_op jit(solution)/shard_map/all_to_all | solution.py:214
  363.3 5.2 %copy-start.23 = (s32[512,12]{0,1:T(8,128)S(1)}, s32[512,12]{0,1:T(8,128)}, u32[]{:S(2)}) copy-start(s32[512,12]{0,1:T(8,128)} %param.18) | copy-start | bytes 73732
  363.3 92.4 %reduce-scatter.6.cloned.1.call-start = ((), (), s32[]{:S(2)}) async-start(), calls=%async_computation.15 | async-start | bytes 7962624 | tf_op jit(solution)/shard_map/reduce_scatter | solution.py:293
  365.2 17.9 %copy-start.27 = (f32[512]{0:T(512)S(1)}, f32[512]{0:T(512)}, u32[]{:S(2)}) copy-start(f32[512]{0:T(512)} %copy-done.26) | copy-start | bytes 6148
  365.2 17.9 %copy-start.32 = (f32[768]{0:T(1024)S(1)}, f32[768]{0:T(1024)}, u32[]{:S(2)}) copy-start(f32[768]{0:T(1024)} %param.19) | copy-start | bytes 9220
  365.2 17.9 %copy-start.45 = (f32[768]{0:T(1024)S(1)}, f32[768]{0:T(1024)}, u32[]{:S(2)}) copy-start(f32[768]{0:T(1024)} %param.20) | copy-start | bytes 9220
  396.4 5.1 copy-start.35
  396.4 75.4 %all-to-all-start.5 = ((bf16[4,512,768]{2,1,0:T(8,128)(2,1)}), bf16[4,512,768]{2,1,0:T(8,128)(2,1)}, u32[]{:S(2)}, u32[]{:S(2)}) async-start(bf16[4,512,768]{2,1,0:T(8,128)(2,1)} %bitcast.89), calls=%async_computation.6 | async-start | bytes 6291456 | tf_op jit(solution)/shard_map/all_to_all | solution.py:37
  471.8 33.5 %all-to-all-start.7 = ((f32[4,24,3084]{2,1,0:T(8,128)}), f32[4,24,3084]{2,1,0:T(8,128)}, u32[]{:S(2)}, u32[]{:S(2)}) async-start(f32[4,24,3084]{2,1,0:T(8,128)} %pad_maximum_fusion.1), calls=%async_computation.10 | async-start | bytes 2457600 | tf_op jit(solution)/shard_map/all_to_all | solution.py:37
  (29 other events, 63.5 us)
Sparse Core Ops, SparseCore 0:
  27.4 65.4 all-gather.5
  94.5 39.7 all-gather.7
  136.4 62.2 all-gather.3
  217.0 59.0 reduce-scatter.3
  290.1 65.2 reduce-scatter.7
  390.0 65.7 reduce-scatter.5

commit v12 on v11

--- a/solution.py
+++ b/solution.py
@@ -36,6 +36,21 @@
     pieces = partial.reshape((group_size, -1) + partial.shape[1:])
     arrived = lax.all_to_all(pieces, "mp", split_axis=0, concat_axis=0, tiled=True)
     return jnp.sum(arrived.astype(jnp.float32), axis=0)
+
+
+def shift_sum(partial, group_size):
+    me = lax.axis_index("mp")
+    pieces = partial.reshape((group_size, -1) + partial.shape[1:])
+    total = lax.dynamic_index_in_dim(pieces, me, 0, keepdims=False).astype(jnp.float32)
+    for step in range(1, group_size):
+        sent = lax.dynamic_index_in_dim(
+            pieces, jnp.remainder(me + step, group_size), 0, keepdims=False
+        )
+        moved = lax.ppermute(
+            sent, "mp", [(i, (i + step) % group_size) for i in range(group_size)]
+        )
+        total = total + moved.astype(jnp.float32)
+    return total
 
 
 def broadcast_gather(local, group_size):
@@ -245,7 +260,7 @@
     incoming = lax.all_to_all(outgoing, "mp", split_axis=0, concat_axis=0, tiled=True)
 
     out_pieces, _ = lax.optimization_barrier((out_partial.astype(jnp.bfloat16), incoming))
-    result = scatter_sum(out_pieces, group_size)
+    result = shift_sum(out_pieces, group_size)
     block_output = (residual + result).astype(jnp.bfloat16)
 
     keys_back = incoming[:, :tok_rows].transpose(1, 0, 2).reshape(tok_rows, model_width)
@@ -295,7 +310,7 @@
     small_sum = lax.dynamic_slice_in_dim(
         lax.psum(small_grads, "dp"), lax.axis_index("dp") * dp_rows, dp_rows, 0
     )
-    reduced = scatter_sum(jnp.concatenate([dp_reduced, ff_grads[2], small_sum], axis=1), group_size)
+    reduced = shift_sum(jnp.concatenate([dp_reduced, ff_grads[2], small_sum], axis=1), group_size)
     up_share = ff_grads[0]
     down_share = ff_grads[1].T
     col = 0

time: 525 us -> 546 us (1.040)
  starting transfers between devices: 33.1 us -> 57.1 us
    ppermute x0 -> x6, waiting for transfers between devices: none -> 38.7 us  [shift_sum(): lax.ppermute(sent, 'mp', [(i, (i + step) % group_size) for i in range(gro...]
    all_to_all x4 -> x2, waiting for transfers between devices: 49.4 us -> 13.8 us  [scatter_sum(): lax.all_to_all(pieces, 'mp', split_axis=0, concat_axis=0, tiled=True)]
    ppermute x0 -> x6, starting transfers between devices: none -> 33.1 us  [shift_sum(): lax.ppermute(sent, 'mp', [(i, (i + step) % group_size) for i in range(gro...]
    all_to_all x4 -> x2, starting transfers between devices: 19.6 us -> 10.3 us  [scatter_sum(): lax.all_to_all(pieces, 'mp', split_axis=0, concat_axis=0, tiled=True)]
  transfers between devices with their start and end apart: 13 -> 17, of which waited for: 11 -> 11; matrix products, arithmetic and copies ran while one was open for 22% -> 20% of each run, Pallas kernels for 0% -> 0%
where the time goes in v12:
time: 546 us; the launch traced here: 538 us
  waiting for transfers between devices  266 us (49%)
  matrix products  75.7 us (14%)
  starting transfers between devices  57.1 us (10%)
  local copies, waits for them, and re-layouts  52.2 us (10%)
  blocking collectives  42 us (8%)
  other arithmetic  29.6 us (5%)
  between operations  15.1 us (3%)
    all_gather x1, waiting for transfers between devices, block_body(): gathered = lax.all_gather(second, 'mp', axis=0, tiled=True)  61.6 us
    all_to_all x1, waiting for transfers between devices, block_body(): lax.all_to_all(packed, 'mp', split_axis=2, concat_axis=0, tiled=True)  55.3 us
    reduce_scatter x1, waiting for transfers between devices, block_body(): lax.psum_scatter(jnp.einsum('tf,df->td', grad_before, w_up, preferred_ele...  47.8 us
    ppermute x6, waiting for transfers between devices, shift_sum(): lax.ppermute(sent, 'mp', [(i, (i + step) % group_size) for i in range(gro...  38.7 us
    ppermute x6, starting transfers between devices, shift_sum(): lax.ppermute(sent, 'mp', [(i, (i + step) % group_size) for i in range(gro...  33.1 us
    psum x1, blocking collectives, block_body(): lax.psum(small_grads, 'dp')  25.5 us
    all_to_all x1, blocking collectives, broadcast_gather(): lax.all_to_all(sent, 'mp', split_axis=0, concat_axis=0, tiled=True)  16.5 us
    all_to_all x1, waiting for transfers between devices, block_body(): lax.all_to_all(outgoing, 'mp', split_axis=0, concat_axis=0, tiled=True)  16.2 us
  transfers between devices with their start and end apart: 17, of which 11 were waited for; matrix products, arithmetic and copies ran while one was open for 20% of the time, Pallas kernels for 0%

profile of v12, /device:TPU:0, one launch (start us, length us, event | category | flops | bytes accessed | tf_op | source)
XLA Modules:
  0.0 538.0 jit_solution(12214296256100885472)
XLA Ops:
  18.5 6.5 %all-to-all-start = ((f32[4,3,100,65]{2,3,1,0:T(8,128)}), f32[4,3,100,65]{2,3,1,0:T(8,128)}, u32[]{:S(2)}, u32[]{:S(2)}) async-start(f32[4,3,100,65]{2,3,1,0:T(8,128)} %pad_maximum_fusion.3), calls=%async_computation | async-start | bytes 884736 | tf_op jit(solution)/shard_map/all_to_all | solution.py:37
  37.8 4.3 all-to-all-start.1
  44.1 55.3 %all-to-all-done.1 = bf16[512,2,4,192]{0,3,1,2:T(8,128)(2,1)} async-done(((bf16[512,2,4,192]{0,3,1,2:T(8,128)(2,1)}), bf16[512,2,4,192]{0,3,1,2:T(8,128)(2,1)}, u32[]{:S(2)}, u32[]{:S(2)}) %all-to-all-start.1) | async-done | bytes 1572896 | tf_op jit(solution)/shard_map/all_to_all | solution.py:121
  103.6 16.5 %all_to_all.43 = bf16[4,3,100,64]{2,3,1,0:T(8,128)(2,1)S(1)} all-to-all(bf16[4,3,100,64]{2,3,1,0:T(8,128)(2,1)S(1)} %broadcast_in_dim.8), channel_id=1, replica_groups=mesh['dp'=8,'mp'=4] {'mp'}, dimensions={0} | all-to-all | bytes 307200 | tf_op jit(solution)/shard_map/all_to_all | solution.py:58
  127.2 7.0 %all-gather.8.cloned.1.call-done = bf16[2048,384]{1,0:T(8,128)(2,1)} async-done(((bf16[512,384]{1,0:T(8,128)(2,1)}), bf16[2048,384]{1,0:T(8,128)(2,1)}) %all-gather.8.cloned.1.call-update) | async-done | bytes 1572880 | tf_op jit(solution)/shard_map/all_gather | solution.py:93
  137.1 61.6 %all-gather.4.cloned.1.call-done = bf16[2048,768]{1,0:T(8,128)(2,1)} async-done(((bf16[512,768]{1,0:T(8,128)(2,1)}), bf16[2048,768]{1,0:T(8,128)(2,1)}) %all-gather.4.cloned.1.call-update) | async-done | bytes 3145744 | tf_op jit(solution)/shard_map/all_gather | solution.py:161
  198.7 6.2 %multiply_convert_fusion = (bf16[2048,768]{1,0:T(8,128)(2,1)}, f32[2048,768]{1,0:T(8,128)S(1)}) fusion(f32[768]{0:T(1024)S(1)} %convert_element_type.150, bf16[2048,768]{1,0:T(8,128)(2,1)} %all-gather.4.cloned.1.call-done, bf16[768,768]{1,0:T(8,128)(2,1)} %param.29), kind=kOutput, calls=%fused_computation.9 | convolution fusion | flops 2425356288 | bytes 13765632 | tf_op jit(solution)/shard_map/dot_general | solution.py:163
  204.9 6.2 %convert_reduce_fusion = (f32[768]{0:T(1024)}, bf16[2048,768]{1,0:T(8,128)(2,1)S(1)}) fusion(f32[2048,768]{1,0:T(8,128)S(1)} %get-tuple-element.58, f32[768]{0:T(1024)S(1)} %convert_element_type.150, bf16[2048,768]{1,0:T(8,128)(2,1)S(1)} %copy-done.21, bf16[768,768]{1,0:T(8,128)(2,1)S(1)} %copy-done.47), kind=kOutput, calls=%fused_computation.8 | convolution fusion | flops 2436365568 | bytes 13768704 | tf_op jit(solution)/shard_map/td,fd->tf/dot_general | solution.py:168
  212.8 4.0 convolution_convert_fusion
  217.0 7.1 %convolution_bitcast_fusion = f32[1,768,768]{2,1,0:T(8,128)} fusion(bf16[2048,768]{1,0:T(8,128)(2,1)} %constant_dynamic-update-slice_fusion, bf16[2048,768]{1,0:T(8,128)(2,1)} %get-tuple-element.57), kind=kOutput, calls=%fused_computation.58 | convolution fusion | flops 2415919104 | bytes 8650752 | tf_op jit(solution)/shard_map/td,tf->df/dot_general | solution.py:183
  224.1 4.2 convolution_bitcast_fusion.1
  228.3 47.8 %reduce-scatter.4.cloned.1.call-done = bf16[512,768]{1,0:T(8,128)(2,1)} async-done(((bf16[2048,768]{1,0:T(8,128)(2,1)}), bf16[512,768]{1,0:T(8,128)(2,1)}) %reduce-scatter.4.cloned.1.call-update) | async-done | bytes 786448 | tf_op jit(solution)/shard_map/reduce_scatter | solution.py:170
  279.2 3.8 convert_reduce_fusion.5
  286.5 3.4 pad_maximum_fusion
  289.9 3.4 convolution_convert_fusion.3
  298.1 3.8 all-to-all-start.3
  302.7 11.0 %all-to-all-done.3 = f32[4,3,100,64]{2,3,1,0:T(8,128)S(1)} async-done(((f32[4,3,100,64]{2,3,1,0:T(8,128)}), f32[4,3,100,64]{2,3,1,0:T(8,128)S(1)}, u32[]{:S(2)}, u32[]{:S(2)}) %all-to-all-start.3) | async-done | bytes 307232 | tf_op jit(solution)/shard_map/all_to_all | solution.py:37
  330.2 4.3 all-to-all-start.4
  334.5 3.3 fusion.9
  342.9 16.2 %all-to-all-done.4 = bf16[4,612,192]{1,2,0:T(8,128)(2,1)} async-done(((bf16[4,612,192]{1,2,0:T(8,128)(2,1)}), bf16[4,612,192]{1,2,0:T(8,128)(2,1)}, u32[]{:S(2)}, u32[]{:S(2)}) %all-to-all-start.4) | async-done | bytes 940064 | tf_op jit(solution)/shard_map/all_to_all | solution.py:260
  359.1 4.2 all-to-all-start.5
  371.0 12.0 %all-to-all-done.5 = bf16[4,512,192]{1,2,0:T(8,128)(2,1)} async-done(((bf16[4,512,192]{1,2,0:T(8,128)(2,1)}), bf16[4,512,192]{1,2,0:T(8,128)(2,1)}, u32[]{:S(2)}, u32[]{:S(2)}) %all-to-all-start.5) | async-done | bytes 786464 | tf_op jit(solution)/shard_map/all_to_all | solution.py:229
  383.0 6.8 %fusion.11 = f32[768,2304]{1,0:T(8,128)} fusion(bf16[512,768]{0,1:T(8,128)(2,1)} %bitcast.25, bf16[512,768]{0,1:T(8,128)(2,1)} %bitcast.122, bf16[512,768]{0,1:T(8,128)(2,1)} %bitcast.120, bf16[512,768]{1,0:T(8,128)(2,1)S(1)} %copy-done.7, f32[768]{0:T(1024)S(1)} %copy-done.52, f32[768]{0:T(1024)S(1)} %copy-done.39, f32[512]{0:T(512)S(1)} %copy-done.34, ...), kind=kOutput, calls=%fused_computation.36 | convolution fusion | flops 1821376512 | bytes 10233856 | tf_op jit(solution)/shard_map/td,te->de/dot_general | solution.py:278
  391.3 6.6 %convolution_convert_fusion.1 = bf16[2048,768]{1,0:T(8,128)(2,1)} fusion(bf16[2048,768]{1,0:T(8,128)(2,1)} %get-tuple-element.57, bf16[768,768]{1,0:T(8,128)(2,1)} %param.31), kind=kOutput, calls=%fused_computation.14 | convolution fusion | flops 2417491968 | bytes 7471104 | tf_op jit(solution)/shard_map/dot_general | solution.py:179
  405.5 25.5 %psum.7 = f32[768,12]{0,1:T(8,128)S(1)} all-reduce(f32[768,12]{0,1:T(8,128)S(1)} %concatenate.47), channel_id=1, replica_groups=mesh['dp'=8,'mp'=4] {'dp'}, use_global_device_ids=true, to_apply=%region_26.27 | all-reduce | flops 9216 | bytes 73728 | tf_op jit(solution)/shard_map/psum | solution.py:311
  431.2 3.3 dynamic-slice_bitcast_fusion.2
  434.5 3.8 collective-permute-start.2
  442.1 13.2 %reduce-scatter.6.cloned.1.call-done = f32[96,2304]{1,0:T(8,128)} async-done(((f32[768,2304]{1,0:T(8,128)}), f32[96,2304]{1,0:T(8,128)}) %reduce-scatter.6.cloned.1.call-update) | async-done | bytes 884752 | tf_op jit(solution)/shard_map/reduce_scatter | solution.py:308
  460.6 25.4 %collective-permute-start.4 = (f32[24,3084]{1,0:T(8,128)S(1)}, f32[24,3084]{1,0:T(8,128)S(1)}, u32[]{:S(2)}, u32[]{:S(2)}) collective-permute-start(f32[24,3084]{1,0:T(8,128)S(1)} %get-tuple-element.44), channel_id=1, source_target_pairs={{0,2},{1,3},{2,0},{3,1},{4,6},{5,7},{6,4},{7,5},{8,10},{9,11},{10,... | collective-permute-start | bytes 888200 | tf_op jit(solution)/shard_map/ppermute | solution.py:49
  486.0 30.9 %collective-permute-done.1 = bf16[512,768]{1,0:T(8,128)(2,1)} collective-permute-done((bf16[512,768]{1,0:T(8,128)(2,1)}, bf16[512,768]{1,0:T(8,128)(2,1)}, u32[]{:S(2)}, u32[]{:S(2)}) %collective-permute-start.1) | collective-permute-done | bytes 786464 | tf_op jit(solution)/shard_map/ppermute | solution.py:49
  517.0 3.3 fusion.50
  520.2 7.8 %collective-permute-done.4 = f32[24,3084]{1,0:T(8,128)S(1)} collective-permute-done((f32[24,3084]{1,0:T(8,128)S(1)}, f32[24,3084]{1,0:T(8,128)S(1)}, u32[]{:S(2)}, u32[]{:S(2)}) %collective-permute-start.4) | collective-permute-done | bytes 296096 | tf_op jit(solution)/shard_map/ppermute | solution.py:49
  (221 shorter events, 104.1 us)
Async XLA Ops:
  7.2 20.0 %copy-start = (bf16[768,1536]{1,0:T(8,128)(2,1)S(1)}, bf16[768,1536]{1,0:T(8,128)(2,1)}, u32[]{:S(2)}) copy-start(bf16[768,1536]{1,0:T(8,128)(2,1)} %param.23) | copy-start | bytes 7077892
  10.2 16.9 %copy-start.33 = (f32[512]{0:T(512)}, f32[512]{0:T(512)S(1)}, u32[]{:S(2)}) copy-start(f32[512]{0:T(512)S(1)} %add_rsqrt_fusion.1) | copy-start | bytes 6148
  18.5 8.6 %copy-start.41 = (f32[768]{0:T(1024)S(1)}, f32[768]{0:T(1024)}, u32[]{:S(2)}) copy-start(f32[768]{0:T(1024)} %param.24) | copy-start | bytes 9220
  18.5 19.3 %all-to-all-start = ((f32[4,3,100,65]{2,3,1,0:T(8,128)}), f32[4,3,100,65]{2,3,1,0:T(8,128)}, u32[]{:S(2)}, u32[]{:S(2)}) async-start(f32[4,3,100,65]{2,3,1,0:T(8,128)} %pad_maximum_fusion.3), calls=%async_computation | async-start | bytes 884736 | tf_op jit(solution)/shard_map/all_to_all | solution.py:37
  25.0 99.5 %all-gather.6.cloned.1.call-start = ((), (), s32[]{:S(2)}) async-start(), calls=%async_computation.10 | async-start | bytes 1966080 | tf_op jit(solution)/shard_map/all_gather | solution.py:92
  37.8 61.5 %all-to-all-start.1 = ((bf16[512,2,4,192]{0,3,1,2:T(8,128)(2,1)}), bf16[512,2,4,192]{0,3,1,2:T(8,128)(2,1)}, u32[]{:S(2)}, u32[]{:S(2)}) async-start(bf16[512,2,4,192]{0,3,1,2:T(8,128)(2,1)} %copy.70), calls=%async_computation.1 | async-start | bytes 3145728 | tf_op jit(solution)/shard_map/all_to_all | solution.py:121
  42.2 92.1 %all-gather.8.cloned.1.call-start = ((), (), s32[]{:S(2)}) async-start(), calls=%async_computation.11 | async-start | bytes 1966080 | tf_op jit(solution)/shard_map/all_gather | solution.py:93
  42.9 155.7 %all-gather.4.cloned.1.call-start = ((), (), s32[]{:S(2)}) async-start(), calls=%async_computation.9 | async-start | bytes 3932160 | tf_op jit(solution)/shard_map/all_gather | solution.py:161
  44.1 57.2 %copy-start.17 = (f32[3,100,65]{1,2,0:T(8,128)}, f32[3,100,65]{1,2,0:T(8,128)S(1)}, u32[]{:S(2)}) copy-start(f32[3,100,65]{1,2,0:T(8,128)S(1)} %reduce_sum.201) | copy-start | bytes 234004
  103.6 17.0 %copy-start.46 = (bf16[768,768]{1,0:T(8,128)(2,1)S(1)}, bf16[768,768]{1,0:T(8,128)(2,1)}, u32[]{:S(2)}) copy-start(bf16[768,768]{1,0:T(8,128)(2,1)} %param.25) | copy-start | bytes 3538948
  103.6 17.0 %copy-start.50 = (f32[768]{0:T(1024)S(1)}, f32[768]{0:T(1024)}, u32[]{:S(2)}) copy-start(f32[768]{0:T(1024)} %param.26) | copy-start | bytes 9220
  123.9 152.1 %reduce-scatter.4.cloned.1.call-start = ((), (), s32[]{:S(2)}) async-start(), calls=%async_computation.12 | async-start | bytes 3932160 | tf_op jit(solution)/shard_map/reduce_scatter | solution.py:170
  204.9 7.9 %copy-start.45 = (bf16[768,768]{1,0:T(8,128)(2,1)S(1)}, bf16[768,768]{1,0:T(8,128)(2,1)}, u32[]{:S(2)}) copy-start(bf16[768,768]{1,0:T(8,128)(2,1)} %param.29) | copy-start | bytes 3538948
  216.9 223.2 %reduce-scatter.8.cloned.1.call-start = ((), (), s32[]{:S(2)}) async-start(), calls=%async_computation.14 | async-start | bytes 7962624 | tf_op jit(solution)/shard_map/reduce_scatter | solution.py:214
  228.3 50.9 %copy-start.37 = (f32[768]{0:T(1024)S(1)}, f32[768]{0:T(1024)}, u32[]{:S(2)}) copy-start(f32[768]{0:T(1024)} %param.32) | copy-start | bytes 9220
  298.1 15.5 %all-to-all-start.3 = ((f32[4,3,100,64]{2,3,1,0:T(8,128)}), f32[4,3,100,64]{2,3,1,0:T(8,128)S(1)}, u32[]{:S(2)}, u32[]{:S(2)}) async-start(f32[4,3,100,64]{2,3,1,0:T(8,128)} %bitcast.126), calls=%async_computation.4 | async-start | bytes 786432 | tf_op jit(solution)/shard_map/all_to_all | solution.py:37
  330.2 28.9 %all-to-all-start.4 = ((bf16[4,612,192]{1,2,0:T(8,128)(2,1)}), bf16[4,612,192]{1,2,0:T(8,128)(2,1)}, u32[]{:S(2)}, u32[]{:S(2)}) async-start(bf16[4,612,192]{1,2,0:T(8,128)(2,1)} %pad_maximum_fusion.2), calls=%async_computation.5 | async-start | bytes 1966080 | tf_op jit(solution)/shard_map/all_to_all | solution.py:260
  359.1 23.9 %all-to-all-start.5 = ((bf16[4,512,192]{1,2,0:T(8,128)(2,1)}), bf16[4,512,192]{1,2,0:T(8,128)(2,1)}, u32[]{:S(2)}, u32[]{:S(2)}) async-start(bf16[4,512,192]{1,2,0:T(8,128)(2,1)} %copy.78), calls=%async_computation.6 | async-start | bytes 1572864 | tf_op jit(solution)/shard_map/all_to_all | solution.py:229
  363.3 92.0 %reduce-scatter.6.cloned.1.call-start = ((), (), s32[]{:S(2)}) async-start(), calls=%async_computation.13 | async-start | bytes 7962624 | tf_op jit(solution)/shard_map/reduce_scatter | solution.py:308
  365.4 17.6 %copy-start.34 = (f32[512]{0:T(512)S(1)}, f32[512]{0:T(512)}, u32[]{:S(2)}) copy-start(f32[512]{0:T(512)} %copy-done.33) | copy-start | bytes 6148
  365.4 17.6 %copy-start.39 = (f32[768]{0:T(1024)S(1)}, f32[768]{0:T(1024)}, u32[]{:S(2)}) copy-start(f32[768]{0:T(1024)} %param.19) | copy-start | bytes 9220
  365.4 17.6 %copy-start.52 = (f32[768]{0:T(1024)S(1)}, f32[768]{0:T(1024)}, u32[]{:S(2)}) copy-start(f32[768]{0:T(1024)} %param.20) | copy-start | bytes 9220
  391.3 8.2 %copy-start.27 = (f32[12,64]{1,0:T(8,128)S(1)}, f32[12,64]{1,0:T(8,128)}, u32[]{:S(2)}) copy-start(f32[12,64]{1,0:T(8,128)} %get-tuple-element.62) | copy-start | bytes 9220
  431.2 7.2 %copy-start.6 = (f32[512,768]{1,0:T(8,128)S(1)}, f32[512,768]{1,0:T(8,128)}, u32[]{:S(2)}) copy-start(f32[512,768]{1,0:T(8,128)} %copy-done.5) | copy-start | bytes 4718596
  431.2 7.2 %copy-start.16 = (f32[512,768]{1,0:T(8,128)S(1)}, f32[512,768]{1,0:T(8,128)}, u32[]{:S(2)}) copy-start(f32[512,768]{1,0:T(8,128)} %get-tuple-element.61) | copy-start | bytes 4718596
  434.5 26.1 %collective-permute-start = (bf16[512,768]{1,0:T(8,128)(2,1)}, bf16[512,768]{1,0:T(8,128)(2,1)}, u32[]{:S(2)}, u32[]{:S(2)}) collective-permute-start(bf16[512,768]{1,0:T(8,128)(2,1)} %get-tuple-element.36), channel_id=1, source_target_pairs={{0,1},{1,2},{2,3},{3,0},{4,5},{5,6},{6,7},{7,4},{8,9},{9,10},{10,1... | collective-permute-start | bytes 2359304 | tf_op jit(solution)/shard_map/ppermute | solution.py:49
  434.5 51.5 %collective-permute-start.2 = (bf16[512,768]{1,0:T(8,128)(2,1)}, bf16[512,768]{1,0:T(8,128)(2,1)}, u32[]{:S(2)}, u32[]{:S(2)}) collective-permute-start(bf16[512,768]{1,0:T(8,128)(2,1)} %get-tuple-element.37), channel_id=1, source_target_pairs={{0,3},{1,0},{2,1},{3,2},{4,7},{5,4},{6,5},{7,6},{8,11},{9,8},{10,9... | collective-permute-start | bytes 2359304 | tf_op jit(solution)/shard_map/ppermute | solution.py:49
  438.3 78.6 %collective-permute-start.1 = (bf16[512,768]{1,0:T(8,128)(2,1)}, bf16[512,768]{1,0:T(8,128)(2,1)}, u32[]{:S(2)}, u32[]{:S(2)}) collective-permute-start(bf16[512,768]{1,0:T(8,128)(2,1)} %get-tuple-element.38), channel_id=1, source_target_pairs={{0,2},{1,3},{2,0},{3,1},{4,6},{5,7},{6,4},{7,5},{8,10},{9,11},{10,... | collective-permute-start | bytes 2359304 | tf_op jit(solution)/shard_map/ppermute | solution.py:49
  455.3 61.7 %copy-start.8 = (f32[512,768]{1,0:T(8,128)S(1)}, f32[512,768]{1,0:T(8,128)}, u32[]{:S(2)}) copy-start(f32[512,768]{1,0:T(8,128)} %get-tuple-element.39) | copy-start | bytes 4718596
  456.7 63.5 %collective-permute-start.3 = (f32[24,3084]{1,0:T(8,128)S(1)}, f32[24,3084]{1,0:T(8,128)S(1)}, u32[]{:S(2)}, u32[]{:S(2)}) collective-permute-start(f32[24,3084]{1,0:T(8,128)S(1)} %get-tuple-element.42), channel_id=1, source_target_pairs={{0,1},{1,2},{2,3},{3,0},{4,5},{5,6},{6,7},{7,4},{8,9},{9,10},{10,1... | collective-permute-start | bytes 888200 | tf_op jit(solution)/shard_map/ppermute | solution.py:49
  458.3 62.0 %collective-permute-start.5 = (f32[24,3084]{1,0:T(8,128)S(1)}, f32[24,3084]{1,0:T(8,128)S(1)}, u32[]{:S(2)}, u32[]{:S(2)}) collective-permute-start(f32[24,3084]{1,0:T(8,128)S(1)} %get-tuple-element.43), channel_id=1, source_target_pairs={{0,3},{1,0},{2,1},{3,2},{4,7},{5,4},{6,5},{7,6},{8,11},{9,8},{10,9... | collective-permute-start | bytes 888200 | tf_op jit(solution)/shard_map/ppermute | solution.py:49
  460.6 67.4 %collective-permute-start.4 = (f32[24,3084]{1,0:T(8,128)S(1)}, f32[24,3084]{1,0:T(8,128)S(1)}, u32[]{:S(2)}, u32[]{:S(2)}) collective-permute-start(f32[24,3084]{1,0:T(8,128)S(1)} %get-tuple-element.44), channel_id=1, source_target_pairs={{0,2},{1,3},{2,0},{3,1},{4,6},{5,7},{6,4},{7,5},{8,10},{9,11},{10,... | collective-permute-start | bytes 888200 | tf_op jit(solution)/shard_map/ppermute | solution.py:49
  (40 other events, 132.8 us)
Sparse Core Ops, SparseCore 0:
  27.4 65.4 all-gather.5
  94.5 39.7 all-gather.7
  136.4 62.2 all-gather.3
  217.0 59.0 reduce-scatter.3
  290.1 65.2 reduce-scatter.7
  390.0 65.1 reduce-scatter.5

commit v13 on v12

--- a/solution.py
+++ b/solution.py
@@ -51,6 +51,25 @@
         )
         total = total + moved.astype(jnp.float32)
     return total
+
+
+def shift_exchange(pieces, group_size):
+    me = lax.axis_index("mp")
+    out = jnp.zeros_like(pieces)
+    out = lax.dynamic_update_index_in_dim(
+        out, lax.dynamic_index_in_dim(pieces, me, 0, keepdims=False), me, 0
+    )
+    for step in range(1, group_size):
+        sent = lax.dynamic_index_in_dim(
+            pieces, jnp.remainder(me + step, group_size), 0, keepdims=False
+        )
+        moved = lax.ppermute(
+            sent, "mp", [(i, (i + step) % group_size) for i in range(group_size)]
+        )
+        out = lax.dynamic_update_index_in_dim(
+            out, moved, jnp.remainder(me + group_size - step, group_size), 0
+        )
+    return out
 
 
 def broadcast_gather(local, group_size):
@@ -215,7 +234,7 @@
         jnp.stack([grad_up, grad_down_t, grad_w_out]), "dp", scatter_dimension=1, tiled=True
     )
 
-    summary_grad = scatter_sum(summary_grad, group_size).astype(jnp.bfloat16)
+    summary_grad = shift_sum(summary_grad, group_size).astype(jnp.bfloat16)
 
     grad_values = jnp.einsum(
         "hcj,hcd->jhd",
@@ -226,7 +245,7 @@
     half_width = local_heads * head_dim
     values_out = grad_values.astype(jnp.bfloat16).reshape(group_size, tok_rows, half_width)
 
-    values_in = lax.all_to_all(values_out, "mp", split_axis=0, concat_axis=0, tiled=True)
+    values_in = shift_exchange(values_out, group_size)
 
     grad_probs = jnp.einsum(
         "hcd,jhd->hcj", summary_grad, value_rows, preferred_element_type=jnp.float32
@@ -257,7 +276,7 @@
         axis=1,
     )
 
-    incoming = lax.all_to_all(outgoing, "mp", split_axis=0, concat_axis=0, tiled=True)
+    incoming = shift_exchange(outgoing, group_size)
 
     out_pieces, _ = lax.optimization_barrier((out_partial.astype(jnp.bfloat16), incoming))
     result = shift_sum(out_pieces, group_size)

time: 546 us -> 510 us (0.934)
  starting transfers between devices: 57.1 us -> 34.9 us
  waiting for transfers between devices: 266 us -> 249 us
  local copies, waits for them, and re-layouts: 52.2 us -> 63.4 us
    all_to_all x2 -> x0, waiting for transfers between devices: 28.2 us -> none  [the longest x1 16.2 us: block_body(): lax.all_to_all(outgoing, 'mp', split_axis=0, concat_axis=0, tiled=True)]
    ppermute x0 -> x6, waiting for transfers between devices: none -> 21.8 us  [shift_exchange(): lax.ppermute(sent, 'mp', [(i, (i + step) % group_size) for i in range(gro...]
    ppermute x6 -> x9, starting transfers between devices: 33.1 us -> 15 us  [shift_sum(): lax.ppermute(sent, 'mp', [(i, (i + step) % group_size) for i in range(gro...]
    all_to_all x2 -> x1, waiting for transfers between devices: 13.8 us -> 2.78 us  [scatter_sum(): lax.all_to_all(pieces, 'mp', split_axis=0, concat_axis=0, tiled=True)]
    all_to_all x2 -> x0, starting transfers between devices: 8.43 us -> none  [the longest x1 4.25 us: block_body(): lax.all_to_all(outgoing, 'mp', split_axis=0, concat_axis=0, tiled=True)]
    ppermute x0 -> x6, starting transfers between devices: none -> 8.21 us  [shift_exchange(): lax.ppermute(sent, 'mp', [(i, (i + step) % group_size) for i in range(gro...]
    dynamic_update_slice x0 -> x7, local copies, waits for them, and re-layouts: none -> 6.89 us  [the longest x6 6.16 us: shift_exchange(): lax.dynamic_update_index_in_dim(out, moved, jnp.remainder(me + group_size...]
    unnamed x112 -> x113, local copies, waits for them, and re-layouts: 10.3 us -> 11.3 us
  transfers between devices with their start and end apart: 17 -> 23, of which waited for: 11 -> 13; matrix products, arithmetic and copies ran while one was open for 20% -> 22% of each run, Pallas kernels for 0% -> 0%
where the time goes in v13:
time: 510 us; the launch traced here: 503 us
  waiting for transfers between devices  249 us (49%)
  matrix products  70.6 us (14%)
  local copies, waits for them, and re-layouts  63.4 us (12%)
  blocking collectives  41.3 us (8%)
  starting transfers between devices  34.9 us (7%)
  other arithmetic  28.8 us (6%)
  between operations  15.2 us (3%)
    all_gather x1, waiting for transfers between devices, block_body(): gathered = lax.all_gather(second, 'mp', axis=0, tiled=True)  61.6 us
    all_to_all x1, waiting for transfers between devices, block_body(): lax.all_to_all(packed, 'mp', split_axis=2, concat_axis=0, tiled=True)  55.3 us
    reduce_scatter x1, waiting for transfers between devices, block_body(): lax.psum_scatter(jnp.einsum('tf,df->td', grad_before, w_up, preferred_ele...  47.8 us
    ppermute x9, waiting for transfers between devices, shift_sum(): lax.ppermute(sent, 'mp', [(i, (i + step) % group_size) for i in range(gro...  38.2 us
    psum x1, blocking collectives, block_body(): lax.psum(small_grads, 'dp')  24.8 us
    ppermute x6, waiting for transfers between devices, shift_exchange(): lax.ppermute(sent, 'mp', [(i, (i + step) % group_size) for i in range(gro...  21.8 us
    all_to_all x1, blocking collectives, broadcast_gather(): lax.all_to_all(sent, 'mp', split_axis=0, concat_axis=0, tiled=True)  16.5 us
    ppermute x9, starting transfers between devices, shift_sum(): lax.ppermute(sent, 'mp', [(i, (i + step) % group_size) for i in range(gro...  15 us
  transfers between devices with their start and end apart: 23, of which 13 were waited for; matrix products, arithmetic and copies ran while one was open for 22% of the time, Pallas kernels for 0%

profile of v13, /device:TPU:0, one launch (start us, length us, event | category | flops | bytes accessed | tf_op | source)
XLA Modules:
  0.0 502.7 jit_solution(3383888271420073260)
XLA Ops:
  18.5 6.5 %all-to-all-start = ((f32[4,3,100,65]{2,3,1,0:T(8,128)}), f32[4,3,100,65]{2,3,1,0:T(8,128)}, u32[]{:S(2)}, u32[]{:S(2)}) async-start(f32[4,3,100,65]{2,3,1,0:T(8,128)} %pad_maximum_fusion.2), calls=%async_computation | async-start | bytes 884736 | tf_op jit(solution)/shard_map/all_to_all | solution.py:37
  37.8 4.4 all-to-all-start.1
  44.1 55.3 %all-to-all-done.1 = bf16[512,2,4,192]{0,3,1,2:T(8,128)(2,1)} async-done(((bf16[512,2,4,192]{0,3,1,2:T(8,128)(2,1)}), bf16[512,2,4,192]{0,3,1,2:T(8,128)(2,1)}, u32[]{:S(2)}, u32[]{:S(2)}) %all-to-all-start.1) | async-done | bytes 1572896 | tf_op jit(solution)/shard_map/all_to_all | solution.py:140
  103.6 16.5 %all_to_all.28 = bf16[4,3,100,64]{2,3,1,0:T(8,128)(2,1)S(1)} all-to-all(bf16[4,3,100,64]{2,3,1,0:T(8,128)(2,1)S(1)} %broadcast_in_dim.33), channel_id=1, replica_groups=mesh['dp'=8,'mp'=4] {'mp'}, dimensions={0} | all-to-all | bytes 307200 | tf_op jit(solution)/shard_map/all_to_all | solution.py:77
  127.2 7.0 %all-gather.8.cloned.1.call-done = bf16[2048,384]{1,0:T(8,128)(2,1)} async-done(((bf16[512,384]{1,0:T(8,128)(2,1)}), bf16[2048,384]{1,0:T(8,128)(2,1)}) %all-gather.8.cloned.1.call-update) | async-done | bytes 1572880 | tf_op jit(solution)/shard_map/all_gather | solution.py:112
  137.0 61.6 %all-gather.4.cloned.1.call-done = bf16[2048,768]{1,0:T(8,128)(2,1)} async-done(((bf16[512,768]{1,0:T(8,128)(2,1)}), bf16[2048,768]{1,0:T(8,128)(2,1)}) %all-gather.4.cloned.1.call-update) | async-done | bytes 3145744 | tf_op jit(solution)/shard_map/all_gather | solution.py:180
  198.7 6.2 %multiply_convert_fusion = (bf16[2048,768]{1,0:T(8,128)(2,1)}, f32[2048,768]{1,0:T(8,128)S(1)}) fusion(f32[768]{0:T(1024)S(1)} %convert_element_type.150, bf16[2048,768]{1,0:T(8,128)(2,1)} %all-gather.4.cloned.1.call-done, bf16[768,768]{1,0:T(8,128)(2,1)} %param.29), kind=kOutput, calls=%fused_computation.9 | convolution fusion | flops 2425356288 | bytes 13765632 | tf_op jit(solution)/shard_map/dot_general | solution.py:182
  204.9 6.2 %convert_reduce_fusion = (f32[768]{0:T(1024)}, bf16[2048,768]{1,0:T(8,128)(2,1)S(1)}) fusion(f32[2048,768]{1,0:T(8,128)S(1)} %get-tuple-element.69, f32[768]{0:T(1024)S(1)} %convert_element_type.150, bf16[2048,768]{1,0:T(8,128)(2,1)S(1)} %copy-done.18, bf16[768,768]{1,0:T(8,128)(2,1)S(1)} %copy-done.46), kind=kOutput, calls=%fused_computation.8 | convolution fusion | flops 2436365568 | bytes 13768704 | tf_op jit(solution)/shard_map/td,fd->tf/dot_general | solution.py:187
  212.8 4.1 convolution_convert_fusion
  217.0 7.1 %convolution_bitcast_fusion = f32[1,768,768]{2,1,0:T(8,128)} fusion(bf16[2048,768]{1,0:T(8,128)(2,1)} %constant_dynamic-update-slice_fusion, bf16[2048,768]{1,0:T(8,128)(2,1)} %get-tuple-element.68), kind=kOutput, calls=%fused_computation.62 | convolution fusion | flops 2415919104 | bytes 8650752 | tf_op jit(solution)/shard_map/td,tf->df/dot_general | solution.py:202
  224.1 4.2 convolution_bitcast_fusion.1
  228.3 47.8 %reduce-scatter.4.cloned.1.call-done = bf16[512,768]{1,0:T(8,128)(2,1)} async-done(((bf16[2048,768]{1,0:T(8,128)(2,1)}), bf16[512,768]{1,0:T(8,128)(2,1)}) %reduce-scatter.4.cloned.1.call-update) | async-done | bytes 786448 | tf_op jit(solution)/shard_map/reduce_scatter | solution.py:189
  276.1 3.1 fusion.42
  279.3 3.8 convert_reduce_fusion.5
  286.6 3.4 pad_maximum_fusion
  290.2 3.4 convolution_convert_fusion.3
  303.4 6.1 %collective-permute-done.1 = f32[3,100,64]{1,2,0:T(8,128)S(1)} collective-permute-done((f32[3,100,64]{1,2,0:T(8,128)S(1)}, f32[3,100,64]{1,2,0:T(8,128)S(1)}, u32[]{:S(2)}, u32[]{:S(2)}) %collective-permute-start.1) | collective-permute-done | bytes 76832 | tf_op jit(solution)/shard_map/ppermute | solution.py:49
  333.3 3.9 constant_dynamic-slice_fusion.1
  339.8 9.3 %collective-permute-done.9 = bf16[512,192]{0,1:T(8,128)(2,1)S(1)} collective-permute-done((bf16[512,192]{0,1:T(8,128)(2,1)S(1)}, bf16[512,192]{0,1:T(8,128)(2,1)S(1)}, u32[]{:S(2)}, u32[]{:S(2)}) %collective-permute-start.9) | collective-permute-done | bytes 196640 | tf_op jit(solution)/shard_map/ppermute | solution.py:66
  352.0 8.7 %collective-permute-done.10 = bf16[512,192]{0,1:T(8,128)(2,1)S(1)} collective-permute-done((bf16[512,192]{0,1:T(8,128)(2,1)S(1)}, bf16[512,192]{0,1:T(8,128)(2,1)S(1)}, u32[]{:S(2)}, u32[]{:S(2)}) %collective-permute-start.10) | collective-permute-done | bytes 196640 | tf_op jit(solution)/shard_map/ppermute | solution.py:66
  361.4 3.8 collective-permute-done.11
  377.5 6.6 %fusion.11 = f32[768,2304]{1,0:T(8,128)} fusion(bf16[512,768]{0,1:T(8,128)(2,1)} %bitcast.41, bf16[512,768]{0,1:T(8,128)(2,1)} %bitcast.161, bf16[512,768]{0,1:T(8,128)(2,1)S(1)} %bitcast.163, bf16[512,768]{1,0:T(8,128)(2,1)S(1)} %copy-done.7, f32[768]{0:T(1024)S(1)} %copy-done.51, f32[768]{0:T(1024)S(1)} %copy-done.38, f32[512]{0:T(512)S(1)} %copy-done.33, ...), kind=kOutput, calls=%fused_computation.36 | convolution fusion | flops 1821376512 | bytes 10233856 | tf_op jit(solution)/shard_map/td,te->de/dot_general | solution.py:297
  385.5 6.5 %convolution_convert_fusion.1 = bf16[2048,768]{1,0:T(8,128)(2,1)} fusion(bf16[2048,768]{1,0:T(8,128)(2,1)} %get-tuple-element.68, bf16[768,768]{1,0:T(8,128)(2,1)} %param.31), kind=kOutput, calls=%fused_computation.14 | convolution fusion | flops 2417491968 | bytes 7471104 | tf_op jit(solution)/shard_map/dot_general | solution.py:198
  393.5 3.7 dynamic-slice_bitcast_fusion.2
  404.3 4.1 fusion.37
  408.5 24.8 %psum.7 = f32[768,12]{0,1:T(8,128)S(1)} all-reduce(f32[768,12]{0,1:T(8,128)S(1)} %concatenate.47), channel_id=1, replica_groups=mesh['dp'=8,'mp'=4] {'dp'}, use_global_device_ids=true, to_apply=%region_25.26 | all-reduce | flops 9216 | bytes 73728 | tf_op jit(solution)/shard_map/psum | solution.py:330
  433.6 3.6 fusion.36
  439.2 13.2 %reduce-scatter.6.cloned.1.call-done = f32[96,2304]{1,0:T(8,128)} async-done(((f32[768,2304]{1,0:T(8,128)}), f32[96,2304]{1,0:T(8,128)}) %reduce-scatter.6.cloned.1.call-update) | async-done | bytes 884752 | tf_op jit(solution)/shard_map/reduce_scatter | solution.py:327
  453.9 3.4 collective-permute-start.14
  458.4 25.4 %collective-permute-done.7 = bf16[512,768]{1,0:T(8,128)(2,1)} collective-permute-done((bf16[512,768]{1,0:T(8,128)(2,1)}, bf16[512,768]{1,0:T(8,128)(2,1)}, u32[]{:S(2)}, u32[]{:S(2)}) %collective-permute-start.7) | collective-permute-done | bytes 786464 | tf_op jit(solution)/shard_map/ppermute | solution.py:49
  483.8 3.3 fusion.50
  487.1 5.7 %collective-permute-done.13 = f32[24,3084]{1,0:T(8,128)S(1)} collective-permute-done((f32[24,3084]{1,0:T(8,128)S(1)}, f32[24,3084]{1,0:T(8,128)S(1)}, u32[]{:S(2)}, u32[]{:S(2)}) %collective-permute-start.13) | collective-permute-done | bytes 296096 | tf_op jit(solution)/shard_map/ppermute | solution.py:49
  (244 shorter events, 114.9 us)
Async XLA Ops:
  7.2 20.0 %copy-start = (bf16[768,1536]{1,0:T(8,128)(2,1)S(1)}, bf16[768,1536]{1,0:T(8,128)(2,1)}, u32[]{:S(2)}) copy-start(bf16[768,1536]{1,0:T(8,128)(2,1)} %param.23) | copy-start | bytes 7077892
  8.7 18.4 %copy-start.26 = (f32[512]{0:T(512)}, f32[512]{0:T(512)S(1)}, u32[]{:S(2)}) copy-start(f32[512]{0:T(512)S(1)} %broadcast_multiply_fusion.5) | copy-start | bytes 6148
  10.2 16.9 %copy-start.32 = (f32[512]{0:T(512)}, f32[512]{0:T(512)S(1)}, u32[]{:S(2)}) copy-start(f32[512]{0:T(512)S(1)} %add_rsqrt_fusion.1) | copy-start | bytes 6148
  18.5 19.3 %all-to-all-start = ((f32[4,3,100,65]{2,3,1,0:T(8,128)}), f32[4,3,100,65]{2,3,1,0:T(8,128)}, u32[]{:S(2)}, u32[]{:S(2)}) async-start(f32[4,3,100,65]{2,3,1,0:T(8,128)} %pad_maximum_fusion.2), calls=%async_computation | async-start | bytes 884736 | tf_op jit(solution)/shard_map/all_to_all | solution.py:37
  25.0 99.5 %all-gather.6.cloned.1.call-start = ((), (), s32[]{:S(2)}) async-start(), calls=%async_computation.7 | async-start | bytes 1966080 | tf_op jit(solution)/shard_map/all_gather | solution.py:111
  37.8 61.5 %all-to-all-start.1 = ((bf16[512,2,4,192]{0,3,1,2:T(8,128)(2,1)}), bf16[512,2,4,192]{0,3,1,2:T(8,128)(2,1)}, u32[]{:S(2)}, u32[]{:S(2)}) async-start(bf16[512,2,4,192]{0,3,1,2:T(8,128)(2,1)} %copy.100), calls=%async_computation.1 | async-start | bytes 3145728 | tf_op jit(solution)/shard_map/all_to_all | solution.py:140
  42.2 92.1 %all-gather.8.cloned.1.call-start = ((), (), s32[]{:S(2)}) async-start(), calls=%async_computation.8 | async-start | bytes 1966080 | tf_op jit(solution)/shard_map/all_gather | solution.py:112
  43.0 155.7 %all-gather.4.cloned.1.call-start = ((), (), s32[]{:S(2)}) async-start(), calls=%async_computation.6 | async-start | bytes 3932160 | tf_op jit(solution)/shard_map/all_gather | solution.py:180
  103.5 17.0 %copy-start.45 = (bf16[768,768]{1,0:T(8,128)(2,1)S(1)}, bf16[768,768]{1,0:T(8,128)(2,1)}, u32[]{:S(2)}) copy-start(bf16[768,768]{1,0:T(8,128)(2,1)} %param.25) | copy-start | bytes 3538948
  103.5 17.1 %copy-start.49 = (f32[768]{0:T(1024)S(1)}, f32[768]{0:T(1024)}, u32[]{:S(2)}) copy-start(f32[768]{0:T(1024)} %param.26) | copy-start | bytes 9220
  123.9 152.2 %reduce-scatter.4.cloned.1.call-start = ((), (), s32[]{:S(2)}) async-start(), calls=%async_computation.9 | async-start | bytes 3932160 | tf_op jit(solution)/shard_map/reduce_scatter | solution.py:189
  216.9 220.3 %reduce-scatter.8.cloned.1.call-start = ((), (), s32[]{:S(2)}) async-start(), calls=%async_computation.11 | async-start | bytes 7962624 | tf_op jit(solution)/shard_map/reduce_scatter | solution.py:233
  228.3 51.0 %copy-start.36 = (f32[768]{0:T(1024)S(1)}, f32[768]{0:T(1024)}, u32[]{:S(2)}) copy-start(f32[768]{0:T(1024)} %param.32) | copy-start | bytes 9220
  290.0 162.5 %reduce-scatter.6.cloned.1.call-start = ((), (), s32[]{:S(2)}) async-start(), calls=%async_computation.10 | async-start | bytes 7962624 | tf_op jit(solution)/shard_map/reduce_scatter | solution.py:327
  296.0 13.5 %copy-start.2 = (f32[3,100,2048]{2,1,0:T(8,128)S(1)}, f32[3,100,2048]{2,1,0:T(8,128)}, u32[]{:S(2)}) copy-start(f32[3,100,2048]{2,1,0:T(8,128)} %copy-done.1) | copy-start | bytes 7372804
  297.9 5.5 %collective-permute-start.2 = (f32[3,100,64]{1,2,0:T(8,128)S(1)}, f32[3,100,64]{1,2,0:T(8,128)S(1)}, u32[]{:S(2)}, u32[]{:S(2)}) collective-permute-start(f32[3,100,64]{1,2,0:T(8,128)S(1)} %get-tuple-element.60), channel_id=1, source_target_pairs={{0,3},{1,0},{2,1},{3,2},{4,7},{5,4},{6,5},{7,6},{8,11},{9,8},{10,9... | collective-permute-start | bytes 230408 | tf_op jit(solution)/shard_map/ppermute | solution.py:49
  300.1 9.3 %collective-permute-start.1 = (f32[3,100,64]{1,2,0:T(8,128)S(1)}, f32[3,100,64]{1,2,0:T(8,128)S(1)}, u32[]{:S(2)}, u32[]{:S(2)}) collective-permute-start(f32[3,100,64]{1,2,0:T(8,128)S(1)} %get-tuple-element.61), channel_id=1, source_target_pairs={{0,2},{1,3},{2,0},{3,1},{4,6},{5,7},{6,4},{7,5},{8,10},{9,11},{10,... | collective-permute-start | bytes 230408 | tf_op jit(solution)/shard_map/ppermute | solution.py:49
  300.4 9.1 %collective-permute-start = (f32[3,100,64]{1,2,0:T(8,128)S(1)}, f32[3,100,64]{1,2,0:T(8,128)S(1)}, u32[]{:S(2)}, u32[]{:S(2)}) collective-permute-start(f32[3,100,64]{1,2,0:T(8,128)S(1)} %get-tuple-element.59), channel_id=1, source_target_pairs={{0,1},{1,2},{2,3},{3,0},{4,5},{5,6},{6,7},{7,4},{8,9},{9,10},{10,1... | collective-permute-start | bytes 230408 | tf_op jit(solution)/shard_map/ppermute | solution.py:49
  323.4 42.5 %collective-permute-start.3 = (bf16[612,192]{0,1:T(8,128)(2,1)}, bf16[612,192]{0,1:T(8,128)(2,1)}, u32[]{:S(2)}, u32[]{:S(2)}) collective-permute-start(bf16[612,192]{0,1:T(8,128)(2,1)} %get-tuple-element.47), channel_id=1, source_target_pairs={{0,1},{1,2},{2,3},{3,0},{4,5},{5,6},{6,7},{7,4},{8,9},{9,10},{10,1... | collective-permute-start | bytes 705032 | tf_op jit(solution)/shard_map/ppermute | solution.py:66
  323.5 44.1 %collective-permute-start.4 = (bf16[612,192]{0,1:T(8,128)(2,1)}, bf16[612,192]{0,1:T(8,128)(2,1)}, u32[]{:S(2)}, u32[]{:S(2)}) collective-permute-start(bf16[612,192]{0,1:T(8,128)(2,1)} %get-tuple-element.48), channel_id=1, source_target_pairs={{0,2},{1,3},{2,0},{3,1},{4,6},{5,7},{6,4},{7,5},{8,10},{9,11},{10,... | collective-permute-start | bytes 705032 | tf_op jit(solution)/shard_map/ppermute | solution.py:66
  325.8 43.4 %collective-permute-start.5 = (bf16[612,192]{0,1:T(8,128)(2,1)}, bf16[612,192]{0,1:T(8,128)(2,1)S(1)}, u32[]{:S(2)}, u32[]{:S(2)}) collective-permute-start(bf16[612,192]{0,1:T(8,128)(2,1)} %get-tuple-element.45), channel_id=1, source_target_pairs={{0,3},{1,0},{2,1},{3,2},{4,7},{5,4},{6,5},{7,6},{8,11},{9,8},{10,9... | collective-permute-start | bytes 705032 | tf_op jit(solution)/shard_map/ppermute | solution.py:66
  337.3 11.9 %collective-permute-start.9 = (bf16[512,192]{0,1:T(8,128)(2,1)S(1)}, bf16[512,192]{0,1:T(8,128)(2,1)S(1)}, u32[]{:S(2)}, u32[]{:S(2)}) collective-permute-start(bf16[512,192]{0,1:T(8,128)(2,1)S(1)} %bitcast.173), channel_id=1, source_target_pairs={{0,1},{1,2},{2,3},{3,0},{4,5},{5,6},{6,7},{7,4},{8,9},{9,10},{10,1... | collective-permute-start | bytes 589832 | tf_op jit(solution)/shard_map/ppermute | solution.py:66
  337.4 23.3 %collective-permute-start.10 = (bf16[512,192]{0,1:T(8,128)(2,1)S(1)}, bf16[512,192]{0,1:T(8,128)(2,1)S(1)}, u32[]{:S(2)}, u32[]{:S(2)}) collective-permute-start(bf16[512,192]{0,1:T(8,128)(2,1)S(1)} %bitcast.172), channel_id=1, source_target_pairs={{0,2},{1,3},{2,0},{3,1},{4,6},{5,7},{6,4},{7,5},{8,10},{9,11},{10,... | collective-permute-start | bytes 589832 | tf_op jit(solution)/shard_map/ppermute | solution.py:66
  349.1 16.1 %collective-permute-start.11 = (bf16[512,192]{0,1:T(8,128)(2,1)S(1)}, bf16[512,192]{0,1:T(8,128)(2,1)S(1)}, u32[]{:S(2)}, u32[]{:S(2)}) collective-permute-start(bf16[512,192]{0,1:T(8,128)(2,1)S(1)} %bitcast.171), channel_id=1, source_target_pairs={{0,3},{1,0},{2,1},{3,2},{4,7},{5,4},{6,5},{7,6},{8,11},{9,8},{10,9... | collective-permute-start | bytes 589832 | tf_op jit(solution)/shard_map/ppermute | solution.py:66
  393.5 9.9 %copy-start.47 = (bf16[768,768]{1,0:T(8,128)(2,1)S(1)}, bf16[768,768]{1,0:T(8,128)(2,1)}, u32[]{:S(2)}) copy-start(bf16[768,768]{1,0:T(8,128)(2,1)} %param.21) | copy-start | bytes 3538948
  397.2 60.1 %collective-permute-start.8 = (bf16[512,768]{1,0:T(8,128)(2,1)}, bf16[512,768]{1,0:T(8,128)(2,1)}, u32[]{:S(2)}, u32[]{:S(2)}) collective-permute-start(bf16[512,768]{1,0:T(8,128)(2,1)} %get-tuple-element.37), channel_id=1, source_target_pairs={{0,3},{1,0},{2,1},{3,2},{4,7},{5,4},{6,5},{7,6},{8,11},{9,8},{10,9... | collective-permute-start | bytes 2359304 | tf_op jit(solution)/shard_map/ppermute | solution.py:49
  400.2 83.6 %collective-permute-start.7 = (bf16[512,768]{1,0:T(8,128)(2,1)}, bf16[512,768]{1,0:T(8,128)(2,1)}, u32[]{:S(2)}, u32[]{:S(2)}) collective-permute-start(bf16[512,768]{1,0:T(8,128)(2,1)} %get-tuple-element.38), channel_id=1, source_target_pairs={{0,2},{1,3},{2,0},{3,1},{4,6},{5,7},{6,4},{7,5},{8,10},{9,11},{10,... | collective-permute-start | bytes 2359304 | tf_op jit(solution)/shard_map/ppermute | solution.py:49
  401.3 82.5 %collective-permute-start.6 = (bf16[512,768]{1,0:T(8,128)(2,1)}, bf16[512,768]{1,0:T(8,128)(2,1)}, u32[]{:S(2)}, u32[]{:S(2)}) collective-permute-start(bf16[512,768]{1,0:T(8,128)(2,1)} %get-tuple-element.36), channel_id=1, source_target_pairs={{0,1},{1,2},{2,3},{3,0},{4,5},{5,6},{6,7},{7,4},{8,9},{9,10},{10,1... | collective-permute-start | bytes 2359304 | tf_op jit(solution)/shard_map/ppermute | solution.py:49
  452.5 31.4 %copy-start.8 = (f32[512,768]{1,0:T(8,128)S(1)}, f32[512,768]{1,0:T(8,128)}, u32[]{:S(2)}) copy-start(f32[512,768]{1,0:T(8,128)} %get-tuple-element.39) | copy-start | bytes 4718596
  453.9 33.2 %collective-permute-start.14 = (f32[24,3084]{1,0:T(8,128)S(1)}, f32[24,3084]{1,0:T(8,128)S(1)}, u32[]{:S(2)}, u32[]{:S(2)}) collective-permute-start(f32[24,3084]{1,0:T(8,128)S(1)} %get-tuple-element.43), channel_id=1, source_target_pairs={{0,3},{1,0},{2,1},{3,2},{4,7},{5,4},{6,5},{7,6},{8,11},{9,8},{10,9... | collective-permute-start | bytes 888200 | tf_op jit(solution)/shard_map/ppermute | solution.py:49
  457.3 35.5 %collective-permute-start.13 = (f32[24,3084]{1,0:T(8,128)S(1)}, f32[24,3084]{1,0:T(8,128)S(1)}, u32[]{:S(2)}, u32[]{:S(2)}) collective-permute-start(f32[24,3084]{1,0:T(8,128)S(1)} %get-tuple-element.44), channel_id=1, source_target_pairs={{0,2},{1,3},{2,0},{3,1},{4,6},{5,7},{6,4},{7,5},{8,10},{9,11},{10,... | collective-permute-start | bytes 888200 | tf_op jit(solution)/shard_map/ppermute | solution.py:49
  457.3 35.4 %collective-permute-start.12 = (f32[24,3084]{1,0:T(8,128)S(1)}, f32[24,3084]{1,0:T(8,128)S(1)}, u32[]{:S(2)}, u32[]{:S(2)}) collective-permute-start(f32[24,3084]{1,0:T(8,128)S(1)} %get-tuple-element.42), channel_id=1, source_target_pairs={{0,1},{1,2},{2,3},{3,0},{4,5},{5,6},{6,7},{7,4},{8,9},{9,10},{10,1... | collective-permute-start | bytes 888200 | tf_op jit(solution)/shard_map/ppermute | solution.py:49
  (45 other events, 179.7 us)
Sparse Core Ops, SparseCore 0:
  27.4 65.4 all-gather.5
  94.5 39.7 all-gather.7
  136.4 62.2 all-gather.3
  217.0 59.0 reduce-scatter.3
  290.1 65.2 reduce-scatter.7
  384.2 68.1 reduce-scatter.5

commit v14 on v13

--- a/solution.py
+++ b/solution.py
@@ -30,12 +30,6 @@
     cumulative = 0.5 * (1.0 + jax.scipy.special.erf(before / math.sqrt(2.0)))
     density = jnp.exp(-0.5 * before * before) / math.sqrt(2.0 * math.pi)
     return (before * cumulative, cumulative + before * density)
-
-
-def scatter_sum(partial, group_size):
-    pieces = partial.reshape((group_size, -1) + partial.shape[1:])
-    arrived = lax.all_to_all(pieces, "mp", split_axis=0, concat_axis=0, tiled=True)
-    return jnp.sum(arrived.astype(jnp.float32), axis=0)
 
 
 def shift_sum(partial, group_size):
@@ -138,7 +132,7 @@
     packed = keyval.reshape(tok_rows, 2, group_size, local_heads * head_dim)
 
     arrived = lax.all_to_all(packed, "mp", split_axis=2, concat_axis=0, tiled=True)
-    sums_and_sizes = scatter_sum(
+    sums_and_sizes = shift_sum(
         jnp.concatenate([query_sums, cluster_sizes[:, :, None]], axis=2), group_size
     )
 

time: 510 us -> 499 us (0.978)
  waiting for transfers between devices: 249 us -> 238 us
    all_to_all x1, waiting for transfers between devices: 55.3 us -> 0.01 us  [block_body(): lax.all_to_all(packed, 'mp', split_axis=2, concat_axis=0, tiled=True)]
    ppermute x9 -> x12, waiting for transfers between devices: 38.2 us -> 92.9 us  [shift_sum(): lax.ppermute(sent, 'mp', [(i, (i + step) % group_size) for i in range(gro...]
    all_gather x1, waiting for transfers between devices: 7.02 us -> 0.43 us  [block_body(): lax.all_gather(cotangent[:, split:], 'mp', axis=0, tiled=True)]
    all_to_all x1 -> x0, starting transfers between devices: 6.48 us -> none  [scatter_sum(): lax.all_to_all(pieces, 'mp', split_axis=0, concat_axis=0, tiled=True)]
    ppermute x9 -> x12, starting transfers between devices: 15 us -> 20 us  [shift_sum(): lax.ppermute(sent, 'mp', [(i, (i + step) % group_size) for i in range(gro...]
    unnamed x113 -> x119, local copies, waits for them, and re-layouts: 11.3 us -> 12.5 us
  transfers between devices with their start and end apart: 23 -> 25, of which waited for: 13 -> 13; matrix products, arithmetic and copies ran while one was open for 22% -> 24% of each run, Pallas kernels for 0% -> 0%
where the time goes in v14:
time: 499 us; the launch traced here: 491 us
  waiting for transfers between devices  238 us (48%)
  matrix products  70.5 us (14%)
  local copies, waits for them, and re-layouts  64.6 us (13%)
  blocking collectives  41.3 us (8%)
  starting transfers between devices  35.5 us (7%)
  other arithmetic  26.3 us (5%)
  between operations  15.1 us (3%)
    ppermute x12, waiting for transfers between devices, shift_sum(): lax.ppermute(sent, 'mp', [(i, (i + step) % group_size) for i in range(gro...  92.9 us
    all_gather x1, waiting for transfers between devices, block_body(): gathered = lax.all_gather(second, 'mp', axis=0, tiled=True)  61.6 us
    reduce_scatter x1, waiting for transfers between devices, block_body(): lax.psum_scatter(jnp.einsum('tf,df->td', grad_before, w_up, preferred_ele...  47.9 us
    psum x1, blocking collectives, block_body(): lax.psum(small_grads, 'dp')  24.8 us
    ppermute x6, waiting for transfers between devices, shift_exchange(): lax.ppermute(sent, 'mp', [(i, (i + step) % group_size) for i in range(gro...  21.8 us
    ppermute x12, starting transfers between devices, shift_sum(): lax.ppermute(sent, 'mp', [(i, (i + step) % group_size) for i in range(gro...  20 us
    all_to_all x1, blocking collectives, broadcast_gather(): lax.all_to_all(sent, 'mp', split_axis=0, concat_axis=0, tiled=True)  16.5 us
    reduce_scatter x1, waiting for transfers between devices, block_body(): lax.psum_scatter(grad_w_attn, 'dp', scatter_dimension=0, tiled=True)  13.3 us
  transfers between devices with their start and end apart: 25, of which 13 were waited for; matrix products, arithmetic and copies ran while one was open for 24% of the time, Pallas kernels for 0%

profile of v14, /device:TPU:0, one launch (start us, length us, event | category | flops | bytes accessed | tf_op | source)
XLA Modules:
  0.0 491.3 jit_solution(10083413880755459603)
XLA Ops:
  18.1 6.5 %all-to-all-start = ((bf16[512,2,4,192]{0,3,1,2:T(8,128)(2,1)}), bf16[512,2,4,192]{0,3,1,2:T(8,128)(2,1)}, u32[]{:S(2)}, u32[]{:S(2)}) async-start(bf16[512,2,4,192]{0,3,1,2:T(8,128)(2,1)} %copy.100), calls=%async_computation | async-start | bytes 3145728 | tf_op jit(solution)/shard_map/all_to_all | solution.py:134
  32.8 3.8 collective-permute-start.2
  37.9 36.1 %collective-permute-done.2 = f32[3,100,65]{1,2,0:T(8,128)} collective-permute-done((f32[3,100,65]{1,2,0:T(8,128)}, f32[3,100,65]{1,2,0:T(8,128)}, u32[]{:S(2)}, u32[]{:S(2)}) %collective-permute-start.2) | collective-permute-done | bytes 78032 | tf_op jit(solution)/shard_map/ppermute | solution.py:43
  73.9 18.5 %collective-permute-done.1 = f32[3,100,65]{1,2,0:T(8,128)} collective-permute-done((f32[3,100,65]{1,2,0:T(8,128)}, f32[3,100,65]{1,2,0:T(8,128)}, u32[]{:S(2)}, u32[]{:S(2)}) %collective-permute-start.1) | collective-permute-done | bytes 78032 | tf_op jit(solution)/shard_map/ppermute | solution.py:43
  98.8 16.5 %all_to_all.23 = bf16[4,3,100,64]{2,3,1,0:T(8,128)(2,1)S(1)} all-to-all(bf16[4,3,100,64]{2,3,1,0:T(8,128)(2,1)S(1)} %broadcast_in_dim.33), channel_id=1, replica_groups=mesh['dp'=8,'mp'=4] {'mp'}, dimensions={0} | all-to-all | bytes 307200 | tf_op jit(solution)/shard_map/all_to_all | solution.py:71
  125.8 61.6 %all-gather.4.cloned.1.call-done = bf16[2048,768]{1,0:T(8,128)(2,1)} async-done(((bf16[512,768]{1,0:T(8,128)(2,1)}), bf16[2048,768]{1,0:T(8,128)(2,1)}) %all-gather.4.cloned.1.call-update) | async-done | bytes 3145744 | tf_op jit(solution)/shard_map/all_gather | solution.py:174
  187.4 6.2 %multiply_convert_fusion = (bf16[2048,768]{1,0:T(8,128)(2,1)}, f32[2048,768]{1,0:T(8,128)S(1)}) fusion(f32[768]{0:T(1024)S(1)} %convert_element_type.150, bf16[2048,768]{1,0:T(8,128)(2,1)} %all-gather.4.cloned.1.call-done, bf16[768,768]{1,0:T(8,128)(2,1)} %param.29), kind=kOutput, calls=%fused_computation.9 | convolution fusion | flops 2425356288 | bytes 13765632 | tf_op jit(solution)/shard_map/dot_general | solution.py:176
  193.6 6.2 %convert_reduce_fusion = (f32[768]{0:T(1024)}, bf16[2048,768]{1,0:T(8,128)(2,1)S(1)}) fusion(f32[2048,768]{1,0:T(8,128)S(1)} %get-tuple-element.72, f32[768]{0:T(1024)S(1)} %convert_element_type.150, bf16[2048,768]{1,0:T(8,128)(2,1)S(1)} %copy-done.20, bf16[768,768]{1,0:T(8,128)(2,1)S(1)} %copy-done.49), kind=kOutput, calls=%fused_computation.8 | convolution fusion | flops 2436365568 | bytes 13768704 | tf_op jit(solution)/shard_map/td,fd->tf/dot_general | solution.py:181
  201.5 4.0 convolution_convert_fusion
  205.7 7.1 %convolution_bitcast_fusion = f32[1,768,768]{2,1,0:T(8,128)} fusion(bf16[2048,768]{1,0:T(8,128)(2,1)} %constant_dynamic-update-slice_fusion, bf16[2048,768]{1,0:T(8,128)(2,1)} %get-tuple-element.71), kind=kOutput, calls=%fused_computation.62 | convolution fusion | flops 2415919104 | bytes 8650752 | tf_op jit(solution)/shard_map/td,tf->df/dot_general | solution.py:196
  212.8 4.2 convolution_bitcast_fusion.1
  216.9 47.9 %reduce-scatter.4.cloned.1.call-done = bf16[512,768]{1,0:T(8,128)(2,1)} async-done(((bf16[2048,768]{1,0:T(8,128)(2,1)}), bf16[512,768]{1,0:T(8,128)(2,1)}) %reduce-scatter.4.cloned.1.call-update) | async-done | bytes 786448 | tf_op jit(solution)/shard_map/reduce_scatter | solution.py:183
  264.8 3.1 fusion.42
  268.0 3.8 convert_reduce_fusion.5
  275.3 3.4 pad_maximum_fusion
  278.9 3.4 convolution_convert_fusion.3
  292.0 6.2 %collective-permute-done.4 = f32[3,100,64]{1,2,0:T(8,128)S(1)} collective-permute-done((f32[3,100,64]{1,2,0:T(8,128)S(1)}, f32[3,100,64]{1,2,0:T(8,128)S(1)}, u32[]{:S(2)}, u32[]{:S(2)}) %collective-permute-start.4) | collective-permute-done | bytes 76832 | tf_op jit(solution)/shard_map/ppermute | solution.py:43
  321.9 4.0 constant_dynamic-slice_fusion.1
  328.5 9.3 %collective-permute-done.12 = bf16[512,192]{0,1:T(8,128)(2,1)S(1)} collective-permute-done((bf16[512,192]{0,1:T(8,128)(2,1)S(1)}, bf16[512,192]{0,1:T(8,128)(2,1)S(1)}, u32[]{:S(2)}, u32[]{:S(2)}) %collective-permute-start.12) | collective-permute-done | bytes 196640 | tf_op jit(solution)/shard_map/ppermute | solution.py:60
  340.7 8.7 %collective-permute-done.13 = bf16[512,192]{0,1:T(8,128)(2,1)S(1)} collective-permute-done((bf16[512,192]{0,1:T(8,128)(2,1)S(1)}, bf16[512,192]{0,1:T(8,128)(2,1)S(1)}, u32[]{:S(2)}, u32[]{:S(2)}) %collective-permute-start.13) | collective-permute-done | bytes 196640 | tf_op jit(solution)/shard_map/ppermute | solution.py:60
  350.1 3.8 collective-permute-done.14
  366.0 6.6 %fusion.11 = f32[768,2304]{1,0:T(8,128)} fusion(bf16[512,768]{0,1:T(8,128)(2,1)} %bitcast.45, bf16[512,768]{0,1:T(8,128)(2,1)} %bitcast.177, bf16[512,768]{0,1:T(8,128)(2,1)S(1)} %bitcast.179, bf16[512,768]{1,0:T(8,128)(2,1)S(1)} %copy-done.7, f32[768]{0:T(1024)S(1)} %copy-done.54, f32[768]{0:T(1024)S(1)} %copy-done.41, f32[512]{0:T(512)S(1)} %copy-done.36, ...), kind=kOutput, calls=%fused_computation.36 | convolution fusion | flops 1821376512 | bytes 10233856 | tf_op jit(solution)/shard_map/td,te->de/dot_general | solution.py:291
  374.1 6.5 %convolution_convert_fusion.1 = bf16[2048,768]{1,0:T(8,128)(2,1)} fusion(bf16[2048,768]{1,0:T(8,128)(2,1)} %get-tuple-element.71, bf16[768,768]{1,0:T(8,128)(2,1)} %param.31), kind=kOutput, calls=%fused_computation.14 | convolution fusion | flops 2417491968 | bytes 7471104 | tf_op jit(solution)/shard_map/dot_general | solution.py:192
  382.0 3.7 dynamic-slice_bitcast_fusion.2
  392.7 4.1 fusion.37
  397.0 24.8 %psum.7 = f32[768,12]{0,1:T(8,128)S(1)} all-reduce(f32[768,12]{0,1:T(8,128)S(1)} %concatenate.47), channel_id=1, replica_groups=mesh['dp'=8,'mp'=4] {'dp'}, use_global_device_ids=true, to_apply=%region_24.25 | all-reduce | flops 9216 | bytes 73728 | tf_op jit(solution)/shard_map/psum | solution.py:324
  422.1 3.6 fusion.36
  427.7 13.3 %reduce-scatter.6.cloned.1.call-done = f32[96,2304]{1,0:T(8,128)} async-done(((f32[768,2304]{1,0:T(8,128)}), f32[96,2304]{1,0:T(8,128)}) %reduce-scatter.6.cloned.1.call-update) | async-done | bytes 884752 | tf_op jit(solution)/shard_map/reduce_scatter | solution.py:321
  442.5 3.4 collective-permute-start.17
  447.0 25.3 %collective-permute-done.10 = bf16[512,768]{1,0:T(8,128)(2,1)} collective-permute-done((bf16[512,768]{1,0:T(8,128)(2,1)}, bf16[512,768]{1,0:T(8,128)(2,1)}, u32[]{:S(2)}, u32[]{:S(2)}) %collective-permute-start.10) | collective-permute-done | bytes 786464 | tf_op jit(solution)/shard_map/ppermute | solution.py:43
  472.3 3.3 fusion.50
  475.6 5.8 %collective-permute-done.16 = f32[24,3084]{1,0:T(8,128)S(1)} collective-permute-done((f32[24,3084]{1,0:T(8,128)S(1)}, f32[24,3084]{1,0:T(8,128)S(1)}, u32[]{:S(2)}, u32[]{:S(2)}) %collective-permute-start.16) | collective-permute-done | bytes 296096 | tf_op jit(solution)/shard_map/ppermute | solution.py:43
  (254 shorter events, 111.5 us)
Async XLA Ops:
  7.2 112.5 %all-gather.6.cloned.1.call-start = ((), (), s32[]{:S(2)}) async-start(), calls=%async_computation.6 | async-start | bytes 1966080 | tf_op jit(solution)/shard_map/all_gather | solution.py:105
  9.8 14.8 %copy-start.29 = (f32[512]{0:T(512)}, f32[512]{0:T(512)S(1)}, u32[]{:S(2)}) copy-start(f32[512]{0:T(512)S(1)} %broadcast_multiply_fusion.5) | copy-start | bytes 6148
  10.2 14.4 %copy-start.35 = (f32[512]{0:T(512)}, f32[512]{0:T(512)S(1)}, u32[]{:S(2)}) copy-start(f32[512]{0:T(512)S(1)} %add_rsqrt_fusion.1) | copy-start | bytes 6148
  18.1 76.0 %all-to-all-start = ((bf16[512,2,4,192]{0,3,1,2:T(8,128)(2,1)}), bf16[512,2,4,192]{0,3,1,2:T(8,128)(2,1)}, u32[]{:S(2)}, u32[]{:S(2)}) async-start(bf16[512,2,4,192]{0,3,1,2:T(8,128)(2,1)} %copy.100), calls=%async_computation | async-start | bytes 3145728 | tf_op jit(solution)/shard_map/all_to_all | solution.py:134
  24.6 98.4 %all-gather.8.cloned.1.call-start = ((), (), s32[]{:S(2)}) async-start(), calls=%async_computation.7 | async-start | bytes 1966080 | tf_op jit(solution)/shard_map/all_gather | solution.py:106
  32.8 41.1 %collective-permute-start.2 = (f32[3,100,65]{1,2,0:T(8,128)}, f32[3,100,65]{1,2,0:T(8,128)}, u32[]{:S(2)}, u32[]{:S(2)}) collective-permute-start(f32[3,100,65]{1,2,0:T(8,128)} %get-tuple-element.61), channel_id=1, source_target_pairs={{0,3},{1,0},{2,1},{3,2},{4,7},{5,4},{6,5},{7,6},{8,11},{9,8},{10,9... | collective-permute-start | bytes 234008 | tf_op jit(solution)/shard_map/ppermute | solution.py:43
  36.7 55.8 %collective-permute-start.1 = (f32[3,100,65]{1,2,0:T(8,128)}, f32[3,100,65]{1,2,0:T(8,128)}, u32[]{:S(2)}, u32[]{:S(2)}) collective-permute-start(f32[3,100,65]{1,2,0:T(8,128)} %get-tuple-element.60), channel_id=1, source_target_pairs={{0,2},{1,3},{2,0},{3,1},{4,6},{5,7},{6,4},{7,5},{8,10},{9,11},{10,... | collective-permute-start | bytes 234008 | tf_op jit(solution)/shard_map/ppermute | solution.py:43
  36.7 55.8 %collective-permute-start = (f32[3,100,65]{1,2,0:T(8,128)}, f32[3,100,65]{1,2,0:T(8,128)}, u32[]{:S(2)}, u32[]{:S(2)}) collective-permute-start(f32[3,100,65]{1,2,0:T(8,128)} %get-tuple-element.59), channel_id=1, source_target_pairs={{0,1},{1,2},{2,3},{3,0},{4,5},{5,6},{6,7},{7,4},{8,9},{9,10},{10,1... | collective-permute-start | bytes 234008 | tf_op jit(solution)/shard_map/ppermute | solution.py:43
  37.8 149.6 %all-gather.4.cloned.1.call-start = ((), (), s32[]{:S(2)}) async-start(), calls=%async_computation.5 | async-start | bytes 3932160 | tf_op jit(solution)/shard_map/all_gather | solution.py:174
  97.8 17.5 %copy-start.25 = (s32[512,12]{0,1:T(8,128)S(1)}, s32[512,12]{0,1:T(8,128)}, u32[]{:S(2)}) copy-start(s32[512,12]{0,1:T(8,128)} %param.18) | copy-start | bytes 73732
  98.8 17.1 %copy-start.48 = (bf16[768,768]{1,0:T(8,128)(2,1)S(1)}, bf16[768,768]{1,0:T(8,128)(2,1)}, u32[]{:S(2)}) copy-start(bf16[768,768]{1,0:T(8,128)(2,1)} %param.25) | copy-start | bytes 3538948
  98.8 17.1 %copy-start.52 = (f32[768]{0:T(1024)S(1)}, f32[768]{0:T(1024)}, u32[]{:S(2)}) copy-start(f32[768]{0:T(1024)} %param.26) | copy-start | bytes 9220
  119.2 145.7 %reduce-scatter.4.cloned.1.call-start = ((), (), s32[]{:S(2)}) async-start(), calls=%async_computation.8 | async-start | bytes 3932160 | tf_op jit(solution)/shard_map/reduce_scatter | solution.py:183
  205.6 220.1 %reduce-scatter.8.cloned.1.call-start = ((), (), s32[]{:S(2)}) async-start(), calls=%async_computation.10 | async-start | bytes 7962624 | tf_op jit(solution)/shard_map/reduce_scatter | solution.py:227
  216.9 51.0 %copy-start.39 = (f32[768]{0:T(1024)S(1)}, f32[768]{0:T(1024)}, u32[]{:S(2)}) copy-start(f32[768]{0:T(1024)} %param.32) | copy-start | bytes 9220
  278.7 162.3 %reduce-scatter.6.cloned.1.call-start = ((), (), s32[]{:S(2)}) async-start(), calls=%async_computation.9 | async-start | bytes 7962624 | tf_op jit(solution)/shard_map/reduce_scatter | solution.py:321
  286.5 5.4 %collective-permute-start.5 = (f32[3,100,64]{1,2,0:T(8,128)S(1)}, f32[3,100,64]{1,2,0:T(8,128)S(1)}, u32[]{:S(2)}, u32[]{:S(2)}) collective-permute-start(f32[3,100,64]{1,2,0:T(8,128)S(1)} %get-tuple-element.63), channel_id=1, source_target_pairs={{0,3},{1,0},{2,1},{3,2},{4,7},{5,4},{6,5},{7,6},{8,11},{9,8},{10,9... | collective-permute-start | bytes 230408 | tf_op jit(solution)/shard_map/ppermute | solution.py:43
  288.7 9.4 %collective-permute-start.4 = (f32[3,100,64]{1,2,0:T(8,128)S(1)}, f32[3,100,64]{1,2,0:T(8,128)S(1)}, u32[]{:S(2)}, u32[]{:S(2)}) collective-permute-start(f32[3,100,64]{1,2,0:T(8,128)S(1)} %get-tuple-element.64), channel_id=1, source_target_pairs={{0,2},{1,3},{2,0},{3,1},{4,6},{5,7},{6,4},{7,5},{8,10},{9,11},{10,... | collective-permute-start | bytes 230408 | tf_op jit(solution)/shard_map/ppermute | solution.py:43
  289.0 9.1 %collective-permute-start.3 = (f32[3,100,64]{1,2,0:T(8,128)S(1)}, f32[3,100,64]{1,2,0:T(8,128)S(1)}, u32[]{:S(2)}, u32[]{:S(2)}) collective-permute-start(f32[3,100,64]{1,2,0:T(8,128)S(1)} %get-tuple-element.62), channel_id=1, source_target_pairs={{0,1},{1,2},{2,3},{3,0},{4,5},{5,6},{6,7},{7,4},{8,9},{9,10},{10,1... | collective-permute-start | bytes 230408 | tf_op jit(solution)/shard_map/ppermute | solution.py:43
  312.1 42.5 %collective-permute-start.6 = (bf16[612,192]{0,1:T(8,128)(2,1)}, bf16[612,192]{0,1:T(8,128)(2,1)}, u32[]{:S(2)}, u32[]{:S(2)}) collective-permute-start(bf16[612,192]{0,1:T(8,128)(2,1)} %get-tuple-element.47), channel_id=1, source_target_pairs={{0,1},{1,2},{2,3},{3,0},{4,5},{5,6},{6,7},{7,4},{8,9},{9,10},{10,1... | collective-permute-start | bytes 705032 | tf_op jit(solution)/shard_map/ppermute | solution.py:60
  312.2 44.0 %collective-permute-start.7 = (bf16[612,192]{0,1:T(8,128)(2,1)}, bf16[612,192]{0,1:T(8,128)(2,1)}, u32[]{:S(2)}, u32[]{:S(2)}) collective-permute-start(bf16[612,192]{0,1:T(8,128)(2,1)} %get-tuple-element.48), channel_id=1, source_target_pairs={{0,2},{1,3},{2,0},{3,1},{4,6},{5,7},{6,4},{7,5},{8,10},{9,11},{10,... | collective-permute-start | bytes 705032 | tf_op jit(solution)/shard_map/ppermute | solution.py:60
  314.5 43.4 %collective-permute-start.8 = (bf16[612,192]{0,1:T(8,128)(2,1)}, bf16[612,192]{0,1:T(8,128)(2,1)S(1)}, u32[]{:S(2)}, u32[]{:S(2)}) collective-permute-start(bf16[612,192]{0,1:T(8,128)(2,1)} %get-tuple-element.45), channel_id=1, source_target_pairs={{0,3},{1,0},{2,1},{3,2},{4,7},{5,4},{6,5},{7,6},{8,11},{9,8},{10,9... | collective-permute-start | bytes 705032 | tf_op jit(solution)/shard_map/ppermute | solution.py:60
  326.0 11.8 %collective-permute-start.12 = (bf16[512,192]{0,1:T(8,128)(2,1)S(1)}, bf16[512,192]{0,1:T(8,128)(2,1)S(1)}, u32[]{:S(2)}, u32[]{:S(2)}) collective-permute-start(bf16[512,192]{0,1:T(8,128)(2,1)S(1)} %bitcast.188), channel_id=1, source_target_pairs={{0,1},{1,2},{2,3},{3,0},{4,5},{5,6},{6,7},{7,4},{8,9},{9,10},{10,1... | collective-permute-start | bytes 589832 | tf_op jit(solution)/shard_map/ppermute | solution.py:60
  326.1 23.3 %collective-permute-start.13 = (bf16[512,192]{0,1:T(8,128)(2,1)S(1)}, bf16[512,192]{0,1:T(8,128)(2,1)S(1)}, u32[]{:S(2)}, u32[]{:S(2)}) collective-permute-start(bf16[512,192]{0,1:T(8,128)(2,1)S(1)} %bitcast.187), channel_id=1, source_target_pairs={{0,2},{1,3},{2,0},{3,1},{4,6},{5,7},{6,4},{7,5},{8,10},{9,11},{10,... | collective-permute-start | bytes 589832 | tf_op jit(solution)/shard_map/ppermute | solution.py:60
  337.8 16.1 %collective-permute-start.14 = (bf16[512,192]{0,1:T(8,128)(2,1)S(1)}, bf16[512,192]{0,1:T(8,128)(2,1)S(1)}, u32[]{:S(2)}, u32[]{:S(2)}) collective-permute-start(bf16[512,192]{0,1:T(8,128)(2,1)S(1)} %bitcast.186), channel_id=1, source_target_pairs={{0,3},{1,0},{2,1},{3,2},{4,7},{5,4},{6,5},{7,6},{8,11},{9,8},{10,9... | collective-permute-start | bytes 589832 | tf_op jit(solution)/shard_map/ppermute | solution.py:60
  385.7 60.1 %collective-permute-start.11 = (bf16[512,768]{1,0:T(8,128)(2,1)}, bf16[512,768]{1,0:T(8,128)(2,1)}, u32[]{:S(2)}, u32[]{:S(2)}) collective-permute-start(bf16[512,768]{1,0:T(8,128)(2,1)} %get-tuple-element.37), channel_id=1, source_target_pairs={{0,3},{1,0},{2,1},{3,2},{4,7},{5,4},{6,5},{7,6},{8,11},{9,8},{10,9... | collective-permute-start | bytes 2359304 | tf_op jit(solution)/shard_map/ppermute | solution.py:43
  388.7 83.6 %collective-permute-start.10 = (bf16[512,768]{1,0:T(8,128)(2,1)}, bf16[512,768]{1,0:T(8,128)(2,1)}, u32[]{:S(2)}, u32[]{:S(2)}) collective-permute-start(bf16[512,768]{1,0:T(8,128)(2,1)} %get-tuple-element.38), channel_id=1, source_target_pairs={{0,2},{1,3},{2,0},{3,1},{4,6},{5,7},{6,4},{7,5},{8,10},{9,11},{10,... | collective-permute-start | bytes 2359304 | tf_op jit(solution)/shard_map/ppermute | solution.py:43
  389.8 82.5 %collective-permute-start.9 = (bf16[512,768]{1,0:T(8,128)(2,1)}, bf16[512,768]{1,0:T(8,128)(2,1)}, u32[]{:S(2)}, u32[]{:S(2)}) collective-permute-start(bf16[512,768]{1,0:T(8,128)(2,1)} %get-tuple-element.36), channel_id=1, source_target_pairs={{0,1},{1,2},{2,3},{3,0},{4,5},{5,6},{6,7},{7,4},{8,9},{9,10},{10,1... | collective-permute-start | bytes 2359304 | tf_op jit(solution)/shard_map/ppermute | solution.py:43
  441.0 31.3 %copy-start.8 = (f32[512,768]{1,0:T(8,128)S(1)}, f32[512,768]{1,0:T(8,128)}, u32[]{:S(2)}) copy-start(f32[512,768]{1,0:T(8,128)} %get-tuple-element.39) | copy-start | bytes 4718596
  442.5 33.1 %collective-permute-start.17 = (f32[24,3084]{1,0:T(8,128)S(1)}, f32[24,3084]{1,0:T(8,128)S(1)}, u32[]{:S(2)}, u32[]{:S(2)}) collective-permute-start(f32[24,3084]{1,0:T(8,128)S(1)} %get-tuple-element.43), channel_id=1, source_target_pairs={{0,3},{1,0},{2,1},{3,2},{4,7},{5,4},{6,5},{7,6},{8,11},{9,8},{10,9... | collective-permute-start | bytes 888200 | tf_op jit(solution)/shard_map/ppermute | solution.py:43
  445.8 35.5 %collective-permute-start.16 = (f32[24,3084]{1,0:T(8,128)S(1)}, f32[24,3084]{1,0:T(8,128)S(1)}, u32[]{:S(2)}, u32[]{:S(2)}) collective-permute-start(f32[24,3084]{1,0:T(8,128)S(1)} %get-tuple-element.44), channel_id=1, source_target_pairs={{0,2},{1,3},{2,0},{3,1},{4,6},{5,7},{6,4},{7,5},{8,10},{9,11},{10,... | collective-permute-start | bytes 888200 | tf_op jit(solution)/shard_map/ppermute | solution.py:43
  445.8 35.5 %collective-permute-start.15 = (f32[24,3084]{1,0:T(8,128)S(1)}, f32[24,3084]{1,0:T(8,128)S(1)}, u32[]{:S(2)}, u32[]{:S(2)}) collective-permute-start(f32[24,3084]{1,0:T(8,128)S(1)} %get-tuple-element.42), channel_id=1, source_target_pairs={{0,1},{1,2},{2,3},{3,0},{4,5},{5,6},{6,7},{7,4},{8,9},{9,10},{10,1... | collective-permute-start | bytes 888200 | tf_op jit(solution)/shard_map/ppermute | solution.py:43
  (50 other events, 203.0 us)
Sparse Core Ops, SparseCore 0:
  9.7 67.2 all-gather.5
  78.5 44.4 all-gather.7
  125.1 62.2 all-gather.3
  205.7 59.0 reduce-scatter.3
  278.8 65.2 reduce-scatter.7
  372.8 68.1 reduce-scatter.5
